TPU v7x, 128 devices: a whole 4x4x4 slice. The times are simulated.
128 devices in a mesh: sx: 8 (over x, core), sy: 8 (over z, y_hi), dp: 2 (over y_lo).
Axes of the slice: x: 4, y: 4 (y_hi: 2, y_lo: 2; y = y_hi * 2 + y_lo), z: 4, core: 2. Of those that a mesh axis runs over, the one named last changes fastest.
Arguments:
- tokens: bfloat16 [2, 32768, 1280], P('dp', ('sx', 'sy')), may hold values from -6 to 6
- lengths: int32 [2, 256], P('dp'), may hold values from 1 to 512, 32768 in all within a row
- ln_gain: float32 [1280], replicated, may hold values from 0.1 to 1.9
- w_qkv: bfloat16 [1280, 3840], P('dp'), may hold values from -4 to 4, as said below
- w_out: bfloat16 [1280, 1280], P('dp'), may hold values from -0.15625 to 0.15625
Outputs:
- hidden: bfloat16 [2, 32768, 1280], P('dp', ('sx', 'sy'))
- pooled: float32 [2, 256, 1280], P('dp')
Inputs may be any that keep to these rules, and one draw needn't show every extreme that they name: The 256 lengths of a row sum to 32768; images are packed end to end in order. `w_qkv`: columns are queries, then keys, then values, each of 16 heads of 80 columns.
All inputs are finite; a program needn't handle non-finite values.
Results may differ from a plain program's by a relative error of at most 0.0051.
Values may be sent and summed in bfloat16 or wider, within the bound.
No kernel may reach another device: no remote copies, remote signals or barrier semaphores. Data moves between devices by JAX's collectives and lax.ppermute only.
A program may use at most 128 MiB of HBM per device.

v0:
```python
import jax
import jax.numpy as jnp
from jax import lax
from jax.sharding import PartitionSpec as P

HEADS = 16
MAXLEN = 512


def from_everyone(shard, axis):
    length = lax.axis_size(axis)
    return lax.all_to_all(
        jnp.broadcast_to(shard[None], (length, *shard.shape)), axis, 0, 0, tiled=True
    )


def laid_out(pieces, dim):
    pieces = jnp.moveaxis(pieces, 0, dim)
    dims = pieces.shape
    return pieces.reshape(*dims[:dim], dims[dim] * dims[dim + 1], *dims[dim + 2 :])


def gather_directly(shard, axis, dim):
    pieces = from_everyone(shard, axis)
    return laid_out(pieces, dim)


def side_by_side(arrays, axis, dim, along):
    both = jnp.concatenate(arrays, axis=along)
    result, at, gathered = (gather_directly(both, axis, dim), 0, [])
    for a in arrays:
        gathered.append(lax.slice_in_dim(result, at, at + a.shape[along], axis=along))
        at += a.shape[along]
    return tuple(gathered)


def with_halo(shard, sides, width):
    edges = {}
    for axis, dim in sides:
        size, length = (lax.axis_size(axis), shard.shape[dim])
        up = [(i, (i + 1) % size) for i in range(size - 1)]
        last = lax.slice_in_dim(shard, length - width, length, axis=dim)
        initial = lax.slice_in_dim(shard, 0, width, axis=dim)
        edges[dim] = (
            lax.ppermute(last, axis, up),
            lax.ppermute(initial, axis, [(b, a) for a, b in up]),
        )
    done = []
    for _, dim in sides:
        low, high = edges[dim]
        around = [(width, width) if d in done else (0, 0) for d in range(shard.ndim)]
        shard = jnp.concatenate([jnp.pad(low, around), shard, jnp.pad(high, around)], axis=dim)
        done.append(dim)
    return shard


def split_up(shard, dim, length):
    dims = shard.shape
    pieces = shard.reshape(*dims[:dim], length, dims[dim] // length, *dims[dim + 1 :])
    return jnp.moveaxis(pieces, dim, 0)


def sent_and_summed(shard, axis, dim):
    pieces = split_up(shard, dim, lax.axis_size(axis))
    arrived = lax.all_to_all(pieces, axis, split_axis=0, concat_axis=0, tiled=True)
    return arrived.sum(axis=0)


def filled_up(lines, length):
    spare = -len(lines) % length
    return jnp.pad(lines, [(0, spare)] + [(0, 0)] * (lines.ndim - 1))


def total_of(shard, axes):
    lines = shard.reshape(-1, shard.shape[-1])
    own = sent_and_summed(filled_up(lines, lax.axis_size(axes)), axes, 0)
    whole = gather_directly(own, axes, 0)
    return whole[: len(lines)].reshape(shard.shape)


def image_ids(lengths, positions, total):
    offsets = jnp.cumsum(lengths) - lengths
    counted = jnp.sum((offsets[None, :] <= positions[:, None]).astype(jnp.int32), axis=1) - 1
    inside = (positions >= 0) & (positions < total)
    return jnp.where(inside, counted, -1)


def normalize(rows, ln_gain):
    values = rows.astype(jnp.float32)
    center = values - jnp.mean(values, axis=-1, keepdims=True)
    spread = jnp.mean(center * center, axis=-1, keepdims=True)
    return (center * lax.rsqrt(spread + 1e-05) * ln_gain).astype(jnp.bfloat16)


def attend(queries, keys, values, q_ids, k_ids):
    length = queries.shape[0]
    heads = queries.shape[1]
    block = min(512, length)
    scale = queries.shape[2] ** (-0.5)

    def one_block(index):
        allowed = q_ids[:, None] == k_ids[None, :]

        def one_head(head):
            q_head = lax.dynamic_index_in_dim(queries, head, 1, keepdims=False)
            k_head = lax.dynamic_index_in_dim(keys, head, 1, keepdims=False)
            v_head = lax.dynamic_index_in_dim(values, head, 1, keepdims=False)
            scores = jnp.dot(q_head, k_head.T, preferred_element_type=jnp.float32) * scale
            scores = jnp.where(allowed, scores, -1e30)
            top = jnp.max(scores, axis=1, keepdims=True)
            weights = jnp.exp(scores - top)
            probs = (weights / jnp.sum(weights, axis=1, keepdims=True)).astype(jnp.bfloat16)
            return jnp.dot(probs, v_head, preferred_element_type=jnp.float32).astype(jnp.bfloat16)

        outcome = lax.map(one_head, jnp.arange(heads, dtype=jnp.int32))
        return jnp.transpose(outcome, (1, 0, 2))

    blocks = lax.map(one_block, jnp.arange(length // block, dtype=jnp.int32))
    return blocks.reshape(length, heads, -1)


def shards(tokens, lengths, ln_gain, w_qkv, w_out):
    qkv_full, out_full = side_by_side((w_qkv, w_out), "dp", 0, 1)
    count_rows = tokens.shape[0]
    local = tokens.shape[1]
    width = tokens.shape[2]
    size = width // HEADS
    images = lengths.shape[1]
    count_x = lax.axis_size("sx")
    count_y = lax.axis_size("sy")
    total = local * count_x * count_y
    shard = lax.axis_index("sx") * count_y + lax.axis_index("sy")
    own_positions = shard * local + jnp.arange(local, dtype=jnp.int32)
    own_list = [image_ids(lengths[0], own_positions, total)]
    normed = normalize(tokens, ln_gain)
    qkv = jnp.dot(
        normed.reshape(count_rows * local, width), qkv_full, preferred_element_type=jnp.float32
    )
    qkv = qkv.astype(jnp.bfloat16).reshape(count_rows, local, 3 * width)
    pieces = qkv.reshape(count_rows, local, 3, HEADS, size)
    keyvals = with_halo(pieces[:, :, 1:3], ((("sx", "sy"), 1),), MAXLEN)
    k_pos = shard * local - MAXLEN + jnp.arange(local + 2 * MAXLEN, dtype=jnp.int32)
    rowidx = 0
    k_ids = image_ids(lengths[rowidx], k_pos, total)
    outcomes = [
        attend(
            pieces[rowidx, :, 0],
            keyvals[rowidx, :, 0],
            keyvals[rowidx, :, 1],
            own_list[rowidx],
            k_ids,
        )
    ]
    context = jnp.stack(outcomes, axis=0).reshape(count_rows * local, width)
    mixed = jnp.dot(context, out_full, preferred_element_type=jnp.float32).reshape(
        count_rows, local, width
    )
    hidden = (tokens.astype(jnp.float32) + mixed).astype(jnp.bfloat16)
    labels = jnp.arange(images, dtype=jnp.int32)
    rowidx = 0
    onehot = (labels[:, None] == own_list[rowidx][None, :]).astype(jnp.bfloat16)
    parts_list = [jnp.dot(onehot, hidden[rowidx], preferred_element_type=jnp.float32)]
    terms = jnp.stack(parts_list, axis=0)
    sums = total_of(terms, ("sx", "sy"))
    pooled = sums / lengths.astype(jnp.float32)[:, :, None]
    return (hidden, pooled)


def solution(mesh):
    in_specs = (P("dp", ("sx", "sy"), None), P("dp", None), P(), P("dp", None), P("dp", None))
    out_specs = (P("dp", ("sx", "sy"), None), P("dp", None, None))
    return jax.shard_map(shards, mesh=mesh, in_specs=in_specs, out_specs=out_specs, check_vma=False)
```

profile of v0, /device:TPU:1, one launch (start us, length us, event | category | flops | bytes accessed | tf_op | source)
XLA Modules:
  0.0 480.5 jit_solution(12452729132204188104)
XLA Ops:
  0.6 3.7 pad_maximum_fusion.1
  4.3 5.4 %broadcast_in_dim.18 = bf16[2,640,5120]{2,1,0:T(8,128)(2,1)} broadcast(bf16[640,5120]{1,0:T(8,128)(2,1)S(1)} %pad_maximum_fusion.1), dimensions={1,2} | broadcast | bytes 19660800 | tf_op jit(solution)/shard_map/broadcast_in_dim | solution.py:13
  9.7 8.7 %all-to-all-start = ((bf16[2,640,5120]{2,1,0:T(8,128)(2,1)}), bf16[2,640,5120]{2,1,0:T(8,128)(2,1)}, u32[]{:S(2)}, u32[]{:S(2)}) async-start(bf16[2,640,5120]{2,1,0:T(8,128)(2,1)} %broadcast_in_dim.18), calls=%async_computation | async-start | bytes 26214400 | tf_op jit(solution)/shard_map/all_to_all | solution.py:12
  19.2 142.1 %all-to-all-done = bf16[2,640,5120]{2,1,0:T(8,128)(2,1)} async-done(((bf16[2,640,5120]{2,1,0:T(8,128)(2,1)}), bf16[2,640,5120]{2,1,0:T(8,128)(2,1)}, u32[]{:S(2)}, u32[]{:S(2)}) %all-to-all-start) | async-done | bytes 13107232 | tf_op jit(solution)/shard_map/all_to_all | solution.py:12
  161.3 10.8 %fusion.18 = bf16[512,3840]{1,0:T(8,128)(2,1)} fusion(bf16[1280,5120]{1,0:T(8,128)(2,1)} %bitcast.1, bf16[1,512,1280]{2,1,0:T(8,128)(2,1)S(1)} %copy-done, f32[1280]{0:T(1024)S(1)} %copy-done.4, f32[512]{0:T(512)S(1)} %add_rsqrt_fusion, f32[512]{0:T(512)S(1)} %broadcast_multiply_fusion), kind=kOutput, calls=%fused_computation.22 | convolution fusion | flops 5038407680 | bytes 15082496 | tf_op jit(solution)/shard_map/dot_general | solution.py:136
  172.1 6.2 %copy.12 = bf16[512,3840]{0,1:T(8,128)(2,1)} copy(bf16[512,3840]{1,0:T(8,128)(2,1)} %fusion.18) | data formatting | bytes 7864320 | tf_op jit(solution)/shard_map/convert_element_type | solution.py:139
  178.3 1.9 slice.35
  180.3 10.0 %collective-permute-start.1 = (bf16[1,512,2,16,80]{1,4,3,2,0:T(8,128)(2,1)S(1)}, bf16[1,512,2,16,80]{1,4,3,2,0:T(8,128)(2,1)}, u32[]{:S(2)}, u32[]{:S(2)}) collective-permute-start(bf16[1,512,2,16,80]{1,4,3,2,0:T(8,128)(2,1)S(1)} %slice.35), channel_id=1, source_target_pairs={{2,0},{4,2},{6,4},{8,6},{10,8},{12,10},{14,12},{16,14},{18,16},{20... | collective-permute-start | bytes 7864328 | tf_op jit(solution)/shard_map/ppermute | solution.py:46
  190.3 1.9 collective-permute-start
  193.6 2.5 slice_bitcast_fusion.2
  196.1 78.1 %collective-permute-done.1 = bf16[1,512,2,16,80]{1,4,3,2,0:T(8,128)(2,1)} collective-permute-done((bf16[1,512,2,16,80]{1,4,3,2,0:T(8,128)(2,1)S(1)}, bf16[1,512,2,16,80]{1,4,3,2,0:T(8,128)(2,1)}, u32[]{:S(2)}, u32[]{:S(2)}) %collective-permute-start.1) | collective-permute-done | bytes 2621472 | tf_op jit(solution)/shard_map/ppermute | solution.py:46
  274.2 28.1 %collective-permute-done = bf16[1,512,2,16,80]{1,4,3,2,0:T(8,128)(2,1)} collective-permute-done((bf16[1,512,2,16,80]{1,4,3,2,0:T(8,128)(2,1)S(1)}, bf16[1,512,2,16,80]{1,4,3,2,0:T(8,128)(2,1)}, u32[]{:S(2)}, u32[]{:S(2)}) %collective-permute-start) | collective-permute-done | bytes 2621472 | tf_op jit(solution)/shard_map/ppermute | solution.py:45
  302.3 3.4 pad_maximum_fusion
  305.7 3.4 slice_bitcast_fusion
  309.1 106.8 %while.18 = (s32[]{:T(128)}, bf16[16,512,80]{1,2,0:T(8,128)(2,1)S(1)}, s32[16]{0:T(128)S(1)}, bf16[512,16,80]{0,2,1:T(8,128)(2,1)}, bf16[1536,16,80]{0,2,1:T(8,1...) while((s32[]{:T(128)}, ...), condition=%wide.region_9.10_spmd.clone, body=%wide.region_6.9_spmd.clone.sunk | while | flops 258776064 | bytes 10112171 | solution.py:115
  327.3 1.8 fusion.56
  334.0 1.8 fusion.56
  354.0 1.8 fusion.56
  360.7 1.8 fusion.56
  380.8 1.8 fusion.56
  387.4 1.8 fusion.56
  416.0 3.8 fusion.30
  421.2 31.1 %all_to_all.15 = f32[64,4,1280]{2,1,0:T(4,128)S(1)} all-to-all(f32[64,4,1280]{2,1,0:T(4,128)S(1)} %copy.13), channel_id=1, replica_groups=mesh['sx'=8,'sy'=8,'dp'=2] {'sx','sy'}, dimensions={0} | all-to-all | bytes 2621440 | tf_op jit(solution)/shard_map/all_to_all | solution.py:65
  452.7 26.1 %all_to_all.16 = f32[64,4,1280]{2,1,0:T(4,128)S(1)} all-to-all(f32[64,4,1280]{2,1,0:T(4,128)S(1)} %broadcast_in_dim.20), channel_id=1, replica_groups=mesh['sx'=8,'sy'=8,'dp'=2] {'sx','sy'}, dimensions={0} | all-to-all | bytes 2621440 | tf_op jit(solution)/shard_map/all_to_all | solution.py:12
  (95 shorter events, 70.3 us)
Async XLA Ops:
  9.7 8.7 %copy-start = (bf16[1,512,1280]{2,1,0:T(8,128)(2,1)S(1)}, bf16[1,512,1280]{2,1,0:T(8,128)(2,1)}, u32[]{:S(2)}) copy-start(bf16[1,512,1280]{2,1,0:T(8,128)(2,1)} %param.7) | copy-start | bytes 3932164
  9.7 151.5 %all-to-all-start = ((bf16[2,640,5120]{2,1,0:T(8,128)(2,1)}), bf16[2,640,5120]{2,1,0:T(8,128)(2,1)}, u32[]{:S(2)}, u32[]{:S(2)}) async-start(bf16[2,640,5120]{2,1,0:T(8,128)(2,1)} %broadcast_in_dim.18), calls=%async_computation | async-start | bytes 26214400 | tf_op jit(solution)/shard_map/all_to_all | solution.py:12
  18.4 142.8 %copy-start.4 = (f32[1280]{0:T(1024)S(1)}, f32[1280]{0:T(1024)}, u32[]{:S(2)}) copy-start(f32[1280]{0:T(1024)} %param.9) | copy-start | bytes 15364
  178.3 13.9 %copy-start.3 = (s32[1,256]{1,0:T(1,128)S(1)}, s32[1,256]{1,0:T(1,128)}, u32[]{:S(2)}) copy-start(s32[1,256]{1,0:T(1,128)} %param.8) | copy-start | bytes 3076
  180.3 93.9 %collective-permute-start.1 = (bf16[1,512,2,16,80]{1,4,3,2,0:T(8,128)(2,1)S(1)}, bf16[1,512,2,16,80]{1,4,3,2,0:T(8,128)(2,1)}, u32[]{:S(2)}, u32[]{:S(2)}) collective-permute-start(bf16[1,512,2,16,80]{1,4,3,2,0:T(8,128)(2,1)S(1)} %slice.35), channel_id=1, source_target_pairs={{2,0},{4,2},{6,4},{8,6},{10,8},{12,10},{14,12},{16,14},{18,16},{20... | collective-permute-start | bytes 7864328 | tf_op jit(solution)/shard_map/ppermute | solution.py:46
  190.3 112.0 %collective-permute-start = (bf16[1,512,2,16,80]{1,4,3,2,0:T(8,128)(2,1)S(1)}, bf16[1,512,2,16,80]{1,4,3,2,0:T(8,128)(2,1)}, u32[]{:S(2)}, u32[]{:S(2)}) collective-permute-start(bf16[1,512,2,16,80]{1,4,3,2,0:T(8,128)(2,1)S(1)} %slice.35), channel_id=1, source_target_pairs={{0,2},{2,4},{4,6},{6,8},{8,10},{10,12},{12,14},{14,16},{16,18},{18... | collective-permute-start | bytes 7864328 | tf_op jit(solution)/shard_map/ppermute | solution.py:45
  305.7 3.4 copy-start.5
  309.1 106.9 %copy-start.1 = (bf16[1,512,1280]{2,1,0:T(8,128)(2,1)S(1)}, bf16[1,512,1280]{2,1,0:T(8,128)(2,1)}, u32[]{:S(2)}) copy-start(bf16[1,512,1280]{2,1,0:T(8,128)(2,1)} %param.7) | copy-start | bytes 3932164
  419.8 1.4 copy-start.2
where the time goes:
time: 482 us; the launch traced here: 480 us
  waiting for transfers between devices  248 us (51%)
  matrix products  72.2 us (15%)
  blocking collectives  57.2 us (12%)
  loops' own time  31.3 us (6%)
  local copies, waits for them, and re-layouts  30.5 us (6%)
  starting transfers between devices  20.6 us (4%)
  other arithmetic  19.6 us (4%)
    all_to_all x1, waiting for transfers between devices, from_everyone(): lax.all_to_all(jnp.broadcast_to(shard[None], (length, *shard.shape)), axi...  142 us
    ppermute x1, waiting for transfers between devices, with_halo(): lax.ppermute(initial, axis, [(b, a) for a, b in up])  78.1 us
    another operation x1, loops' own time, one_block(): outcome = lax.map(one_head, jnp.arange(heads, dtype=jnp.int32))  31.3 us
    all_to_all x1, blocking collectives, sent_and_summed(): lax.all_to_all(pieces, axis, split_axis=0, concat_axis=0, tiled=True)  31.1 us
    dot_general x16, matrix products, one_head(): jnp.dot(probs, v_head, preferred_element_type=jnp.float32)  28.8 us
    dot_general x16, matrix products, one_head(): jnp.dot(q_head, k_head.T, preferred_element_type=jnp.float32) * scale  28.1 us
    ppermute x1, waiting for transfers between devices, with_halo(): lax.ppermute(last, axis, up)  28.1 us
    all_to_all x1, blocking collectives, from_everyone(): lax.all_to_all(jnp.broadcast_to(shard[None], (length, *shard.shape)), axi...  26.1 us
  transfers between devices with their start and end apart: 3, of which 3 were waited for; matrix products, arithmetic and copies ran while one was open for 1% of the time, Pallas kernels for 0%

commit v1 on v0

v1 whole, which is shorter than its diff:
```python
import itertools

import jax
import jax.numpy as jnp
from jax import lax
from jax.experimental import pallas as pl
from jax.experimental.pallas import tpu as pltpu
from jax.sharding import Mesh
from jax.sharding import PartitionSpec as P

HEADS = 16
SIZE = 80
D = HEADS * SIZE
LOCAL = 512
WIN = 2 * LOCAL
PAD = WIN + 256
QB = 256
IMAGES = 256
WIDTHS = (256, 384, 512, 640, 768, 896, 1024)
HALF = D // 2
KR = 160
CG = 640
TOKEN_AXES = ("x", "co", "z", "yh")
ALL_AXES = TOKEN_AXES + ("dp",)
LOG2E = 1.4426950408889634


def permutation(move):
    def index(x, co, z, y):
        return ((x * 2 + co) * 8 + (z * 2 + y // 2)) * 2 + y % 2

    places = itertools.product(range(4), range(2), range(4), range(4))
    return [(index(*place), index(*move(*place))) for place in places]


Y_UP = permutation(lambda x, co, z, y: (x, co, z, (y + 1) % 4))
Y_DOWN = permutation(lambda x, co, z, y: (x, co, z, (y - 1) % 4))
X_UP = permutation(lambda x, co, z, y: ((x + 1) % 4, co, z, y))
X_DOWN = permutation(lambda x, co, z, y: ((x - 1) % 4, co, z, y))
Z_UP = permutation(lambda x, co, z, y: (x, co, (z + 1) % 4, y))
Z_DOWN = permutation(lambda x, co, z, y: (x, co, (z - 1) % 4, y))
CORE = permutation(lambda x, co, z, y: (x, 1 - co, z, y))


def moved(piece, pairs):
    return lax.ppermute(piece, ALL_AXES, pairs)


def first_pieces(w_qkv, w_out):
    x, co, z = (lax.axis_index(a) for a in ("x", "co", "z"))
    pieces = []
    for side in range(2):
        a = lax.dynamic_slice(w_qkv, (x * KR, (co * 2 + side) * CG), (KR, CG))
        b = lax.dynamic_slice(w_qkv, (z * KR, (4 + side) * CG), (KR, CG))
        c = lax.dynamic_slice(w_out, (z * KR, side * CG), (KR, CG))
        pieces.append(jnp.stack([a, jnp.where(co == 0, b, c)]))
    return pieces


def attention_kernel(
    place_ref, ends_ref, own_ref, prev_ref, gain_ref, wqkv_ref, wout_ref, mine_ref, other_ref,
    spans_ref, image_ref, lens_ref,
    hprev_ref, hown_ref, pooled_ref,
    x_ref, w_ref, wo_ref, q_ref, k_ref, vt_ref, ctx_ref, bias_ref, hid_ref, sem,
):
    x, z, co, dp = (place_ref[i] for i in range(4))
    lo = ends_ref[0, LOCAL]
    hi = jnp.where(ends_ref[1, WIN - 1] == WIN, WIN, ends_ref[0, WIN - 1])
    base = (lo // 128) * 128
    blocks = (hi - base + QB - 1) // QB

    copies = [
        pltpu.make_async_copy(prev_ref, x_ref.at[pl.ds(0, LOCAL)], sem.at[0]),
        pltpu.make_async_copy(own_ref, x_ref.at[pl.ds(LOCAL, LOCAL)], sem.at[0]),
        pltpu.make_async_copy(wqkv_ref, w_ref.at[pl.ds(dp * HALF, HALF)], sem.at[1]),
        pltpu.make_async_copy(wout_ref, wo_ref.at[pl.ds(dp * HALF, HALF)], sem.at[1]),
    ]
    far = (1 - dp) * HALF
    order = (
        [(0, x, 0), (0, x, 1), (1, z, 0), (1, z, 1)]
        + [(0, (x + 3) % 4, 0), (0, (x + 3) % 4, 1), (0, (x + 1) % 4, 0), (0, (x + 1) % 4, 1)]
        + [(1, (z + 3) % 4, 0), (1, (z + 3) % 4, 1), (1, (z + 1) % 4, 0), (1, (z + 1) % 4, 1)]
        + [(0, (x + 2) % 4, 0), (0, (x + 2) % 4, 1), (1, (z + 2) % 4, 0), (1, (z + 2) % 4, 1)]
    )
    for c in copies:
        c.start()
    for source, core in ((mine_ref, co), (other_ref, 1 - co)):
        for slot, (part, row, side) in enumerate(order):
            rows = pl.ds(pl.multiple_of(far + row * KR, 16), KR)
            if part == 0:
                cols = pl.ds(pl.multiple_of((core * 2 + side) * CG, 128), CG)
                pltpu.make_async_copy(source.at[slot], w_ref.at[rows, cols], sem.at[1]).start()
            else:

                @pl.when(core == 0)
                def _(source=source, slot=slot, rows=rows, side=side):
                    cols = pl.ds((4 + side) * CG, CG)
                    pltpu.make_async_copy(source.at[slot], w_ref.at[rows, cols], sem.at[1]).start()

                @pl.when(core == 1)
                def _(source=source, slot=slot, rows=rows, side=side):
                    cols = pl.ds(side * CG, CG)
                    pltpu.make_async_copy(source.at[slot], wo_ref.at[rows, cols], sem.at[1]).start()

    x_ref[WIN:, :] = jnp.zeros((PAD - WIN, D), jnp.bfloat16)
    k_ref[...] = jnp.zeros_like(k_ref)
    vt_ref[...] = jnp.zeros_like(vt_ref)
    hid_ref[...] = jnp.zeros_like(hid_ref)
    copies[0].wait()
    copies[1].wait()
    copies[2].wait()
    copies[3].wait()
    for source in (mine_ref, other_ref):
        for slot in range(16):
            pltpu.make_async_copy(
                source.at[slot], w_ref.at[pl.ds(0, KR), pl.ds(0, CG)], sem.at[1]
            ).wait()

    def project(j, carry):
        row0 = pl.multiple_of(base + j * QB, 128)
        rows = pl.ds(row0, QB)
        values = x_ref[rows, :].astype(jnp.float32)
        center = values - jnp.mean(values, axis=1, keepdims=True)
        spread = jnp.mean(center * center, axis=1, keepdims=True)
        normed = (center * lax.rsqrt(spread + 1e-05) * gain_ref[...]).astype(jnp.bfloat16)
        q = jnp.dot(normed, w_ref[:, 0:D], preferred_element_type=jnp.float32)
        q_ref[rows, :] = (q * (LOG2E * SIZE**-0.5)).astype(jnp.bfloat16)
        k = jnp.dot(normed, w_ref[:, D : 2 * D], preferred_element_type=jnp.float32)
        k_ref[rows, :] = k.astype(jnp.bfloat16)
        v = jnp.dot(normed, w_ref[:, 2 * D : 3 * D], preferred_element_type=jnp.float32)
        vt_ref[:, rows] = v.T.astype(jnp.bfloat16)
        return carry

    lax.fori_loop(0, blocks, project, 0)

    def attend(j, carry):
        row0 = pl.multiple_of(base + j * QB, 128)
        rows = pl.ds(row0, QB)
        least = ends_ref[0, jnp.maximum(row0, lo)]
        most = ends_ref[1, jnp.minimum(row0 + QB, hi) - 1]
        k0 = pl.multiple_of((least // 128) * 128, 128)
        need = most - k0
        start = spans_ref[0:1, rows]
        end = spans_ref[1:2, rows]
        for i, width in enumerate(WIDTHS):
            above = WIDTHS[i - 1] if i else 0

            @pl.when((need > above) & (need <= width))
            def _(width=width):
                keys = pl.ds(k0, width)
                at = lax.broadcasted_iota(jnp.int32, (width, QB), 0) + k0
                bias_ref[0:width, :] = jnp.where((at >= start) & (at < end), 0.0, -1e30)

                def one_head(h, inner):
                    w0 = pl.multiple_of(jnp.minimum((h * SIZE) // 128 * 128, D - 256), 128)
                    window = pl.ds(w0, 256)
                    lane = lax.broadcasted_iota(jnp.int32, (QB, 256), 1) + (w0 - h * SIZE)
                    q = jnp.where((lane >= 0) & (lane < SIZE), q_ref[rows, window], 0)
                    s = lax.dot_general(
                        k_ref[keys, window], q.astype(jnp.bfloat16), (((1,), (1,)), ((), ())),
                        preferred_element_type=jnp.float32,
                    )
                    s = s + bias_ref[0:width, :]
                    top = jnp.max(s, axis=0, keepdims=True)
                    p = jnp.exp2(s - top)
                    total = jnp.sum(p, axis=0, keepdims=True)
                    features = pl.ds(pl.multiple_of(h * SIZE, 16), SIZE)
                    c = jnp.dot(
                        vt_ref[features, keys], p.astype(jnp.bfloat16),
                        preferred_element_type=jnp.float32,
                    )
                    ctx_ref[features, :] = (c * (1.0 / total)).astype(jnp.bfloat16)
                    return inner

                lax.fori_loop(0, HEADS, one_head, 0, unroll=2)

        mixed = lax.dot_general(
            ctx_ref[...], wo_ref[...], (((0,), (0,)), ((), ())),
            preferred_element_type=jnp.float32,
        )
        hidden = x_ref[rows, :].astype(jnp.float32) + mixed
        at = lax.broadcasted_iota(jnp.int32, (QB, D), 0) + row0
        hidden = jnp.where((at >= lo) & (at < hi), hidden, 0.0)
        hid_ref[rows, :] = hidden.astype(jnp.bfloat16)
        return carry

    lax.fori_loop(0, blocks, attend, 0)

    hprev_ref[...] = hid_ref[0:LOCAL, :]
    hown_ref[...] = hid_ref[LOCAL:WIN, :]
    label = lax.broadcasted_iota(jnp.int32, (IMAGES, WIN), 0)
    at = lax.broadcasted_iota(jnp.int32, (IMAGES, WIN), 1)
    member = (label == image_ref[...]) & (at >= lo) & (at < hi)
    sums = jnp.dot(
        jnp.where(member, 1.0, 0.0).astype(jnp.bfloat16), hid_ref[0:WIN, :],
        preferred_element_type=jnp.float32,
    )
    pooled_ref[...] = (sums / lens_ref[...]).astype(jnp.bfloat16)


def attention(place, spans, image, lens, own, prev, gain, w_qkv, w_out, mine, other):
    hbm = pl.BlockSpec(memory_space=pltpu.HBM)
    vmem = pl.BlockSpec(memory_space=pltpu.VMEM)
    smem = pl.BlockSpec(memory_space=pltpu.SMEM)
    return pl.pallas_call(
        attention_kernel,
        out_shape=(
            jax.ShapeDtypeStruct((LOCAL, D), jnp.bfloat16),
            jax.ShapeDtypeStruct((LOCAL, D), jnp.bfloat16),
            jax.ShapeDtypeStruct((IMAGES, D), jnp.bfloat16),
        ),
        in_specs=[smem, smem, hbm, hbm, vmem, hbm, hbm, hbm, hbm, vmem, vmem, vmem],
        out_specs=(vmem, vmem, vmem),
        scratch_shapes=[
            pltpu.VMEM((PAD, D), jnp.bfloat16),
            pltpu.VMEM((D, 3 * D), jnp.bfloat16),
            pltpu.VMEM((D, D), jnp.bfloat16),
            pltpu.VMEM((PAD, D), jnp.bfloat16),
            pltpu.VMEM((PAD, D), jnp.bfloat16),
            pltpu.VMEM((D, PAD), jnp.bfloat16),
            pltpu.VMEM((D, QB), jnp.bfloat16),
            pltpu.VMEM((WIDTHS[-1], QB), jnp.float32),
            pltpu.VMEM((PAD, D), jnp.bfloat16),
            pltpu.SemaphoreType.DMA((2,)),
        ],
        compiler_params=pltpu.CompilerParams(vmem_limit_bytes=60 * 2**20),
        cost_estimate=pl.CostEstimate(
            flops=30_000_000_000, bytes_accessed=20_000_000, transcendentals=10_000_000
        ),
        name="attention",
    )(place, spans, own, prev, gain, w_qkv, w_out, mine, other, spans, image, lens)


def shards(tokens, lengths, ln_gain, w_qkv, w_out):
    x, co, z, yh, dp = (lax.axis_index(a) for a in ALL_AXES)
    shard = (x * 2 + co) * 8 + z * 2 + yh
    own = tokens[0]

    p0, p1 = first_pieces(w_qkv, w_out)
    r0 = moved(p0, Y_UP)
    r1 = moved(p1, Y_DOWN)
    a0 = jnp.stack([r0[0], r1[0]])
    b0 = jnp.stack([r0[1], r1[1]])
    sent, a0, b0 = lax.optimization_barrier((own, a0, b0))
    prev = lax.ppermute(sent, TOKEN_AXES, [(i, i + 1) for i in range(63)])
    a1, a2 = moved(a0, X_UP), moved(a0, X_DOWN)
    b1, b2 = moved(b0, Z_UP), moved(b0, Z_DOWN)
    a3, a4 = moved(a1[0], X_UP), moved(a2[1], X_DOWN)
    b3, b4 = moved(b1[0], Z_UP), moved(b2[1], Z_DOWN)
    mine = jnp.concatenate(
        [a0, b0, a1, a2, b1, b2, a3[None], a4[None], b3[None], b4[None]], axis=0
    )
    other = moved(mine, CORE)

    lens = lengths[0]
    ends = jnp.cumsum(lens)
    offsets = ends - lens
    first = (shard - 1) * LOCAL
    at = first + jnp.arange(PAD, dtype=jnp.int32)
    begun = offsets[:, None] <= at[None, :]
    image = jnp.sum(begun.astype(jnp.int32), axis=0) - 1
    start = jnp.max(jnp.where(begun, offsets[:, None], -WIN), axis=0) - first
    end = jnp.min(jnp.where(ends[:, None] > at[None, :], ends[:, None], 1 << 20), axis=0) - first
    spans = jnp.stack([start, end]).astype(jnp.int32)
    place = jnp.stack([x, z, co, dp]).astype(jnp.int32)

    hprev, hown, part = attention(
        place, spans, image[None, :WIN], lens.astype(jnp.float32)[:, None], own, prev,
        ln_gain[None], w_qkv, w_out, mine, other,
    )
    back = lax.ppermute(hprev, TOKEN_AXES, [(i + 1, i) for i in range(63)])

    swap = [(0, 1), (1, 0)]
    group = ("x", "z", "yh")
    part = part.reshape(2, IMAGES // 2, D)
    kept = lax.dynamic_index_in_dim(part, co, 0, keepdims=False)
    given = lax.dynamic_index_in_dim(part, 1 - co, 0, keepdims=False)
    kept = kept.astype(jnp.float32) + lax.ppermute(given, "co", swap).astype(jnp.float32)
    kept = kept.astype(jnp.bfloat16).reshape(32, 4, D)
    rows = lax.all_to_all(kept, group, 0, 0, tiled=True).astype(jnp.float32)
    rows = jnp.sum(rows, axis=0).astype(jnp.bfloat16)
    half = lax.all_to_all(jnp.broadcast_to(rows[None], (32, 4, D)), group, 0, 0, tiled=True)
    half = half.reshape(IMAGES // 2, D)
    rest = lax.ppermute(half, "co", swap)
    pooled = jnp.where(co == 0, jnp.stack([half, rest]), jnp.stack([rest, half]))
    pooled = pooled.reshape(1, IMAGES, D).astype(jnp.float32)

    limit = jnp.where(end[WIN - 1] == WIN, WIN, start[WIN - 1]) - LOCAL
    here = jnp.arange(LOCAL, dtype=jnp.int32)[:, None] < limit
    hidden = jnp.where(here, hown, back)[None]
    return hidden, pooled


def solution(mesh):
    fine = Mesh(mesh.devices.reshape(4, 2, 4, 2, 2), ALL_AXES)
    in_specs = (P("dp", TOKEN_AXES, None), P("dp", None), P(), P("dp", None), P("dp", None))
    out_specs = (P("dp", TOKEN_AXES, None), P("dp", None, None))
    return jax.shard_map(
        shards, mesh=fine, in_specs=in_specs, out_specs=out_specs, check_vma=False
    )
```

time: 482 us -> 205 us (0.43)
  waiting for transfers between devices: 248 us -> 66.1 us
  matrix products: 72.2 us -> 0 us
  Pallas kernels: 0 us -> 59.3 us
  blocking collectives: 57.2 us -> 22.8 us
  loops' own time: 31.3 us -> 0 us
  local copies, waits for them, and re-layouts: 30.5 us -> 6.2 us
  starting transfers between devices: 20.6 us -> 39.2 us
  other arithmetic: 19.6 us -> 9.21 us
    all_to_all x1, waiting for transfers between devices: 142 us -> 1.27 us  [shards(): lax.all_to_all(jnp.broadcast_to(rows[None], (32, 4, D)), group, 0, 0, til...]
    dot_general x35 -> x0, matrix products: 72.2 us -> none  [the longest x16 28.8 us: one_head(): jnp.dot(probs, v_head, preferred_element_type=jnp.float32)]
    pallas_call x0 -> x1, Pallas kernels: none -> 59.3 us  [attention(): pl.pallas_call(attention_kernel, out_shape=(jax.ShapeDtypeStruct((LOCAL,...]
    ppermute x2 -> x15, waiting for transfers between devices: 106 us -> 64.9 us  [the longest x1 24.7 us: shards(): prev = lax.ppermute(sent, TOKEN_AXES, [(i, i + 1) for i in range(63)])]
    all_to_all x2 -> x1, blocking collectives: 57.2 us -> 22.8 us  [shards(): rows = lax.all_to_all(kept, group, 0, 0, tiled=True).astype(jnp.float32)]
    another operation x1 -> x0, loops' own time: 31.3 us -> none  [one_block(): outcome = lax.map(one_head, jnp.arange(heads, dtype=jnp.int32))]
    ppermute x2 -> x15, starting transfers between devices: 11.9 us -> 35.3 us  [the longest x11 21.9 us: moved(): return lax.ppermute(piece, ALL_AXES, pairs)]
    reduce_sum x21 -> x2, other arithmetic: 10.8 us -> 0.68 us  [the longest x1 0.53 us: shards(): image = jnp.sum(begun.astype(jnp.int32), axis=0) - 1]
  transfers between devices with their start and end apart: 3 -> 16, of which waited for: 3 -> 9; matrix products, arithmetic and copies ran while one was open for 1% -> 5% of each run, Pallas kernels for 0% -> 0%
where the time goes in v1:
time: 205 us
  waiting for transfers between devices  66.1 us (32%)
  Pallas kernels  59.3 us (29%)
  starting transfers between devices  39.2 us (19%)
  blocking collectives  22.8 us (11%)
  other arithmetic  9.21 us (4%)
  local copies, waits for them, and re-layouts  6.2 us (3%)
  between operations  2.29 us (1%)
    pallas_call x1, Pallas kernels, attention(): pl.pallas_call(attention_kernel, out_shape=(jax.ShapeDtypeStruct((LOCAL,...  59.3 us
    ppermute x1, waiting for transfers between devices, shards(): prev = lax.ppermute(sent, TOKEN_AXES, [(i, i + 1) for i in range(63)])  24.7 us
    all_to_all x1, blocking collectives, shards(): rows = lax.all_to_all(kept, group, 0, 0, tiled=True).astype(jnp.float32)  22.8 us
    ppermute x11, starting transfers between devices, moved(): return lax.ppermute(piece, ALL_AXES, pairs)  21.9 us
    ppermute x11, waiting for transfers between devices, moved(): return lax.ppermute(piece, ALL_AXES, pairs)  19.9 us
    ppermute x1, waiting for transfers between devices, shards(): back = lax.ppermute(hprev, TOKEN_AXES, [(i + 1, i) for i in range(63)])  18.7 us
    ppermute x1, starting transfers between devices, shards(): back = lax.ppermute(hprev, TOKEN_AXES, [(i + 1, i) for i in range(63)])  8.58 us
  transfers between devices with their start and end apart: 16, of which 9 were waited for; matrix products, arithmetic and copies ran while one was open for 5% of the time, Pallas kernels for 0%

profile of v1, /device:TPU:1, one launch (start us, length us, event | category | flops | bytes accessed | tf_op | source)
XLA Modules:
  0.0 205.1 jit_solution(10406417709913224100)
XLA Ops:
  0.6 1.5 dynamic-slice_bitcast_fusion.2
  2.2 3.6 %collective-permute-start.1 = (bf16[2,160,640]{2,1,0:T(8,128)(2,1)S(1)}, bf16[2,160,640]{2,1,0:T(8,128)(2,1)S(1)}, u32[]{:S(2)}, u32[]{:S(2)}) collective-permute-start(bf16[2,160,640]{2,1,0:T(8,128)(2,1)S(1)} %pad_maximum_fusion.1), channel_id=1, source_target_pairs={{0,3},{1,0},{2,1},{3,2},{4,7},{5,4},{6,5},{7,6},{8,11},{9,8},{10,9... | collective-permute-start | bytes 1228808 | tf_op jit(solution)/shard_map/ppermute | solution.py:46
  5.9 8.0 %collective-permute-done.1 = bf16[2,160,640]{2,1,0:T(8,128)(2,1)S(1)} collective-permute-done((bf16[2,160,640]{2,1,0:T(8,128)(2,1)S(1)}, bf16[2,160,640]{2,1,0:T(8,128)(2,1)S(1)}, u32[]{:S(2)}, u32[]{:S(2)}) %collective-permute-start.1) | collective-permute-done | bytes 409632 | tf_op jit(solution)/shard_map/ppermute | solution.py:46
  14.0 3.2 %collective-permute-done = bf16[2,160,640]{2,1,0:T(8,128)(2,1)S(1)} collective-permute-done((bf16[2,160,640]{2,1,0:T(8,128)(2,1)S(1)}, bf16[2,160,640]{2,1,0:T(8,128)(2,1)S(1)}, u32[]{:S(2)}, u32[]{:S(2)}) %collective-permute-start) | collective-permute-done | bytes 409632 | tf_op jit(solution)/shard_map/ppermute | solution.py:46
  17.3 2.5 %collective-permute-start.4 = (bf16[2,160,640]{2,1,0:T(8,128)(2,1)S(1)}, bf16[2,160,640]{2,1,0:T(8,128)(2,1)S(1)}, u32[]{:S(2)}, u32[]{:S(2)}) collective-permute-start(bf16[2,160,640]{2,1,0:T(8,128)(2,1)S(1)} %get-tuple-element.9), channel_id=1, source_target_pairs={{0,96},{1,97},{2,98},{3,99},{4,100},{5,101},{6,102},{7,103},{8,104... | collective-permute-start | bytes 1228808 | tf_op jit(solution)/shard_map/ppermute | solution.py:46
  19.9 3.8 %collective-permute-start.6 = (bf16[2,160,640]{2,1,0:T(8,128)(2,1)S(1)}, bf16[2,160,640]{2,1,0:T(8,128)(2,1)S(1)}, u32[]{:S(2)}, u32[]{:S(2)}) collective-permute-start(bf16[2,160,640]{2,1,0:T(8,128)(2,1)S(1)} %get-tuple-element.10), channel_id=1, source_target_pairs={{0,12},{1,13},{2,14},{3,15},{4,0},{5,1},{6,2},{7,3},{8,4},{9,5},{1... | collective-permute-start | bytes 1228808 | tf_op jit(solution)/shard_map/ppermute | solution.py:46
  23.8 3.1 %collective-permute-done.4 = bf16[2,160,640]{2,1,0:T(8,128)(2,1)S(1)} collective-permute-done((bf16[2,160,640]{2,1,0:T(8,128)(2,1)S(1)}, bf16[2,160,640]{2,1,0:T(8,128)(2,1)S(1)}, u32[]{:S(2)}, u32[]{:S(2)}) %collective-permute-start.4) | collective-permute-done | bytes 409632 | tf_op jit(solution)/shard_map/ppermute | solution.py:46
  26.9 3.5 %collective-permute-start.8 = (bf16[160,640]{1,0:T(8,128)(2,1)S(1)}, bf16[160,640]{1,0:T(8,128)(2,1)S(1)}, u32[]{:S(2)}, u32[]{:S(2)}) collective-permute-start(bf16[160,640]{1,0:T(8,128)(2,1)S(1)} %slice_bitcast_fusion.2), channel_id=1, source_target_pairs={{0,96},{1,97},{2,98},{3,99},{4,100},{5,101},{6,102},{7,103},{8,104... | collective-permute-start | bytes 614408 | tf_op jit(solution)/shard_map/ppermute | solution.py:46
  30.6 3.8 %collective-permute-start.10 = (bf16[160,640]{1,0:T(8,128)(2,1)S(1)}, bf16[160,640]{1,0:T(8,128)(2,1)S(1)}, u32[]{:S(2)}, u32[]{:S(2)}) collective-permute-start(bf16[160,640]{1,0:T(8,128)(2,1)S(1)} %slice_bitcast_fusion), channel_id=1, source_target_pairs={{0,12},{1,13},{2,14},{3,15},{4,0},{5,1},{6,2},{7,3},{8,4},{9,5},{1... | collective-permute-start | bytes 614408 | tf_op jit(solution)/shard_map/ppermute | solution.py:46
  34.7 1.6 collective-permute-done.7
  36.4 3.9 %collective-permute-done.9 = bf16[160,640]{1,0:T(8,128)(2,1)S(1)} collective-permute-done((bf16[160,640]{1,0:T(8,128)(2,1)S(1)}, bf16[160,640]{1,0:T(8,128)(2,1)S(1)}, u32[]{:S(2)}, u32[]{:S(2)}) %collective-permute-start.9) | collective-permute-done | bytes 204832 | tf_op jit(solution)/shard_map/ppermute | solution.py:46
  40.4 4.5 %collective-permute-start.11 = (bf16[16,160,640]{2,1,0:T(8,128)(2,1)S(1)}, bf16[16,160,640]{2,1,0:T(8,128)(2,1)}, u32[]{:S(2)}, u32[]{:S(2)}) collective-permute-start(bf16[16,160,640]{2,1,0:T(8,128)(2,1)S(1)} %bitcast_dynamic-update-slice_fusion.mine_ref), channel_id=1, source_target_pairs={{0,16},{1,17},{2,18},{3,19},{4,20},{5,21},{6,22},{7,23},{8,24},{9,... | collective-permute-start | bytes 9830408 | tf_op jit(solution)/shard_map/ppermute | solution.py:46
  45.4 1.9 collective-permute-start.2
  51.2 24.7 %collective-permute-done.2.prev_ref = bf16[512,1280]{1,0:T(8,128)(2,1)} collective-permute-done((bf16[512,1280]{1,0:T(8,128)(2,1)}, bf16[512,1280]{1,0:T(8,128)(2,1)}, u32[]{:S(2)}, u32[]{:S(2)}) %collective-permute-start.2) | collective-permute-done | bytes 1310752 | tf_op jit(solution)/shard_map/ppermute | solution.py:245
  75.9 59.3 %attention.1 = (bf16[512,1280]{1,0:T(8,128)(2,1)}, bf16[512,1280]{1,0:T(8,128)(2,1)}, bf16[256,1280]{1,0:T(8,128)(2,1)}) custom-call(s32[4]{0:T(128)} %pad_add_fusion.1.place_ref, s32[2,1280]{1,0:T(2,128)} %pad_add_fusion.ends_ref.spans_ref, bf16[512,1280]{1,0:T(8,128)(2,1)} %bitcast.58, bf16[512,1280]{1,0:T(8,128)(2,1)} %collective-permute-done.2.prev_ref, ...), custom_call_target="tpu_custom_call" | custom-call | flops 30000001024 | bytes 20000000 | tf_op jit(solution)/shard_map/attention/pallas_call | solution.py:205
  136.2 1.6 collective-permute-done.13
  139.0 22.8 %all_to_all.10 = bf16[32,4,1280]{2,1,0:T(4,128)(2,1)S(1)} all-to-all(bf16[32,4,1280]{2,1,0:T(4,128)(2,1)S(1)} %reshape.130), channel_id=1, replica_groups=mesh['x'=4,'co'=2,'z'=4,'yh'=2,'dp'=2] {'x','z','yh'}, dimensions={0} | all-to-all | bytes 655360 | tf_op jit(solution)/shard_map/all_to_all | solution.py:280
  162.8 4.0 %all-to-all-start.1 = ((bf16[32,4,1280]{2,1,0:T(4,128)(2,1)}), bf16[32,4,1280]{2,1,0:T(4,128)(2,1)S(1)}, u32[]{:S(2)}, u32[]{:S(2)}) async-start(bf16[32,4,1280]{2,1,0:T(4,128)(2,1)} %broadcast_in_dim.69), calls=%async_computation.1 | async-start | bytes 655360 | tf_op jit(solution)/shard_map/all_to_all | solution.py:282
  166.8 8.6 %collective-permute-start.12 = (bf16[512,1280]{1,0:T(8,128)(2,1)}, bf16[512,1280]{1,0:T(8,128)(2,1)S(1)}, u32[]{:S(2)}, u32[]{:S(2)}) collective-permute-start(bf16[512,1280]{1,0:T(8,128)(2,1)} %get-tuple-element.12), channel_id=1, source_target_pairs={{2,0},{4,2},{6,4},{8,6},{10,8},{12,10},{14,12},{16,14},{18,16},{20... | collective-permute-start | bytes 3932168 | tf_op jit(solution)/shard_map/ppermute | solution.py:271
  175.3 1.3 all-to-all-done.1
  177.4 2.8 %collective-permute-start.14 = (bf16[128,1280]{1,0:T(8,128)(2,1)}, bf16[128,1280]{1,0:T(8,128)(2,1)}, u32[]{:S(2)}, u32[]{:S(2)}) collective-permute-start(bf16[128,1280]{1,0:T(8,128)(2,1)} %reshape.131), channel_id=1, source_target_pairs={{0,16},{16,0},{1,17},{17,1},{2,18},{18,2},{3,19},{19,3},{4,20},{20... | collective-permute-start | bytes 983048 | tf_op jit(solution)/shard_map/ppermute | solution.py:284
  182.9 1.2 maximum_select_fusion
  185.2 18.7 %collective-permute-done.12 = bf16[512,1280]{1,0:T(8,128)(2,1)S(1)} collective-permute-done((bf16[512,1280]{1,0:T(8,128)(2,1)}, bf16[512,1280]{1,0:T(8,128)(2,1)S(1)}, u32[]{:S(2)}, u32[]{:S(2)}) %collective-permute-start.12) | collective-permute-done | bytes 1310752 | tf_op jit(solution)/shard_map/ppermute | solution.py:271
  203.9 1.3 select_bitcast_fusion
  (67 shorter events, 11.8 us)
Async XLA Ops:
  2.2 11.8 %collective-permute-start.1 = (bf16[2,160,640]{2,1,0:T(8,128)(2,1)S(1)}, bf16[2,160,640]{2,1,0:T(8,128)(2,1)S(1)}, u32[]{:S(2)}, u32[]{:S(2)}) collective-permute-start(bf16[2,160,640]{2,1,0:T(8,128)(2,1)S(1)} %pad_maximum_fusion.1), channel_id=1, source_target_pairs={{0,3},{1,0},{2,1},{3,2},{4,7},{5,4},{6,5},{7,6},{8,11},{9,8},{10,9... | collective-permute-start | bytes 1228808 | tf_op jit(solution)/shard_map/ppermute | solution.py:46
  5.9 11.4 %collective-permute-start = (bf16[2,160,640]{2,1,0:T(8,128)(2,1)S(1)}, bf16[2,160,640]{2,1,0:T(8,128)(2,1)S(1)}, u32[]{:S(2)}, u32[]{:S(2)}) collective-permute-start(bf16[2,160,640]{2,1,0:T(8,128)(2,1)S(1)} %pad_maximum_fusion), channel_id=1, source_target_pairs={{0,1},{1,2},{2,3},{3,0},{4,5},{5,6},{6,7},{7,4},{8,9},{9,10},{10,1... | collective-permute-start | bytes 1228808 | tf_op jit(solution)/shard_map/ppermute | solution.py:46
  17.3 9.6 %collective-permute-start.4 = (bf16[2,160,640]{2,1,0:T(8,128)(2,1)S(1)}, bf16[2,160,640]{2,1,0:T(8,128)(2,1)S(1)}, u32[]{:S(2)}, u32[]{:S(2)}) collective-permute-start(bf16[2,160,640]{2,1,0:T(8,128)(2,1)S(1)} %get-tuple-element.9), channel_id=1, source_target_pairs={{0,96},{1,97},{2,98},{3,99},{4,100},{5,101},{6,102},{7,103},{8,104... | collective-permute-start | bytes 1228808 | tf_op jit(solution)/shard_map/ppermute | solution.py:46
  19.9 10.5 %collective-permute-start.3 = (bf16[2,160,640]{2,1,0:T(8,128)(2,1)S(1)}, bf16[2,160,640]{2,1,0:T(8,128)(2,1)S(1)}, u32[]{:S(2)}, u32[]{:S(2)}) collective-permute-start(bf16[2,160,640]{2,1,0:T(8,128)(2,1)S(1)} %get-tuple-element.9), channel_id=1, source_target_pairs={{0,32},{1,33},{2,34},{3,35},{4,36},{5,37},{6,38},{7,39},{8,40},{9,... | collective-permute-start | bytes 1228808 | tf_op jit(solution)/shard_map/ppermute | solution.py:46
  19.9 10.6 %collective-permute-start.6 = (bf16[2,160,640]{2,1,0:T(8,128)(2,1)S(1)}, bf16[2,160,640]{2,1,0:T(8,128)(2,1)S(1)}, u32[]{:S(2)}, u32[]{:S(2)}) collective-permute-start(bf16[2,160,640]{2,1,0:T(8,128)(2,1)S(1)} %get-tuple-element.10), channel_id=1, source_target_pairs={{0,12},{1,13},{2,14},{3,15},{4,0},{5,1},{6,2},{7,3},{8,4},{9,5},{1... | collective-permute-start | bytes 1228808 | tf_op jit(solution)/shard_map/ppermute | solution.py:46
  23.7 10.7 %collective-permute-start.5 = (bf16[2,160,640]{2,1,0:T(8,128)(2,1)S(1)}, bf16[2,160,640]{2,1,0:T(8,128)(2,1)S(1)}, u32[]{:S(2)}, u32[]{:S(2)}) collective-permute-start(bf16[2,160,640]{2,1,0:T(8,128)(2,1)S(1)} %get-tuple-element.10), channel_id=1, source_target_pairs={{0,4},{1,5},{2,6},{3,7},{4,8},{5,9},{6,10},{7,11},{8,12},{9,13},{1... | collective-permute-start | bytes 1228808 | tf_op jit(solution)/shard_map/ppermute | solution.py:46
  23.8 21.1 %copy-start.2 = (s32[1,256]{1,0:T(1,128)S(1)}, s32[1,256]{1,0:T(1,128)}, u32[]{:S(2)}) copy-start(s32[1,256]{1,0:T(1,128)} %param.6) | copy-start | bytes 3076
  23.8 23.6 %copy-start.3 = (f32[1280]{0:T(1024)S(1)}, f32[1280]{0:T(1024)}, u32[]{:S(2)}) copy-start(f32[1280]{0:T(1024)} %param.7) | copy-start | bytes 15364
  26.9 9.5 %collective-permute-start.8 = (bf16[160,640]{1,0:T(8,128)(2,1)S(1)}, bf16[160,640]{1,0:T(8,128)(2,1)S(1)}, u32[]{:S(2)}, u32[]{:S(2)}) collective-permute-start(bf16[160,640]{1,0:T(8,128)(2,1)S(1)} %slice_bitcast_fusion.2), channel_id=1, source_target_pairs={{0,96},{1,97},{2,98},{3,99},{4,100},{5,101},{6,102},{7,103},{8,104... | collective-permute-start | bytes 614408 | tf_op jit(solution)/shard_map/ppermute | solution.py:46
  30.4 5.9 %collective-permute-start.7 = (bf16[160,640]{1,0:T(8,128)(2,1)S(1)}, bf16[160,640]{1,0:T(8,128)(2,1)S(1)}, u32[]{:S(2)}, u32[]{:S(2)}) collective-permute-start(bf16[160,640]{1,0:T(8,128)(2,1)S(1)} %slice_bitcast_fusion.3), channel_id=1, source_target_pairs={{0,32},{1,33},{2,34},{3,35},{4,36},{5,37},{6,38},{7,39},{8,40},{9,... | collective-permute-start | bytes 614408 | tf_op jit(solution)/shard_map/ppermute | solution.py:46
  30.6 9.8 %collective-permute-start.10 = (bf16[160,640]{1,0:T(8,128)(2,1)S(1)}, bf16[160,640]{1,0:T(8,128)(2,1)S(1)}, u32[]{:S(2)}, u32[]{:S(2)}) collective-permute-start(bf16[160,640]{1,0:T(8,128)(2,1)S(1)} %slice_bitcast_fusion), channel_id=1, source_target_pairs={{0,12},{1,13},{2,14},{3,15},{4,0},{5,1},{6,2},{7,3},{8,4},{9,5},{1... | collective-permute-start | bytes 614408 | tf_op jit(solution)/shard_map/ppermute | solution.py:46
  34.4 5.9 %collective-permute-start.9 = (bf16[160,640]{1,0:T(8,128)(2,1)S(1)}, bf16[160,640]{1,0:T(8,128)(2,1)S(1)}, u32[]{:S(2)}, u32[]{:S(2)}) collective-permute-start(bf16[160,640]{1,0:T(8,128)(2,1)S(1)} %slice_bitcast_fusion.1), channel_id=1, source_target_pairs={{0,4},{1,5},{2,6},{3,7},{4,8},{5,9},{6,10},{7,11},{8,12},{9,13},{1... | collective-permute-start | bytes 614408 | tf_op jit(solution)/shard_map/ppermute | solution.py:46
  40.4 35.5 %copy-start.1 = (bf16[16,160,640]{2,1,0:T(8,128)(2,1)}, bf16[16,160,640]{2,1,0:T(8,128)(2,1)S(1)}, u32[]{:S(2)}) copy-start(bf16[16,160,640]{2,1,0:T(8,128)(2,1)S(1)} %bitcast_dynamic-update-slice_fusion.mine_ref) | copy-start | bytes 9830404
  40.4 35.5 %collective-permute-start.11 = (bf16[16,160,640]{2,1,0:T(8,128)(2,1)S(1)}, bf16[16,160,640]{2,1,0:T(8,128)(2,1)}, u32[]{:S(2)}, u32[]{:S(2)}) collective-permute-start(bf16[16,160,640]{2,1,0:T(8,128)(2,1)S(1)} %bitcast_dynamic-update-slice_fusion.mine_ref), channel_id=1, source_target_pairs={{0,16},{1,17},{2,18},{3,19},{4,20},{5,21},{6,22},{7,23},{8,24},{9,... | collective-permute-start | bytes 9830408 | tf_op jit(solution)/shard_map/ppermute | solution.py:46
  45.4 30.5 %collective-permute-start.2 = (bf16[512,1280]{1,0:T(8,128)(2,1)}, bf16[512,1280]{1,0:T(8,128)(2,1)}, u32[]{:S(2)}, u32[]{:S(2)}) collective-permute-start(bf16[512,1280]{1,0:T(8,128)(2,1)} %bitcast.57), channel_id=1, source_target_pairs={{0,2},{2,4},{4,6},{6,8},{8,10},{10,12},{12,14},{14,16},{16,18},{18... | collective-permute-start | bytes 3932168 | tf_op jit(solution)/shard_map/ppermute | solution.py:245
  136.1 1.7 collective-permute-start.13
  139.0 64.9 %copy-start = (bf16[512,1280]{1,0:T(8,128)(2,1)S(1)}, bf16[512,1280]{1,0:T(8,128)(2,1)}, u32[]{:S(2)}) copy-start(bf16[512,1280]{1,0:T(8,128)(2,1)} %get-tuple-element.11) | copy-start | bytes 3932164
  162.8 13.8 %all-to-all-start.1 = ((bf16[32,4,1280]{2,1,0:T(4,128)(2,1)}), bf16[32,4,1280]{2,1,0:T(4,128)(2,1)S(1)}, u32[]{:S(2)}, u32[]{:S(2)}) async-start(bf16[32,4,1280]{2,1,0:T(4,128)(2,1)} %broadcast_in_dim.69), calls=%async_computation.1 | async-start | bytes 655360 | tf_op jit(solution)/shard_map/all_to_all | solution.py:282
  166.8 37.1 %collective-permute-start.12 = (bf16[512,1280]{1,0:T(8,128)(2,1)}, bf16[512,1280]{1,0:T(8,128)(2,1)S(1)}, u32[]{:S(2)}, u32[]{:S(2)}) collective-permute-start(bf16[512,1280]{1,0:T(8,128)(2,1)} %get-tuple-element.12), channel_id=1, source_target_pairs={{2,0},{4,2},{6,4},{8,6},{10,8},{12,10},{14,12},{16,14},{18,16},{20... | collective-permute-start | bytes 3932168 | tf_op jit(solution)/shard_map/ppermute | solution.py:271
  177.4 5.4 %collective-permute-start.14 = (bf16[128,1280]{1,0:T(8,128)(2,1)}, bf16[128,1280]{1,0:T(8,128)(2,1)}, u32[]{:S(2)}, u32[]{:S(2)}) collective-permute-start(bf16[128,1280]{1,0:T(8,128)(2,1)} %reshape.131), channel_id=1, source_target_pairs={{0,16},{16,0},{1,17},{17,1},{2,18},{18,2},{3,19},{19,3},{4,20},{20... | collective-permute-start | bytes 983048 | tf_op jit(solution)/shard_map/ppermute | solution.py:284

commit v2 on v1

--- a/solution.py
+++ b/solution.py
@@ -8,8 +8,10 @@
 from jax.sharding import Mesh
 from jax.sharding import PartitionSpec as P
 
+
 HEADS = 16
 SIZE = 80
+VROWS = 96
 D = HEADS * SIZE
 LOCAL = 512
 WIN = 2 * LOCAL
@@ -61,7 +63,8 @@
     place_ref, ends_ref, own_ref, prev_ref, gain_ref, wqkv_ref, wout_ref, mine_ref, other_ref,
     spans_ref, image_ref, lens_ref,
     hprev_ref, hown_ref, pooled_ref,
-    x_ref, w_ref, wo_ref, q_ref, k_ref, vt_ref, ctx_ref, bias_ref, hid_ref, sem,
+    x_ref, n_ref, w_ref, wo_ref, q_ref, k_ref, vt_ref, ctx_ref, bias_ref, hid_ref,
+    s0_ref, s1_ref, p0_ref, p1_ref, top0_ref, top1_ref, sem,
 ):
     x, z, co, dp = (place_ref[i] for i in range(4))
     lo = ends_ref[0, LOCAL]
@@ -69,12 +72,6 @@
     base = (lo // 128) * 128
     blocks = (hi - base + QB - 1) // QB
 
-    copies = [
-        pltpu.make_async_copy(prev_ref, x_ref.at[pl.ds(0, LOCAL)], sem.at[0]),
-        pltpu.make_async_copy(own_ref, x_ref.at[pl.ds(LOCAL, LOCAL)], sem.at[0]),
-        pltpu.make_async_copy(wqkv_ref, w_ref.at[pl.ds(dp * HALF, HALF)], sem.at[1]),
-        pltpu.make_async_copy(wout_ref, wo_ref.at[pl.ds(dp * HALF, HALF)], sem.at[1]),
-    ]
     far = (1 - dp) * HALF
     order = (
         [(0, x, 0), (0, x, 1), (1, z, 0), (1, z, 1)]
@@ -82,60 +79,92 @@
         + [(1, (z + 3) % 4, 0), (1, (z + 3) % 4, 1), (1, (z + 1) % 4, 0), (1, (z + 1) % 4, 1)]
         + [(0, (x + 2) % 4, 0), (0, (x + 2) % 4, 1), (1, (z + 2) % 4, 0), (1, (z + 2) % 4, 1)]
     )
-    for c in copies:
-        c.start()
-    for source, core in ((mine_ref, co), (other_ref, 1 - co)):
-        for slot, (part, row, side) in enumerate(order):
-            rows = pl.ds(pl.multiple_of(far + row * KR, 16), KR)
-            if part == 0:
-                cols = pl.ds(pl.multiple_of((core * 2 + side) * CG, 128), CG)
-                pltpu.make_async_copy(source.at[slot], w_ref.at[rows, cols], sem.at[1]).start()
-            else:
-
-                @pl.when(core == 0)
-                def _(source=source, slot=slot, rows=rows, side=side):
-                    cols = pl.ds((4 + side) * CG, CG)
-                    pltpu.make_async_copy(source.at[slot], w_ref.at[rows, cols], sem.at[1]).start()
-
-                @pl.when(core == 1)
-                def _(source=source, slot=slot, rows=rows, side=side):
-                    cols = pl.ds(side * CG, CG)
-                    pltpu.make_async_copy(source.at[slot], wo_ref.at[rows, cols], sem.at[1]).start()
+
+    pltpu.make_async_copy(prev_ref, x_ref.at[pl.ds(0, LOCAL)], sem.at[0]).start()
+    pltpu.make_async_copy(own_ref, x_ref.at[pl.ds(LOCAL, LOCAL)], sem.at[0]).start()
+
+    def near(part, target, cols):
+        return pltpu.make_async_copy(
+            wout_ref if part == 3 else wqkv_ref.at[:, cols],
+            target.at[pl.ds(pl.multiple_of(dp * HALF, 16), HALF), cols],
+            sem.at[1 + part],
+        )
+
+    def distant(part, source, slot, row, side):
+        target = wo_ref if part == 3 else w_ref
+        rows = pl.ds(pl.multiple_of(far + row * KR, 16), KR)
+        cols = pl.ds((0 if part == 3 else part * D) + side * CG, CG)
+        return pltpu.make_async_copy(source.at[slot], target.at[rows, cols], sem.at[1 + part])
+
+    columns = [pl.ds(0, D), pl.ds(D, D), pl.ds(2 * D, D), pl.ds(0, D)]
+    targets = [w_ref, w_ref, w_ref, wo_ref]
+    for part in range(4):
+        near(part, targets[part], columns[part]).start()
+        for source, core in ((mine_ref, co), (other_ref, 1 - co)):
+
+            @pl.when(core == part % 2)
+            def _(source=source, part=part):
+                for slot, (kind, row, side) in enumerate(order):
+                    if kind == part // 2:
+                        distant(part, source, slot, row, side).start()
+
+    def arrived(part):
+        near(part, targets[part], columns[part]).wait()
+        for slot in range(8):
+            distant(part, mine_ref, slot, 0, 0).wait()
 
     x_ref[WIN:, :] = jnp.zeros((PAD - WIN, D), jnp.bfloat16)
+    pltpu.make_async_copy(prev_ref, x_ref.at[pl.ds(0, LOCAL)], sem.at[0]).wait()
+    pltpu.make_async_copy(own_ref, x_ref.at[pl.ds(LOCAL, LOCAL)], sem.at[0]).wait()
+
+    def block_rows(j):
+        row0 = pl.multiple_of(base + j * QB, 128)
+        return row0, pl.ds(row0, QB)
+
+    def normalize(j, carry):
+        _, rows = block_rows(j)
+        values = x_ref[rows, :].astype(jnp.float32)
+        center = values - jnp.mean(values, axis=1, keepdims=True)
+        spread = jnp.mean(center * center, axis=1, keepdims=True)
+        normed = center * lax.rsqrt(spread + 1e-05) * gain_ref[...]
+        n_ref[rows, :] = normed.astype(jnp.bfloat16)
+        return carry
+
+    lax.fori_loop(0, blocks, normalize, 0)
     k_ref[...] = jnp.zeros_like(k_ref)
     vt_ref[...] = jnp.zeros_like(vt_ref)
     hid_ref[...] = jnp.zeros_like(hid_ref)
-    copies[0].wait()
-    copies[1].wait()
-    copies[2].wait()
-    copies[3].wait()
-    for source in (mine_ref, other_ref):
-        for slot in range(16):
-            pltpu.make_async_copy(
-                source.at[slot], w_ref.at[pl.ds(0, KR), pl.ds(0, CG)], sem.at[1]
-            ).wait()
-
-    def project(j, carry):
-        row0 = pl.multiple_of(base + j * QB, 128)
-        rows = pl.ds(row0, QB)
-        values = x_ref[rows, :].astype(jnp.float32)
-        center = values - jnp.mean(values, axis=1, keepdims=True)
-        spread = jnp.mean(center * center, axis=1, keepdims=True)
-        normed = (center * lax.rsqrt(spread + 1e-05) * gain_ref[...]).astype(jnp.bfloat16)
-        q = jnp.dot(normed, w_ref[:, 0:D], preferred_element_type=jnp.float32)
+
+    def project_q(j, carry):
+        _, rows = block_rows(j)
+        q = jnp.dot(n_ref[rows, :], w_ref[:, 0:D], preferred_element_type=jnp.float32)
         q_ref[rows, :] = (q * (LOG2E * SIZE**-0.5)).astype(jnp.bfloat16)
-        k = jnp.dot(normed, w_ref[:, D : 2 * D], preferred_element_type=jnp.float32)
+        return carry
+
+    def project_k(j, carry):
+        _, rows = block_rows(j)
+        k = jnp.dot(n_ref[rows, :], w_ref[:, D : 2 * D], preferred_element_type=jnp.float32)
         k_ref[rows, :] = k.astype(jnp.bfloat16)
-        v = jnp.dot(normed, w_ref[:, 2 * D : 3 * D], preferred_element_type=jnp.float32)
-        vt_ref[:, rows] = v.T.astype(jnp.bfloat16)
-        return carry
-
-    lax.fori_loop(0, blocks, project, 0)
+        return carry
+
+    def project_v(j, carry):
+        _, rows = block_rows(j)
+        v = jnp.dot(n_ref[rows, :], w_ref[:, 2 * D :], preferred_element_type=jnp.float32)
+        vt = v.T.astype(jnp.bfloat16)
+        for h in range(HEADS):
+            vt_ref[pl.ds(h * VROWS, SIZE), rows] = vt[h * SIZE : (h + 1) * SIZE]
+            vt_ref[pl.ds(h * VROWS + SIZE, VROWS - SIZE), rows] = jnp.ones(
+                (VROWS - SIZE, QB), jnp.bfloat16
+            )
+        return carry
+
+    for part, project in enumerate((project_q, project_k, project_v)):
+        arrived(part)
+        lax.fori_loop(0, blocks, project, 0)
+    arrived(3)
 
     def attend(j, carry):
-        row0 = pl.multiple_of(base + j * QB, 128)
-        rows = pl.ds(row0, QB)
+        row0, rows = block_rows(j)
         least = ends_ref[0, jnp.maximum(row0, lo)]
         most = ends_ref[1, jnp.minimum(row0 + QB, hi) - 1]
         k0 = pl.multiple_of((least // 128) * 128, 128)
@@ -151,28 +180,49 @@
                 at = lax.broadcasted_iota(jnp.int32, (width, QB), 0) + k0
                 bias_ref[0:width, :] = jnp.where((at >= start) & (at < end), 0.0, -1e30)
 
-                def one_head(h, inner):
+                def scores(h, s_ref, top_ref):
                     w0 = pl.multiple_of(jnp.minimum((h * SIZE) // 128 * 128, D - 256), 128)
                     window = pl.ds(w0, 256)
-                    lane = lax.broadcasted_iota(jnp.int32, (QB, 256), 1) + (w0 - h * SIZE)
-                    q = jnp.where((lane >= 0) & (lane < SIZE), q_ref[rows, window], 0)
+                    lane = lax.broadcasted_iota(jnp.int32, (1, 256), 1) + (w0 - h * SIZE)
+                    inside = jnp.where((lane >= 0) & (lane < SIZE), 1.0, 0.0)
+                    q = q_ref[rows, window] * inside.astype(jnp.bfloat16)
                     s = lax.dot_general(
-                        k_ref[keys, window], q.astype(jnp.bfloat16), (((1,), (1,)), ((), ())),
+                        k_ref[keys, window], q, (((1,), (1,)), ((), ())),
                         preferred_element_type=jnp.float32,
                     )
                     s = s + bias_ref[0:width, :]
-                    top = jnp.max(s, axis=0, keepdims=True)
-                    p = jnp.exp2(s - top)
-                    total = jnp.sum(p, axis=0, keepdims=True)
-                    features = pl.ds(pl.multiple_of(h * SIZE, 16), SIZE)
+                    s_ref[0:width, :] = s
+                    top_ref[...] = jnp.max(s, axis=0, keepdims=True)
+
+                def weights(s_ref, top_ref, p_ref):
+                    p_ref[0:width, :] = jnp.exp2(s_ref[0:width, :] - top_ref[...]).astype(
+                        jnp.bfloat16
+                    )
+
+                def mix(h, p_ref):
+                    features = pl.ds(pl.multiple_of(h * VROWS, 16), VROWS)
                     c = jnp.dot(
-                        vt_ref[features, keys], p.astype(jnp.bfloat16),
+                        vt_ref[features, keys], p_ref[0:width, :],
                         preferred_element_type=jnp.float32,
                     )
-                    ctx_ref[features, :] = (c * (1.0 / total)).astype(jnp.bfloat16)
+                    ctx_ref[pl.ds(pl.multiple_of(h * SIZE, 16), SIZE), :] = (
+                        c[0:SIZE] * (1.0 / c[SIZE : SIZE + 1])
+                    ).astype(jnp.bfloat16)
+
+                scores(0, s0_ref, top0_ref)
+
+                def two_heads(i, inner):
+                    h = i * 2
+                    scores(h + 1, s1_ref, top1_ref)
+                    weights(s0_ref, top0_ref, p0_ref)
+                    mix(jnp.maximum(h - 1, 0), p1_ref)
+                    scores(jnp.minimum(h + 2, HEADS - 1), s0_ref, top0_ref)
+                    weights(s1_ref, top1_ref, p1_ref)
+                    mix(h, p0_ref)
                     return inner
 
-                lax.fori_loop(0, HEADS, one_head, 0, unroll=2)
+                lax.fori_loop(0, HEADS // 2, two_heads, 0)
+                mix(HEADS - 1, p1_ref)
 
         mixed = lax.dot_general(
             ctx_ref[...], wo_ref[...], (((0,), (0,)), ((), ())),
@@ -213,15 +263,22 @@
         out_specs=(vmem, vmem, vmem),
         scratch_shapes=[
             pltpu.VMEM((PAD, D), jnp.bfloat16),
+            pltpu.VMEM((PAD, D), jnp.bfloat16),
             pltpu.VMEM((D, 3 * D), jnp.bfloat16),
             pltpu.VMEM((D, D), jnp.bfloat16),
             pltpu.VMEM((PAD, D), jnp.bfloat16),
             pltpu.VMEM((PAD, D), jnp.bfloat16),
-            pltpu.VMEM((D, PAD), jnp.bfloat16),
+            pltpu.VMEM((HEADS * VROWS, PAD), jnp.bfloat16),
             pltpu.VMEM((D, QB), jnp.bfloat16),
             pltpu.VMEM((WIDTHS[-1], QB), jnp.float32),
             pltpu.VMEM((PAD, D), jnp.bfloat16),
-            pltpu.SemaphoreType.DMA((2,)),
+            pltpu.VMEM((WIDTHS[-1], QB), jnp.float32),
+            pltpu.VMEM((WIDTHS[-1], QB), jnp.float32),
+            pltpu.VMEM((WIDTHS[-1], QB), jnp.bfloat16),
+            pltpu.VMEM((WIDTHS[-1], QB), jnp.bfloat16),
+            pltpu.VMEM((1, QB), jnp.float32),
+            pltpu.VMEM((1, QB), jnp.float32),
+            pltpu.SemaphoreType.DMA((5,)),
         ],
         compiler_params=pltpu.CompilerParams(vmem_limit_bytes=60 * 2**20),
         cost_estimate=pl.CostEstimate(
@@ -231,7 +288,7 @@
     )(place, spans, own, prev, gain, w_qkv, w_out, mine, other, spans, image, lens)
 
 
-def shards(tokens, lengths, ln_gain, w_qkv, w_out):
+def layer(tokens, lengths, ln_gain, w_qkv, w_out):
     x, co, z, yh, dp = (lax.axis_index(a) for a in ALL_AXES)
     shard = (x * 2 + co) * 8 + z * 2 + yh
     own = tokens[0]
@@ -241,8 +298,7 @@
     r1 = moved(p1, Y_DOWN)
     a0 = jnp.stack([r0[0], r1[0]])
     b0 = jnp.stack([r0[1], r1[1]])
-    sent, a0, b0 = lax.optimization_barrier((own, a0, b0))
-    prev = lax.ppermute(sent, TOKEN_AXES, [(i, i + 1) for i in range(63)])
+    prev = lax.ppermute(own, TOKEN_AXES, [(i, i + 1) for i in range(63)])
     a1, a2 = moved(a0, X_UP), moved(a0, X_DOWN)
     b1, b2 = moved(b0, Z_UP), moved(b0, Z_DOWN)
     a3, a4 = moved(a1[0], X_UP), moved(a2[1], X_DOWN)
@@ -275,7 +331,8 @@
     part = part.reshape(2, IMAGES // 2, D)
     kept = lax.dynamic_index_in_dim(part, co, 0, keepdims=False)
     given = lax.dynamic_index_in_dim(part, 1 - co, 0, keepdims=False)
-    kept = kept.astype(jnp.float32) + lax.ppermute(given, "co", swap).astype(jnp.float32)
+    given = lax.ppermute(given, "co", swap)
+    kept = kept.astype(jnp.float32) + given.astype(jnp.float32)
     kept = kept.astype(jnp.bfloat16).reshape(32, 4, D)
     rows = lax.all_to_all(kept, group, 0, 0, tiled=True).astype(jnp.float32)
     rows = jnp.sum(rows, axis=0).astype(jnp.bfloat16)
@@ -295,6 +352,4 @@
     fine = Mesh(mesh.devices.reshape(4, 2, 4, 2, 2), ALL_AXES)
     in_specs = (P("dp", TOKEN_AXES, None), P("dp", None), P(), P("dp", None), P("dp", None))
     out_specs = (P("dp", TOKEN_AXES, None), P("dp", None, None))
-    return jax.shard_map(
-        shards, mesh=fine, in_specs=in_specs, out_specs=out_specs, check_vma=False
-    )
+    return jax.shard_map(layer, mesh=fine, in_specs=in_specs, out_specs=out_specs, check_vma=False)

time: 205 us -> 187 us (0.912)
  Pallas kernels: 59.3 us -> 33.3 us
  local copies, waits for them, and re-layouts: 6.2 us -> 15.6 us
  waiting for transfers between devices: 66.1 us -> 57.5 us
  blocking collectives: 22.8 us -> 28.5 us
    pallas_call x1, Pallas kernels: 59.3 us -> 33.3 us  [attention(): pl.pallas_call(attention_kernel, out_shape=(jax.ShapeDtypeStruct((LOCAL,...]
    ppermute x11, waiting for transfers between devices: 19.9 us -> 12.2 us  [moved(): return lax.ppermute(piece, ALL_AXES, pairs)]
    unnamed x17 -> x19, local copies, waits for them, and re-layouts: 0.39 us -> 7.76 us
    all_to_all x1, blocking collectives: 22.8 us -> 28.5 us  [layer(): rows = lax.all_to_all(kept, group, 0, 0, tiled=True).astype(jnp.float32)]
  transfers between devices with their start and end apart: 16 -> 16, of which waited for: 9 -> 7; matrix products, arithmetic and copies ran while one was open for 5% -> 9% of each run, Pallas kernels for 0% -> 0%
where the time goes in v2:
time: 187 us
  waiting for transfers between devices  57.5 us (31%)
  starting transfers between devices  40.3 us (22%)
  Pallas kernels  33.3 us (18%)
  blocking collectives  28.5 us (15%)
  local copies, waits for them, and re-layouts  15.6 us (8%)
  other arithmetic  9.24 us (5%)
  between operations  2.19 us (1%)
    pallas_call x1, Pallas kernels, attention(): pl.pallas_call(attention_kernel, out_shape=(jax.ShapeDtypeStruct((LOCAL,...  33.3 us
    all_to_all x1, blocking collectives, layer(): rows = lax.all_to_all(kept, group, 0, 0, tiled=True).astype(jnp.float32)  28.5 us
    ppermute x1, waiting for transfers between devices, layer(): prev = lax.ppermute(own, TOKEN_AXES, [(i, i + 1) for i in range(63)])  23.7 us
    ppermute x11, starting transfers between devices, moved(): return lax.ppermute(piece, ALL_AXES, pairs)  21.5 us
    ppermute x1, waiting for transfers between devices, layer(): back = lax.ppermute(hprev, TOKEN_AXES, [(i + 1, i) for i in range(63)])  18.7 us
    ppermute x11, waiting for transfers between devices, moved(): return lax.ppermute(piece, ALL_AXES, pairs)  12.2 us
    ppermute x1, starting transfers between devices, layer(): back = lax.ppermute(hprev, TOKEN_AXES, [(i + 1, i) for i in range(63)])  8.52 us
    unnamed x19, local copies, waits for them, and re-layouts  7.76 us
  transfers between devices with their start and end apart: 16, of which 7 were waited for; matrix products, arithmetic and copies ran while one was open for 9% of the time, Pallas kernels for 0%

profile of v2, /device:TPU:1, one launch (start us, length us, event | category | flops | bytes accessed | tf_op | source)
XLA Modules:
  0.0 186.6 jit_solution(2288276279662337089)
XLA Ops:
  0.6 1.5 dynamic-slice_bitcast_fusion.1
  2.2 2.2 %collective-permute-start.1 = (bf16[2,160,640]{2,1,0:T(8,128)(2,1)S(1)}, bf16[2,160,640]{2,1,0:T(8,128)(2,1)S(1)}, u32[]{:S(2)}, u32[]{:S(2)}) collective-permute-start(bf16[2,160,640]{2,1,0:T(8,128)(2,1)S(1)} %pad_maximum_fusion), channel_id=1, source_target_pairs={{0,1},{1,2},{2,3},{3,0},{4,5},{5,6},{6,7},{7,4},{8,9},{9,10},{10,1... | collective-permute-start | bytes 1228808 | tf_op jit(solution)/shard_map/ppermute | solution.py:48
  4.4 1.5 collective-permute-start.2
  5.9 8.9 %collective-permute-done.1 = bf16[2,160,640]{2,1,0:T(8,128)(2,1)S(1)} collective-permute-done((bf16[2,160,640]{2,1,0:T(8,128)(2,1)S(1)}, bf16[2,160,640]{2,1,0:T(8,128)(2,1)S(1)}, u32[]{:S(2)}, u32[]{:S(2)}) %collective-permute-start.1) | collective-permute-done | bytes 409632 | tf_op jit(solution)/shard_map/ppermute | solution.py:48
  16.4 2.4 %collective-permute-start.4 = (bf16[2,160,640]{2,1,0:T(8,128)(2,1)S(1)}, bf16[2,160,640]{2,1,0:T(8,128)(2,1)S(1)}, u32[]{:S(2)}, u32[]{:S(2)}) collective-permute-start(bf16[2,160,640]{2,1,0:T(8,128)(2,1)S(1)} %pad_maximum_fusion.2), channel_id=1, source_target_pairs={{0,96},{1,97},{2,98},{3,99},{4,100},{5,101},{6,102},{7,103},{8,104... | collective-permute-start | bytes 1228808 | tf_op jit(solution)/shard_map/ppermute | solution.py:48
  18.9 3.8 %collective-permute-start.6 = (bf16[2,160,640]{2,1,0:T(8,128)(2,1)S(1)}, bf16[2,160,640]{2,1,0:T(8,128)(2,1)S(1)}, u32[]{:S(2)}, u32[]{:S(2)}) collective-permute-start(bf16[2,160,640]{2,1,0:T(8,128)(2,1)S(1)} %pad_maximum_fusion.3), channel_id=1, source_target_pairs={{0,12},{1,13},{2,14},{3,15},{4,0},{5,1},{6,2},{7,3},{8,4},{9,5},{1... | collective-permute-start | bytes 1228808 | tf_op jit(solution)/shard_map/ppermute | solution.py:48
  24.1 2.1 %collective-permute-done.4 = bf16[2,160,640]{2,1,0:T(8,128)(2,1)S(1)} collective-permute-done((bf16[2,160,640]{2,1,0:T(8,128)(2,1)S(1)}, bf16[2,160,640]{2,1,0:T(8,128)(2,1)S(1)}, u32[]{:S(2)}, u32[]{:S(2)}) %collective-permute-start.4) | collective-permute-done | bytes 409632 | tf_op jit(solution)/shard_map/ppermute | solution.py:48
  26.2 3.5 %collective-permute-start.8 = (bf16[160,640]{1,0:T(8,128)(2,1)S(1)}, bf16[160,640]{1,0:T(8,128)(2,1)S(1)}, u32[]{:S(2)}, u32[]{:S(2)}) collective-permute-start(bf16[160,640]{1,0:T(8,128)(2,1)S(1)} %slice_bitcast_fusion.2), channel_id=1, source_target_pairs={{0,96},{1,97},{2,98},{3,99},{4,100},{5,101},{6,102},{7,103},{8,104... | collective-permute-start | bytes 614408 | tf_op jit(solution)/shard_map/ppermute | solution.py:48
  29.8 3.8 %collective-permute-start.10 = (bf16[160,640]{1,0:T(8,128)(2,1)S(1)}, bf16[160,640]{1,0:T(8,128)(2,1)S(1)}, u32[]{:S(2)}, u32[]{:S(2)}) collective-permute-start(bf16[160,640]{1,0:T(8,128)(2,1)S(1)} %slice_bitcast_fusion), channel_id=1, source_target_pairs={{0,12},{1,13},{2,14},{3,15},{4,0},{5,1},{6,2},{7,3},{8,4},{9,5},{1... | collective-permute-start | bytes 614408 | tf_op jit(solution)/shard_map/ppermute | solution.py:48
  38.4 1.2 collective-permute-done.9
  40.9 4.0 %collective-permute-start.11 = (bf16[16,160,640]{2,1,0:T(8,128)(2,1)}, bf16[16,160,640]{2,1,0:T(8,128)(2,1)}, u32[]{:S(2)}, u32[]{:S(2)}) collective-permute-start(bf16[16,160,640]{2,1,0:T(8,128)(2,1)} %bitcast_dynamic-update-slice_fusion.mine_ref), channel_id=1, source_target_pairs={{0,16},{1,17},{2,18},{3,19},{4,20},{5,21},{6,22},{7,23},{8,24},{9,... | collective-permute-start | bytes 9830408 | tf_op jit(solution)/shard_map/ppermute | solution.py:48
  45.0 3.6 %collective-permute-start = (bf16[512,1280]{1,0:T(8,128)(2,1)S(1)}, bf16[512,1280]{1,0:T(8,128)(2,1)S(1)}, u32[]{:S(2)}, u32[]{:S(2)}) collective-permute-start(bf16[512,1280]{1,0:T(8,128)(2,1)S(1)} %bitcast.58), channel_id=1, source_target_pairs={{0,2},{2,4},{4,6},{6,8},{8,10},{10,12},{12,14},{14,16},{16,18},{18... | collective-permute-start | bytes 3932168 | tf_op jit(solution)/shard_map/ppermute | solution.py:301
  53.0 23.7 %collective-permute-done.prev_ref = bf16[512,1280]{1,0:T(8,128)(2,1)S(1)} collective-permute-done((bf16[512,1280]{1,0:T(8,128)(2,1)S(1)}, bf16[512,1280]{1,0:T(8,128)(2,1)S(1)}, u32[]{:S(2)}, u32[]{:S(2)}) %collective-permute-start) | collective-permute-done | bytes 1310752 | tf_op jit(solution)/shard_map/ppermute | solution.py:301
  77.7 33.3 %attention.1 = (bf16[512,1280]{1,0:T(8,128)(2,1)}, bf16[512,1280]{1,0:T(8,128)(2,1)}, bf16[256,1280]{1,0:T(8,128)(2,1)}) custom-call(s32[4]{0:T(128)} %pad_add_fusion.1.place_ref, s32[2,1280]{1,0:T(2,128)} %pad_add_fusion.ends_ref.spans_ref, bf16[512,1280]{1,0:T(8,128)(2,1)} %bitcast.57, bf16[512,1280]{1,0:T(8,128)(2,1)} %copy-done.4, ...), custom_call_target="tpu_custom_call" | custom-call | flops 30000001024 | bytes 20000000 | tf_op jit(solution)/shard_map/attention/pallas_call | solution.py:255
  112.2 1.6 collective-permute-done.13
  114.9 28.5 %all_to_all.10 = bf16[32,4,1280]{2,1,0:T(4,128)(2,1)S(1)} all-to-all(bf16[32,4,1280]{2,1,0:T(4,128)(2,1)S(1)} %reshape.130), channel_id=1, replica_groups=mesh['x'=4,'co'=2,'z'=4,'yh'=2,'dp'=2] {'x','z','yh'}, dimensions={0} | all-to-all | bytes 655360 | tf_op jit(solution)/shard_map/all_to_all | solution.py:337
  144.4 3.9 %all-to-all-start.1 = ((bf16[32,4,1280]{2,1,0:T(4,128)(2,1)}), bf16[32,4,1280]{2,1,0:T(4,128)(2,1)S(1)}, u32[]{:S(2)}, u32[]{:S(2)}) async-start(bf16[32,4,1280]{2,1,0:T(4,128)(2,1)} %broadcast_in_dim.69), calls=%async_computation.1 | async-start | bytes 655360 | tf_op jit(solution)/shard_map/all_to_all | solution.py:339
  148.3 8.5 %collective-permute-start.12 = (bf16[512,1280]{1,0:T(8,128)(2,1)}, bf16[512,1280]{1,0:T(8,128)(2,1)S(1)}, u32[]{:S(2)}, u32[]{:S(2)}) collective-permute-start(bf16[512,1280]{1,0:T(8,128)(2,1)} %get-tuple-element.6), channel_id=1, source_target_pairs={{2,0},{4,2},{6,4},{8,6},{10,8},{12,10},{14,12},{16,14},{18,16},{20... | collective-permute-start | bytes 3932168 | tf_op jit(solution)/shard_map/ppermute | solution.py:327
  156.8 1.3 all-to-all-done.1
  158.9 2.7 %collective-permute-start.14 = (bf16[128,1280]{1,0:T(8,128)(2,1)}, bf16[128,1280]{1,0:T(8,128)(2,1)}, u32[]{:S(2)}, u32[]{:S(2)}) collective-permute-start(bf16[128,1280]{1,0:T(8,128)(2,1)} %reshape.131), channel_id=1, source_target_pairs={{0,16},{16,0},{1,17},{17,1},{2,18},{18,2},{3,19},{19,3},{4,20},{20... | collective-permute-start | bytes 983048 | tf_op jit(solution)/shard_map/ppermute | solution.py:341
  164.4 1.2 maximum_select_fusion
  165.6 1.1 bitcast_convert_fusion
  166.7 18.7 %collective-permute-done.12 = bf16[512,1280]{1,0:T(8,128)(2,1)S(1)} collective-permute-done((bf16[512,1280]{1,0:T(8,128)(2,1)}, bf16[512,1280]{1,0:T(8,128)(2,1)S(1)}, u32[]{:S(2)}, u32[]{:S(2)}) %collective-permute-start.12) | collective-permute-done | bytes 1310752 | tf_op jit(solution)/shard_map/ppermute | solution.py:327
  185.4 1.3 select_bitcast_fusion
  (70 shorter events, 20.0 us)
Async XLA Ops:
  2.2 12.7 %collective-permute-start.1 = (bf16[2,160,640]{2,1,0:T(8,128)(2,1)S(1)}, bf16[2,160,640]{2,1,0:T(8,128)(2,1)S(1)}, u32[]{:S(2)}, u32[]{:S(2)}) collective-permute-start(bf16[2,160,640]{2,1,0:T(8,128)(2,1)S(1)} %pad_maximum_fusion), channel_id=1, source_target_pairs={{0,1},{1,2},{2,3},{3,0},{4,5},{5,6},{6,7},{7,4},{8,9},{9,10},{10,1... | collective-permute-start | bytes 1228808 | tf_op jit(solution)/shard_map/ppermute | solution.py:48
  4.4 11.2 %collective-permute-start.2 = (bf16[2,160,640]{2,1,0:T(8,128)(2,1)S(1)}, bf16[2,160,640]{2,1,0:T(8,128)(2,1)S(1)}, u32[]{:S(2)}, u32[]{:S(2)}) collective-permute-start(bf16[2,160,640]{2,1,0:T(8,128)(2,1)S(1)} %pad_maximum_fusion.1), channel_id=1, source_target_pairs={{0,3},{1,0},{2,1},{3,2},{4,7},{5,4},{6,5},{7,6},{8,11},{9,8},{10,9... | collective-permute-start | bytes 1228808 | tf_op jit(solution)/shard_map/ppermute | solution.py:48
  16.4 9.8 %collective-permute-start.4 = (bf16[2,160,640]{2,1,0:T(8,128)(2,1)S(1)}, bf16[2,160,640]{2,1,0:T(8,128)(2,1)S(1)}, u32[]{:S(2)}, u32[]{:S(2)}) collective-permute-start(bf16[2,160,640]{2,1,0:T(8,128)(2,1)S(1)} %pad_maximum_fusion.2), channel_id=1, source_target_pairs={{0,96},{1,97},{2,98},{3,99},{4,100},{5,101},{6,102},{7,103},{8,104... | collective-permute-start | bytes 1228808 | tf_op jit(solution)/shard_map/ppermute | solution.py:48
  18.8 10.9 %collective-permute-start.3 = (bf16[2,160,640]{2,1,0:T(8,128)(2,1)S(1)}, bf16[2,160,640]{2,1,0:T(8,128)(2,1)S(1)}, u32[]{:S(2)}, u32[]{:S(2)}) collective-permute-start(bf16[2,160,640]{2,1,0:T(8,128)(2,1)S(1)} %pad_maximum_fusion.2), channel_id=1, source_target_pairs={{0,32},{1,33},{2,34},{3,35},{4,36},{5,37},{6,38},{7,39},{8,40},{9,... | collective-permute-start | bytes 1228808 | tf_op jit(solution)/shard_map/ppermute | solution.py:48
  18.9 10.9 %collective-permute-start.6 = (bf16[2,160,640]{2,1,0:T(8,128)(2,1)S(1)}, bf16[2,160,640]{2,1,0:T(8,128)(2,1)S(1)}, u32[]{:S(2)}, u32[]{:S(2)}) collective-permute-start(bf16[2,160,640]{2,1,0:T(8,128)(2,1)S(1)} %pad_maximum_fusion.3), channel_id=1, source_target_pairs={{0,12},{1,13},{2,14},{3,15},{4,0},{5,1},{6,2},{7,3},{8,4},{9,5},{1... | collective-permute-start | bytes 1228808 | tf_op jit(solution)/shard_map/ppermute | solution.py:48
  22.7 11.0 %collective-permute-start.5 = (bf16[2,160,640]{2,1,0:T(8,128)(2,1)S(1)}, bf16[2,160,640]{2,1,0:T(8,128)(2,1)S(1)}, u32[]{:S(2)}, u32[]{:S(2)}) collective-permute-start(bf16[2,160,640]{2,1,0:T(8,128)(2,1)S(1)} %pad_maximum_fusion.3), channel_id=1, source_target_pairs={{0,4},{1,5},{2,6},{3,7},{4,8},{5,9},{6,10},{7,11},{8,12},{9,13},{1... | collective-permute-start | bytes 1228808 | tf_op jit(solution)/shard_map/ppermute | solution.py:48
  24.1 20.9 %copy-start.3 = (bf16[1,512,1280]{2,1,0:T(8,128)(2,1)S(1)}, bf16[1,512,1280]{2,1,0:T(8,128)(2,1)}, u32[]{:S(2)}) copy-start(bf16[1,512,1280]{2,1,0:T(8,128)(2,1)} %param.5) | copy-start | bytes 3932164
  24.1 24.5 %copy-start.1 = (s32[1,256]{1,0:T(1,128)S(1)}, s32[1,256]{1,0:T(1,128)}, u32[]{:S(2)}) copy-start(s32[1,256]{1,0:T(1,128)} %param.6) | copy-start | bytes 3076
  24.1 25.1 %copy-start.2 = (f32[1280]{0:T(1024)S(1)}, f32[1280]{0:T(1024)}, u32[]{:S(2)}) copy-start(f32[1280]{0:T(1024)} %param.7) | copy-start | bytes 15364
  26.2 11.5 %collective-permute-start.8 = (bf16[160,640]{1,0:T(8,128)(2,1)S(1)}, bf16[160,640]{1,0:T(8,128)(2,1)S(1)}, u32[]{:S(2)}, u32[]{:S(2)}) collective-permute-start(bf16[160,640]{1,0:T(8,128)(2,1)S(1)} %slice_bitcast_fusion.2), channel_id=1, source_target_pairs={{0,96},{1,97},{2,98},{3,99},{4,100},{5,101},{6,102},{7,103},{8,104... | collective-permute-start | bytes 614408 | tf_op jit(solution)/shard_map/ppermute | solution.py:48
  29.7 7.2 %collective-permute-start.7 = (bf16[160,640]{1,0:T(8,128)(2,1)S(1)}, bf16[160,640]{1,0:T(8,128)(2,1)S(1)}, u32[]{:S(2)}, u32[]{:S(2)}) collective-permute-start(bf16[160,640]{1,0:T(8,128)(2,1)S(1)} %slice_bitcast_fusion.3), channel_id=1, source_target_pairs={{0,32},{1,33},{2,34},{3,35},{4,36},{5,37},{6,38},{7,39},{8,40},{9,... | collective-permute-start | bytes 614408 | tf_op jit(solution)/shard_map/ppermute | solution.py:48
  29.8 10.4 %collective-permute-start.10 = (bf16[160,640]{1,0:T(8,128)(2,1)S(1)}, bf16[160,640]{1,0:T(8,128)(2,1)S(1)}, u32[]{:S(2)}, u32[]{:S(2)}) collective-permute-start(bf16[160,640]{1,0:T(8,128)(2,1)S(1)} %slice_bitcast_fusion), channel_id=1, source_target_pairs={{0,12},{1,13},{2,14},{3,15},{4,0},{5,1},{6,2},{7,3},{8,4},{9,5},{1... | collective-permute-start | bytes 614408 | tf_op jit(solution)/shard_map/ppermute | solution.py:48
  33.7 5.9 %collective-permute-start.9 = (bf16[160,640]{1,0:T(8,128)(2,1)S(1)}, bf16[160,640]{1,0:T(8,128)(2,1)S(1)}, u32[]{:S(2)}, u32[]{:S(2)}) collective-permute-start(bf16[160,640]{1,0:T(8,128)(2,1)S(1)} %slice_bitcast_fusion.1), channel_id=1, source_target_pairs={{0,4},{1,5},{2,6},{3,7},{4,8},{5,9},{6,10},{7,11},{8,12},{9,13},{1... | collective-permute-start | bytes 614408 | tf_op jit(solution)/shard_map/ppermute | solution.py:48
  40.9 35.7 %collective-permute-start.11 = (bf16[16,160,640]{2,1,0:T(8,128)(2,1)}, bf16[16,160,640]{2,1,0:T(8,128)(2,1)}, u32[]{:S(2)}, u32[]{:S(2)}) collective-permute-start(bf16[16,160,640]{2,1,0:T(8,128)(2,1)} %bitcast_dynamic-update-slice_fusion.mine_ref), channel_id=1, source_target_pairs={{0,16},{1,17},{2,18},{3,19},{4,20},{5,21},{6,22},{7,23},{8,24},{9,... | collective-permute-start | bytes 9830408 | tf_op jit(solution)/shard_map/ppermute | solution.py:48
  45.0 31.7 %collective-permute-start = (bf16[512,1280]{1,0:T(8,128)(2,1)S(1)}, bf16[512,1280]{1,0:T(8,128)(2,1)S(1)}, u32[]{:S(2)}, u32[]{:S(2)}) collective-permute-start(bf16[512,1280]{1,0:T(8,128)(2,1)S(1)} %bitcast.58), channel_id=1, source_target_pairs={{0,2},{2,4},{4,6},{6,8},{8,10},{10,12},{12,14},{14,16},{16,18},{18... | collective-permute-start | bytes 3932168 | tf_op jit(solution)/shard_map/ppermute | solution.py:301
  76.7 1.1 copy-start.4
  112.1 1.7 collective-permute-start.13
  114.9 70.4 %copy-start = (bf16[512,1280]{1,0:T(8,128)(2,1)S(1)}, bf16[512,1280]{1,0:T(8,128)(2,1)}, u32[]{:S(2)}) copy-start(bf16[512,1280]{1,0:T(8,128)(2,1)} %get-tuple-element.5) | copy-start | bytes 3932164
  144.4 13.7 %all-to-all-start.1 = ((bf16[32,4,1280]{2,1,0:T(4,128)(2,1)}), bf16[32,4,1280]{2,1,0:T(4,128)(2,1)S(1)}, u32[]{:S(2)}, u32[]{:S(2)}) async-start(bf16[32,4,1280]{2,1,0:T(4,128)(2,1)} %broadcast_in_dim.69), calls=%async_computation.1 | async-start | bytes 655360 | tf_op jit(solution)/shard_map/all_to_all | solution.py:339
  148.3 37.1 %collective-permute-start.12 = (bf16[512,1280]{1,0:T(8,128)(2,1)}, bf16[512,1280]{1,0:T(8,128)(2,1)S(1)}, u32[]{:S(2)}, u32[]{:S(2)}) collective-permute-start(bf16[512,1280]{1,0:T(8,128)(2,1)} %get-tuple-element.6), channel_id=1, source_target_pairs={{2,0},{4,2},{6,4},{8,6},{10,8},{12,10},{14,12},{16,14},{18,16},{20... | collective-permute-start | bytes 3932168 | tf_op jit(solution)/shard_map/ppermute | solution.py:327
  158.9 5.4 %collective-permute-start.14 = (bf16[128,1280]{1,0:T(8,128)(2,1)}, bf16[128,1280]{1,0:T(8,128)(2,1)}, u32[]{:S(2)}, u32[]{:S(2)}) collective-permute-start(bf16[128,1280]{1,0:T(8,128)(2,1)} %reshape.131), channel_id=1, source_target_pairs={{0,16},{16,0},{1,17},{17,1},{2,18},{18,2},{3,19},{19,3},{4,20},{20... | collective-permute-start | bytes 983048 | tf_op jit(solution)/shard_map/ppermute | solution.py:341

commit v3 on v2

--- a/solution.py
+++ b/solution.py
@@ -21,7 +21,6 @@
 WIDTHS = (256, 384, 512, 640, 768, 896, 1024)
 HALF = D // 2
 KR = 160
-CG = 640
 TOKEN_AXES = ("x", "co", "z", "yh")
 ALL_AXES = TOKEN_AXES + ("dp",)
 LOG2E = 1.4426950408889634
@@ -49,36 +48,32 @@
 
 
 def first_pieces(w_qkv, w_out):
-    x, co, z = (lax.axis_index(a) for a in ("x", "co", "z"))
+    x, co = lax.axis_index("x"), lax.axis_index("co")
     pieces = []
     for side in range(2):
-        a = lax.dynamic_slice(w_qkv, (x * KR, (co * 2 + side) * CG), (KR, CG))
-        b = lax.dynamic_slice(w_qkv, (z * KR, (4 + side) * CG), (KR, CG))
-        c = lax.dynamic_slice(w_out, (z * KR, side * CG), (KR, CG))
-        pieces.append(jnp.stack([a, jnp.where(co == 0, b, c)]))
+        part = co * 2 + side
+        q = lax.dynamic_slice(w_qkv, (x * KR, jnp.minimum(part, 2) * D), (KR, D))
+        o = lax.dynamic_slice(w_out, (x * KR, 0), (KR, D))
+        pieces.append(q if side == 0 else jnp.where(co == 0, q, o))
     return pieces
 
 
 def attention_kernel(
-    place_ref, ends_ref, own_ref, prev_ref, gain_ref, wqkv_ref, wout_ref, mine_ref, other_ref,
-    spans_ref, image_ref, lens_ref,
-    hprev_ref, hown_ref, pooled_ref,
-    x_ref, n_ref, w_ref, wo_ref, q_ref, k_ref, vt_ref, ctx_ref, bias_ref, hid_ref,
-    s0_ref, s1_ref, p0_ref, p1_ref, top0_ref, top1_ref, sem,
+    place_ref, ends_ref, own_ref, prev_ref, gain_ref, wqkv_ref, wout_ref, *refs
 ):
-    x, z, co, dp = (place_ref[i] for i in range(4))
+    mine_refs, other_refs, refs = refs[:8], refs[8:16], refs[16:]
+    (
+        spans_ref, image_ref, lens_ref, hprev_ref, hown_ref, pooled_ref,
+        x_ref, n_ref, w_ref, wo_ref, q_ref, k_ref, vt_ref, ctx_ref, bias_ref, hid_ref,
+        s0_ref, s1_ref, p0_ref, p1_ref, top0_ref, top1_ref, sem,
+    ) = refs
+    x, co, dp = (place_ref[i] for i in range(3))
     lo = ends_ref[0, LOCAL]
     hi = jnp.where(ends_ref[1, WIN - 1] == WIN, WIN, ends_ref[0, WIN - 1])
     base = (lo // 128) * 128
     blocks = (hi - base + QB - 1) // QB
 
     far = (1 - dp) * HALF
-    order = (
-        [(0, x, 0), (0, x, 1), (1, z, 0), (1, z, 1)]
-        + [(0, (x + 3) % 4, 0), (0, (x + 3) % 4, 1), (0, (x + 1) % 4, 0), (0, (x + 1) % 4, 1)]
-        + [(1, (z + 3) % 4, 0), (1, (z + 3) % 4, 1), (1, (z + 1) % 4, 0), (1, (z + 1) % 4, 1)]
-        + [(0, (x + 2) % 4, 0), (0, (x + 2) % 4, 1), (1, (z + 2) % 4, 0), (1, (z + 2) % 4, 1)]
-    )
 
     pltpu.make_async_copy(prev_ref, x_ref.at[pl.ds(0, LOCAL)], sem.at[0]).start()
     pltpu.make_async_copy(own_ref, x_ref.at[pl.ds(LOCAL, LOCAL)], sem.at[0]).start()
@@ -90,28 +85,28 @@
             sem.at[1 + part],
         )
 
-    def distant(part, source, slot, row, side):
+    def distant(part, source, row):
         target = wo_ref if part == 3 else w_ref
         rows = pl.ds(pl.multiple_of(far + row * KR, 16), KR)
-        cols = pl.ds((0 if part == 3 else part * D) + side * CG, CG)
-        return pltpu.make_async_copy(source.at[slot], target.at[rows, cols], sem.at[1 + part])
+        return pltpu.make_async_copy(source, target.at[rows, columns[part]], sem.at[1 + part])
 
     columns = [pl.ds(0, D), pl.ds(D, D), pl.ds(2 * D, D), pl.ds(0, D)]
     targets = [w_ref, w_ref, w_ref, wo_ref]
+    shift = (0, 3, 1, 2)
     for part in range(4):
         near(part, targets[part], columns[part]).start()
-        for source, core in ((mine_ref, co), (other_ref, 1 - co)):
-
-            @pl.when(core == part % 2)
-            def _(source=source, part=part):
-                for slot, (kind, row, side) in enumerate(order):
-                    if kind == part // 2:
-                        distant(part, source, slot, row, side).start()
+        for held, core in ((mine_refs, co), (other_refs, 1 - co)):
+
+            @pl.when(core == part // 2)
+            def _(held=held, part=part):
+                for slot in range(4):
+                    row = lax.rem(x + shift[slot], 4)
+                    distant(part, held[slot * 2 + part % 2], row).start()
 
     def arrived(part):
         near(part, targets[part], columns[part]).wait()
-        for slot in range(8):
-            distant(part, mine_ref, slot, 0, 0).wait()
+        for _ in range(4):
+            distant(part, mine_refs[0], 0).wait()
 
     x_ref[WIN:, :] = jnp.zeros((PAD - WIN, D), jnp.bfloat16)
     pltpu.make_async_copy(prev_ref, x_ref.at[pl.ds(0, LOCAL)], sem.at[0]).wait()
@@ -259,7 +254,7 @@
             jax.ShapeDtypeStruct((LOCAL, D), jnp.bfloat16),
             jax.ShapeDtypeStruct((IMAGES, D), jnp.bfloat16),
         ),
-        in_specs=[smem, smem, hbm, hbm, vmem, hbm, hbm, hbm, hbm, vmem, vmem, vmem],
+        in_specs=[smem, smem, hbm, hbm, vmem, hbm, hbm] + [hbm] * 16 + [vmem] * 3,
         out_specs=(vmem, vmem, vmem),
         scratch_shapes=[
             pltpu.VMEM((PAD, D), jnp.bfloat16),
@@ -285,7 +280,7 @@
             flops=30_000_000_000, bytes_accessed=20_000_000, transcendentals=10_000_000
         ),
         name="attention",
-    )(place, spans, own, prev, gain, w_qkv, w_out, mine, other, spans, image, lens)
+    )(place, spans, own, prev, gain, w_qkv, w_out, *mine, *other, spans, image, lens)
 
 
 def layer(tokens, lengths, ln_gain, w_qkv, w_out):
@@ -296,17 +291,18 @@
     p0, p1 = first_pieces(w_qkv, w_out)
     r0 = moved(p0, Y_UP)
     r1 = moved(p1, Y_DOWN)
-    a0 = jnp.stack([r0[0], r1[0]])
-    b0 = jnp.stack([r0[1], r1[1]])
     prev = lax.ppermute(own, TOKEN_AXES, [(i, i + 1) for i in range(63)])
-    a1, a2 = moved(a0, X_UP), moved(a0, X_DOWN)
-    b1, b2 = moved(b0, Z_UP), moved(b0, Z_DOWN)
-    a3, a4 = moved(a1[0], X_UP), moved(a2[1], X_DOWN)
-    b3, b4 = moved(b1[0], Z_UP), moved(b2[1], Z_DOWN)
-    mine = jnp.concatenate(
-        [a0, b0, a1, a2, b1, b2, a3[None], a4[None], b3[None], b4[None]], axis=0
-    )
-    other = moved(mine, CORE)
+    u0 = moved(r0, X_UP)
+    d1 = moved(r1, X_DOWN)
+    u1 = moved(r1, X_UP)
+    d0 = moved(r0, X_DOWN)
+    f0 = moved(u0, X_UP)
+    f1 = moved(d1, X_DOWN)
+    near = [moved(a, CORE) for a in (r0, r1)]
+    ring = [moved(a, CORE) for a in (u0, u1, d0, d1)]
+    last = [moved(a, CORE) for a in (f0, f1)]
+    mine = [r0, r1, u0, u1, d0, d1, f0, f1]
+    other = near + ring + last
 
     lens = lengths[0]
     ends = jnp.cumsum(lens)
@@ -318,7 +314,7 @@
     start = jnp.max(jnp.where(begun, offsets[:, None], -WIN), axis=0) - first
     end = jnp.min(jnp.where(ends[:, None] > at[None, :], ends[:, None], 1 << 20), axis=0) - first
     spans = jnp.stack([start, end]).astype(jnp.int32)
-    place = jnp.stack([x, z, co, dp]).astype(jnp.int32)
+    place = jnp.stack([x, co, dp]).astype(jnp.int32)
 
     hprev, hown, part = attention(
         place, spans, image[None, :WIN], lens.astype(jnp.float32)[:, None], own, prev,

time: 187 us -> 177 us (0.947)
  the two profiles are of different devices: /device:TPU:1 before, /device:TPU:9 now
where the time goes in v3:
time: 177 us; the launch traced here: 176 us
  waiting for transfers between devices  46.5 us (26%)
  blocking collectives  46.2 us (26%)
  starting transfers between devices  42.1 us (24%)
  Pallas kernels  23.9 us (14%)
  other arithmetic  7.97 us (5%)
  local copies, waits for them, and re-layouts  7.22 us (4%)
  between operations  2.18 us (1%)
    all_to_all x1, blocking collectives, layer(): rows = lax.all_to_all(kept, group, 0, 0, tiled=True).astype(jnp.float32)  46.2 us
    pallas_call x1, Pallas kernels, attention(): pl.pallas_call(attention_kernel, out_shape=(jax.ShapeDtypeStruct((LOCAL,...  23.9 us
    ppermute x16, waiting for transfers between devices, moved(): return lax.ppermute(piece, ALL_AXES, pairs)  23.2 us
    ppermute x16, starting transfers between devices, moved(): return lax.ppermute(piece, ALL_AXES, pairs)  21.5 us
    ppermute x1, waiting for transfers between devices, layer(): back = lax.ppermute(hprev, TOKEN_AXES, [(i + 1, i) for i in range(63)])  20.5 us
    ppermute x1, starting transfers between devices, layer(): back = lax.ppermute(hprev, TOKEN_AXES, [(i + 1, i) for i in range(63)])  8.58 us
    ppermute x1, starting transfers between devices, layer(): prev = lax.ppermute(own, TOKEN_AXES, [(i, i + 1) for i in range(63)])  5.12 us
    all_to_all x1, starting transfers between devices, layer(): lax.all_to_all(jnp.broadcast_to(rows[None], (32, 4, D)), group, 0, 0, til...  3.95 us
  transfers between devices with their start and end apart: 21, of which 8 were waited for; matrix products, arithmetic and copies ran while one was open for 4% of the time, Pallas kernels for 0%

profile of v3, /device:TPU:9, one launch (start us, length us, event | category | flops | bytes accessed | tf_op | source)
XLA Modules:
  0.0 176.1 jit_solution(8744812358072242797)
XLA Ops:
  0.7 1.4 dynamic-slice_select_fusion
  2.2 1.5 collective-permute-start.1
  3.7 8.9 %collective-permute-done.2.refs_1_ = bf16[160,1280]{1,0:T(8,128)(2,1)S(1)} collective-permute-done((bf16[160,1280]{1,0:T(8,128)(2,1)S(1)}, bf16[160,1280]{1,0:T(8,128)(2,1)S(1)}, u32[]{:S(2)}, u32[]{:S(2)}) %collective-permute-start.2) | collective-permute-done | bytes 409632 | tf_op jit(solution)/shard_map/ppermute | solution.py:47
  12.6 1.5 collective-permute-start.10
  14.1 2.5 %collective-permute-start.6 = (bf16[160,1280]{1,0:T(8,128)(2,1)S(1)}, bf16[160,1280]{1,0:T(8,128)(2,1)S(1)}, u32[]{:S(2)}, u32[]{:S(2)}) collective-permute-start(bf16[160,1280]{1,0:T(8,128)(2,1)S(1)} %collective-permute-done.2.refs_1_), channel_id=1, source_target_pairs={{0,96},{1,97},{2,98},{3,99},{4,100},{5,101},{6,102},{7,103},{8,104... | collective-permute-start | bytes 1228808 | tf_op jit(solution)/shard_map/ppermute | solution.py:47
  16.6 5.1 %collective-permute-start = (bf16[512,1280]{1,0:T(8,128)(2,1)S(1)}, bf16[512,1280]{1,0:T(8,128)(2,1)}, u32[]{:S(2)}, u32[]{:S(2)}) collective-permute-start(bf16[512,1280]{1,0:T(8,128)(2,1)S(1)} %bitcast.34), channel_id=1, source_target_pairs={{0,2},{2,4},{4,6},{6,8},{8,10},{10,12},{12,14},{14,16},{16,18},{18... | collective-permute-start | bytes 3932168 | tf_op jit(solution)/shard_map/ppermute | solution.py:294
  22.3 1.7 collective-permute-start.9
  24.0 2.8 %collective-permute-start.5 = (bf16[160,1280]{1,0:T(8,128)(2,1)S(1)}, bf16[160,1280]{1,0:T(8,128)(2,1)}, u32[]{:S(2)}, u32[]{:S(2)}) collective-permute-start(bf16[160,1280]{1,0:T(8,128)(2,1)S(1)} %collective-permute-done.1.refs_0_), channel_id=1, source_target_pairs={{0,96},{1,97},{2,98},{3,99},{4,100},{5,101},{6,102},{7,103},{8,104... | collective-permute-start | bytes 1228808 | tf_op jit(solution)/shard_map/ppermute | solution.py:47
  27.5 5.5 %collective-permute-done.4.refs_3_ = bf16[160,1280]{1,0:T(8,128)(2,1)} collective-permute-done((bf16[160,1280]{1,0:T(8,128)(2,1)S(1)}, bf16[160,1280]{1,0:T(8,128)(2,1)}, u32[]{:S(2)}, u32[]{:S(2)}) %collective-permute-start.4) | collective-permute-done | bytes 409632 | tf_op jit(solution)/shard_map/ppermute | solution.py:47
  33.0 4.6 %collective-permute-start.14 = (bf16[160,1280]{1,0:T(8,128)(2,1)S(1)}, bf16[160,1280]{1,0:T(8,128)(2,1)}, u32[]{:S(2)}, u32[]{:S(2)}) collective-permute-start(bf16[160,1280]{1,0:T(8,128)(2,1)S(1)} %collective-permute-done.6.refs_5_), channel_id=1, source_target_pairs={{0,16},{1,17},{2,18},{3,19},{4,20},{5,21},{6,22},{7,23},{8,24},{9,... | collective-permute-start | bytes 1228808 | tf_op jit(solution)/shard_map/ppermute | solution.py:47
  37.7 4.1 %collective-permute-done.3.refs_2_ = bf16[160,1280]{1,0:T(8,128)(2,1)} collective-permute-done((bf16[160,1280]{1,0:T(8,128)(2,1)S(1)}, bf16[160,1280]{1,0:T(8,128)(2,1)}, u32[]{:S(2)}, u32[]{:S(2)}) %collective-permute-start.3) | collective-permute-done | bytes 409632 | tf_op jit(solution)/shard_map/ppermute | solution.py:47
  43.9 2.5 %collective-permute-start.11 = (bf16[160,1280]{1,0:T(8,128)(2,1)}, bf16[160,1280]{1,0:T(8,128)(2,1)S(1)}, u32[]{:S(2)}, u32[]{:S(2)}) collective-permute-start(bf16[160,1280]{1,0:T(8,128)(2,1)} %collective-permute-done.3.refs_2_), channel_id=1, source_target_pairs={{0,16},{1,17},{2,18},{3,19},{4,20},{5,21},{6,22},{7,23},{8,24},{9,... | collective-permute-start | bytes 1228808 | tf_op jit(solution)/shard_map/ppermute | solution.py:47
  46.3 2.4 %collective-permute-done.8.refs_7_ = bf16[160,1280]{1,0:T(8,128)(2,1)} collective-permute-done((bf16[160,1280]{1,0:T(8,128)(2,1)S(1)}, bf16[160,1280]{1,0:T(8,128)(2,1)}, u32[]{:S(2)}, u32[]{:S(2)}) %collective-permute-start.8) | collective-permute-done | bytes 409632 | tf_op jit(solution)/shard_map/ppermute | solution.py:47
  49.6 2.3 %collective-permute-done.7.refs_6_ = bf16[160,1280]{1,0:T(8,128)(2,1)} collective-permute-done((bf16[160,1280]{1,0:T(8,128)(2,1)}, bf16[160,1280]{1,0:T(8,128)(2,1)}, u32[]{:S(2)}, u32[]{:S(2)}) %collective-permute-start.7) | collective-permute-done | bytes 409632 | tf_op jit(solution)/shard_map/ppermute | solution.py:47
  51.9 3.3 %collective-permute-start.15 = (bf16[160,1280]{1,0:T(8,128)(2,1)}, bf16[160,1280]{1,0:T(8,128)(2,1)S(1)}, u32[]{:S(2)}, u32[]{:S(2)}) collective-permute-start(bf16[160,1280]{1,0:T(8,128)(2,1)} %collective-permute-done.7.refs_6_), channel_id=1, source_target_pairs={{0,16},{1,17},{2,18},{3,19},{4,20},{5,21},{6,22},{7,23},{8,24},{9,... | collective-permute-start | bytes 1228808 | tf_op jit(solution)/shard_map/ppermute | solution.py:47
  58.8 23.9 %attention.1 = (bf16[512,1280]{1,0:T(8,128)(2,1)}, bf16[512,1280]{1,0:T(8,128)(2,1)}, bf16[256,1280]{1,0:T(8,128)(2,1)}) custom-call(s32[3]{0:T(128)} %pad_add_fusion.1.place_ref, s32[2,1280]{1,0:T(2,128)} %pad_add_fusion.ends_ref.refs_16_, bf16[512,1280]{1,0:T(8,128)(2,1)} %bitcast.33, bf16[512,1280]{1,0:T(8,128)(2,1)} %collective-permute-done.prev_ref, ...), custom_call_target="tpu_custom_call" | custom-call | flops 30000001024 | bytes 20000000 | tf_op jit(solution)/shard_map/attention/pallas_call | solution.py:250
  83.8 1.6 collective-permute-done.18
  86.5 46.2 %all_to_all.10 = bf16[32,4,1280]{2,1,0:T(4,128)(2,1)S(1)} all-to-all(bf16[32,4,1280]{2,1,0:T(4,128)(2,1)S(1)} %reshape.130), channel_id=1, replica_groups=mesh['x'=4,'co'=2,'z'=4,'yh'=2,'dp'=2] {'x','z','yh'}, dimensions={0} | all-to-all | bytes 655360 | tf_op jit(solution)/shard_map/all_to_all | solution.py:333
  133.7 4.0 %all-to-all-start.1 = ((bf16[32,4,1280]{2,1,0:T(4,128)(2,1)}), bf16[32,4,1280]{2,1,0:T(4,128)(2,1)S(1)}, u32[]{:S(2)}, u32[]{:S(2)}) async-start(bf16[32,4,1280]{2,1,0:T(4,128)(2,1)} %broadcast_in_dim.53), calls=%async_computation.1 | async-start | bytes 655360 | tf_op jit(solution)/shard_map/all_to_all | solution.py:335
  137.7 8.6 %collective-permute-start.17 = (bf16[512,1280]{1,0:T(8,128)(2,1)}, bf16[512,1280]{1,0:T(8,128)(2,1)S(1)}, u32[]{:S(2)}, u32[]{:S(2)}) collective-permute-start(bf16[512,1280]{1,0:T(8,128)(2,1)} %get-tuple-element.6), channel_id=1, source_target_pairs={{2,0},{4,2},{6,4},{8,6},{10,8},{12,10},{14,12},{16,14},{18,16},{20... | collective-permute-start | bytes 3932168 | tf_op jit(solution)/shard_map/ppermute | solution.py:323
  146.3 1.3 all-to-all-done.1
  147.7 2.8 %collective-permute-start.19 = (bf16[128,1280]{1,0:T(8,128)(2,1)S(1)}, bf16[128,1280]{1,0:T(8,128)(2,1)S(1)}, u32[]{:S(2)}, u32[]{:S(2)}) collective-permute-start(bf16[128,1280]{1,0:T(8,128)(2,1)S(1)} %reshape.131), channel_id=1, source_target_pairs={{0,16},{16,0},{1,17},{17,1},{2,18},{18,2},{3,19},{19,3},{4,20},{20... | collective-permute-start | bytes 983048 | tf_op jit(solution)/shard_map/ppermute | solution.py:337
  154.4 20.5 %collective-permute-done.17 = bf16[512,1280]{1,0:T(8,128)(2,1)S(1)} collective-permute-done((bf16[512,1280]{1,0:T(8,128)(2,1)}, bf16[512,1280]{1,0:T(8,128)(2,1)S(1)}, u32[]{:S(2)}, u32[]{:S(2)}) %collective-permute-start.17) | collective-permute-done | bytes 1310752 | tf_op jit(solution)/shard_map/ppermute | solution.py:323
  174.8 1.3 select_bitcast_fusion
  (74 shorter events, 13.7 us)
Async XLA Ops:
  0.7 41.2 %copy-start.2 = (f32[1280]{0:T(1024)S(1)}, f32[1280]{0:T(1024)}, u32[]{:S(2)}) copy-start(f32[1280]{0:T(1024)} %param.7) | copy-start | bytes 15364
  2.1 10.4 %collective-permute-start.2 = (bf16[160,1280]{1,0:T(8,128)(2,1)S(1)}, bf16[160,1280]{1,0:T(8,128)(2,1)S(1)}, u32[]{:S(2)}, u32[]{:S(2)}) collective-permute-start(bf16[160,1280]{1,0:T(8,128)(2,1)S(1)} %get-tuple-element.13), channel_id=1, source_target_pairs={{0,3},{1,0},{2,1},{3,2},{4,7},{5,4},{6,5},{7,6},{8,11},{9,8},{10,9... | collective-permute-start | bytes 1228808 | tf_op jit(solution)/shard_map/ppermute | solution.py:47
  2.2 20.1 %collective-permute-start.1 = (bf16[160,1280]{1,0:T(8,128)(2,1)S(1)}, bf16[160,1280]{1,0:T(8,128)(2,1)S(1)}, u32[]{:S(2)}, u32[]{:S(2)}) collective-permute-start(bf16[160,1280]{1,0:T(8,128)(2,1)S(1)} %get-tuple-element.14), channel_id=1, source_target_pairs={{0,1},{1,2},{2,3},{3,0},{4,5},{5,6},{6,7},{7,4},{8,9},{9,10},{10,1... | collective-permute-start | bytes 1228808 | tf_op jit(solution)/shard_map/ppermute | solution.py:47
  12.5 46.2 %copy-start.4 = (bf16[160,1280]{1,0:T(8,128)(2,1)}, bf16[160,1280]{1,0:T(8,128)(2,1)S(1)}, u32[]{:S(2)}) copy-start(bf16[160,1280]{1,0:T(8,128)(2,1)S(1)} %collective-permute-done.2.refs_1_) | copy-start | bytes 1228804
  12.6 11.5 %collective-permute-start.10 = (bf16[160,1280]{1,0:T(8,128)(2,1)S(1)}, bf16[160,1280]{1,0:T(8,128)(2,1)S(1)}, u32[]{:S(2)}, u32[]{:S(2)}) collective-permute-start(bf16[160,1280]{1,0:T(8,128)(2,1)S(1)} %collective-permute-done.2.refs_1_), channel_id=1, source_target_pairs={{0,16},{1,17},{2,18},{3,19},{4,20},{5,21},{6,22},{7,23},{8,24},{9,... | collective-permute-start | bytes 1228808 | tf_op jit(solution)/shard_map/ppermute | solution.py:47
  14.1 12.8 %collective-permute-start.6 = (bf16[160,1280]{1,0:T(8,128)(2,1)S(1)}, bf16[160,1280]{1,0:T(8,128)(2,1)S(1)}, u32[]{:S(2)}, u32[]{:S(2)}) collective-permute-start(bf16[160,1280]{1,0:T(8,128)(2,1)S(1)} %collective-permute-done.2.refs_1_), channel_id=1, source_target_pairs={{0,96},{1,97},{2,98},{3,99},{4,100},{5,101},{6,102},{7,103},{8,104... | collective-permute-start | bytes 1228808 | tf_op jit(solution)/shard_map/ppermute | solution.py:47
  16.6 39.9 %collective-permute-start = (bf16[512,1280]{1,0:T(8,128)(2,1)S(1)}, bf16[512,1280]{1,0:T(8,128)(2,1)}, u32[]{:S(2)}, u32[]{:S(2)}) collective-permute-start(bf16[512,1280]{1,0:T(8,128)(2,1)S(1)} %bitcast.34), channel_id=1, source_target_pairs={{0,2},{2,4},{4,6},{6,8},{8,10},{10,12},{12,14},{14,16},{16,18},{18... | collective-permute-start | bytes 3932168 | tf_op jit(solution)/shard_map/ppermute | solution.py:294
  22.2 10.8 %collective-permute-start.4 = (bf16[160,1280]{1,0:T(8,128)(2,1)S(1)}, bf16[160,1280]{1,0:T(8,128)(2,1)}, u32[]{:S(2)}, u32[]{:S(2)}) collective-permute-start(bf16[160,1280]{1,0:T(8,128)(2,1)S(1)} %collective-permute-done.2.refs_1_), channel_id=1, source_target_pairs={{0,32},{1,33},{2,34},{3,35},{4,36},{5,37},{6,38},{7,39},{8,40},{9,... | collective-permute-start | bytes 1228808 | tf_op jit(solution)/shard_map/ppermute | solution.py:47
  22.3 36.4 %copy-start.5 = (bf16[160,1280]{1,0:T(8,128)(2,1)}, bf16[160,1280]{1,0:T(8,128)(2,1)S(1)}, u32[]{:S(2)}) copy-start(bf16[160,1280]{1,0:T(8,128)(2,1)S(1)} %collective-permute-done.1.refs_0_) | copy-start | bytes 1228804
  22.3 15.2 %collective-permute-start.9 = (bf16[160,1280]{1,0:T(8,128)(2,1)S(1)}, bf16[160,1280]{1,0:T(8,128)(2,1)}, u32[]{:S(2)}, u32[]{:S(2)}) collective-permute-start(bf16[160,1280]{1,0:T(8,128)(2,1)S(1)} %collective-permute-done.1.refs_0_), channel_id=1, source_target_pairs={{0,16},{1,17},{2,18},{3,19},{4,20},{5,21},{6,22},{7,23},{8,24},{9,... | collective-permute-start | bytes 1228808 | tf_op jit(solution)/shard_map/ppermute | solution.py:47
  24.0 13.5 %collective-permute-start.5 = (bf16[160,1280]{1,0:T(8,128)(2,1)S(1)}, bf16[160,1280]{1,0:T(8,128)(2,1)}, u32[]{:S(2)}, u32[]{:S(2)}) collective-permute-start(bf16[160,1280]{1,0:T(8,128)(2,1)S(1)} %collective-permute-done.1.refs_0_), channel_id=1, source_target_pairs={{0,96},{1,97},{2,98},{3,99},{4,100},{5,101},{6,102},{7,103},{8,104... | collective-permute-start | bytes 1228808 | tf_op jit(solution)/shard_map/ppermute | solution.py:47
  26.9 14.9 %collective-permute-start.3 = (bf16[160,1280]{1,0:T(8,128)(2,1)S(1)}, bf16[160,1280]{1,0:T(8,128)(2,1)}, u32[]{:S(2)}, u32[]{:S(2)}) collective-permute-start(bf16[160,1280]{1,0:T(8,128)(2,1)S(1)} %collective-permute-done.1.refs_0_), channel_id=1, source_target_pairs={{0,32},{1,33},{2,34},{3,35},{4,36},{5,37},{6,38},{7,39},{8,40},{9,... | collective-permute-start | bytes 1228808 | tf_op jit(solution)/shard_map/ppermute | solution.py:47
  33.0 10.8 %collective-permute-start.14 = (bf16[160,1280]{1,0:T(8,128)(2,1)S(1)}, bf16[160,1280]{1,0:T(8,128)(2,1)}, u32[]{:S(2)}, u32[]{:S(2)}) collective-permute-start(bf16[160,1280]{1,0:T(8,128)(2,1)S(1)} %collective-permute-done.6.refs_5_), channel_id=1, source_target_pairs={{0,16},{1,17},{2,18},{3,19},{4,20},{5,21},{6,22},{7,23},{8,24},{9,... | collective-permute-start | bytes 1228808 | tf_op jit(solution)/shard_map/ppermute | solution.py:47
  37.6 11.1 %collective-permute-start.8 = (bf16[160,1280]{1,0:T(8,128)(2,1)S(1)}, bf16[160,1280]{1,0:T(8,128)(2,1)}, u32[]{:S(2)}, u32[]{:S(2)}) collective-permute-start(bf16[160,1280]{1,0:T(8,128)(2,1)S(1)} %collective-permute-done.6.refs_5_), channel_id=1, source_target_pairs={{0,96},{1,97},{2,98},{3,99},{4,100},{5,101},{6,102},{7,103},{8,104... | collective-permute-start | bytes 1228808 | tf_op jit(solution)/shard_map/ppermute | solution.py:47
  37.6 12.0 %collective-permute-start.12 = (bf16[160,1280]{1,0:T(8,128)(2,1)}, bf16[160,1280]{1,0:T(8,128)(2,1)}, u32[]{:S(2)}, u32[]{:S(2)}) collective-permute-start(bf16[160,1280]{1,0:T(8,128)(2,1)} %collective-permute-done.4.refs_3_), channel_id=1, source_target_pairs={{0,16},{1,17},{2,18},{3,19},{4,20},{5,21},{6,22},{7,23},{8,24},{9,... | collective-permute-start | bytes 1228808 | tf_op jit(solution)/shard_map/ppermute | solution.py:47
  41.8 10.1 %collective-permute-start.7 = (bf16[160,1280]{1,0:T(8,128)(2,1)}, bf16[160,1280]{1,0:T(8,128)(2,1)}, u32[]{:S(2)}, u32[]{:S(2)}) collective-permute-start(bf16[160,1280]{1,0:T(8,128)(2,1)} %collective-permute-done.3.refs_2_), channel_id=1, source_target_pairs={{0,32},{1,33},{2,34},{3,35},{4,36},{5,37},{6,38},{7,39},{8,40},{9,... | collective-permute-start | bytes 1228808 | tf_op jit(solution)/shard_map/ppermute | solution.py:47
  43.9 12.6 %collective-permute-start.11 = (bf16[160,1280]{1,0:T(8,128)(2,1)}, bf16[160,1280]{1,0:T(8,128)(2,1)S(1)}, u32[]{:S(2)}, u32[]{:S(2)}) collective-permute-start(bf16[160,1280]{1,0:T(8,128)(2,1)} %collective-permute-done.3.refs_2_), channel_id=1, source_target_pairs={{0,16},{1,17},{2,18},{3,19},{4,20},{5,21},{6,22},{7,23},{8,24},{9,... | collective-permute-start | bytes 1228808 | tf_op jit(solution)/shard_map/ppermute | solution.py:47
  48.7 7.7 %collective-permute-start.13 = (bf16[160,1280]{1,0:T(8,128)(2,1)}, bf16[160,1280]{1,0:T(8,128)(2,1)S(1)}, u32[]{:S(2)}, u32[]{:S(2)}) collective-permute-start(bf16[160,1280]{1,0:T(8,128)(2,1)} %collective-permute-done.5.refs_4_), channel_id=1, source_target_pairs={{0,16},{1,17},{2,18},{3,19},{4,20},{5,21},{6,22},{7,23},{8,24},{9,... | collective-permute-start | bytes 1228808 | tf_op jit(solution)/shard_map/ppermute | solution.py:47
  49.6 7.6 %collective-permute-start.16 = (bf16[160,1280]{1,0:T(8,128)(2,1)}, bf16[160,1280]{1,0:T(8,128)(2,1)S(1)}, u32[]{:S(2)}, u32[]{:S(2)}) collective-permute-start(bf16[160,1280]{1,0:T(8,128)(2,1)} %collective-permute-done.8.refs_7_), channel_id=1, source_target_pairs={{0,16},{1,17},{2,18},{3,19},{4,20},{5,21},{6,22},{7,23},{8,24},{9,... | collective-permute-start | bytes 1228808 | tf_op jit(solution)/shard_map/ppermute | solution.py:47
  51.9 6.1 %collective-permute-start.15 = (bf16[160,1280]{1,0:T(8,128)(2,1)}, bf16[160,1280]{1,0:T(8,128)(2,1)S(1)}, u32[]{:S(2)}, u32[]{:S(2)}) collective-permute-start(bf16[160,1280]{1,0:T(8,128)(2,1)} %collective-permute-done.7.refs_6_), channel_id=1, source_target_pairs={{0,16},{1,17},{2,18},{3,19},{4,20},{5,21},{6,22},{7,23},{8,24},{9,... | collective-permute-start | bytes 1228808 | tf_op jit(solution)/shard_map/ppermute | solution.py:47
  83.7 1.7 collective-permute-start.18
  133.7 13.8 %all-to-all-start.1 = ((bf16[32,4,1280]{2,1,0:T(4,128)(2,1)}), bf16[32,4,1280]{2,1,0:T(4,128)(2,1)S(1)}, u32[]{:S(2)}, u32[]{:S(2)}) async-start(bf16[32,4,1280]{2,1,0:T(4,128)(2,1)} %broadcast_in_dim.53), calls=%async_computation.1 | async-start | bytes 655360 | tf_op jit(solution)/shard_map/all_to_all | solution.py:335
  137.7 37.1 %collective-permute-start.17 = (bf16[512,1280]{1,0:T(8,128)(2,1)}, bf16[512,1280]{1,0:T(8,128)(2,1)S(1)}, u32[]{:S(2)}, u32[]{:S(2)}) collective-permute-start(bf16[512,1280]{1,0:T(8,128)(2,1)} %get-tuple-element.6), channel_id=1, source_target_pairs={{2,0},{4,2},{6,4},{8,6},{10,8},{12,10},{14,12},{16,14},{18,16},{20... | collective-permute-start | bytes 3932168 | tf_op jit(solution)/shard_map/ppermute | solution.py:323
  147.7 5.4 %collective-permute-start.19 = (bf16[128,1280]{1,0:T(8,128)(2,1)S(1)}, bf16[128,1280]{1,0:T(8,128)(2,1)S(1)}, u32[]{:S(2)}, u32[]{:S(2)}) collective-permute-start(bf16[128,1280]{1,0:T(8,128)(2,1)S(1)} %reshape.131), channel_id=1, source_target_pairs={{0,16},{16,0},{1,17},{17,1},{2,18},{18,2},{3,19},{19,3},{4,20},{20... | collective-permute-start | bytes 983048 | tf_op jit(solution)/shard_map/ppermute | solution.py:337
  (9 other events, 129.8 us)

commit v4 on v3

--- a/solution.py
+++ b/solution.py
@@ -1,3 +1,4 @@
+import functools
 import itertools
 
 import jax
@@ -15,10 +16,10 @@
 D = HEADS * SIZE
 LOCAL = 512
 WIN = 2 * LOCAL
-PAD = WIN + 256
 QB = 256
 IMAGES = 256
-WIDTHS = (256, 384, 512, 640, 768, 896, 1024)
+EDGE_WIDTHS = (256, 384, 512, 640)
+OWN_WIDTHS = (256, 384, 512)
 HALF = D // 2
 KR = 160
 TOKEN_AXES = ("x", "co", "z", "yh")
@@ -41,6 +42,9 @@
 Z_UP = permutation(lambda x, co, z, y: (x, co, (z + 1) % 4, y))
 Z_DOWN = permutation(lambda x, co, z, y: (x, co, (z - 1) % 4, y))
 CORE = permutation(lambda x, co, z, y: (x, 1 - co, z, y))
+
+
+WRAPS = [i for i in range(63) if i % 16 == 15]
 
 
 def moved(piece, pairs):
@@ -58,25 +62,42 @@
     return pieces
 
 
-def attention_kernel(
-    place_ref, ends_ref, own_ref, prev_ref, gain_ref, wqkv_ref, wout_ref, *refs
-):
-    mine_refs, other_refs, refs = refs[:8], refs[8:16], refs[16:]
+def attention_kernel(edge, place_ref, ends_ref, *refs):
+    widths = EDGE_WIDTHS if edge else OWN_WIDTHS
+    window = WIN if edge else LOCAL
+    if edge:
+        prev_ref, late_ref, refs = refs[0], refs[1], refs[2:]
+    own_ref, gain_ref, wqkv_ref, wout_ref, refs = *refs[:4], refs[4:]
+    mine_refs, other_refs, spans_ref, refs = refs[:8], refs[8:16], refs[16], refs[17:]
+    if edge:
+        hprev_ref, hown_ref, sum_ref, refs = *refs[:3], refs[3:]
+    else:
+        image_ref, lens_ref, hedge_ref, sum_ref, hown_ref, pooled_ref, refs = *refs[:6], refs[6:]
     (
-        spans_ref, image_ref, lens_ref, hprev_ref, hown_ref, pooled_ref,
         x_ref, n_ref, w_ref, wo_ref, q_ref, k_ref, vt_ref, ctx_ref, bias_ref, hid_ref,
         s0_ref, s1_ref, p0_ref, p1_ref, top0_ref, top1_ref, sem,
     ) = refs
-    x, co, dp = (place_ref[i] for i in range(3))
-    lo = ends_ref[0, LOCAL]
-    hi = jnp.where(ends_ref[1, WIN - 1] == WIN, WIN, ends_ref[0, WIN - 1])
+    x, co, dp, lo, hi, wrap = (place_ref[i] for i in range(6))
     base = (lo // 128) * 128
     blocks = (hi - base + QB - 1) // QB
 
     far = (1 - dp) * HALF
 
-    pltpu.make_async_copy(prev_ref, x_ref.at[pl.ds(0, LOCAL)], sem.at[0]).start()
-    pltpu.make_async_copy(own_ref, x_ref.at[pl.ds(LOCAL, LOCAL)], sem.at[0]).start()
+    inputs = [pltpu.make_async_copy(own_ref, x_ref.at[pl.ds(window - LOCAL, LOCAL)], sem.at[0])]
+    inputs[0].start()
+    if edge:
+        inputs.append(pltpu.make_async_copy(prev_ref, x_ref.at[pl.ds(0, LOCAL)], sem.at[0]))
+
+        @pl.when(wrap == 0)
+        def _():
+            inputs[1].start()
+
+        @pl.when(wrap == 1)
+        def _():
+            pltpu.make_async_copy(late_ref, x_ref.at[pl.ds(0, LOCAL)], sem.at[0]).start()
+    else:
+        inputs.append(pltpu.make_async_copy(hedge_ref, hid_ref.at[pl.ds(0, LOCAL)], sem.at[5]))
+        inputs[1].start()
 
     def near(part, target, cols):
         return pltpu.make_async_copy(
@@ -108,9 +129,9 @@
         for _ in range(4):
             distant(part, mine_refs[0], 0).wait()
 
-    x_ref[WIN:, :] = jnp.zeros((PAD - WIN, D), jnp.bfloat16)
-    pltpu.make_async_copy(prev_ref, x_ref.at[pl.ds(0, LOCAL)], sem.at[0]).wait()
-    pltpu.make_async_copy(own_ref, x_ref.at[pl.ds(LOCAL, LOCAL)], sem.at[0]).wait()
+    x_ref[window:, :] = jnp.zeros((x_ref.shape[0] - window, D), jnp.bfloat16)
+    for copy in inputs:
+        copy.wait()
 
     def block_rows(j):
         row0 = pl.multiple_of(base + j * QB, 128)
@@ -128,7 +149,8 @@
     lax.fori_loop(0, blocks, normalize, 0)
     k_ref[...] = jnp.zeros_like(k_ref)
     vt_ref[...] = jnp.zeros_like(vt_ref)
-    hid_ref[...] = jnp.zeros_like(hid_ref)
+    if edge:
+        hid_ref[...] = jnp.zeros_like(hid_ref)
 
     def project_q(j, carry):
         _, rows = block_rows(j)
@@ -166,8 +188,8 @@
         need = most - k0
         start = spans_ref[0:1, rows]
         end = spans_ref[1:2, rows]
-        for i, width in enumerate(WIDTHS):
-            above = WIDTHS[i - 1] if i else 0
+        for i, width in enumerate(widths):
+            above = widths[i - 1] if i else 0
 
             @pl.when((need > above) & (need <= width))
             def _(width=width):
@@ -177,12 +199,12 @@
 
                 def scores(h, s_ref, top_ref):
                     w0 = pl.multiple_of(jnp.minimum((h * SIZE) // 128 * 128, D - 256), 128)
-                    window = pl.ds(w0, 256)
+                    lanes = pl.ds(w0, 256)
                     lane = lax.broadcasted_iota(jnp.int32, (1, 256), 1) + (w0 - h * SIZE)
                     inside = jnp.where((lane >= 0) & (lane < SIZE), 1.0, 0.0)
-                    q = q_ref[rows, window] * inside.astype(jnp.bfloat16)
+                    q = q_ref[rows, lanes] * inside.astype(jnp.bfloat16)
                     s = lax.dot_general(
-                        k_ref[keys, window], q, (((1,), (1,)), ((), ())),
+                        k_ref[keys, lanes], q, (((1,), (1,)), ((), ())),
                         preferred_element_type=jnp.float32,
                     )
                     s = s + bias_ref[0:width, :]
@@ -225,62 +247,79 @@
         )
         hidden = x_ref[rows, :].astype(jnp.float32) + mixed
         at = lax.broadcasted_iota(jnp.int32, (QB, D), 0) + row0
-        hidden = jnp.where((at >= lo) & (at < hi), hidden, 0.0)
-        hid_ref[rows, :] = hidden.astype(jnp.bfloat16)
+        inside = (at >= lo) & (at < hi)
+        hidden = hidden.astype(jnp.bfloat16)
+        if edge:
+            hid_ref[rows, :] = jnp.where(inside, hidden, jnp.zeros_like(hidden))
+        else:
+            hid_ref[rows, :] = jnp.where(inside, hidden, hid_ref[rows, :])
         return carry
 
     lax.fori_loop(0, blocks, attend, 0)
 
-    hprev_ref[...] = hid_ref[0:LOCAL, :]
-    hown_ref[...] = hid_ref[LOCAL:WIN, :]
-    label = lax.broadcasted_iota(jnp.int32, (IMAGES, WIN), 0)
-    at = lax.broadcasted_iota(jnp.int32, (IMAGES, WIN), 1)
+    if edge:
+        hprev_ref[...] = hid_ref[0:LOCAL, :]
+        hown_ref[...] = hid_ref[LOCAL:WIN, :]
+        sum_ref[...] = jnp.dot(
+            jnp.ones((8, WIN), jnp.bfloat16), hid_ref[0:WIN, :], preferred_element_type=jnp.float32
+        )
+        return
+    hown_ref[...] = hid_ref[0:LOCAL, :]
+    label = lax.broadcasted_iota(jnp.int32, (IMAGES, LOCAL), 0)
+    at = lax.broadcasted_iota(jnp.int32, (IMAGES, LOCAL), 1)
     member = (label == image_ref[...]) & (at >= lo) & (at < hi)
     sums = jnp.dot(
-        jnp.where(member, 1.0, 0.0).astype(jnp.bfloat16), hid_ref[0:WIN, :],
+        jnp.where(member, 1.0, 0.0).astype(jnp.bfloat16), hid_ref[0:LOCAL, :],
         preferred_element_type=jnp.float32,
     )
+    label = lax.broadcasted_iota(jnp.int32, (IMAGES, D), 0)
+    sums = sums + jnp.where(label == place_ref[6], sum_ref[0:1, :], 0.0)
     pooled_ref[...] = (sums / lens_ref[...]).astype(jnp.bfloat16)
 
 
-def attention(place, spans, image, lens, own, prev, gain, w_qkv, w_out, mine, other):
+def attention(edge, place, spans, inputs, gain, weights, extra):
     hbm = pl.BlockSpec(memory_space=pltpu.HBM)
     vmem = pl.BlockSpec(memory_space=pltpu.VMEM)
     smem = pl.BlockSpec(memory_space=pltpu.SMEM)
+    rows = WIN + 256 if edge else LOCAL + 256
+    width = (EDGE_WIDTHS if edge else OWN_WIDTHS)[-1]
+    hidden = jax.ShapeDtypeStruct((LOCAL, D), jnp.bfloat16)
+    if edge:
+        outs = (hidden, hidden, jax.ShapeDtypeStruct((8, D), jnp.float32))
+        tail = []
+    else:
+        outs = (hidden, jax.ShapeDtypeStruct((IMAGES, D), jnp.bfloat16))
+        tail = [vmem, vmem, hbm, vmem]
     return pl.pallas_call(
-        attention_kernel,
-        out_shape=(
-            jax.ShapeDtypeStruct((LOCAL, D), jnp.bfloat16),
-            jax.ShapeDtypeStruct((LOCAL, D), jnp.bfloat16),
-            jax.ShapeDtypeStruct((IMAGES, D), jnp.bfloat16),
-        ),
-        in_specs=[smem, smem, hbm, hbm, vmem, hbm, hbm] + [hbm] * 16 + [vmem] * 3,
-        out_specs=(vmem, vmem, vmem),
+        functools.partial(attention_kernel, edge),
+        out_shape=outs,
+        in_specs=[smem, smem] + [hbm] * len(inputs) + [vmem] + [hbm] * 18 + [vmem] + tail,
+        out_specs=(vmem,) * len(outs),
         scratch_shapes=[
-            pltpu.VMEM((PAD, D), jnp.bfloat16),
-            pltpu.VMEM((PAD, D), jnp.bfloat16),
+            pltpu.VMEM((rows, D), jnp.bfloat16),
+            pltpu.VMEM((rows, D), jnp.bfloat16),
             pltpu.VMEM((D, 3 * D), jnp.bfloat16),
             pltpu.VMEM((D, D), jnp.bfloat16),
-            pltpu.VMEM((PAD, D), jnp.bfloat16),
-            pltpu.VMEM((PAD, D), jnp.bfloat16),
-            pltpu.VMEM((HEADS * VROWS, PAD), jnp.bfloat16),
+            pltpu.VMEM((rows, D), jnp.bfloat16),
+            pltpu.VMEM((rows, D), jnp.bfloat16),
+            pltpu.VMEM((HEADS * VROWS, rows), jnp.bfloat16),
             pltpu.VMEM((D, QB), jnp.bfloat16),
-            pltpu.VMEM((WIDTHS[-1], QB), jnp.float32),
-            pltpu.VMEM((PAD, D), jnp.bfloat16),
-            pltpu.VMEM((WIDTHS[-1], QB), jnp.float32),
-            pltpu.VMEM((WIDTHS[-1], QB), jnp.float32),
-            pltpu.VMEM((WIDTHS[-1], QB), jnp.bfloat16),
-            pltpu.VMEM((WIDTHS[-1], QB), jnp.bfloat16),
+            pltpu.VMEM((width, QB), jnp.float32),
+            pltpu.VMEM((rows, D), jnp.bfloat16),
+            pltpu.VMEM((width, QB), jnp.float32),
+            pltpu.VMEM((width, QB), jnp.float32),
+            pltpu.VMEM((width, QB), jnp.bfloat16),
+            pltpu.VMEM((width, QB), jnp.bfloat16),
             pltpu.VMEM((1, QB), jnp.float32),
             pltpu.VMEM((1, QB), jnp.float32),
-            pltpu.SemaphoreType.DMA((5,)),
+            pltpu.SemaphoreType.DMA((6,)),
         ],
-        compiler_params=pltpu.CompilerParams(vmem_limit_bytes=60 * 2**20),
+        compiler_params=pltpu.CompilerParams(vmem_limit_bytes=50 * 2**20),
         cost_estimate=pl.CostEstimate(
-            flops=30_000_000_000, bytes_accessed=20_000_000, transcendentals=10_000_000
+            flops=15_000_000_000, bytes_accessed=20_000_000, transcendentals=5_000_000
         ),
-        name="attention",
-    )(place, spans, own, prev, gain, w_qkv, w_out, *mine, *other, spans, image, lens)
+        name="edge_attention" if edge else "own_attention",
+    )(place, spans, *inputs, gain, *weights, spans, *extra)
 
 
 def layer(tokens, lengths, ln_gain, w_qkv, w_out):
@@ -289,11 +328,13 @@
     own = tokens[0]
 
     p0, p1 = first_pieces(w_qkv, w_out)
+    lent = lax.ppermute(own, TOKEN_AXES, [(i, i + 8) for i in WRAPS])
     r0 = moved(p0, Y_UP)
     r1 = moved(p1, Y_DOWN)
-    prev = lax.ppermute(own, TOKEN_AXES, [(i, i + 1) for i in range(63)])
+    prev = lax.ppermute(own, TOKEN_AXES, [(i, i + 1) for i in range(63) if i not in WRAPS])
     u0 = moved(r0, X_UP)
     d1 = moved(r1, X_DOWN)
+    late = lax.ppermute(lent, TOKEN_AXES, [(i + 8, i + 1) for i in WRAPS])
     u1 = moved(r1, X_UP)
     d0 = moved(r0, X_DOWN)
     f0 = moved(u0, X_UP)
@@ -308,19 +349,29 @@
     ends = jnp.cumsum(lens)
     offsets = ends - lens
     first = (shard - 1) * LOCAL
-    at = first + jnp.arange(PAD, dtype=jnp.int32)
+    at = first + jnp.arange(WIN + 256, dtype=jnp.int32)
     begun = offsets[:, None] <= at[None, :]
     image = jnp.sum(begun.astype(jnp.int32), axis=0) - 1
     start = jnp.max(jnp.where(begun, offsets[:, None], -WIN), axis=0) - first
     end = jnp.min(jnp.where(ends[:, None] > at[None, :], ends[:, None], 1 << 20), axis=0) - first
     spans = jnp.stack([start, end]).astype(jnp.int32)
-    place = jnp.stack([x, co, dp]).astype(jnp.int32)
-
-    hprev, hown, part = attention(
-        place, spans, image[None, :WIN], lens.astype(jnp.float32)[:, None], own, prev,
-        ln_gain[None], w_qkv, w_out, mine, other,
+    low = start[LOCAL]
+    cut = jnp.where(low < LOCAL, end[LOCAL], LOCAL)
+    limit = jnp.where(end[WIN - 1] == WIN, WIN, start[WIN - 1])
+    wrap = (co + z + yh == 0) & (x > 0)
+    places = [
+        jnp.stack([x, co, dp, lo, hi, wrap, image[LOCAL]]).astype(jnp.int32)
+        for lo, hi in ((low, cut), (cut - LOCAL, limit - LOCAL))
+    ]
+    gain = ln_gain[None]
+    weights = [w_qkv, w_out, *mine, *other]
+
+    hprev, hedge, total = attention(True, places[0], spans, [prev, late, own], gain, weights, [])
+    back = lax.ppermute(hprev, TOKEN_AXES, [(i + 1, i) for i in range(63)])
+    hown, part = attention(
+        False, places[1], spans[:, LOCAL:] - LOCAL, [own], gain, weights,
+        [image[None, LOCAL:WIN], lens.astype(jnp.float32)[:, None], hedge, total],
     )
-    back = lax.ppermute(hprev, TOKEN_AXES, [(i + 1, i) for i in range(63)])
 
     swap = [(0, 1), (1, 0)]
     group = ("x", "z", "yh")
@@ -338,8 +389,7 @@
     pooled = jnp.where(co == 0, jnp.stack([half, rest]), jnp.stack([rest, half]))
     pooled = pooled.reshape(1, IMAGES, D).astype(jnp.float32)
 
-    limit = jnp.where(end[WIN - 1] == WIN, WIN, start[WIN - 1]) - LOCAL
-    here = jnp.arange(LOCAL, dtype=jnp.int32)[:, None] < limit
+    here = jnp.arange(LOCAL, dtype=jnp.int32)[:, None] < limit - LOCAL
     hidden = jnp.where(here, hown, back)[None]
     return hidden, pooled
 

time: 177 us -> 197 us (1.11)
  the two profiles are of different devices: /device:TPU:9 before, /device:TPU:1 now
where the time goes in v4:
time: 197 us; the launch traced here: 196 us
  waiting for transfers between devices  54.6 us (28%)
  starting transfers between devices  44 us (22%)
  Pallas kernels  44 us (22%)
  blocking collectives  36.3 us (18%)
  local copies, waits for them, and re-layouts  8.05 us (4%)
  other arithmetic  6.08 us (3%)
  between operations  3.29 us (2%)
    pallas_call x2, Pallas kernels, attention(): pl.pallas_call(functools.partial(attention_kernel, edge), out_shape=outs,...  44 us
    all_to_all x1, blocking collectives, layer(): rows = lax.all_to_all(kept, group, 0, 0, tiled=True).astype(jnp.float32)  36.3 us
    ppermute x1, waiting for transfers between devices, layer(): back = lax.ppermute(hprev, TOKEN_AXES, [(i + 1, i) for i in range(63)])  21.8 us
    ppermute x16, starting transfers between devices, moved(): return lax.ppermute(piece, ALL_AXES, pairs)  21.6 us
    ppermute x16, waiting for transfers between devices, moved(): return lax.ppermute(piece, ALL_AXES, pairs)  18.6 us
    ppermute x1, waiting for transfers between devices, layer(): lax.ppermute(own, TOKEN_AXES, [(i, i + 1) for i in range(63) if i not in...  10.1 us
    ppermute x1, starting transfers between devices, layer(): back = lax.ppermute(hprev, TOKEN_AXES, [(i + 1, i) for i in range(63)])  8.52 us
  transfers between devices with their start and end apart: 23, of which 8 were waited for; matrix products, arithmetic and copies ran while one was open for 4% of the time, Pallas kernels for 0%

profile of v4, /device:TPU:1, one launch (start us, length us, event | category | flops | bytes accessed | tf_op | source)
XLA Modules:
  0.0 196.3 jit_solution(8600567712064391685)
XLA Ops:
  0.6 1.9 collective-permute-start.17
  2.5 1.3 dynamic-slice_select_fusion
  3.9 2.2 %collective-permute-start = (bf16[160,1280]{1,0:T(8,128)(2,1)S(1)}, bf16[160,1280]{1,0:T(8,128)(2,1)S(1)}, u32[]{:S(2)}, u32[]{:S(2)}) collective-permute-start(bf16[160,1280]{1,0:T(8,128)(2,1)S(1)} %get-tuple-element.18), channel_id=1, source_target_pairs={{0,1},{1,2},{2,3},{3,0},{4,5},{5,6},{6,7},{7,4},{8,9},{9,10},{10,1... | collective-permute-start | bytes 1228808 | tf_op jit(solution)/shard_map/ppermute | solution.py:51
  6.1 1.5 collective-permute-start.1
  7.6 9.0 %collective-permute-done.refs_6_.refs_4_ = bf16[160,1280]{1,0:T(8,128)(2,1)S(1)} collective-permute-done((bf16[160,1280]{1,0:T(8,128)(2,1)S(1)}, bf16[160,1280]{1,0:T(8,128)(2,1)S(1)}, u32[]{:S(2)}, u32[]{:S(2)}) %collective-permute-start) | collective-permute-done | bytes 409632 | tf_op jit(solution)/shard_map/ppermute | solution.py:51
  17.7 1.6 collective-permute-start.5
  19.3 2.7 %collective-permute-start.4 = (bf16[160,1280]{1,0:T(8,128)(2,1)S(1)}, bf16[160,1280]{1,0:T(8,128)(2,1)S(1)}, u32[]{:S(2)}, u32[]{:S(2)}) collective-permute-start(bf16[160,1280]{1,0:T(8,128)(2,1)S(1)} %collective-permute-done.refs_6_.refs_4_), channel_id=1, source_target_pairs={{0,96},{1,97},{2,98},{3,99},{4,100},{5,101},{6,102},{7,103},{8,104... | collective-permute-start | bytes 1228808 | tf_op jit(solution)/shard_map/ppermute | solution.py:51
  22.4 5.1 %collective-permute-done.2.refs_8_.refs_6_ = bf16[160,1280]{1,0:T(8,128)(2,1)S(1)} collective-permute-done((bf16[160,1280]{1,0:T(8,128)(2,1)S(1)}, bf16[160,1280]{1,0:T(8,128)(2,1)S(1)}, u32[]{:S(2)}, u32[]{:S(2)}) %collective-permute-start.2) | collective-permute-done | bytes 409632 | tf_op jit(solution)/shard_map/ppermute | solution.py:51
  27.5 4.0 %collective-permute-start.8 = (bf16[160,1280]{1,0:T(8,128)(2,1)S(1)}, bf16[160,1280]{1,0:T(8,128)(2,1)S(1)}, u32[]{:S(2)}, u32[]{:S(2)}) collective-permute-start(bf16[160,1280]{1,0:T(8,128)(2,1)S(1)} %collective-permute-done.refs_6_.refs_4_), channel_id=1, source_target_pairs={{0,16},{1,17},{2,18},{3,19},{4,20},{5,21},{6,22},{7,23},{8,24},{9,... | collective-permute-start | bytes 1228808 | tf_op jit(solution)/shard_map/ppermute | solution.py:51
  31.8 4.5 %collective-permute-done.3.refs_9_.refs_7_ = bf16[160,1280]{1,0:T(8,128)(2,1)S(1)} collective-permute-done((bf16[160,1280]{1,0:T(8,128)(2,1)S(1)}, bf16[160,1280]{1,0:T(8,128)(2,1)S(1)}, u32[]{:S(2)}, u32[]{:S(2)}) %collective-permute-start.3) | collective-permute-done | bytes 409632 | tf_op jit(solution)/shard_map/ppermute | solution.py:51
  36.2 2.7 %collective-permute-start.7 = (bf16[160,1280]{1,0:T(8,128)(2,1)S(1)}, bf16[160,1280]{1,0:T(8,128)(2,1)S(1)}, u32[]{:S(2)}, u32[]{:S(2)}) collective-permute-start(bf16[160,1280]{1,0:T(8,128)(2,1)S(1)} %collective-permute-done.5.refs_11_.refs_9_), channel_id=1, source_target_pairs={{0,96},{1,97},{2,98},{3,99},{4,100},{5,101},{6,102},{7,103},{8,104... | collective-permute-start | bytes 1228808 | tf_op jit(solution)/shard_map/ppermute | solution.py:51
  38.9 3.4 %collective-permute-start.16 = (bf16[512,1280]{1,0:T(8,128)(2,1)}, bf16[512,1280]{1,0:T(8,128)(2,1)}, u32[]{:S(2)}, u32[]{:S(2)}) collective-permute-start(bf16[512,1280]{1,0:T(8,128)(2,1)} %bitcast.35), channel_id=1, source_target_pairs={{0,2},{2,4},{4,6},{6,8},{8,10},{10,12},{12,14},{14,16},{16,18},{18... | collective-permute-start | bytes 3932168 | tf_op jit(solution)/shard_map/ppermute | solution.py:334
  42.4 1.7 collective-permute-start.18
  44.7 4.4 %collective-permute-start.10 = (bf16[160,1280]{1,0:T(8,128)(2,1)S(1)}, bf16[160,1280]{1,0:T(8,128)(2,1)}, u32[]{:S(2)}, u32[]{:S(2)}) collective-permute-start(bf16[160,1280]{1,0:T(8,128)(2,1)S(1)} %collective-permute-done.2.refs_8_.refs_6_), channel_id=1, source_target_pairs={{0,16},{1,17},{2,18},{3,19},{4,20},{5,21},{6,22},{7,23},{8,24},{9,... | collective-permute-start | bytes 1228808 | tf_op jit(solution)/shard_map/ppermute | solution.py:51
  55.6 1.3 stack.50.place_ref
  57.8 10.1 %collective-permute-done.16.refs_0_ = bf16[512,1280]{1,0:T(8,128)(2,1)} collective-permute-done((bf16[512,1280]{1,0:T(8,128)(2,1)}, bf16[512,1280]{1,0:T(8,128)(2,1)}, u32[]{:S(2)}, u32[]{:S(2)}) %collective-permute-start.16) | collective-permute-done | bytes 1310752 | tf_op jit(solution)/shard_map/ppermute | solution.py:334
  68.9 22.9 %edge_attention.1 = (bf16[512,1280]{1,0:T(8,128)(2,1)}, bf16[512,1280]{1,0:T(8,128)(2,1)}, f32[8,1280]{1,0:T(8,128)S(1)}) custom-call(s32[7]{0:T(128)S(1)} %stack.50.place_ref, s32[2,1280]{1,0:T(2,128)S(1)} %pad_add_fusion.ends_ref.refs_22_, bf16[512,1280]{1,0:T(8,128)(2,1)} %collective-permute-done.16.refs_0_, ...), custom_call_target="tpu_custom_call" | custom-call | flops 15000000512 | bytes 20000000 | tf_op jit(solution)/shard_map/edge_attention/pallas_call | solution.py:293
  91.8 21.1 %own_attention.1 = (bf16[512,1280]{1,0:T(8,128)(2,1)}, bf16[256,1280]{1,0:T(8,128)(2,1)}) custom-call(s32[7]{0:T(128)S(1)} %stack.48.place_ref, s32[2,768]{1,0:T(2,128)S(1)} %fusion.4.ends_ref.refs_20_, bf16[512,1280]{1,0:T(8,128)(2,1)} %bitcast.37, f32[1,1280]{1,0:T(1,128)S(1)} %broadcast_in_dim.50.refs_3_.refs_1_, bf16[640,3840]{1,0:T(8,128)(2,1)} %refs_2_.1, ...), custom_call_target="tpu_custom_call" | custom-call | flops 15000000512 | bytes 20000000 | tf_op jit(solution)/shard_map/own_attention/pallas_call | solution.py:293
  114.0 1.6 collective-permute-done.20
  116.8 36.3 %all_to_all.10 = bf16[32,4,1280]{2,1,0:T(4,128)(2,1)S(1)} all-to-all(bf16[32,4,1280]{2,1,0:T(4,128)(2,1)S(1)} %reshape.139), channel_id=1, replica_groups=mesh['x'=4,'co'=2,'z'=4,'yh'=2,'dp'=2] {'x','z','yh'}, dimensions={0} | all-to-all | bytes 655360 | tf_op jit(solution)/shard_map/all_to_all | solution.py:384
  154.1 3.9 %all-to-all-start.1 = ((bf16[32,4,1280]{2,1,0:T(4,128)(2,1)}), bf16[32,4,1280]{2,1,0:T(4,128)(2,1)S(1)}, u32[]{:S(2)}, u32[]{:S(2)}) async-start(bf16[32,4,1280]{2,1,0:T(4,128)(2,1)} %broadcast_in_dim.53), calls=%async_computation.1 | async-start | bytes 655360 | tf_op jit(solution)/shard_map/all_to_all | solution.py:386
  157.9 8.5 %collective-permute-start.19 = (bf16[512,1280]{1,0:T(8,128)(2,1)}, bf16[512,1280]{1,0:T(8,128)(2,1)S(1)}, u32[]{:S(2)}, u32[]{:S(2)}) collective-permute-start(bf16[512,1280]{1,0:T(8,128)(2,1)} %get-tuple-element.10), channel_id=1, source_target_pairs={{2,0},{4,2},{6,4},{8,6},{10,8},{12,10},{14,12},{16,14},{18,16},{20... | collective-permute-start | bytes 3932168 | tf_op jit(solution)/shard_map/ppermute | solution.py:370
  167.8 2.8 %collective-permute-start.21 = (bf16[128,1280]{1,0:T(8,128)(2,1)S(1)}, bf16[128,1280]{1,0:T(8,128)(2,1)S(1)}, u32[]{:S(2)}, u32[]{:S(2)}) collective-permute-start(bf16[128,1280]{1,0:T(8,128)(2,1)S(1)} %reshape.140), channel_id=1, source_target_pairs={{0,16},{16,0},{1,17},{17,1},{2,18},{18,2},{3,19},{19,3},{4,20},{20... | collective-permute-start | bytes 983048 | tf_op jit(solution)/shard_map/ppermute | solution.py:388
  173.2 21.8 %collective-permute-done.19 = bf16[512,1280]{1,0:T(8,128)(2,1)S(1)} collective-permute-done((bf16[512,1280]{1,0:T(8,128)(2,1)}, bf16[512,1280]{1,0:T(8,128)(2,1)S(1)}, u32[]{:S(2)}, u32[]{:S(2)}) %collective-permute-start.19) | collective-permute-done | bytes 1310752 | tf_op jit(solution)/shard_map/ppermute | solution.py:370
  (73 shorter events, 16.6 us)
Async XLA Ops:
  0.6 50.3 %copy-start.5 = (f32[1280]{0:T(1024)S(1)}, f32[1280]{0:T(1024)}, u32[]{:S(2)}) copy-start(f32[1280]{0:T(1024)} %param.7) | copy-start | bytes 15364
  0.6 41.7 %collective-permute-start.17 = (bf16[512,1280]{1,0:T(8,128)(2,1)}, bf16[512,1280]{1,0:T(8,128)(2,1)}, u32[]{:S(2)}, u32[]{:S(2)}) collective-permute-start(bf16[512,1280]{1,0:T(8,128)(2,1)} %bitcast.34), channel_id=1, source_target_pairs={{30,46},{62,78},{94,110},{31,47},{63,79},{95,111}} | collective-permute-start | bytes 3932168 | tf_op jit(solution)/shard_map/ppermute | solution.py:331
  3.9 12.7 %collective-permute-start = (bf16[160,1280]{1,0:T(8,128)(2,1)S(1)}, bf16[160,1280]{1,0:T(8,128)(2,1)S(1)}, u32[]{:S(2)}, u32[]{:S(2)}) collective-permute-start(bf16[160,1280]{1,0:T(8,128)(2,1)S(1)} %get-tuple-element.18), channel_id=1, source_target_pairs={{0,1},{1,2},{2,3},{3,0},{4,5},{5,6},{6,7},{7,4},{8,9},{9,10},{10,1... | collective-permute-start | bytes 1228808 | tf_op jit(solution)/shard_map/ppermute | solution.py:51
  6.1 11.6 %collective-permute-start.1 = (bf16[160,1280]{1,0:T(8,128)(2,1)S(1)}, bf16[160,1280]{1,0:T(8,128)(2,1)S(1)}, u32[]{:S(2)}, u32[]{:S(2)}) collective-permute-start(bf16[160,1280]{1,0:T(8,128)(2,1)S(1)} %get-tuple-element.17), channel_id=1, source_target_pairs={{0,3},{1,0},{2,1},{3,2},{4,7},{5,4},{6,5},{7,6},{8,11},{9,8},{10,9... | collective-permute-start | bytes 1228808 | tf_op jit(solution)/shard_map/ppermute | solution.py:51
  16.6 10.9 %collective-permute-start.2 = (bf16[160,1280]{1,0:T(8,128)(2,1)S(1)}, bf16[160,1280]{1,0:T(8,128)(2,1)S(1)}, u32[]{:S(2)}, u32[]{:S(2)}) collective-permute-start(bf16[160,1280]{1,0:T(8,128)(2,1)S(1)} %collective-permute-done.refs_6_.refs_4_), channel_id=1, source_target_pairs={{0,32},{1,33},{2,34},{3,35},{4,36},{5,37},{6,38},{7,39},{8,40},{9,... | collective-permute-start | bytes 1228808 | tf_op jit(solution)/shard_map/ppermute | solution.py:51
  17.7 14.0 %collective-permute-start.5 = (bf16[160,1280]{1,0:T(8,128)(2,1)S(1)}, bf16[160,1280]{1,0:T(8,128)(2,1)S(1)}, u32[]{:S(2)}, u32[]{:S(2)}) collective-permute-start(bf16[160,1280]{1,0:T(8,128)(2,1)S(1)} %collective-permute-done.1.refs_7_.refs_5_), channel_id=1, source_target_pairs={{0,96},{1,97},{2,98},{3,99},{4,100},{5,101},{6,102},{7,103},{8,104... | collective-permute-start | bytes 1228808 | tf_op jit(solution)/shard_map/ppermute | solution.py:51
  19.3 17.0 %collective-permute-start.3 = (bf16[160,1280]{1,0:T(8,128)(2,1)S(1)}, bf16[160,1280]{1,0:T(8,128)(2,1)S(1)}, u32[]{:S(2)}, u32[]{:S(2)}) collective-permute-start(bf16[160,1280]{1,0:T(8,128)(2,1)S(1)} %collective-permute-done.1.refs_7_.refs_5_), channel_id=1, source_target_pairs={{0,32},{1,33},{2,34},{3,35},{4,36},{5,37},{6,38},{7,39},{8,40},{9,... | collective-permute-start | bytes 1228808 | tf_op jit(solution)/shard_map/ppermute | solution.py:51
  19.3 17.0 %collective-permute-start.4 = (bf16[160,1280]{1,0:T(8,128)(2,1)S(1)}, bf16[160,1280]{1,0:T(8,128)(2,1)S(1)}, u32[]{:S(2)}, u32[]{:S(2)}) collective-permute-start(bf16[160,1280]{1,0:T(8,128)(2,1)S(1)} %collective-permute-done.refs_6_.refs_4_), channel_id=1, source_target_pairs={{0,96},{1,97},{2,98},{3,99},{4,100},{5,101},{6,102},{7,103},{8,104... | collective-permute-start | bytes 1228808 | tf_op jit(solution)/shard_map/ppermute | solution.py:51
  27.5 11.5 %collective-permute-start.8 = (bf16[160,1280]{1,0:T(8,128)(2,1)S(1)}, bf16[160,1280]{1,0:T(8,128)(2,1)S(1)}, u32[]{:S(2)}, u32[]{:S(2)}) collective-permute-start(bf16[160,1280]{1,0:T(8,128)(2,1)S(1)} %collective-permute-done.refs_6_.refs_4_), channel_id=1, source_target_pairs={{0,16},{1,17},{2,18},{3,19},{4,20},{5,21},{6,22},{7,23},{8,24},{9,... | collective-permute-start | bytes 1228808 | tf_op jit(solution)/shard_map/ppermute | solution.py:51
  31.7 13.0 %collective-permute-start.9 = (bf16[160,1280]{1,0:T(8,128)(2,1)S(1)}, bf16[160,1280]{1,0:T(8,128)(2,1)S(1)}, u32[]{:S(2)}, u32[]{:S(2)}) collective-permute-start(bf16[160,1280]{1,0:T(8,128)(2,1)S(1)} %collective-permute-done.1.refs_7_.refs_5_), channel_id=1, source_target_pairs={{0,16},{1,17},{2,18},{3,19},{4,20},{5,21},{6,22},{7,23},{8,24},{9,... | collective-permute-start | bytes 1228808 | tf_op jit(solution)/shard_map/ppermute | solution.py:51
  36.2 12.8 %collective-permute-start.6 = (bf16[160,1280]{1,0:T(8,128)(2,1)S(1)}, bf16[160,1280]{1,0:T(8,128)(2,1)S(1)}, u32[]{:S(2)}, u32[]{:S(2)}) collective-permute-start(bf16[160,1280]{1,0:T(8,128)(2,1)S(1)} %collective-permute-done.2.refs_8_.refs_6_), channel_id=1, source_target_pairs={{0,32},{1,33},{2,34},{3,35},{4,36},{5,37},{6,38},{7,39},{8,40},{9,... | collective-permute-start | bytes 1228808 | tf_op jit(solution)/shard_map/ppermute | solution.py:51
  36.2 13.1 %collective-permute-start.7 = (bf16[160,1280]{1,0:T(8,128)(2,1)S(1)}, bf16[160,1280]{1,0:T(8,128)(2,1)S(1)}, u32[]{:S(2)}, u32[]{:S(2)}) collective-permute-start(bf16[160,1280]{1,0:T(8,128)(2,1)S(1)} %collective-permute-done.5.refs_11_.refs_9_), channel_id=1, source_target_pairs={{0,96},{1,97},{2,98},{3,99},{4,100},{5,101},{6,102},{7,103},{8,104... | collective-permute-start | bytes 1228808 | tf_op jit(solution)/shard_map/ppermute | solution.py:51
  38.9 28.9 %collective-permute-start.16 = (bf16[512,1280]{1,0:T(8,128)(2,1)}, bf16[512,1280]{1,0:T(8,128)(2,1)}, u32[]{:S(2)}, u32[]{:S(2)}) collective-permute-start(bf16[512,1280]{1,0:T(8,128)(2,1)} %bitcast.35), channel_id=1, source_target_pairs={{0,2},{2,4},{4,6},{6,8},{8,10},{10,12},{12,14},{14,16},{16,18},{18... | collective-permute-start | bytes 3932168 | tf_op jit(solution)/shard_map/ppermute | solution.py:334
  42.4 25.5 %collective-permute-start.18 = (bf16[512,1280]{1,0:T(8,128)(2,1)}, bf16[512,1280]{1,0:T(8,128)(2,1)}, u32[]{:S(2)}, u32[]{:S(2)}) collective-permute-start(bf16[512,1280]{1,0:T(8,128)(2,1)} %collective-permute-done.17), channel_id=1, source_target_pairs={{46,32},{78,64},{110,96},{47,33},{79,65},{111,97}} | collective-permute-start | bytes 3932168 | tf_op jit(solution)/shard_map/ppermute | solution.py:337
  44.7 7.4 %collective-permute-start.10 = (bf16[160,1280]{1,0:T(8,128)(2,1)S(1)}, bf16[160,1280]{1,0:T(8,128)(2,1)}, u32[]{:S(2)}, u32[]{:S(2)}) collective-permute-start(bf16[160,1280]{1,0:T(8,128)(2,1)S(1)} %collective-permute-done.2.refs_8_.refs_6_), channel_id=1, source_target_pairs={{0,16},{1,17},{2,18},{3,19},{4,20},{5,21},{6,22},{7,23},{8,24},{9,... | collective-permute-start | bytes 1228808 | tf_op jit(solution)/shard_map/ppermute | solution.py:51
  49.0 3.4 %collective-permute-start.13 = (bf16[160,1280]{1,0:T(8,128)(2,1)S(1)}, bf16[160,1280]{1,0:T(8,128)(2,1)}, u32[]{:S(2)}, u32[]{:S(2)}) collective-permute-start(bf16[160,1280]{1,0:T(8,128)(2,1)S(1)} %collective-permute-done.5.refs_11_.refs_9_), channel_id=1, source_target_pairs={{0,16},{1,17},{2,18},{3,19},{4,20},{5,21},{6,22},{7,23},{8,24},{9,... | collective-permute-start | bytes 1228808 | tf_op jit(solution)/shard_map/ppermute | solution.py:51
  50.1 2.6 %collective-permute-start.11 = (bf16[160,1280]{1,0:T(8,128)(2,1)S(1)}, bf16[160,1280]{1,0:T(8,128)(2,1)}, u32[]{:S(2)}, u32[]{:S(2)}) collective-permute-start(bf16[160,1280]{1,0:T(8,128)(2,1)S(1)} %collective-permute-done.3.refs_9_.refs_7_), channel_id=1, source_target_pairs={{0,16},{1,17},{2,18},{3,19},{4,20},{5,21},{6,22},{7,23},{8,24},{9,... | collective-permute-start | bytes 1228808 | tf_op jit(solution)/shard_map/ppermute | solution.py:51
  52.1 5.7 %collective-permute-start.12 = (bf16[160,1280]{1,0:T(8,128)(2,1)S(1)}, bf16[160,1280]{1,0:T(8,128)(2,1)}, u32[]{:S(2)}, u32[]{:S(2)}) collective-permute-start(bf16[160,1280]{1,0:T(8,128)(2,1)S(1)} %collective-permute-done.4.refs_10_.refs_8_), channel_id=1, source_target_pairs={{0,16},{1,17},{2,18},{3,19},{4,20},{5,21},{6,22},{7,23},{8,24},{9,... | collective-permute-start | bytes 1228808 | tf_op jit(solution)/shard_map/ppermute | solution.py:51
  52.5 15.4 %collective-permute-start.14 = (bf16[160,1280]{1,0:T(8,128)(2,1)S(1)}, bf16[160,1280]{1,0:T(8,128)(2,1)}, u32[]{:S(2)}, u32[]{:S(2)}) collective-permute-start(bf16[160,1280]{1,0:T(8,128)(2,1)S(1)} %collective-permute-done.6.refs_12_.refs_10_), channel_id=1, source_target_pairs={{0,16},{1,17},{2,18},{3,19},{4,20},{5,21},{6,22},{7,23},{8,24},{9,... | collective-permute-start | bytes 1228808 | tf_op jit(solution)/shard_map/ppermute | solution.py:51
  52.7 15.2 %collective-permute-start.15 = (bf16[160,1280]{1,0:T(8,128)(2,1)}, bf16[160,1280]{1,0:T(8,128)(2,1)}, u32[]{:S(2)}, u32[]{:S(2)}) collective-permute-start(bf16[160,1280]{1,0:T(8,128)(2,1)} %copy-done), channel_id=1, source_target_pairs={{0,16},{1,17},{2,18},{3,19},{4,20},{5,21},{6,22},{7,23},{8,24},{9,... | collective-permute-start | bytes 1228808 | tf_op jit(solution)/shard_map/ppermute | solution.py:51
  113.9 1.7 collective-permute-start.20
  154.1 13.7 %all-to-all-start.1 = ((bf16[32,4,1280]{2,1,0:T(4,128)(2,1)}), bf16[32,4,1280]{2,1,0:T(4,128)(2,1)S(1)}, u32[]{:S(2)}, u32[]{:S(2)}) async-start(bf16[32,4,1280]{2,1,0:T(4,128)(2,1)} %broadcast_in_dim.53), calls=%async_computation.1 | async-start | bytes 655360 | tf_op jit(solution)/shard_map/all_to_all | solution.py:386
  157.9 37.1 %collective-permute-start.19 = (bf16[512,1280]{1,0:T(8,128)(2,1)}, bf16[512,1280]{1,0:T(8,128)(2,1)S(1)}, u32[]{:S(2)}, u32[]{:S(2)}) collective-permute-start(bf16[512,1280]{1,0:T(8,128)(2,1)} %get-tuple-element.10), channel_id=1, source_target_pairs={{2,0},{4,2},{6,4},{8,6},{10,8},{12,10},{14,12},{16,14},{18,16},{20... | collective-permute-start | bytes 3932168 | tf_op jit(solution)/shard_map/ppermute | solution.py:370
  167.8 4.1 %collective-permute-start.21 = (bf16[128,1280]{1,0:T(8,128)(2,1)S(1)}, bf16[128,1280]{1,0:T(8,128)(2,1)S(1)}, u32[]{:S(2)}, u32[]{:S(2)}) collective-permute-start(bf16[128,1280]{1,0:T(8,128)(2,1)S(1)} %reshape.140), channel_id=1, source_target_pairs={{0,16},{16,0},{1,17},{17,1},{2,18},{18,2},{3,19},{19,3},{4,20},{20... | collective-permute-start | bytes 983048 | tf_op jit(solution)/shard_map/ppermute | solution.py:388
  (6 other events, 74.6 us)

commit v5 on v4

--- a/solution.py
+++ b/solution.py
@@ -18,8 +18,8 @@
 WIN = 2 * LOCAL
 QB = 256
 IMAGES = 256
-EDGE_WIDTHS = (256, 384, 512, 640)
-OWN_WIDTHS = (256, 384, 512)
+WIDTHS = (256, 384, 512)
+SHIFT = 16
 HALF = D // 2
 KR = 160
 TOKEN_AXES = ("x", "co", "z", "yh")
@@ -63,8 +63,6 @@
 
 
 def attention_kernel(edge, place_ref, ends_ref, *refs):
-    widths = EDGE_WIDTHS if edge else OWN_WIDTHS
-    window = WIN if edge else LOCAL
     if edge:
         prev_ref, late_ref, refs = refs[0], refs[1], refs[2:]
     own_ref, gain_ref, wqkv_ref, wout_ref, refs = *refs[:4], refs[4:]
@@ -73,20 +71,32 @@
         hprev_ref, hown_ref, sum_ref, refs = *refs[:3], refs[3:]
     else:
         image_ref, lens_ref, hedge_ref, sum_ref, hown_ref, pooled_ref, refs = *refs[:6], refs[6:]
+    if edge:
+        wide_ref, refs = refs[0], refs[1:]
     (
         x_ref, n_ref, w_ref, wo_ref, q_ref, k_ref, vt_ref, ctx_ref, bias_ref, hid_ref,
         s0_ref, s1_ref, p0_ref, p1_ref, top0_ref, top1_ref, sem,
     ) = refs
     x, co, dp, lo, hi, wrap = (place_ref[i] for i in range(6))
-    base = (lo // 128) * 128
+    if edge:
+        first = pl.multiple_of(lo // SHIFT * SHIFT, SHIFT)
+        offset = lo - first
+        base, lo, hi = 0, 0, hi - lo
+    else:
+        base = (lo // 128) * 128
     blocks = (hi - base + QB - 1) // QB
 
     far = (1 - dp) * HALF
 
-    inputs = [pltpu.make_async_copy(own_ref, x_ref.at[pl.ds(window - LOCAL, LOCAL)], sem.at[0])]
+    tokens_ref = wide_ref if edge else x_ref
+    inputs = [
+        pltpu.make_async_copy(
+            own_ref, tokens_ref.at[pl.ds(LOCAL if edge else 0, LOCAL)], sem.at[0]
+        )
+    ]
     inputs[0].start()
     if edge:
-        inputs.append(pltpu.make_async_copy(prev_ref, x_ref.at[pl.ds(0, LOCAL)], sem.at[0]))
+        inputs.append(pltpu.make_async_copy(prev_ref, wide_ref.at[pl.ds(0, LOCAL)], sem.at[0]))
 
         @pl.when(wrap == 0)
         def _():
@@ -94,7 +104,7 @@
 
         @pl.when(wrap == 1)
         def _():
-            pltpu.make_async_copy(late_ref, x_ref.at[pl.ds(0, LOCAL)], sem.at[0]).start()
+            pltpu.make_async_copy(late_ref, wide_ref.at[pl.ds(0, LOCAL)], sem.at[0]).start()
     else:
         inputs.append(pltpu.make_async_copy(hedge_ref, hid_ref.at[pl.ds(0, LOCAL)], sem.at[5]))
         inputs[1].start()
@@ -129,9 +139,27 @@
         for _ in range(4):
             distant(part, mine_refs[0], 0).wait()
 
-    x_ref[window:, :] = jnp.zeros((x_ref.shape[0] - window, D), jnp.bfloat16)
+    if not edge:
+        x_ref[LOCAL:, :] = jnp.zeros((x_ref.shape[0] - LOCAL, D), jnp.bfloat16)
     for copy in inputs:
         copy.wait()
+
+    def mover(lag):
+        out = lax.broadcasted_iota(jnp.int32, (QB, QB + SHIFT), 0)
+        source = lax.broadcasted_iota(jnp.int32, (QB, QB + SHIFT), 1)
+        return jnp.where(source == out + lag, 1.0, 0.0).astype(jnp.bfloat16)
+
+    if edge:
+        wide_ref[WIN:, :] = jnp.zeros((wide_ref.shape[0] - WIN, D), jnp.bfloat16)
+        pick = mover(offset)
+
+        def align(j, carry):
+            rows = pl.ds(pl.multiple_of(first + j * QB, SHIFT), QB + SHIFT)
+            taken = jnp.dot(pick, wide_ref[rows, :], preferred_element_type=jnp.float32)
+            x_ref[pl.ds(pl.multiple_of(j * QB, QB), QB), :] = taken.astype(jnp.bfloat16)
+            return carry
+
+        lax.fori_loop(0, blocks, align, 0)
 
     def block_rows(j):
         row0 = pl.multiple_of(base + j * QB, 128)
@@ -151,6 +179,7 @@
     vt_ref[...] = jnp.zeros_like(vt_ref)
     if edge:
         hid_ref[...] = jnp.zeros_like(hid_ref)
+        wide_ref[...] = jnp.zeros_like(wide_ref)
 
     def project_q(j, carry):
         _, rows = block_rows(j)
@@ -182,14 +211,18 @@
 
     def attend(j, carry):
         row0, rows = block_rows(j)
-        least = ends_ref[0, jnp.maximum(row0, lo)]
-        most = ends_ref[1, jnp.minimum(row0 + QB, hi) - 1]
-        k0 = pl.multiple_of((least // 128) * 128, 128)
-        need = most - k0
-        start = spans_ref[0:1, rows]
-        end = spans_ref[1:2, rows]
-        for i, width in enumerate(widths):
-            above = widths[i - 1] if i else 0
+        if edge:
+            k0, need = 0, hi
+            start, end = 0, hi
+        else:
+            least = ends_ref[0, jnp.maximum(row0, lo)]
+            most = ends_ref[1, jnp.minimum(row0 + QB, hi) - 1]
+            k0 = pl.multiple_of((least // 128) * 128, 128)
+            need = most - k0
+            start = spans_ref[0:1, rows]
+            end = spans_ref[1:2, rows]
+        for i, width in enumerate(WIDTHS):
+            above = WIDTHS[i - 1] if i else 0
 
             @pl.when((need > above) & (need <= width))
             def _(width=width):
@@ -250,7 +283,9 @@
         inside = (at >= lo) & (at < hi)
         hidden = hidden.astype(jnp.bfloat16)
         if edge:
-            hid_ref[rows, :] = jnp.where(inside, hidden, jnp.zeros_like(hidden))
+            hid_ref[pl.ds(pl.multiple_of(row0 + SHIFT, SHIFT), QB), :] = jnp.where(
+                inside, hidden, jnp.zeros_like(hidden)
+            )
         else:
             hid_ref[rows, :] = jnp.where(inside, hidden, hid_ref[rows, :])
         return carry
@@ -258,10 +293,23 @@
     lax.fori_loop(0, blocks, attend, 0)
 
     if edge:
-        hprev_ref[...] = hid_ref[0:LOCAL, :]
-        hown_ref[...] = hid_ref[LOCAL:WIN, :]
+        put = mover(SHIFT - offset)
+
+        @pl.when(hi > 0)
+        def _():
+            for j in range(3):
+                moved_rows = jnp.dot(
+                    put, hid_ref[j * QB : (j + 1) * QB + SHIFT, :],
+                    preferred_element_type=jnp.float32,
+                )
+                rows = pl.ds(pl.multiple_of(first + j * QB, SHIFT), QB)
+                wide_ref[rows, :] = moved_rows.astype(jnp.bfloat16)
+
+        hprev_ref[...] = wide_ref[0:LOCAL, :]
+        hown_ref[...] = wide_ref[LOCAL:WIN, :]
         sum_ref[...] = jnp.dot(
-            jnp.ones((8, WIN), jnp.bfloat16), hid_ref[0:WIN, :], preferred_element_type=jnp.float32
+            jnp.ones((8, LOCAL + SHIFT), jnp.bfloat16), hid_ref[0 : LOCAL + SHIFT, :],
+            preferred_element_type=jnp.float32,
         )
         return
     hown_ref[...] = hid_ref[0:LOCAL, :]
@@ -281,8 +329,8 @@
     hbm = pl.BlockSpec(memory_space=pltpu.HBM)
     vmem = pl.BlockSpec(memory_space=pltpu.VMEM)
     smem = pl.BlockSpec(memory_space=pltpu.SMEM)
-    rows = WIN + 256 if edge else LOCAL + 256
-    width = (EDGE_WIDTHS if edge else OWN_WIDTHS)[-1]
+    rows = LOCAL + 256
+    width = WIDTHS[-1]
     hidden = jax.ShapeDtypeStruct((LOCAL, D), jnp.bfloat16)
     if edge:
         outs = (hidden, hidden, jax.ShapeDtypeStruct((8, D), jnp.float32))
@@ -295,7 +343,8 @@
         out_shape=outs,
         in_specs=[smem, smem] + [hbm] * len(inputs) + [vmem] + [hbm] * 18 + [vmem] + tail,
         out_specs=(vmem,) * len(outs),
-        scratch_shapes=[
+        scratch_shapes=([pltpu.VMEM((WIN + 3 * QB, D), jnp.bfloat16)] if edge else [])
+        + [
             pltpu.VMEM((rows, D), jnp.bfloat16),
             pltpu.VMEM((rows, D), jnp.bfloat16),
             pltpu.VMEM((D, 3 * D), jnp.bfloat16),
@@ -305,7 +354,7 @@
             pltpu.VMEM((HEADS * VROWS, rows), jnp.bfloat16),
             pltpu.VMEM((D, QB), jnp.bfloat16),
             pltpu.VMEM((width, QB), jnp.float32),
-            pltpu.VMEM((rows, D), jnp.bfloat16),
+            pltpu.VMEM((rows + 2 * SHIFT, D), jnp.bfloat16),
             pltpu.VMEM((width, QB), jnp.float32),
             pltpu.VMEM((width, QB), jnp.float32),
             pltpu.VMEM((width, QB), jnp.bfloat16),

time: 197 us -> 189 us (0.959)
  blocking collectives: 36.3 us -> 27.1 us
    all_to_all x1, blocking collectives: 36.3 us -> 27.1 us  [layer(): rows = lax.all_to_all(kept, group, 0, 0, tiled=True).astype(jnp.float32)]
where the time goes in v5:
time: 189 us; the launch traced here: 188 us
  waiting for transfers between devices  54.6 us (29%)
  Pallas kernels  45.2 us (24%)
  starting transfers between devices  44 us (23%)
  blocking collectives  27.1 us (14%)
  local copies, waits for them, and re-layouts  8.05 us (4%)
  other arithmetic  6.08 us (3%)
  between operations  3.29 us (2%)
    pallas_call x2, Pallas kernels, attention(): pl.pallas_call(functools.partial(attention_kernel, edge), out_shape=outs,...  45.2 us
    all_to_all x1, blocking collectives, layer(): rows = lax.all_to_all(kept, group, 0, 0, tiled=True).astype(jnp.float32)  27.1 us
    ppermute x1, waiting for transfers between devices, layer(): back = lax.ppermute(hprev, TOKEN_AXES, [(i + 1, i) for i in range(63)])  21.8 us
    ppermute x16, starting transfers between devices, moved(): return lax.ppermute(piece, ALL_AXES, pairs)  21.6 us
    ppermute x16, waiting for transfers between devices, moved(): return lax.ppermute(piece, ALL_AXES, pairs)  18.6 us
    ppermute x1, waiting for transfers between devices, layer(): lax.ppermute(own, TOKEN_AXES, [(i, i + 1) for i in range(63) if i not in...  10.1 us
    ppermute x1, starting transfers between devices, layer(): back = lax.ppermute(hprev, TOKEN_AXES, [(i + 1, i) for i in range(63)])  8.52 us
    all_to_all x1, starting transfers between devices, layer(): lax.all_to_all(jnp.broadcast_to(rows[None], (32, 4, D)), group, 0, 0, til...  3.87 us
  transfers between devices with their start and end apart: 23, of which 8 were waited for; matrix products, arithmetic and copies ran while one was open for 4% of the time, Pallas kernels for 0%

profile of v5, /device:TPU:1, one launch (start us, length us, event | category | flops | bytes accessed | tf_op | source)
XLA Modules:
  0.0 188.2 jit_solution(3339760398150901995)
XLA Ops:
  0.6 1.9 %collective-permute-start.17 = (bf16[512,1280]{1,0:T(8,128)(2,1)}, bf16[512,1280]{1,0:T(8,128)(2,1)}, u32[]{:S(2)}, u32[]{:S(2)}) collective-permute-start(bf16[512,1280]{1,0:T(8,128)(2,1)} %bitcast.34), channel_id=1, source_target_pairs={{30,46},{62,78},{94,110},{31,47},{63,79},{95,111}} | collective-permute-start | bytes 3932168 | tf_op jit(solution)/shard_map/ppermute | solution.py:380
  2.5 1.3 dynamic-slice_select_fusion
  3.9 2.2 %collective-permute-start = (bf16[160,1280]{1,0:T(8,128)(2,1)S(1)}, bf16[160,1280]{1,0:T(8,128)(2,1)S(1)}, u32[]{:S(2)}, u32[]{:S(2)}) collective-permute-start(bf16[160,1280]{1,0:T(8,128)(2,1)S(1)} %get-tuple-element.18), channel_id=1, source_target_pairs={{0,1},{1,2},{2,3},{3,0},{4,5},{5,6},{6,7},{7,4},{8,9},{9,10},{10,1... | collective-permute-start | bytes 1228808 | tf_op jit(solution)/shard_map/ppermute | solution.py:51
  6.1 1.5 collective-permute-start.1
  7.6 9.0 %collective-permute-done.refs_6_.refs_4_ = bf16[160,1280]{1,0:T(8,128)(2,1)S(1)} collective-permute-done((bf16[160,1280]{1,0:T(8,128)(2,1)S(1)}, bf16[160,1280]{1,0:T(8,128)(2,1)S(1)}, u32[]{:S(2)}, u32[]{:S(2)}) %collective-permute-start) | collective-permute-done | bytes 409632 | tf_op jit(solution)/shard_map/ppermute | solution.py:51
  17.7 1.6 collective-permute-start.5
  19.3 2.7 %collective-permute-start.4 = (bf16[160,1280]{1,0:T(8,128)(2,1)S(1)}, bf16[160,1280]{1,0:T(8,128)(2,1)S(1)}, u32[]{:S(2)}, u32[]{:S(2)}) collective-permute-start(bf16[160,1280]{1,0:T(8,128)(2,1)S(1)} %collective-permute-done.refs_6_.refs_4_), channel_id=1, source_target_pairs={{0,96},{1,97},{2,98},{3,99},{4,100},{5,101},{6,102},{7,103},{8,104... | collective-permute-start | bytes 1228808 | tf_op jit(solution)/shard_map/ppermute | solution.py:51
  22.4 5.1 %collective-permute-done.2.refs_8_.refs_6_ = bf16[160,1280]{1,0:T(8,128)(2,1)S(1)} collective-permute-done((bf16[160,1280]{1,0:T(8,128)(2,1)S(1)}, bf16[160,1280]{1,0:T(8,128)(2,1)S(1)}, u32[]{:S(2)}, u32[]{:S(2)}) %collective-permute-start.2) | collective-permute-done | bytes 409632 | tf_op jit(solution)/shard_map/ppermute | solution.py:51
  27.5 4.0 %collective-permute-start.8 = (bf16[160,1280]{1,0:T(8,128)(2,1)S(1)}, bf16[160,1280]{1,0:T(8,128)(2,1)S(1)}, u32[]{:S(2)}, u32[]{:S(2)}) collective-permute-start(bf16[160,1280]{1,0:T(8,128)(2,1)S(1)} %collective-permute-done.refs_6_.refs_4_), channel_id=1, source_target_pairs={{0,16},{1,17},{2,18},{3,19},{4,20},{5,21},{6,22},{7,23},{8,24},{9,... | collective-permute-start | bytes 1228808 | tf_op jit(solution)/shard_map/ppermute | solution.py:51
  31.8 4.5 %collective-permute-done.3.refs_9_.refs_7_ = bf16[160,1280]{1,0:T(8,128)(2,1)S(1)} collective-permute-done((bf16[160,1280]{1,0:T(8,128)(2,1)S(1)}, bf16[160,1280]{1,0:T(8,128)(2,1)S(1)}, u32[]{:S(2)}, u32[]{:S(2)}) %collective-permute-start.3) | collective-permute-done | bytes 409632 | tf_op jit(solution)/shard_map/ppermute | solution.py:51
  36.2 2.7 %collective-permute-start.7 = (bf16[160,1280]{1,0:T(8,128)(2,1)S(1)}, bf16[160,1280]{1,0:T(8,128)(2,1)S(1)}, u32[]{:S(2)}, u32[]{:S(2)}) collective-permute-start(bf16[160,1280]{1,0:T(8,128)(2,1)S(1)} %collective-permute-done.5.refs_11_.refs_9_), channel_id=1, source_target_pairs={{0,96},{1,97},{2,98},{3,99},{4,100},{5,101},{6,102},{7,103},{8,104... | collective-permute-start | bytes 1228808 | tf_op jit(solution)/shard_map/ppermute | solution.py:51
  38.9 3.4 %collective-permute-start.16 = (bf16[512,1280]{1,0:T(8,128)(2,1)}, bf16[512,1280]{1,0:T(8,128)(2,1)}, u32[]{:S(2)}, u32[]{:S(2)}) collective-permute-start(bf16[512,1280]{1,0:T(8,128)(2,1)} %bitcast.35), channel_id=1, source_target_pairs={{0,2},{2,4},{4,6},{6,8},{8,10},{10,12},{12,14},{14,16},{16,18},{18... | collective-permute-start | bytes 3932168 | tf_op jit(solution)/shard_map/ppermute | solution.py:383
  42.4 1.7 collective-permute-start.18
  44.7 4.4 %collective-permute-start.10 = (bf16[160,1280]{1,0:T(8,128)(2,1)S(1)}, bf16[160,1280]{1,0:T(8,128)(2,1)}, u32[]{:S(2)}, u32[]{:S(2)}) collective-permute-start(bf16[160,1280]{1,0:T(8,128)(2,1)S(1)} %collective-permute-done.2.refs_8_.refs_6_), channel_id=1, source_target_pairs={{0,16},{1,17},{2,18},{3,19},{4,20},{5,21},{6,22},{7,23},{8,24},{9,... | collective-permute-start | bytes 1228808 | tf_op jit(solution)/shard_map/ppermute | solution.py:51
  55.6 1.3 stack.50.place_ref
  57.8 10.1 %collective-permute-done.16.refs_0_ = bf16[512,1280]{1,0:T(8,128)(2,1)} collective-permute-done((bf16[512,1280]{1,0:T(8,128)(2,1)}, bf16[512,1280]{1,0:T(8,128)(2,1)}, u32[]{:S(2)}, u32[]{:S(2)}) %collective-permute-start.16) | collective-permute-done | bytes 1310752 | tf_op jit(solution)/shard_map/ppermute | solution.py:383
  68.9 24.0 %edge_attention.1 = (bf16[512,1280]{1,0:T(8,128)(2,1)}, bf16[512,1280]{1,0:T(8,128)(2,1)}, f32[8,1280]{1,0:T(8,128)S(1)}) custom-call(s32[7]{0:T(128)S(1)} %stack.50.place_ref, s32[2,1280]{1,0:T(2,128)S(1)} %pad_add_fusion.ends_ref.refs_22_, bf16[512,1280]{1,0:T(8,128)(2,1)} %collective-permute-done.16.refs_0_, ...), custom_call_target="tpu_custom_call" | custom-call | flops 15000000512 | bytes 20000000 | tf_op jit(solution)/shard_map/edge_attention/pallas_call | solution.py:341
  92.9 21.1 %own_attention.1 = (bf16[512,1280]{1,0:T(8,128)(2,1)}, bf16[256,1280]{1,0:T(8,128)(2,1)}) custom-call(s32[7]{0:T(128)S(1)} %stack.48.place_ref, s32[2,768]{1,0:T(2,128)S(1)} %fusion.4.ends_ref.refs_20_, bf16[512,1280]{1,0:T(8,128)(2,1)} %bitcast.37, f32[1,1280]{1,0:T(1,128)S(1)} %broadcast_in_dim.50.refs_3_.refs_1_, bf16[640,3840]{1,0:T(8,128)(2,1)} %refs_2_.1, ...), custom_call_target="tpu_custom_call" | custom-call | flops 15000000512 | bytes 20000000 | tf_op jit(solution)/shard_map/own_attention/pallas_call | solution.py:341
  115.2 1.6 collective-permute-done.20
  117.9 27.1 %all_to_all.10 = bf16[32,4,1280]{2,1,0:T(4,128)(2,1)S(1)} all-to-all(bf16[32,4,1280]{2,1,0:T(4,128)(2,1)S(1)} %reshape.139), channel_id=1, replica_groups=mesh['x'=4,'co'=2,'z'=4,'yh'=2,'dp'=2] {'x','z','yh'}, dimensions={0} | all-to-all | bytes 655360 | tf_op jit(solution)/shard_map/all_to_all | solution.py:433
  146.0 3.9 %all-to-all-start.1 = ((bf16[32,4,1280]{2,1,0:T(4,128)(2,1)}), bf16[32,4,1280]{2,1,0:T(4,128)(2,1)S(1)}, u32[]{:S(2)}, u32[]{:S(2)}) async-start(bf16[32,4,1280]{2,1,0:T(4,128)(2,1)} %broadcast_in_dim.53), calls=%async_computation.1 | async-start | bytes 655360 | tf_op jit(solution)/shard_map/all_to_all | solution.py:435
  149.9 8.5 %collective-permute-start.19 = (bf16[512,1280]{1,0:T(8,128)(2,1)}, bf16[512,1280]{1,0:T(8,128)(2,1)S(1)}, u32[]{:S(2)}, u32[]{:S(2)}) collective-permute-start(bf16[512,1280]{1,0:T(8,128)(2,1)} %get-tuple-element.10), channel_id=1, source_target_pairs={{2,0},{4,2},{6,4},{8,6},{10,8},{12,10},{14,12},{16,14},{18,16},{20... | collective-permute-start | bytes 3932168 | tf_op jit(solution)/shard_map/ppermute | solution.py:419
  159.8 2.8 %collective-permute-start.21 = (bf16[128,1280]{1,0:T(8,128)(2,1)S(1)}, bf16[128,1280]{1,0:T(8,128)(2,1)S(1)}, u32[]{:S(2)}, u32[]{:S(2)}) collective-permute-start(bf16[128,1280]{1,0:T(8,128)(2,1)S(1)} %reshape.140), channel_id=1, source_target_pairs={{0,16},{16,0},{1,17},{17,1},{2,18},{18,2},{3,19},{19,3},{4,20},{20... | collective-permute-start | bytes 983048 | tf_op jit(solution)/shard_map/ppermute | solution.py:437
  165.1 21.8 %collective-permute-done.19 = bf16[512,1280]{1,0:T(8,128)(2,1)S(1)} collective-permute-done((bf16[512,1280]{1,0:T(8,128)(2,1)}, bf16[512,1280]{1,0:T(8,128)(2,1)S(1)}, u32[]{:S(2)}, u32[]{:S(2)}) %collective-permute-start.19) | collective-permute-done | bytes 1310752 | tf_op jit(solution)/shard_map/ppermute | solution.py:419
  (73 shorter events, 16.6 us)
Async XLA Ops:
  0.6 50.3 %copy-start.5 = (f32[1280]{0:T(1024)S(1)}, f32[1280]{0:T(1024)}, u32[]{:S(2)}) copy-start(f32[1280]{0:T(1024)} %param.7) | copy-start | bytes 15364
  0.6 41.7 %collective-permute-start.17 = (bf16[512,1280]{1,0:T(8,128)(2,1)}, bf16[512,1280]{1,0:T(8,128)(2,1)}, u32[]{:S(2)}, u32[]{:S(2)}) collective-permute-start(bf16[512,1280]{1,0:T(8,128)(2,1)} %bitcast.34), channel_id=1, source_target_pairs={{30,46},{62,78},{94,110},{31,47},{63,79},{95,111}} | collective-permute-start | bytes 3932168 | tf_op jit(solution)/shard_map/ppermute | solution.py:380
  3.9 12.7 %collective-permute-start = (bf16[160,1280]{1,0:T(8,128)(2,1)S(1)}, bf16[160,1280]{1,0:T(8,128)(2,1)S(1)}, u32[]{:S(2)}, u32[]{:S(2)}) collective-permute-start(bf16[160,1280]{1,0:T(8,128)(2,1)S(1)} %get-tuple-element.18), channel_id=1, source_target_pairs={{0,1},{1,2},{2,3},{3,0},{4,5},{5,6},{6,7},{7,4},{8,9},{9,10},{10,1... | collective-permute-start | bytes 1228808 | tf_op jit(solution)/shard_map/ppermute | solution.py:51
  6.1 11.6 %collective-permute-start.1 = (bf16[160,1280]{1,0:T(8,128)(2,1)S(1)}, bf16[160,1280]{1,0:T(8,128)(2,1)S(1)}, u32[]{:S(2)}, u32[]{:S(2)}) collective-permute-start(bf16[160,1280]{1,0:T(8,128)(2,1)S(1)} %get-tuple-element.17), channel_id=1, source_target_pairs={{0,3},{1,0},{2,1},{3,2},{4,7},{5,4},{6,5},{7,6},{8,11},{9,8},{10,9... | collective-permute-start | bytes 1228808 | tf_op jit(solution)/shard_map/ppermute | solution.py:51
  16.6 10.9 %collective-permute-start.2 = (bf16[160,1280]{1,0:T(8,128)(2,1)S(1)}, bf16[160,1280]{1,0:T(8,128)(2,1)S(1)}, u32[]{:S(2)}, u32[]{:S(2)}) collective-permute-start(bf16[160,1280]{1,0:T(8,128)(2,1)S(1)} %collective-permute-done.refs_6_.refs_4_), channel_id=1, source_target_pairs={{0,32},{1,33},{2,34},{3,35},{4,36},{5,37},{6,38},{7,39},{8,40},{9,... | collective-permute-start | bytes 1228808 | tf_op jit(solution)/shard_map/ppermute | solution.py:51
  17.7 14.0 %collective-permute-start.5 = (bf16[160,1280]{1,0:T(8,128)(2,1)S(1)}, bf16[160,1280]{1,0:T(8,128)(2,1)S(1)}, u32[]{:S(2)}, u32[]{:S(2)}) collective-permute-start(bf16[160,1280]{1,0:T(8,128)(2,1)S(1)} %collective-permute-done.1.refs_7_.refs_5_), channel_id=1, source_target_pairs={{0,96},{1,97},{2,98},{3,99},{4,100},{5,101},{6,102},{7,103},{8,104... | collective-permute-start | bytes 1228808 | tf_op jit(solution)/shard_map/ppermute | solution.py:51
  19.3 17.0 %collective-permute-start.3 = (bf16[160,1280]{1,0:T(8,128)(2,1)S(1)}, bf16[160,1280]{1,0:T(8,128)(2,1)S(1)}, u32[]{:S(2)}, u32[]{:S(2)}) collective-permute-start(bf16[160,1280]{1,0:T(8,128)(2,1)S(1)} %collective-permute-done.1.refs_7_.refs_5_), channel_id=1, source_target_pairs={{0,32},{1,33},{2,34},{3,35},{4,36},{5,37},{6,38},{7,39},{8,40},{9,... | collective-permute-start | bytes 1228808 | tf_op jit(solution)/shard_map/ppermute | solution.py:51
  19.3 17.0 %collective-permute-start.4 = (bf16[160,1280]{1,0:T(8,128)(2,1)S(1)}, bf16[160,1280]{1,0:T(8,128)(2,1)S(1)}, u32[]{:S(2)}, u32[]{:S(2)}) collective-permute-start(bf16[160,1280]{1,0:T(8,128)(2,1)S(1)} %collective-permute-done.refs_6_.refs_4_), channel_id=1, source_target_pairs={{0,96},{1,97},{2,98},{3,99},{4,100},{5,101},{6,102},{7,103},{8,104... | collective-permute-start | bytes 1228808 | tf_op jit(solution)/shard_map/ppermute | solution.py:51
  27.5 11.5 %collective-permute-start.8 = (bf16[160,1280]{1,0:T(8,128)(2,1)S(1)}, bf16[160,1280]{1,0:T(8,128)(2,1)S(1)}, u32[]{:S(2)}, u32[]{:S(2)}) collective-permute-start(bf16[160,1280]{1,0:T(8,128)(2,1)S(1)} %collective-permute-done.refs_6_.refs_4_), channel_id=1, source_target_pairs={{0,16},{1,17},{2,18},{3,19},{4,20},{5,21},{6,22},{7,23},{8,24},{9,... | collective-permute-start | bytes 1228808 | tf_op jit(solution)/shard_map/ppermute | solution.py:51
  31.7 13.0 %collective-permute-start.9 = (bf16[160,1280]{1,0:T(8,128)(2,1)S(1)}, bf16[160,1280]{1,0:T(8,128)(2,1)S(1)}, u32[]{:S(2)}, u32[]{:S(2)}) collective-permute-start(bf16[160,1280]{1,0:T(8,128)(2,1)S(1)} %collective-permute-done.1.refs_7_.refs_5_), channel_id=1, source_target_pairs={{0,16},{1,17},{2,18},{3,19},{4,20},{5,21},{6,22},{7,23},{8,24},{9,... | collective-permute-start | bytes 1228808 | tf_op jit(solution)/shard_map/ppermute | solution.py:51
  36.2 12.8 %collective-permute-start.6 = (bf16[160,1280]{1,0:T(8,128)(2,1)S(1)}, bf16[160,1280]{1,0:T(8,128)(2,1)S(1)}, u32[]{:S(2)}, u32[]{:S(2)}) collective-permute-start(bf16[160,1280]{1,0:T(8,128)(2,1)S(1)} %collective-permute-done.2.refs_8_.refs_6_), channel_id=1, source_target_pairs={{0,32},{1,33},{2,34},{3,35},{4,36},{5,37},{6,38},{7,39},{8,40},{9,... | collective-permute-start | bytes 1228808 | tf_op jit(solution)/shard_map/ppermute | solution.py:51
  36.2 13.1 %collective-permute-start.7 = (bf16[160,1280]{1,0:T(8,128)(2,1)S(1)}, bf16[160,1280]{1,0:T(8,128)(2,1)S(1)}, u32[]{:S(2)}, u32[]{:S(2)}) collective-permute-start(bf16[160,1280]{1,0:T(8,128)(2,1)S(1)} %collective-permute-done.5.refs_11_.refs_9_), channel_id=1, source_target_pairs={{0,96},{1,97},{2,98},{3,99},{4,100},{5,101},{6,102},{7,103},{8,104... | collective-permute-start | bytes 1228808 | tf_op jit(solution)/shard_map/ppermute | solution.py:51
  38.9 28.9 %collective-permute-start.16 = (bf16[512,1280]{1,0:T(8,128)(2,1)}, bf16[512,1280]{1,0:T(8,128)(2,1)}, u32[]{:S(2)}, u32[]{:S(2)}) collective-permute-start(bf16[512,1280]{1,0:T(8,128)(2,1)} %bitcast.35), channel_id=1, source_target_pairs={{0,2},{2,4},{4,6},{6,8},{8,10},{10,12},{12,14},{14,16},{16,18},{18... | collective-permute-start | bytes 3932168 | tf_op jit(solution)/shard_map/ppermute | solution.py:383
  42.4 25.5 %collective-permute-start.18 = (bf16[512,1280]{1,0:T(8,128)(2,1)}, bf16[512,1280]{1,0:T(8,128)(2,1)}, u32[]{:S(2)}, u32[]{:S(2)}) collective-permute-start(bf16[512,1280]{1,0:T(8,128)(2,1)} %collective-permute-done.17), channel_id=1, source_target_pairs={{46,32},{78,64},{110,96},{47,33},{79,65},{111,97}} | collective-permute-start | bytes 3932168 | tf_op jit(solution)/shard_map/ppermute | solution.py:386
  44.7 7.4 %collective-permute-start.10 = (bf16[160,1280]{1,0:T(8,128)(2,1)S(1)}, bf16[160,1280]{1,0:T(8,128)(2,1)}, u32[]{:S(2)}, u32[]{:S(2)}) collective-permute-start(bf16[160,1280]{1,0:T(8,128)(2,1)S(1)} %collective-permute-done.2.refs_8_.refs_6_), channel_id=1, source_target_pairs={{0,16},{1,17},{2,18},{3,19},{4,20},{5,21},{6,22},{7,23},{8,24},{9,... | collective-permute-start | bytes 1228808 | tf_op jit(solution)/shard_map/ppermute | solution.py:51
  49.0 3.4 %collective-permute-start.13 = (bf16[160,1280]{1,0:T(8,128)(2,1)S(1)}, bf16[160,1280]{1,0:T(8,128)(2,1)}, u32[]{:S(2)}, u32[]{:S(2)}) collective-permute-start(bf16[160,1280]{1,0:T(8,128)(2,1)S(1)} %collective-permute-done.5.refs_11_.refs_9_), channel_id=1, source_target_pairs={{0,16},{1,17},{2,18},{3,19},{4,20},{5,21},{6,22},{7,23},{8,24},{9,... | collective-permute-start | bytes 1228808 | tf_op jit(solution)/shard_map/ppermute | solution.py:51
  50.1 2.6 %collective-permute-start.11 = (bf16[160,1280]{1,0:T(8,128)(2,1)S(1)}, bf16[160,1280]{1,0:T(8,128)(2,1)}, u32[]{:S(2)}, u32[]{:S(2)}) collective-permute-start(bf16[160,1280]{1,0:T(8,128)(2,1)S(1)} %collective-permute-done.3.refs_9_.refs_7_), channel_id=1, source_target_pairs={{0,16},{1,17},{2,18},{3,19},{4,20},{5,21},{6,22},{7,23},{8,24},{9,... | collective-permute-start | bytes 1228808 | tf_op jit(solution)/shard_map/ppermute | solution.py:51
  52.1 5.7 %collective-permute-start.12 = (bf16[160,1280]{1,0:T(8,128)(2,1)S(1)}, bf16[160,1280]{1,0:T(8,128)(2,1)}, u32[]{:S(2)}, u32[]{:S(2)}) collective-permute-start(bf16[160,1280]{1,0:T(8,128)(2,1)S(1)} %collective-permute-done.4.refs_10_.refs_8_), channel_id=1, source_target_pairs={{0,16},{1,17},{2,18},{3,19},{4,20},{5,21},{6,22},{7,23},{8,24},{9,... | collective-permute-start | bytes 1228808 | tf_op jit(solution)/shard_map/ppermute | solution.py:51
  52.5 15.4 %collective-permute-start.14 = (bf16[160,1280]{1,0:T(8,128)(2,1)S(1)}, bf16[160,1280]{1,0:T(8,128)(2,1)}, u32[]{:S(2)}, u32[]{:S(2)}) collective-permute-start(bf16[160,1280]{1,0:T(8,128)(2,1)S(1)} %collective-permute-done.6.refs_12_.refs_10_), channel_id=1, source_target_pairs={{0,16},{1,17},{2,18},{3,19},{4,20},{5,21},{6,22},{7,23},{8,24},{9,... | collective-permute-start | bytes 1228808 | tf_op jit(solution)/shard_map/ppermute | solution.py:51
  52.7 15.2 %collective-permute-start.15 = (bf16[160,1280]{1,0:T(8,128)(2,1)}, bf16[160,1280]{1,0:T(8,128)(2,1)}, u32[]{:S(2)}, u32[]{:S(2)}) collective-permute-start(bf16[160,1280]{1,0:T(8,128)(2,1)} %copy-done), channel_id=1, source_target_pairs={{0,16},{1,17},{2,18},{3,19},{4,20},{5,21},{6,22},{7,23},{8,24},{9,... | collective-permute-start | bytes 1228808 | tf_op jit(solution)/shard_map/ppermute | solution.py:51
  115.1 1.7 collective-permute-start.20
  146.0 13.7 %all-to-all-start.1 = ((bf16[32,4,1280]{2,1,0:T(4,128)(2,1)}), bf16[32,4,1280]{2,1,0:T(4,128)(2,1)S(1)}, u32[]{:S(2)}, u32[]{:S(2)}) async-start(bf16[32,4,1280]{2,1,0:T(4,128)(2,1)} %broadcast_in_dim.53), calls=%async_computation.1 | async-start | bytes 655360 | tf_op jit(solution)/shard_map/all_to_all | solution.py:435
  149.9 37.1 %collective-permute-start.19 = (bf16[512,1280]{1,0:T(8,128)(2,1)}, bf16[512,1280]{1,0:T(8,128)(2,1)S(1)}, u32[]{:S(2)}, u32[]{:S(2)}) collective-permute-start(bf16[512,1280]{1,0:T(8,128)(2,1)} %get-tuple-element.10), channel_id=1, source_target_pairs={{2,0},{4,2},{6,4},{8,6},{10,8},{12,10},{14,12},{16,14},{18,16},{20... | collective-permute-start | bytes 3932168 | tf_op jit(solution)/shard_map/ppermute | solution.py:419
  159.8 4.1 %collective-permute-start.21 = (bf16[128,1280]{1,0:T(8,128)(2,1)S(1)}, bf16[128,1280]{1,0:T(8,128)(2,1)S(1)}, u32[]{:S(2)}, u32[]{:S(2)}) collective-permute-start(bf16[128,1280]{1,0:T(8,128)(2,1)S(1)} %reshape.140), channel_id=1, source_target_pairs={{0,16},{16,0},{1,17},{17,1},{2,18},{18,2},{3,19},{19,3},{4,20},{20... | collective-permute-start | bytes 983048 | tf_op jit(solution)/shard_map/ppermute | solution.py:437
  (6 other events, 75.7 us)

commit v6 on v5

--- a/solution.py
+++ b/solution.py
@@ -20,10 +20,13 @@
 IMAGES = 256
 WIDTHS = (256, 384, 512)
 SHIFT = 16
+SLOTS = 16
 HALF = D // 2
 KR = 160
 TOKEN_AXES = ("x", "co", "z", "yh")
 ALL_AXES = TOKEN_AXES + ("dp",)
+GROUP = ("x", "z", "yh")
+SWAP = [(0, 1), (1, 0)]
 LOG2E = 1.4426950408889634
 
 
@@ -70,7 +73,7 @@
     if edge:
         hprev_ref, hown_ref, sum_ref, refs = *refs[:3], refs[3:]
     else:
-        image_ref, lens_ref, hedge_ref, sum_ref, hown_ref, pooled_ref, refs = *refs[:6], refs[6:]
+        image_ref, lens_ref, hedge_ref, sum_ref, hown_ref, pooled_ref, few_ref, refs = *refs[:7], refs[7:]
     if edge:
         wide_ref, refs = refs[0], refs[1:]
     (
@@ -323,6 +326,36 @@
     label = lax.broadcasted_iota(jnp.int32, (IMAGES, D), 0)
     sums = sums + jnp.where(label == place_ref[6], sum_ref[0:1, :], 0.0)
     pooled_ref[...] = (sums / lens_ref[...]).astype(jnp.bfloat16)
+    label = lax.broadcasted_iota(jnp.int32, (SLOTS, LOCAL), 0) + place_ref[6]
+    at = lax.broadcasted_iota(jnp.int32, (SLOTS, LOCAL), 1)
+    member = (label == image_ref[...]) & (at >= lo) & (at < hi)
+    sums = jnp.dot(
+        jnp.where(member, 1.0, 0.0).astype(jnp.bfloat16), hid_ref[0:LOCAL, :],
+        preferred_element_type=jnp.float32,
+    )
+    label = lax.broadcasted_iota(jnp.int32, (SLOTS, D), 0)
+    sums = sums + jnp.where(label == 0, sum_ref[0:1, :], 0.0)
+    few_ref[...] = sums.astype(jnp.bfloat16)
+
+
+def unpack_kernel(near_ref, far_ref, slot_ref, lens_ref, out_ref):
+    at = lax.broadcasted_iota(jnp.int32, (IMAGES, 32 * SLOTS), 1)
+    sums = jnp.zeros((IMAGES, D), jnp.float32)
+    for i, ref in enumerate((near_ref, far_ref)):
+        pick = jnp.where(slot_ref[...] == at + i * 32 * SLOTS, 1.0, 0.0).astype(jnp.bfloat16)
+        sums = sums + jnp.dot(pick, ref[...], preferred_element_type=jnp.float32)
+    out_ref[...] = sums / lens_ref[...]
+
+
+def unpack(near, far, slot, lens):
+    vmem = pl.BlockSpec(memory_space=pltpu.VMEM)
+    return pl.pallas_call(
+        unpack_kernel,
+        out_shape=jax.ShapeDtypeStruct((IMAGES, D), jnp.float32),
+        in_specs=[vmem] * 4,
+        out_specs=vmem,
+        name="unpack",
+    )(near, far, slot, lens)
 
 
 def attention(edge, place, spans, inputs, gain, weights, extra):
@@ -336,7 +369,11 @@
         outs = (hidden, hidden, jax.ShapeDtypeStruct((8, D), jnp.float32))
         tail = []
     else:
-        outs = (hidden, jax.ShapeDtypeStruct((IMAGES, D), jnp.bfloat16))
+        outs = (
+            hidden,
+            jax.ShapeDtypeStruct((IMAGES, D), jnp.bfloat16),
+            jax.ShapeDtypeStruct((SLOTS, D), jnp.bfloat16),
+        )
         tail = [vmem, vmem, hbm, vmem]
     return pl.pallas_call(
         functools.partial(attention_kernel, edge),
@@ -412,31 +449,51 @@
         jnp.stack([x, co, dp, lo, hi, wrap, image[LOCAL]]).astype(jnp.int32)
         for lo, hi in ((low, cut), (cut - LOCAL, limit - LOCAL))
     ]
+    owner = (ends - 1) // LOCAL
+    leader = jnp.sum((offsets[None, :] <= owner[:, None] * LOCAL).astype(jnp.int32), axis=1) - 1
+    rank = jnp.arange(IMAGES, dtype=jnp.int32) - leader
+    group = owner // 16 * 8 + owner % 8
+    slot = jnp.where(owner // 8 % 2 == co, 0, 32 * SLOTS) + group * SLOTS + rank
+    slot = slot[:, None]
+    crowded = jnp.full((8, 128), jnp.max(rank) >= SLOTS).astype(jnp.float32)
+    elsewhere = lax.ppermute(crowded, "dp", SWAP)
+    fits = crowded[0, 0] + elsewhere[0, 0] == 0.0
+
     gain = ln_gain[None]
     weights = [w_qkv, w_out, *mine, *other]
 
     hprev, hedge, total = attention(True, places[0], spans, [prev, late, own], gain, weights, [])
     back = lax.ppermute(hprev, TOKEN_AXES, [(i + 1, i) for i in range(63)])
-    hown, part = attention(
+    hown, part, few = attention(
         False, places[1], spans[:, LOCAL:] - LOCAL, [own], gain, weights,
         [image[None, LOCAL:WIN], lens.astype(jnp.float32)[:, None], hedge, total],
     )
 
-    swap = [(0, 1), (1, 0)]
-    group = ("x", "z", "yh")
-    part = part.reshape(2, IMAGES // 2, D)
-    kept = lax.dynamic_index_in_dim(part, co, 0, keepdims=False)
-    given = lax.dynamic_index_in_dim(part, 1 - co, 0, keepdims=False)
-    given = lax.ppermute(given, "co", swap)
-    kept = kept.astype(jnp.float32) + given.astype(jnp.float32)
-    kept = kept.astype(jnp.bfloat16).reshape(32, 4, D)
-    rows = lax.all_to_all(kept, group, 0, 0, tiled=True).astype(jnp.float32)
-    rows = jnp.sum(rows, axis=0).astype(jnp.bfloat16)
-    half = lax.all_to_all(jnp.broadcast_to(rows[None], (32, 4, D)), group, 0, 0, tiled=True)
-    half = half.reshape(IMAGES // 2, D)
-    rest = lax.ppermute(half, "co", swap)
-    pooled = jnp.where(co == 0, jnp.stack([half, rest]), jnp.stack([rest, half]))
-    pooled = pooled.reshape(1, IMAGES, D).astype(jnp.float32)
+    lens_column = lens.astype(jnp.float32)[:, None]
+
+    def pooled_directly(few, part):
+        near = lax.all_to_all(
+            jnp.broadcast_to(few[None], (32, SLOTS, D)), GROUP, 0, 0, tiled=True
+        ).reshape(32 * SLOTS, D)
+        far = lax.ppermute(near, "co", SWAP)
+        return unpack(near, far, slot, lens_column)
+
+    def pooled_by_sums(few, part):
+        part = part.reshape(2, IMAGES // 2, D)
+        kept = lax.dynamic_index_in_dim(part, co, 0, keepdims=False)
+        given = lax.dynamic_index_in_dim(part, 1 - co, 0, keepdims=False)
+        given = lax.ppermute(given, "co", SWAP)
+        kept = kept.astype(jnp.float32) + given.astype(jnp.float32)
+        kept = kept.astype(jnp.bfloat16).reshape(32, 4, D)
+        rows = lax.all_to_all(kept, GROUP, 0, 0, tiled=True).astype(jnp.float32)
+        rows = jnp.sum(rows, axis=0).astype(jnp.bfloat16)
+        half = lax.all_to_all(jnp.broadcast_to(rows[None], (32, 4, D)), GROUP, 0, 0, tiled=True)
+        half = half.reshape(IMAGES // 2, D)
+        rest = lax.ppermute(half, "co", SWAP)
+        pooled = jnp.where(co == 0, jnp.stack([half, rest]), jnp.stack([rest, half]))
+        return pooled.reshape(IMAGES, D).astype(jnp.float32)
+
+    pooled = lax.cond(fits, pooled_directly, pooled_by_sums, few, part)[None]
 
     here = jnp.arange(LOCAL, dtype=jnp.int32)[:, None] < limit - LOCAL
     hidden = jnp.where(here, hown, back)[None]

time: 189 us -> 164 us (0.87)
  waiting for transfers between devices: 54.6 us -> 16.3 us
  blocking collectives: 27.1 us -> 36 us
  starting transfers between devices: 44 us -> 39.9 us
  other arithmetic: 6.08 us -> 9.94 us
  Pallas kernels: 45.2 us -> 48.9 us
    ppermute x1, waiting for transfers between devices: 21.8 us -> 0.01 us  [layer(): back = lax.ppermute(hprev, TOKEN_AXES, [(i + 1, i) for i in range(63)])]
    all_to_all x1, blocking collectives: 27.1 us -> 36 us  [pooled_directly(): lax.all_to_all(jnp.broadcast_to(few[None], (32, SLOTS, D)), GROUP, 0, 0,...]
    ppermute x16, waiting for transfers between devices: 18.6 us -> 11.2 us  [moved(): return lax.ppermute(piece, ALL_AXES, pairs)]
    ppermute x1, waiting for transfers between devices: 10.1 us -> 4.92 us  [layer(): lax.ppermute(own, TOKEN_AXES, [(i, i + 1) for i in range(63) if i not in...]
    all_to_all x1 -> x0, starting transfers between devices: 3.87 us -> none  [layer(): lax.all_to_all(jnp.broadcast_to(rows[None], (32, 4, D)), group, 0, 0, til...]
    pallas_call x0 -> x1, Pallas kernels: none -> 3.7 us  [unpack(): pl.pallas_call(unpack_kernel, out_shape=jax.ShapeDtypeStruct((IMAGES, D),...]
    ppermute x2, waiting for transfers between devices: 2.78 us -> 0.22 us  [the longest x1 0.22 us: layer(): elsewhere = lax.ppermute(crowded, 'dp', SWAP)]
    convert_element_type x3 -> x0, other arithmetic: 2.2 us -> none  [the longest x1 1.14 us: layer(): pooled = pooled.reshape(1, IMAGES, D).astype(jnp.float32)]
  transfers between devices with their start and end apart: 23 -> 22, of which waited for: 8 -> 5; matrix products, arithmetic and copies ran while one was open for 4% -> 8% of each run, Pallas kernels for 0% -> 15%
where the time goes in v6:
time: 164 us
  Pallas kernels  48.9 us (30%)
  starting transfers between devices  39.9 us (24%)
  blocking collectives  36 us (22%)
  waiting for transfers between devices  16.3 us (10%)
  other arithmetic  9.94 us (6%)
  local copies, waits for them, and re-layouts  7.91 us (5%)
  between operations  4.83 us (3%)
    pallas_call x2, Pallas kernels, attention(): pl.pallas_call(functools.partial(attention_kernel, edge), out_shape=outs,...  45.2 us
    all_to_all x1, blocking collectives, pooled_directly(): lax.all_to_all(jnp.broadcast_to(few[None], (32, SLOTS, D)), GROUP, 0, 0,...  36 us
    ppermute x16, starting transfers between devices, moved(): return lax.ppermute(piece, ALL_AXES, pairs)  21.6 us
    ppermute x16, waiting for transfers between devices, moved(): return lax.ppermute(piece, ALL_AXES, pairs)  11.2 us
    ppermute x1, starting transfers between devices, layer(): back = lax.ppermute(hprev, TOKEN_AXES, [(i + 1, i) for i in range(63)])  9.58 us
    ppermute x1, waiting for transfers between devices, layer(): lax.ppermute(own, TOKEN_AXES, [(i, i + 1) for i in range(63) if i not in...  4.92 us
    pallas_call x1, Pallas kernels, unpack(): pl.pallas_call(unpack_kernel, out_shape=jax.ShapeDtypeStruct((IMAGES, D),...  3.7 us
    ppermute x1, starting transfers between devices, layer(): lax.ppermute(own, TOKEN_AXES, [(i, i + 1) for i in range(63) if i not in...  3.55 us
  transfers between devices with their start and end apart: 22, of which 5 were waited for; matrix products, arithmetic and copies ran while one was open for 8% of the time, Pallas kernels for 15%

profile of v6, /device:TPU:1, one launch (start us, length us, event | category | flops | bytes accessed | tf_op | source)
XLA Modules:
  0.0 163.9 jit_solution(17265131070155286557)
XLA Ops:
  2.0 2.2 %collective-permute-start.3 = (bf16[160,1280]{1,0:T(8,128)(2,1)S(1)}, bf16[160,1280]{1,0:T(8,128)(2,1)S(1)}, u32[]{:S(2)}, u32[]{:S(2)}) collective-permute-start(bf16[160,1280]{1,0:T(8,128)(2,1)S(1)} %get-tuple-element.215), channel_id=1, source_target_pairs={{0,1},{1,2},{2,3},{3,0},{4,5},{5,6},{6,7},{7,4},{8,9},{9,10},{10,1... | collective-permute-start | bytes 1228808 | tf_op jit(solution)/shard_map/ppermute | solution.py:54
  4.2 1.5 collective-permute-start.4
  5.7 1.7 %collective-permute-start.20 = (bf16[512,1280]{1,0:T(8,128)(2,1)}, bf16[512,1280]{1,0:T(8,128)(2,1)}, u32[]{:S(2)}, u32[]{:S(2)}) collective-permute-start(bf16[512,1280]{1,0:T(8,128)(2,1)} %bitcast.18.refs_2_.refs_0_), channel_id=1, source_target_pairs={{30,46},{62,78},{94,110},{31,47},{63,79},{95,111}} | collective-permute-start | bytes 3932168 | tf_op jit(solution)/shard_map/ppermute | solution.py:417
  8.3 6.4 %collective-permute-done.3.refs_6_.refs_4_ = bf16[160,1280]{1,0:T(8,128)(2,1)S(1)} collective-permute-done((bf16[160,1280]{1,0:T(8,128)(2,1)S(1)}, bf16[160,1280]{1,0:T(8,128)(2,1)S(1)}, u32[]{:S(2)}, u32[]{:S(2)}) %collective-permute-start.3) | collective-permute-done | bytes 409632 | tf_op jit(solution)/shard_map/ppermute | solution.py:54
  17.8 1.6 %collective-permute-start.8 = (bf16[160,1280]{1,0:T(8,128)(2,1)S(1)}, bf16[160,1280]{1,0:T(8,128)(2,1)S(1)}, u32[]{:S(2)}, u32[]{:S(2)}) collective-permute-start(bf16[160,1280]{1,0:T(8,128)(2,1)S(1)} %collective-permute-done.4.refs_7_.refs_5_), channel_id=1, source_target_pairs={{0,96},{1,97},{2,98},{3,99},{4,100},{5,101},{6,102},{7,103},{8,104... | collective-permute-start | bytes 1228808 | tf_op jit(solution)/shard_map/ppermute | solution.py:54
  19.6 2.5 %collective-permute-start.7 = (bf16[160,1280]{1,0:T(8,128)(2,1)S(1)}, bf16[160,1280]{1,0:T(8,128)(2,1)S(1)}, u32[]{:S(2)}, u32[]{:S(2)}) collective-permute-start(bf16[160,1280]{1,0:T(8,128)(2,1)S(1)} %collective-permute-done.3.refs_6_.refs_4_), channel_id=1, source_target_pairs={{0,96},{1,97},{2,98},{3,99},{4,100},{5,101},{6,102},{7,103},{8,104... | collective-permute-start | bytes 1228808 | tf_op jit(solution)/shard_map/ppermute | solution.py:54
  22.1 3.5 %collective-permute-done.5.refs_8_.refs_6_ = bf16[160,1280]{1,0:T(8,128)(2,1)S(1)} collective-permute-done((bf16[160,1280]{1,0:T(8,128)(2,1)S(1)}, bf16[160,1280]{1,0:T(8,128)(2,1)S(1)}, u32[]{:S(2)}, u32[]{:S(2)}) %collective-permute-start.5) | collective-permute-done | bytes 409632 | tf_op jit(solution)/shard_map/ppermute | solution.py:54
  25.6 4.0 %collective-permute-start.11 = (bf16[160,1280]{1,0:T(8,128)(2,1)S(1)}, bf16[160,1280]{1,0:T(8,128)(2,1)S(1)}, u32[]{:S(2)}, u32[]{:S(2)}) collective-permute-start(bf16[160,1280]{1,0:T(8,128)(2,1)S(1)} %collective-permute-done.3.refs_6_.refs_4_), channel_id=1, source_target_pairs={{0,16},{1,17},{2,18},{3,19},{4,20},{5,21},{6,22},{7,23},{8,24},{9,... | collective-permute-start | bytes 1228808 | tf_op jit(solution)/shard_map/ppermute | solution.py:54
  29.6 3.6 %collective-permute-start.19 = (bf16[512,1280]{1,0:T(8,128)(2,1)}, bf16[512,1280]{1,0:T(8,128)(2,1)}, u32[]{:S(2)}, u32[]{:S(2)}) collective-permute-start(bf16[512,1280]{1,0:T(8,128)(2,1)} %bitcast.18.refs_2_.refs_0_), channel_id=1, source_target_pairs={{0,2},{2,4},{4,6},{6,8},{8,10},{10,12},{12,14},{14,16},{16,18},{18... | collective-permute-start | bytes 3932168 | tf_op jit(solution)/shard_map/ppermute | solution.py:420
  34.4 3.7 %collective-permute-start.12 = (bf16[160,1280]{1,0:T(8,128)(2,1)S(1)}, bf16[160,1280]{1,0:T(8,128)(2,1)}, u32[]{:S(2)}, u32[]{:S(2)}) collective-permute-start(bf16[160,1280]{1,0:T(8,128)(2,1)S(1)} %collective-permute-done.4.refs_7_.refs_5_), channel_id=1, source_target_pairs={{0,16},{1,17},{2,18},{3,19},{4,20},{5,21},{6,22},{7,23},{8,24},{9,... | collective-permute-start | bytes 1228808 | tf_op jit(solution)/shard_map/ppermute | solution.py:54
  39.3 1.5 collective-permute-start.10
  40.8 1.7 %collective-permute-start.21 = (bf16[512,1280]{1,0:T(8,128)(2,1)}, bf16[512,1280]{1,0:T(8,128)(2,1)}, u32[]{:S(2)}, u32[]{:S(2)}) collective-permute-start(bf16[512,1280]{1,0:T(8,128)(2,1)} %collective-permute-done.20), channel_id=1, source_target_pairs={{46,32},{78,64},{110,96},{47,33},{79,65},{111,97}} | collective-permute-start | bytes 3932168 | tf_op jit(solution)/shard_map/ppermute | solution.py:423
  47.9 1.4 stack.50.place_ref
  51.6 1.6 %broadcast_and_fusion = (s32[256,1]{1,0:T(8,128)}, s32[256,1]{1,0:T(8,128)S(1)}) fusion(s32[256,1]{1,0:T(8,128)} %copy.22), kind=kLoop, calls=%fused_computation.43 | loop fusion | flops 4864 | bytes 3072 | tf_op jit(solution)/shard_map/jit(floor_divide)/rem | solution.py:456
  55.9 4.9 %collective-permute-done.19.refs_0_ = bf16[512,1280]{1,0:T(8,128)(2,1)} collective-permute-done((bf16[512,1280]{1,0:T(8,128)(2,1)}, bf16[512,1280]{1,0:T(8,128)(2,1)}, u32[]{:S(2)}, u32[]{:S(2)}) %collective-permute-start.19) | collective-permute-done | bytes 1310752 | tf_op jit(solution)/shard_map/ppermute | solution.py:420
  60.8 24.1 %edge_attention.1 = (bf16[512,1280]{1,0:T(8,128)(2,1)}, bf16[512,1280]{1,0:T(8,128)(2,1)}, f32[8,1280]{1,0:T(8,128)S(1)}) custom-call(s32[7]{0:T(128)S(1)} %stack.50.place_ref, s32[2,1280]{1,0:T(2,128)S(1)} %pad_add_fusion.ends_ref.refs_22_, bf16[512,1280]{1,0:T(8,128)(2,1)} %collective-permute-done.19.refs_0_, ...), custom_call_target="tpu_custom_call" | custom-call | flops 15000000512 | bytes 20000000 | tf_op jit(solution)/shard_map/edge_attention/pallas_call | solution.py:378
  84.9 9.6 %collective-permute-start.22 = (bf16[512,1280]{1,0:T(8,128)(2,1)}, bf16[512,1280]{1,0:T(8,128)(2,1)}, u32[]{:S(2)}, u32[]{:S(2)}) collective-permute-start(bf16[512,1280]{1,0:T(8,128)(2,1)} %get-tuple-element.131), channel_id=1, source_target_pairs={{2,0},{4,2},{6,4},{8,6},{10,8},{12,10},{14,12},{16,14},{18,16},{20... | collective-permute-start | bytes 3932168 | tf_op jit(solution)/shard_map/ppermute | solution.py:466
  94.5 21.2 %own_attention.1 = (bf16[512,1280]{1,0:T(8,128)(2,1)}, bf16[256,1280]{1,0:T(8,128)(2,1)}, bf16[16,1280]{1,0:T(8,128)(2,1)S(1)}) custom-call(s32[7]{0:T(128)S(1)} %stack.48.place_ref, s32[2,768]{1,0:T(2,128)S(1)} %fusion.15.ends_ref.refs_20_, bf16[512,1280]{1,0:T(8,128)(2,1)} %bitcast.18.refs_2_.refs_0_, f32[1,1280]{1,0:T(1,128)S(1)} %broadcast_in_dim.72.refs_3_.refs_1_, ...), custom_call_target="tpu_custom_call" | custom-call | flops 15000000512 | bytes 20000000 | tf_op jit(solution)/shard_map/own_attention/pallas_call | solution.py:378
  116.3 44.9 %conditional.1 = (f32[1,256,1280]{2,1,0:T(8,128)}) conditional(s32[]{:T(128)} %convert_element_type.59, (s32[]{:T(128)}, bf16[256,1280]{1,0:T(8,128)(2,1)}) %tuple.26, (bf16[16,1280]{1,0:T(8,128)(2,1)S(1)}, s32[256,1]{1,0:T(8,128)}, s32[]{:T(128)}, s32[]{:T(128)}, s32[256,1]{1,0:T(8,128)}, /*index=5*/pred[256,1]{1,0:T(8,128)(4,1)S(1)}, (), ...), branch_computations={%region_7.9_spmd, %region_9.10_spmd} | conditional | flops 2124808 | bytes 14494692 | solution.py:496
  116.5 36.0 %all_to_all.14 = bf16[32,16,1280]{2,1,0:T(8,128)(2,1)S(1)} all-to-all(bf16[32,16,1280]{2,1,0:T(8,128)(2,1)S(1)} %broadcast_in_dim.36), channel_id=1, replica_groups=mesh['x'=4,'co'=2,'z'=4,'yh'=2,'dp'=2] {'x','z','yh'}, dimensions={0} | all-to-all | bytes 2621440 | tf_op jit(solution)/shard_map/cond/branch_1_fun/all_to_all | solution.py:475
  152.5 1.6 collective-permute-start.2
  155.8 1.8 %fusion.8.slot_ref = s32[256,1]{1,0:T(8,128)} fusion(s32[256,1]{1,0:T(8,128)S(1)} %copy-done.7, pred[256,1]{1,0:T(8,128)(4,1)S(1)} %get-tuple-element.201, s32[256,1]{1,0:T(8,128)S(1)} %get-tuple-element.117, s32[256,1]{1,0:T(8,128)} %copy.20, s32[256,1]{1,0:T(8,128)S(1)} %copy-done.6, pred[256,1]{1,0:T(8,128)(4,1)S(1)} %get-tuple-element.201, ...), kind=kLoop, calls=%fused_computation.20 | loop fusion | flops 11520 | bytes 11020 | tf_op jit(solution)/shard_map/add | solution.py:456
  157.6 3.7 %unpack.1 = f32[256,1280]{1,0:T(8,128)} custom-call(bf16[512,1280]{1,0:T(8,128)(2,1)} %bitcast.36, bf16[512,1280]{1,0:T(8,128)(2,1)} %collective-permute-done.2.far_ref, s32[256,1]{1,0:T(8,128)} %fusion.8.slot_ref, f32[256,1]{1,0:T(8,128)} %copy.26.lens_ref), custom_call_target="tpu_custom_call" | custom-call | tf_op jit(solution)/shard_map/cond/branch_1_fun/unpack/pallas_call | solution.py:352
  161.3 2.6 %select_bitcast_fusion = bf16[1,512,1280]{2,1,0:T(8,128)(2,1)} fusion(bf16[512,1280]{1,0:T(8,128)(2,1)S(1)} %copy-done.3, bf16[512,1280]{1,0:T(8,128)(2,1)} %collective-permute-done.22, pred[512]{0:T(512)(128)(4,1)S(1)} %iota_compare_fusion), kind=kLoop, calls=%fused_computation.30 | loop fusion | flops 655360 | bytes 3932672 | tf_op jit(solution)/shard_map/broadcast_in_dim | solution.py:499
  (91 shorter events, 16.5 us)
Async XLA Ops:
  0.6 43.1 %copy-start.9 = (f32[1280]{0:T(1024)S(1)}, f32[1280]{0:T(1024)}, u32[]{:S(2)}) copy-start(f32[1280]{0:T(1024)} %param.9) | copy-start | bytes 15364
  2.0 12.7 %collective-permute-start.3 = (bf16[160,1280]{1,0:T(8,128)(2,1)S(1)}, bf16[160,1280]{1,0:T(8,128)(2,1)S(1)}, u32[]{:S(2)}, u32[]{:S(2)}) collective-permute-start(bf16[160,1280]{1,0:T(8,128)(2,1)S(1)} %get-tuple-element.215), channel_id=1, source_target_pairs={{0,1},{1,2},{2,3},{3,0},{4,5},{5,6},{6,7},{7,4},{8,9},{9,10},{10,1... | collective-permute-start | bytes 1228808 | tf_op jit(solution)/shard_map/ppermute | solution.py:54
  4.2 13.6 %collective-permute-start.4 = (bf16[160,1280]{1,0:T(8,128)(2,1)S(1)}, bf16[160,1280]{1,0:T(8,128)(2,1)S(1)}, u32[]{:S(2)}, u32[]{:S(2)}) collective-permute-start(bf16[160,1280]{1,0:T(8,128)(2,1)S(1)} %get-tuple-element.214), channel_id=1, source_target_pairs={{0,3},{1,0},{2,1},{3,2},{4,7},{5,4},{6,5},{7,6},{8,11},{9,8},{10,9... | collective-permute-start | bytes 1228808 | tf_op jit(solution)/shard_map/ppermute | solution.py:54
  5.7 35.1 %collective-permute-start.20 = (bf16[512,1280]{1,0:T(8,128)(2,1)}, bf16[512,1280]{1,0:T(8,128)(2,1)}, u32[]{:S(2)}, u32[]{:S(2)}) collective-permute-start(bf16[512,1280]{1,0:T(8,128)(2,1)} %bitcast.18.refs_2_.refs_0_), channel_id=1, source_target_pairs={{30,46},{62,78},{94,110},{31,47},{63,79},{95,111}} | collective-permute-start | bytes 3932168 | tf_op jit(solution)/shard_map/ppermute | solution.py:417
  14.7 10.9 %collective-permute-start.5 = (bf16[160,1280]{1,0:T(8,128)(2,1)S(1)}, bf16[160,1280]{1,0:T(8,128)(2,1)S(1)}, u32[]{:S(2)}, u32[]{:S(2)}) collective-permute-start(bf16[160,1280]{1,0:T(8,128)(2,1)S(1)} %collective-permute-done.3.refs_6_.refs_4_), channel_id=1, source_target_pairs={{0,32},{1,33},{2,34},{3,35},{4,36},{5,37},{6,38},{7,39},{8,40},{9,... | collective-permute-start | bytes 1228808 | tf_op jit(solution)/shard_map/ppermute | solution.py:54
  17.1 2.5 %collective-permute-start.23 = (f32[8,128]{1,0:T(8,128)S(1)}, f32[8,128]{1,0:T(8,128)S(1)}, u32[]{:S(2)}, u32[]{:S(2)}) collective-permute-start(f32[8,128]{1,0:T(8,128)S(1)} %broadcast_in_dim.75), channel_id=1, source_target_pairs={{0,1},{1,0},{2,3},{3,2},{4,5},{5,4},{6,7},{7,6},{8,9},{9,8},{10,11... | collective-permute-start | bytes 12296 | tf_op jit(solution)/shard_map/ppermute | solution.py:459
  17.8 11.9 %collective-permute-start.8 = (bf16[160,1280]{1,0:T(8,128)(2,1)S(1)}, bf16[160,1280]{1,0:T(8,128)(2,1)S(1)}, u32[]{:S(2)}, u32[]{:S(2)}) collective-permute-start(bf16[160,1280]{1,0:T(8,128)(2,1)S(1)} %collective-permute-done.4.refs_7_.refs_5_), channel_id=1, source_target_pairs={{0,96},{1,97},{2,98},{3,99},{4,100},{5,101},{6,102},{7,103},{8,104... | collective-permute-start | bytes 1228808 | tf_op jit(solution)/shard_map/ppermute | solution.py:54
  19.4 14.9 %collective-permute-start.6 = (bf16[160,1280]{1,0:T(8,128)(2,1)S(1)}, bf16[160,1280]{1,0:T(8,128)(2,1)S(1)}, u32[]{:S(2)}, u32[]{:S(2)}) collective-permute-start(bf16[160,1280]{1,0:T(8,128)(2,1)S(1)} %collective-permute-done.4.refs_7_.refs_5_), channel_id=1, source_target_pairs={{0,32},{1,33},{2,34},{3,35},{4,36},{5,37},{6,38},{7,39},{8,40},{9,... | collective-permute-start | bytes 1228808 | tf_op jit(solution)/shard_map/ppermute | solution.py:54
  19.6 18.4 %collective-permute-start.7 = (bf16[160,1280]{1,0:T(8,128)(2,1)S(1)}, bf16[160,1280]{1,0:T(8,128)(2,1)S(1)}, u32[]{:S(2)}, u32[]{:S(2)}) collective-permute-start(bf16[160,1280]{1,0:T(8,128)(2,1)S(1)} %collective-permute-done.3.refs_6_.refs_4_), channel_id=1, source_target_pairs={{0,96},{1,97},{2,98},{3,99},{4,100},{5,101},{6,102},{7,103},{8,104... | collective-permute-start | bytes 1228808 | tf_op jit(solution)/shard_map/ppermute | solution.py:54
  25.6 13.7 %collective-permute-start.11 = (bf16[160,1280]{1,0:T(8,128)(2,1)S(1)}, bf16[160,1280]{1,0:T(8,128)(2,1)S(1)}, u32[]{:S(2)}, u32[]{:S(2)}) collective-permute-start(bf16[160,1280]{1,0:T(8,128)(2,1)S(1)} %collective-permute-done.3.refs_6_.refs_4_), channel_id=1, source_target_pairs={{0,16},{1,17},{2,18},{3,19},{4,20},{5,21},{6,22},{7,23},{8,24},{9,... | collective-permute-start | bytes 1228808 | tf_op jit(solution)/shard_map/ppermute | solution.py:54
  29.6 31.2 %collective-permute-start.19 = (bf16[512,1280]{1,0:T(8,128)(2,1)}, bf16[512,1280]{1,0:T(8,128)(2,1)}, u32[]{:S(2)}, u32[]{:S(2)}) collective-permute-start(bf16[512,1280]{1,0:T(8,128)(2,1)} %bitcast.18.refs_2_.refs_0_), channel_id=1, source_target_pairs={{0,2},{2,4},{4,6},{6,8},{8,10},{10,12},{12,14},{14,16},{16,18},{18... | collective-permute-start | bytes 3932168 | tf_op jit(solution)/shard_map/ppermute | solution.py:420
  34.4 15.7 %collective-permute-start.12 = (bf16[160,1280]{1,0:T(8,128)(2,1)S(1)}, bf16[160,1280]{1,0:T(8,128)(2,1)}, u32[]{:S(2)}, u32[]{:S(2)}) collective-permute-start(bf16[160,1280]{1,0:T(8,128)(2,1)S(1)} %collective-permute-done.4.refs_7_.refs_5_), channel_id=1, source_target_pairs={{0,16},{1,17},{2,18},{3,19},{4,20},{5,21},{6,22},{7,23},{8,24},{9,... | collective-permute-start | bytes 1228808 | tf_op jit(solution)/shard_map/ppermute | solution.py:54
  38.1 13.0 %collective-permute-start.9 = (bf16[160,1280]{1,0:T(8,128)(2,1)S(1)}, bf16[160,1280]{1,0:T(8,128)(2,1)S(1)}, u32[]{:S(2)}, u32[]{:S(2)}) collective-permute-start(bf16[160,1280]{1,0:T(8,128)(2,1)S(1)} %collective-permute-done.5.refs_8_.refs_6_), channel_id=1, source_target_pairs={{0,32},{1,33},{2,34},{3,35},{4,36},{5,37},{6,38},{7,39},{8,40},{9,... | collective-permute-start | bytes 1228808 | tf_op jit(solution)/shard_map/ppermute | solution.py:54
  39.3 11.8 %collective-permute-start.10 = (bf16[160,1280]{1,0:T(8,128)(2,1)S(1)}, bf16[160,1280]{1,0:T(8,128)(2,1)}, u32[]{:S(2)}, u32[]{:S(2)}) collective-permute-start(bf16[160,1280]{1,0:T(8,128)(2,1)S(1)} %collective-permute-done.8.refs_11_.refs_9_), channel_id=1, source_target_pairs={{0,96},{1,97},{2,98},{3,99},{4,100},{5,101},{6,102},{7,103},{8,104... | collective-permute-start | bytes 1228808 | tf_op jit(solution)/shard_map/ppermute | solution.py:54
  40.8 20.0 %collective-permute-start.21 = (bf16[512,1280]{1,0:T(8,128)(2,1)}, bf16[512,1280]{1,0:T(8,128)(2,1)}, u32[]{:S(2)}, u32[]{:S(2)}) collective-permute-start(bf16[512,1280]{1,0:T(8,128)(2,1)} %collective-permute-done.20), channel_id=1, source_target_pairs={{46,32},{78,64},{110,96},{47,33},{79,65},{111,97}} | collective-permute-start | bytes 3932168 | tf_op jit(solution)/shard_map/ppermute | solution.py:423
  50.1 3.2 %collective-permute-start.13 = (bf16[160,1280]{1,0:T(8,128)(2,1)S(1)}, bf16[160,1280]{1,0:T(8,128)(2,1)S(1)}, u32[]{:S(2)}, u32[]{:S(2)}) collective-permute-start(bf16[160,1280]{1,0:T(8,128)(2,1)S(1)} %collective-permute-done.5.refs_8_.refs_6_), channel_id=1, source_target_pairs={{0,16},{1,17},{2,18},{3,19},{4,20},{5,21},{6,22},{7,23},{8,24},{9,... | collective-permute-start | bytes 1228808 | tf_op jit(solution)/shard_map/ppermute | solution.py:54
  51.1 2.4 %collective-permute-start.16 = (bf16[160,1280]{1,0:T(8,128)(2,1)S(1)}, bf16[160,1280]{1,0:T(8,128)(2,1)S(1)}, u32[]{:S(2)}, u32[]{:S(2)}) collective-permute-start(bf16[160,1280]{1,0:T(8,128)(2,1)S(1)} %collective-permute-done.8.refs_11_.refs_9_), channel_id=1, source_target_pairs={{0,16},{1,17},{2,18},{3,19},{4,20},{5,21},{6,22},{7,23},{8,24},{9,... | collective-permute-start | bytes 1228808 | tf_op jit(solution)/shard_map/ppermute | solution.py:54
  51.2 2.7 %collective-permute-start.14 = (bf16[160,1280]{1,0:T(8,128)(2,1)S(1)}, bf16[160,1280]{1,0:T(8,128)(2,1)S(1)}, u32[]{:S(2)}, u32[]{:S(2)}) collective-permute-start(bf16[160,1280]{1,0:T(8,128)(2,1)S(1)} %collective-permute-done.6.refs_9_.refs_7_), channel_id=1, source_target_pairs={{0,16},{1,17},{2,18},{3,19},{4,20},{5,21},{6,22},{7,23},{8,24},{9,... | collective-permute-start | bytes 1228808 | tf_op jit(solution)/shard_map/ppermute | solution.py:54
  53.3 2.6 %collective-permute-start.15 = (bf16[160,1280]{1,0:T(8,128)(2,1)S(1)}, bf16[160,1280]{1,0:T(8,128)(2,1)}, u32[]{:S(2)}, u32[]{:S(2)}) collective-permute-start(bf16[160,1280]{1,0:T(8,128)(2,1)S(1)} %collective-permute-done.7.refs_10_.refs_8_), channel_id=1, source_target_pairs={{0,16},{1,17},{2,18},{3,19},{4,20},{5,21},{6,22},{7,23},{8,24},{9,... | collective-permute-start | bytes 1228808 | tf_op jit(solution)/shard_map/ppermute | solution.py:54
  53.5 7.4 %collective-permute-start.17 = (bf16[160,1280]{1,0:T(8,128)(2,1)S(1)}, bf16[160,1280]{1,0:T(8,128)(2,1)}, u32[]{:S(2)}, u32[]{:S(2)}) collective-permute-start(bf16[160,1280]{1,0:T(8,128)(2,1)S(1)} %collective-permute-done.9.refs_12_.refs_10_), channel_id=1, source_target_pairs={{0,16},{1,17},{2,18},{3,19},{4,20},{5,21},{6,22},{7,23},{8,24},{9,... | collective-permute-start | bytes 1228808 | tf_op jit(solution)/shard_map/ppermute | solution.py:54
  53.9 7.0 %collective-permute-start.18 = (bf16[160,1280]{1,0:T(8,128)(2,1)}, bf16[160,1280]{1,0:T(8,128)(2,1)}, u32[]{:S(2)}, u32[]{:S(2)}) collective-permute-start(bf16[160,1280]{1,0:T(8,128)(2,1)} %collective-permute-done.10.refs_13_.refs_11_), channel_id=1, source_target_pairs={{0,16},{1,17},{2,18},{3,19},{4,20},{5,21},{6,22},{7,23},{8,24},{9,... | collective-permute-start | bytes 1228808 | tf_op jit(solution)/shard_map/ppermute | solution.py:54
  84.9 76.4 %collective-permute-start.22 = (bf16[512,1280]{1,0:T(8,128)(2,1)}, bf16[512,1280]{1,0:T(8,128)(2,1)}, u32[]{:S(2)}, u32[]{:S(2)}) collective-permute-start(bf16[512,1280]{1,0:T(8,128)(2,1)} %get-tuple-element.131), channel_id=1, source_target_pairs={{2,0},{4,2},{6,4},{8,6},{10,8},{12,10},{14,12},{16,14},{18,16},{20... | collective-permute-start | bytes 3932168 | tf_op jit(solution)/shard_map/ppermute | solution.py:466
  116.3 45.0 %copy-start.3 = (bf16[512,1280]{1,0:T(8,128)(2,1)S(1)}, bf16[512,1280]{1,0:T(8,128)(2,1)}, u32[]{:S(2)}) copy-start(bf16[512,1280]{1,0:T(8,128)(2,1)} %get-tuple-element.130) | copy-start | bytes 3932164
  152.5 5.1 %collective-permute-start.2 = (bf16[512,1280]{1,0:T(8,128)(2,1)S(1)}, bf16[512,1280]{1,0:T(8,128)(2,1)}, u32[]{:S(2)}, u32[]{:S(2)}) collective-permute-start(bf16[512,1280]{1,0:T(8,128)(2,1)S(1)} %bitcast.35), channel_id=1, source_target_pairs={{0,16},{16,0},{1,17},{17,1},{2,18},{18,2},{3,19},{19,3},{4,20},{20... | collective-permute-start | bytes 3932168 | tf_op jit(solution)/shard_map/cond/branch_1_fun/ppermute | solution.py:478
  (11 other events, 213.8 us)

commit v7 on v6

--- a/solution.py
+++ b/solution.py
@@ -47,40 +47,35 @@
 CORE = permutation(lambda x, co, z, y: (x, 1 - co, z, y))
 
 
-WRAPS = [i for i in range(63) if i % 16 == 15]
-
-
 def moved(piece, pairs):
     return lax.ppermute(piece, ALL_AXES, pairs)
 
 
 def first_pieces(w_qkv, w_out):
-    x, co = lax.axis_index("x"), lax.axis_index("co")
-    pieces = []
-    for side in range(2):
-        part = co * 2 + side
-        q = lax.dynamic_slice(w_qkv, (x * KR, jnp.minimum(part, 2) * D), (KR, D))
-        o = lax.dynamic_slice(w_out, (x * KR, 0), (KR, D))
-        pieces.append(q if side == 0 else jnp.where(co == 0, q, o))
-    return pieces
+    x, co, z = (lax.axis_index(a) for a in ("x", "co", "z"))
+    near = lax.dynamic_slice(w_qkv, (x * KR, co * 2 * D), (KR, D))
+    q = lax.dynamic_slice(w_qkv, (z * KR, D), (KR, D))
+    o = lax.dynamic_slice(w_out, (z * KR, 0), (KR, D))
+    return near, jnp.where(co == 0, q, o)
 
 
 def attention_kernel(edge, place_ref, ends_ref, *refs):
     if edge:
-        prev_ref, late_ref, refs = refs[0], refs[1], refs[2:]
+        prev_ref, refs = refs[0], refs[1:]
     own_ref, gain_ref, wqkv_ref, wout_ref, refs = *refs[:4], refs[4:]
-    mine_refs, other_refs, spans_ref, refs = refs[:8], refs[8:16], refs[16], refs[17:]
-    if edge:
-        hprev_ref, hown_ref, sum_ref, refs = *refs[:3], refs[3:]
+    mine_refs, other_refs, spans_ref, refs = refs[:10], refs[10:20], refs[20], refs[21:]
+    if edge:
+        lens_ref, hin_ref, sum_ref, refs = *refs[:3], refs[3:]
+        hprev_ref, hown_ref, pooled_ref, few_ref, refs = *refs[:4], refs[4:]
     else:
-        image_ref, lens_ref, hedge_ref, sum_ref, hown_ref, pooled_ref, few_ref, refs = *refs[:7], refs[7:]
+        image_ref, hown_ref, sum_ref, refs = *refs[:3], refs[3:]
     if edge:
         wide_ref, refs = refs[0], refs[1:]
     (
         x_ref, n_ref, w_ref, wo_ref, q_ref, k_ref, vt_ref, ctx_ref, bias_ref, hid_ref,
         s0_ref, s1_ref, p0_ref, p1_ref, top0_ref, top1_ref, sem,
     ) = refs
-    x, co, dp, lo, hi, wrap = (place_ref[i] for i in range(6))
+    x, co, dp, lo, hi, z = (place_ref[i] for i in range(6))
     if edge:
         first = pl.multiple_of(lo // SHIFT * SHIFT, SHIFT)
         offset = lo - first
@@ -100,16 +95,6 @@
     inputs[0].start()
     if edge:
         inputs.append(pltpu.make_async_copy(prev_ref, wide_ref.at[pl.ds(0, LOCAL)], sem.at[0]))
-
-        @pl.when(wrap == 0)
-        def _():
-            inputs[1].start()
-
-        @pl.when(wrap == 1)
-        def _():
-            pltpu.make_async_copy(late_ref, wide_ref.at[pl.ds(0, LOCAL)], sem.at[0]).start()
-    else:
-        inputs.append(pltpu.make_async_copy(hedge_ref, hid_ref.at[pl.ds(0, LOCAL)], sem.at[5]))
         inputs[1].start()
 
     def near(part, target, cols):
@@ -119,28 +104,32 @@
             sem.at[1 + part],
         )
 
-    def distant(part, source, row):
+    def distant(part, source, row, count):
         target = wo_ref if part == 3 else w_ref
-        rows = pl.ds(pl.multiple_of(far + row * KR, 16), KR)
+        rows = pl.ds(pl.multiple_of(far + row, 16), count)
         return pltpu.make_async_copy(source, target.at[rows, columns[part]], sem.at[1 + part])
 
     columns = [pl.ds(0, D), pl.ds(D, D), pl.ds(2 * D, D), pl.ds(0, D)]
     targets = [w_ref, w_ref, w_ref, wo_ref]
-    shift = (0, 3, 1, 2)
     for part in range(4):
         near(part, targets[part], columns[part]).start()
+        side = part % 2
+        turn = z if side else x
         for held, core in ((mine_refs, co), (other_refs, 1 - co)):
 
             @pl.when(core == part // 2)
-            def _(held=held, part=part):
-                for slot in range(4):
-                    row = lax.rem(x + shift[slot], 4)
-                    distant(part, held[slot * 2 + part % 2], row).start()
+            def _(held=held, part=part, side=side, turn=turn):
+                for slot, shift in enumerate((0, 3, 1)):
+                    row = lax.rem(turn + shift, 4) * KR
+                    distant(part, held[slot * 2 + side], row, KR).start()
+                row = lax.rem(turn + 2, 4) * KR
+                distant(part, held[6 + side], row, KR // 2).start()
+                distant(part, held[8 + side], row + KR // 2, KR // 2).start()
 
     def arrived(part):
         near(part, targets[part], columns[part]).wait()
         for _ in range(4):
-            distant(part, mine_refs[0], 0).wait()
+            distant(part, mine_refs[0], 0, KR).wait()
 
     if not edge:
         x_ref[LOCAL:, :] = jnp.zeros((x_ref.shape[0] - LOCAL, D), jnp.bfloat16)
@@ -180,8 +169,8 @@
     lax.fori_loop(0, blocks, normalize, 0)
     k_ref[...] = jnp.zeros_like(k_ref)
     vt_ref[...] = jnp.zeros_like(vt_ref)
-    if edge:
-        hid_ref[...] = jnp.zeros_like(hid_ref)
+    hid_ref[...] = jnp.zeros_like(hid_ref)
+    if edge:
         wide_ref[...] = jnp.zeros_like(wide_ref)
 
     def project_q(j, carry):
@@ -309,11 +298,21 @@
                 wide_ref[rows, :] = moved_rows.astype(jnp.bfloat16)
 
         hprev_ref[...] = wide_ref[0:LOCAL, :]
-        hown_ref[...] = wide_ref[LOCAL:WIN, :]
-        sum_ref[...] = jnp.dot(
+        hown_ref[...] = hin_ref[...] + wide_ref[LOCAL:WIN, :]
+        extra = jnp.dot(
             jnp.ones((8, LOCAL + SHIFT), jnp.bfloat16), hid_ref[0 : LOCAL + SHIFT, :],
             preferred_element_type=jnp.float32,
         )
+        label = lax.broadcasted_iota(jnp.int32, (IMAGES, D), 0)
+        sums = sum_ref[...] + jnp.where(label == place_ref[6], extra[0:1, :], 0.0)
+        pooled = (sums / lens_ref[...]).astype(jnp.bfloat16)
+        pooled_ref[...] = pooled
+        label = lax.broadcasted_iota(jnp.int32, (SLOTS, IMAGES), 0) + place_ref[6]
+        pick = lax.broadcasted_iota(jnp.int32, (SLOTS, IMAGES), 1) == label
+        few_ref[...] = jnp.dot(
+            jnp.where(pick, 1.0, 0.0).astype(jnp.bfloat16), pooled,
+            preferred_element_type=jnp.float32,
+        ).astype(jnp.bfloat16)
         return
     hown_ref[...] = hid_ref[0:LOCAL, :]
     label = lax.broadcasted_iota(jnp.int32, (IMAGES, LOCAL), 0)
@@ -323,39 +322,30 @@
         jnp.where(member, 1.0, 0.0).astype(jnp.bfloat16), hid_ref[0:LOCAL, :],
         preferred_element_type=jnp.float32,
     )
-    label = lax.broadcasted_iota(jnp.int32, (IMAGES, D), 0)
-    sums = sums + jnp.where(label == place_ref[6], sum_ref[0:1, :], 0.0)
-    pooled_ref[...] = (sums / lens_ref[...]).astype(jnp.bfloat16)
-    label = lax.broadcasted_iota(jnp.int32, (SLOTS, LOCAL), 0) + place_ref[6]
-    at = lax.broadcasted_iota(jnp.int32, (SLOTS, LOCAL), 1)
-    member = (label == image_ref[...]) & (at >= lo) & (at < hi)
-    sums = jnp.dot(
-        jnp.where(member, 1.0, 0.0).astype(jnp.bfloat16), hid_ref[0:LOCAL, :],
-        preferred_element_type=jnp.float32,
-    )
-    label = lax.broadcasted_iota(jnp.int32, (SLOTS, D), 0)
-    sums = sums + jnp.where(label == 0, sum_ref[0:1, :], 0.0)
-    few_ref[...] = sums.astype(jnp.bfloat16)
-
-
-def unpack_kernel(near_ref, far_ref, slot_ref, lens_ref, out_ref):
-    at = lax.broadcasted_iota(jnp.int32, (IMAGES, 32 * SLOTS), 1)
-    sums = jnp.zeros((IMAGES, D), jnp.float32)
+    sum_ref[...] = sums
+
+
+def unpack_kernel(near_ref, far_ref, slot_ref, out_ref):
+    at = lax.broadcasted_iota(jnp.int32, (32 * SLOTS, IMAGES), 0)
+    means = jnp.zeros((IMAGES, D), jnp.float32)
     for i, ref in enumerate((near_ref, far_ref)):
         pick = jnp.where(slot_ref[...] == at + i * 32 * SLOTS, 1.0, 0.0).astype(jnp.bfloat16)
-        sums = sums + jnp.dot(pick, ref[...], preferred_element_type=jnp.float32)
-    out_ref[...] = sums / lens_ref[...]
-
-
-def unpack(near, far, slot, lens):
+        means = means + lax.dot_general(
+            pick, ref[...], (((0,), (0,)), ((), ())), preferred_element_type=jnp.float32
+        )
+    out_ref[...] = means
+
+
+def unpack(near, far, slot):
     vmem = pl.BlockSpec(memory_space=pltpu.VMEM)
     return pl.pallas_call(
         unpack_kernel,
         out_shape=jax.ShapeDtypeStruct((IMAGES, D), jnp.float32),
-        in_specs=[vmem] * 4,
+        in_specs=[vmem] * 3,
         out_specs=vmem,
+        compiler_params=pltpu.CompilerParams(vmem_limit_bytes=16 * 2**20),
         name="unpack",
-    )(near, far, slot, lens)
+    )(near, far, slot)
 
 
 def attention(edge, place, spans, inputs, gain, weights, extra):
@@ -365,20 +355,18 @@
     rows = LOCAL + 256
     width = WIDTHS[-1]
     hidden = jax.ShapeDtypeStruct((LOCAL, D), jnp.bfloat16)
-    if edge:
-        outs = (hidden, hidden, jax.ShapeDtypeStruct((8, D), jnp.float32))
-        tail = []
+    sums = jax.ShapeDtypeStruct((IMAGES, D), jnp.float32)
+    if edge:
+        pooled = jax.ShapeDtypeStruct((IMAGES, D), jnp.bfloat16)
+        outs = (hidden, hidden, pooled, jax.ShapeDtypeStruct((SLOTS, D), jnp.bfloat16))
+        tail = [vmem, vmem, vmem]
     else:
-        outs = (
-            hidden,
-            jax.ShapeDtypeStruct((IMAGES, D), jnp.bfloat16),
-            jax.ShapeDtypeStruct((SLOTS, D), jnp.bfloat16),
-        )
-        tail = [vmem, vmem, hbm, vmem]
+        outs = (hidden, sums)
+        tail = [vmem]
     return pl.pallas_call(
         functools.partial(attention_kernel, edge),
         out_shape=outs,
-        in_specs=[smem, smem] + [hbm] * len(inputs) + [vmem] + [hbm] * 18 + [vmem] + tail,
+        in_specs=[smem, smem] + [hbm] * len(inputs) + [vmem] + [hbm] * 22 + [vmem] + tail,
         out_specs=(vmem,) * len(outs),
         scratch_shapes=([pltpu.VMEM((WIN + 3 * QB, D), jnp.bfloat16)] if edge else [])
         + [
@@ -414,22 +402,18 @@
     own = tokens[0]
 
     p0, p1 = first_pieces(w_qkv, w_out)
-    lent = lax.ppermute(own, TOKEN_AXES, [(i, i + 8) for i in WRAPS])
     r0 = moved(p0, Y_UP)
     r1 = moved(p1, Y_DOWN)
-    prev = lax.ppermute(own, TOKEN_AXES, [(i, i + 1) for i in range(63) if i not in WRAPS])
-    u0 = moved(r0, X_UP)
-    d1 = moved(r1, X_DOWN)
-    late = lax.ppermute(lent, TOKEN_AXES, [(i + 8, i + 1) for i in WRAPS])
-    u1 = moved(r1, X_UP)
-    d0 = moved(r0, X_DOWN)
-    f0 = moved(u0, X_UP)
-    f1 = moved(d1, X_DOWN)
-    near = [moved(a, CORE) for a in (r0, r1)]
-    ring = [moved(a, CORE) for a in (u0, u1, d0, d1)]
-    last = [moved(a, CORE) for a in (f0, f1)]
-    mine = [r0, r1, u0, u1, d0, d1, f0, f1]
-    other = near + ring + last
+    ux, dx = moved(r0, X_UP), moved(r0, X_DOWN)
+    uz, dz = moved(r1, Z_UP), moved(r1, Z_DOWN)
+    half = KR // 2
+    fx, fz = moved(ux[:half], X_UP), moved(uz[:half], Z_UP)
+    gx, gz = moved(dx[half:], X_DOWN), moved(dz[half:], Z_DOWN)
+    prev = lax.ppermute(own, TOKEN_AXES, [(i, i + 1) for i in range(63)])
+    near = [moved(a, CORE) for a in (r0, r1, ux, uz, dx, dz)]
+    last = [moved(a, CORE) for a in (fx, fz, gx, gz)]
+    mine = [r0, r1, ux, uz, dx, dz, fx, fz, gx, gz]
+    other = near + last
 
     lens = lengths[0]
     ends = jnp.cumsum(lens)
@@ -444,9 +428,8 @@
     low = start[LOCAL]
     cut = jnp.where(low < LOCAL, end[LOCAL], LOCAL)
     limit = jnp.where(end[WIN - 1] == WIN, WIN, start[WIN - 1])
-    wrap = (co + z + yh == 0) & (x > 0)
     places = [
-        jnp.stack([x, co, dp, lo, hi, wrap, image[LOCAL]]).astype(jnp.int32)
+        jnp.stack([x, co, dp, lo, hi, z, image[LOCAL]]).astype(jnp.int32)
         for lo, hi in ((low, cut), (cut - LOCAL, limit - LOCAL))
     ]
     owner = (ends - 1) // LOCAL
@@ -454,7 +437,7 @@
     rank = jnp.arange(IMAGES, dtype=jnp.int32) - leader
     group = owner // 16 * 8 + owner % 8
     slot = jnp.where(owner // 8 % 2 == co, 0, 32 * SLOTS) + group * SLOTS + rank
-    slot = slot[:, None]
+    slot = slot[None]
     crowded = jnp.full((8, 128), jnp.max(rank) >= SLOTS).astype(jnp.float32)
     elsewhere = lax.ppermute(crowded, "dp", SWAP)
     fits = crowded[0, 0] + elsewhere[0, 0] == 0.0
@@ -462,21 +445,21 @@
     gain = ln_gain[None]
     weights = [w_qkv, w_out, *mine, *other]
 
-    hprev, hedge, total = attention(True, places[0], spans, [prev, late, own], gain, weights, [])
+    hown, sums = attention(
+        False, places[1], spans[:, LOCAL:] - LOCAL, [own], gain, weights, [image[None, LOCAL:WIN]]
+    )
+    hprev, hown, part, few = attention(
+        True, places[0], spans, [prev, own], gain, weights,
+        [lens.astype(jnp.float32)[:, None], hown, sums],
+    )
     back = lax.ppermute(hprev, TOKEN_AXES, [(i + 1, i) for i in range(63)])
-    hown, part, few = attention(
-        False, places[1], spans[:, LOCAL:] - LOCAL, [own], gain, weights,
-        [image[None, LOCAL:WIN], lens.astype(jnp.float32)[:, None], hedge, total],
-    )
-
-    lens_column = lens.astype(jnp.float32)[:, None]
 
     def pooled_directly(few, part):
         near = lax.all_to_all(
             jnp.broadcast_to(few[None], (32, SLOTS, D)), GROUP, 0, 0, tiled=True
         ).reshape(32 * SLOTS, D)
         far = lax.ppermute(near, "co", SWAP)
-        return unpack(near, far, slot, lens_column)
+        return unpack(near, far, slot)
 
     def pooled_by_sums(few, part):
         part = part.reshape(2, IMAGES // 2, D)

time: 164 us -> 182 us (1.11)
  waiting for transfers between devices: 16.3 us -> 38.1 us
  blocking collectives: 36 us -> 30 us
  other arithmetic: 9.94 us -> 4.47 us
  starting transfers between devices: 39.9 us -> 45.3 us
  local copies, waits for them, and re-layouts: 7.91 us -> 9.83 us
    ppermute x1, waiting for transfers between devices: 0.22 us -> 18.3 us  [layer(): elsewhere = lax.ppermute(crowded, 'dp', SWAP)]
    ppermute x1, starting transfers between devices: 0.09 us -> 9.1 us  [layer(): elsewhere = lax.ppermute(crowded, 'dp', SWAP)]
    ppermute x1, starting transfers between devices: 9.58 us -> 1.92 us  [layer(): back = lax.ppermute(hprev, TOKEN_AXES, [(i + 1, i) for i in range(63)])]
    ppermute x16 -> x20, starting transfers between devices: 21.6 us -> 27.7 us  [moved(): return lax.ppermute(piece, ALL_AXES, pairs)]
    all_to_all x1, blocking collectives: 36 us -> 30 us  [pooled_directly(): lax.all_to_all(jnp.broadcast_to(few[None], (32, SLOTS, D)), GROUP, 0, 0,...]
    unnamed x14 -> x18, local copies, waits for them, and re-layouts: 0.03 us -> 4.29 us
    ppermute x3 -> x1, starting transfers between devices: 7.01 us -> 3.48 us  [layer(): prev = lax.ppermute(own, TOKEN_AXES, [(i, i + 1) for i in range(63)])]
    ppermute x1, waiting for transfers between devices: 0.01 us -> 2.64 us  [pooled_directly(): far = lax.ppermute(near, 'co', SWAP)]
  transfers between devices with their start and end apart: 22 -> 24, of which waited for: 5 -> 7; matrix products, arithmetic and copies ran while one was open for 8% -> 4% of each run, Pallas kernels for 15% -> 13%
where the time goes in v7:
time: 182 us
  Pallas kernels  49.2 us (27%)
  starting transfers between devices  45.3 us (25%)
  waiting for transfers between devices  38.1 us (21%)
  blocking collectives  30 us (16%)
  local copies, waits for them, and re-layouts  9.83 us (5%)
  between operations  4.84 us (3%)
  other arithmetic  4.47 us (2%)
    pallas_call x2, Pallas kernels, attention(): pl.pallas_call(functools.partial(attention_kernel, edge), out_shape=outs,...  47.3 us
    all_to_all x1, blocking collectives, pooled_directly(): lax.all_to_all(jnp.broadcast_to(few[None], (32, SLOTS, D)), GROUP, 0, 0,...  30 us
    ppermute x20, starting transfers between devices, moved(): return lax.ppermute(piece, ALL_AXES, pairs)  27.7 us
    ppermute x1, waiting for transfers between devices, layer(): elsewhere = lax.ppermute(crowded, 'dp', SWAP)  18.3 us
    ppermute x20, waiting for transfers between devices, moved(): return lax.ppermute(piece, ALL_AXES, pairs)  12.5 us
    ppermute x1, starting transfers between devices, layer(): elsewhere = lax.ppermute(crowded, 'dp', SWAP)  9.1 us
    ppermute x1, waiting for transfers between devices, layer(): prev = lax.ppermute(own, TOKEN_AXES, [(i, i + 1) for i in range(63)])  4.75 us
    unnamed x18, local copies, waits for them, and re-layouts  4.29 us
  transfers between devices with their start and end apart: 24, of which 7 were waited for; matrix products, arithmetic and copies ran while one was open for 4% of the time, Pallas kernels for 13%

profile of v7, /device:TPU:1, one launch (start us, length us, event | category | flops | bytes accessed | tf_op | source)
XLA Modules:
  0.0 181.9 jit_solution(11615232010096169464)
XLA Ops:
  2.0 2.2 %collective-permute-start.4 = (bf16[160,1280]{1,0:T(8,128)(2,1)S(1)}, bf16[160,1280]{1,0:T(8,128)(2,1)S(1)}, u32[]{:S(2)}, u32[]{:S(2)}) collective-permute-start(bf16[160,1280]{1,0:T(8,128)(2,1)S(1)} %get-tuple-element.162), channel_id=1, source_target_pairs={{0,1},{1,2},{2,3},{3,0},{4,5},{5,6},{6,7},{7,4},{8,9},{9,10},{10,1... | collective-permute-start | bytes 1228808 | tf_op jit(solution)/shard_map/ppermute | solution.py:51
  6.4 8.4 %collective-permute-done.4.refs_4_.refs_5_ = bf16[160,1280]{1,0:T(8,128)(2,1)S(1)} collective-permute-done((bf16[160,1280]{1,0:T(8,128)(2,1)S(1)}, bf16[160,1280]{1,0:T(8,128)(2,1)S(1)}, u32[]{:S(2)}, u32[]{:S(2)}) %collective-permute-start.4) | collective-permute-done | bytes 409632 | tf_op jit(solution)/shard_map/ppermute | solution.py:51
  15.8 1.6 collective-permute-start.8
  17.4 1.5 collective-permute-start.7
  19.4 2.2 %collective-permute-start.9 = (bf16[160,1280]{1,0:T(8,128)(2,1)S(1)}, bf16[160,1280]{1,0:T(8,128)(2,1)S(1)}, u32[]{:S(2)}, u32[]{:S(2)}) collective-permute-start(bf16[160,1280]{1,0:T(8,128)(2,1)S(1)} %collective-permute-done.5.refs_5_.refs_6_), channel_id=1, source_target_pairs={{0,12},{1,13},{2,14},{3,15},{4,0},{5,1},{6,2},{7,3},{8,4},{9,5},{1... | collective-permute-start | bytes 1228808 | tf_op jit(solution)/shard_map/ppermute | solution.py:51
  21.6 2.3 %collective-permute-start.14 = (bf16[160,1280]{1,0:T(8,128)(2,1)S(1)}, bf16[160,1280]{1,0:T(8,128)(2,1)}, u32[]{:S(2)}, u32[]{:S(2)}) collective-permute-start(bf16[160,1280]{1,0:T(8,128)(2,1)S(1)} %collective-permute-done.4.refs_4_.refs_5_), channel_id=1, source_target_pairs={{0,16},{1,17},{2,18},{3,19},{4,20},{5,21},{6,22},{7,23},{8,24},{9,... | collective-permute-start | bytes 1228808 | tf_op jit(solution)/shard_map/ppermute | solution.py:51
  24.0 1.6 collective-permute-done.6.refs_6_.refs_7_
  25.6 2.2 %collective-permute-start.15 = (bf16[160,1280]{1,0:T(8,128)(2,1)S(1)}, bf16[160,1280]{1,0:T(8,128)(2,1)}, u32[]{:S(2)}, u32[]{:S(2)}) collective-permute-start(bf16[160,1280]{1,0:T(8,128)(2,1)S(1)} %collective-permute-done.5.refs_5_.refs_6_), channel_id=1, source_target_pairs={{0,16},{1,17},{2,18},{3,19},{4,20},{5,21},{6,22},{7,23},{8,24},{9,... | collective-permute-start | bytes 1228808 | tf_op jit(solution)/shard_map/ppermute | solution.py:51
  32.0 2.7 %collective-permute-start.12 = (bf16[80,1280]{1,0:T(8,128)(2,1)S(1)}, bf16[80,1280]{1,0:T(8,128)(2,1)S(1)}, u32[]{:S(2)}, u32[]{:S(2)}) collective-permute-start(bf16[80,1280]{1,0:T(8,128)(2,1)S(1)} %slice.66), channel_id=1, source_target_pairs={{0,96},{1,97},{2,98},{3,99},{4,100},{5,101},{6,102},{7,103},{8,104... | collective-permute-start | bytes 614408 | tf_op jit(solution)/shard_map/ppermute | solution.py:51
  34.8 2.2 %collective-permute-start.13 = (bf16[80,1280]{1,0:T(8,128)(2,1)S(1)}, bf16[80,1280]{1,0:T(8,128)(2,1)S(1)}, u32[]{:S(2)}, u32[]{:S(2)}) collective-permute-start(bf16[80,1280]{1,0:T(8,128)(2,1)S(1)} %slice.67), channel_id=1, source_target_pairs={{0,12},{1,13},{2,14},{3,15},{4,0},{5,1},{6,2},{7,3},{8,4},{9,5},{1... | collective-permute-start | bytes 614408 | tf_op jit(solution)/shard_map/ppermute | solution.py:51
  36.9 3.7 %collective-permute-start.20 = (bf16[80,1280]{1,0:T(8,128)(2,1)S(1)}, bf16[80,1280]{1,0:T(8,128)(2,1)S(1)}, u32[]{:S(2)}, u32[]{:S(2)}) collective-permute-start(bf16[80,1280]{1,0:T(8,128)(2,1)S(1)} %collective-permute-done.10.refs_10_.refs_11_), channel_id=1, source_target_pairs={{0,16},{1,17},{2,18},{3,19},{4,20},{5,21},{6,22},{7,23},{8,24},{9,... | collective-permute-start | bytes 614408 | tf_op jit(solution)/shard_map/ppermute | solution.py:51
  41.4 2.5 %collective-permute-start.18 = (bf16[160,1280]{1,0:T(8,128)(2,1)S(1)}, bf16[160,1280]{1,0:T(8,128)(2,1)}, u32[]{:S(2)}, u32[]{:S(2)}) collective-permute-start(bf16[160,1280]{1,0:T(8,128)(2,1)S(1)} %collective-permute-done.8.refs_8_.refs_9_), channel_id=1, source_target_pairs={{0,16},{1,17},{2,18},{3,19},{4,20},{5,21},{6,22},{7,23},{8,24},{9,... | collective-permute-start | bytes 1228808 | tf_op jit(solution)/shard_map/ppermute | solution.py:51
  52.2 3.5 %collective-permute-start.3 = (bf16[512,1280]{1,0:T(8,128)(2,1)}, bf16[512,1280]{1,0:T(8,128)(2,1)S(1)}, u32[]{:S(2)}, u32[]{:S(2)}) collective-permute-start(bf16[512,1280]{1,0:T(8,128)(2,1)} %bitcast.46), channel_id=1, source_target_pairs={{0,2},{2,4},{4,6},{6,8},{8,10},{10,12},{12,14},{14,16},{16,18},{18... | collective-permute-start | bytes 3932168 | tf_op jit(solution)/shard_map/ppermute | solution.py:412
  57.6 21.6 %own_attention.1 = (bf16[512,1280]{1,0:T(8,128)(2,1)}, f32[256,1280]{1,0:T(8,128)}) custom-call(s32[7]{0:T(128)S(1)} %stack.46.place_ref, s32[2,768]{1,0:T(2,128)S(1)} %fusion.9.ends_ref.refs_24_, bf16[512,1280]{1,0:T(8,128)(2,1)} %bitcast.47, f32[1,1280]{1,0:T(1,128)S(1)} %broadcast_in_dim.71.refs_1_.refs_2_, bf16[640,3840]{1,0:T(8,128)(2,1)} %refs_3_.3, ...), custom_call_target="tpu_custom_call" | custom-call | flops 15000000512 | bytes 20000000 | tf_op jit(solution)/shard_map/own_attention/pallas_call | solution.py:366
  79.2 4.7 %collective-permute-done.3.refs_0_ = bf16[512,1280]{1,0:T(8,128)(2,1)S(1)} collective-permute-done((bf16[512,1280]{1,0:T(8,128)(2,1)}, bf16[512,1280]{1,0:T(8,128)(2,1)S(1)}, u32[]{:S(2)}, u32[]{:S(2)}) %collective-permute-start.3) | collective-permute-done | bytes 1310752 | tf_op jit(solution)/shard_map/ppermute | solution.py:412
  85.0 25.6 %edge_attention.1 = (bf16[512,1280]{1,0:T(8,128)(2,1)}, bf16[512,1280]{1,0:T(8,128)(2,1)}, bf16[256,1280]{1,0:T(8,128)(2,1)}, bf16[16,1280]{1,0:T(8,128)(2,1)S(1)}) custom-call(s32[7]{0:T(128)S(1)} %stack.44.place_ref, s32[2,1280]{1,0:T(2,128)S(1)} %pad_add_fusion.ends_ref.refs_25_, bf16[512,1280]{1,0:T(8,128)(2,1)} %copy-done.8, ...), custom_call_target="tpu_custom_call" | custom-call | flops 15000000512 | bytes 20000000 | tf_op jit(solution)/shard_map/edge_attention/pallas_call | solution.py:366
  110.7 1.9 %collective-permute-start.24 = (bf16[512,1280]{1,0:T(8,128)(2,1)}, bf16[512,1280]{1,0:T(8,128)(2,1)S(1)}, u32[]{:S(2)}, u32[]{:S(2)}) collective-permute-start(bf16[512,1280]{1,0:T(8,128)(2,1)} %get-tuple-element.128), channel_id=1, source_target_pairs={{2,0},{4,2},{6,4},{8,6},{10,8},{12,10},{14,12},{16,14},{18,16},{20... | collective-permute-start | bytes 3932168 | tf_op jit(solution)/shard_map/ppermute | solution.py:455
  114.1 9.1 %collective-permute-start.25 = (f32[8,128]{1,0:T(8,128)S(1)}, f32[8,128]{1,0:T(8,128)S(1)}, u32[]{:S(2)}, u32[]{:S(2)}) collective-permute-start(f32[8,128]{1,0:T(8,128)S(1)} %broadcast_in_dim.74), channel_id=1, source_target_pairs={{0,1},{1,0},{2,3},{3,2},{4,5},{5,4},{6,7},{7,6},{8,9},{9,8},{10,11... | collective-permute-start | bytes 12296 | tf_op jit(solution)/shard_map/ppermute | solution.py:442
  123.2 18.3 %collective-permute-done.25 = f32[8,128]{1,0:T(8,128)S(1)} collective-permute-done((f32[8,128]{1,0:T(8,128)S(1)}, f32[8,128]{1,0:T(8,128)S(1)}, u32[]{:S(2)}, u32[]{:S(2)}) %collective-permute-start.25) | collective-permute-done | bytes 4128 | tf_op jit(solution)/shard_map/ppermute | solution.py:442
  142.7 37.9 %conditional.1 = (f32[1,256,1280]{2,1,0:T(8,128)}) conditional(s32[]{:T(128)} %convert_element_type.56, (s32[]{:T(128)}, bf16[256,1280]{1,0:T(8,128)(2,1)}) %tuple.26, (bf16[16,1280]{1,0:T(8,128)(2,1)S(1)}, s32[1,256]{1,0:T(1,128)S(1)}, s32[]{:T(128)}, s32[]{:T(128)}, s32[1,256]{1,0:T(1,128)S(1)}, /*index=5*/pred[1,256]{1,0:T(4,128)(4,1)S(1)}, (), ...), branch_computations={%region_7.9_spmd, %region_9.10_spmd} | conditional | flops 2124808 | bytes 11489468 | solution.py:479
  142.8 30.0 %all_to_all.14 = bf16[32,16,1280]{2,1,0:T(8,128)(2,1)S(1)} all-to-all(bf16[32,16,1280]{2,1,0:T(8,128)(2,1)S(1)} %broadcast_in_dim.36), channel_id=1, replica_groups=mesh['x'=4,'co'=2,'z'=4,'yh'=2,'dp'=2] {'x','z','yh'}, dimensions={0} | all-to-all | bytes 2621440 | tf_op jit(solution)/shard_map/cond/branch_1_fun/all_to_all | solution.py:458
  172.8 3.2 %collective-permute-start.2 = (bf16[512,1280]{1,0:T(8,128)(2,1)S(1)}, bf16[512,1280]{1,0:T(8,128)(2,1)S(1)}, u32[]{:S(2)}, u32[]{:S(2)}) collective-permute-start(bf16[512,1280]{1,0:T(8,128)(2,1)S(1)} %bitcast.33), channel_id=1, source_target_pairs={{0,16},{16,0},{1,17},{17,1},{2,18},{18,2},{3,19},{19,3},{4,20},{20... | collective-permute-start | bytes 3932168 | tf_op jit(solution)/shard_map/cond/branch_1_fun/ppermute | solution.py:461
  176.0 2.6 %collective-permute-done.2.far_ref = bf16[512,1280]{1,0:T(8,128)(2,1)S(1)} collective-permute-done((bf16[512,1280]{1,0:T(8,128)(2,1)S(1)}, bf16[512,1280]{1,0:T(8,128)(2,1)S(1)}, u32[]{:S(2)}, u32[]{:S(2)}) %collective-permute-start.2) | collective-permute-done | bytes 1310752 | tf_op jit(solution)/shard_map/cond/branch_1_fun/ppermute | solution.py:461
  178.7 1.9 %unpack.1 = f32[256,1280]{1,0:T(8,128)} custom-call(bf16[512,1280]{1,0:T(8,128)(2,1)S(1)} %bitcast.34, bf16[512,1280]{1,0:T(8,128)(2,1)S(1)} %collective-permute-done.2.far_ref, s32[1,256]{1,0:T(1,128)S(1)} %fusion.4.slot_ref), custom_call_target="tpu_custom_call" | custom-call | tf_op jit(solution)/shard_map/cond/branch_1_fun/unpack/pallas_call | solution.py:341
  (87 shorter events, 21.3 us)
Async XLA Ops:
  2.0 12.7 %collective-permute-start.4 = (bf16[160,1280]{1,0:T(8,128)(2,1)S(1)}, bf16[160,1280]{1,0:T(8,128)(2,1)S(1)}, u32[]{:S(2)}, u32[]{:S(2)}) collective-permute-start(bf16[160,1280]{1,0:T(8,128)(2,1)S(1)} %get-tuple-element.162), channel_id=1, source_target_pairs={{0,1},{1,2},{2,3},{3,0},{4,5},{5,6},{6,7},{7,4},{8,9},{9,10},{10,1... | collective-permute-start | bytes 1228808 | tf_op jit(solution)/shard_map/ppermute | solution.py:51
  4.2 13.2 %collective-permute-start.5 = (bf16[160,1280]{1,0:T(8,128)(2,1)S(1)}, bf16[160,1280]{1,0:T(8,128)(2,1)S(1)}, u32[]{:S(2)}, u32[]{:S(2)}) collective-permute-start(bf16[160,1280]{1,0:T(8,128)(2,1)S(1)} %get-tuple-element.161), channel_id=1, source_target_pairs={{0,3},{1,0},{2,1},{3,2},{4,7},{5,4},{6,5},{7,6},{8,11},{9,8},{10,9... | collective-permute-start | bytes 1228808 | tf_op jit(solution)/shard_map/ppermute | solution.py:51
  14.7 10.9 %collective-permute-start.6 = (bf16[160,1280]{1,0:T(8,128)(2,1)S(1)}, bf16[160,1280]{1,0:T(8,128)(2,1)S(1)}, u32[]{:S(2)}, u32[]{:S(2)}) collective-permute-start(bf16[160,1280]{1,0:T(8,128)(2,1)S(1)} %collective-permute-done.4.refs_4_.refs_5_), channel_id=1, source_target_pairs={{0,32},{1,33},{2,34},{3,35},{4,36},{5,37},{6,38},{7,39},{8,40},{9,... | collective-permute-start | bytes 1228808 | tf_op jit(solution)/shard_map/ppermute | solution.py:51
  15.8 13.7 %collective-permute-start.8 = (bf16[160,1280]{1,0:T(8,128)(2,1)S(1)}, bf16[160,1280]{1,0:T(8,128)(2,1)S(1)}, u32[]{:S(2)}, u32[]{:S(2)}) collective-permute-start(bf16[160,1280]{1,0:T(8,128)(2,1)S(1)} %collective-permute-done.4.refs_4_.refs_5_), channel_id=1, source_target_pairs={{0,96},{1,97},{2,98},{3,99},{4,100},{5,101},{6,102},{7,103},{8,104... | collective-permute-start | bytes 1228808 | tf_op jit(solution)/shard_map/ppermute | solution.py:51
  17.4 11.5 %collective-permute-start.7 = (bf16[160,1280]{1,0:T(8,128)(2,1)S(1)}, bf16[160,1280]{1,0:T(8,128)(2,1)S(1)}, u32[]{:S(2)}, u32[]{:S(2)}) collective-permute-start(bf16[160,1280]{1,0:T(8,128)(2,1)S(1)} %collective-permute-done.5.refs_5_.refs_6_), channel_id=1, source_target_pairs={{0,4},{1,5},{2,6},{3,7},{4,8},{5,9},{6,10},{7,11},{8,12},{9,13},{1... | collective-permute-start | bytes 1228808 | tf_op jit(solution)/shard_map/ppermute | solution.py:51
  19.4 12.5 %collective-permute-start.9 = (bf16[160,1280]{1,0:T(8,128)(2,1)S(1)}, bf16[160,1280]{1,0:T(8,128)(2,1)S(1)}, u32[]{:S(2)}, u32[]{:S(2)}) collective-permute-start(bf16[160,1280]{1,0:T(8,128)(2,1)S(1)} %collective-permute-done.5.refs_5_.refs_6_), channel_id=1, source_target_pairs={{0,12},{1,13},{2,14},{3,15},{4,0},{5,1},{6,2},{7,3},{8,4},{9,5},{1... | collective-permute-start | bytes 1228808 | tf_op jit(solution)/shard_map/ppermute | solution.py:51
  21.6 13.1 %collective-permute-start.14 = (bf16[160,1280]{1,0:T(8,128)(2,1)S(1)}, bf16[160,1280]{1,0:T(8,128)(2,1)}, u32[]{:S(2)}, u32[]{:S(2)}) collective-permute-start(bf16[160,1280]{1,0:T(8,128)(2,1)S(1)} %collective-permute-done.4.refs_4_.refs_5_), channel_id=1, source_target_pairs={{0,16},{1,17},{2,18},{3,19},{4,20},{5,21},{6,22},{7,23},{8,24},{9,... | collective-permute-start | bytes 1228808 | tf_op jit(solution)/shard_map/ppermute | solution.py:51
  25.6 15.2 %collective-permute-start.15 = (bf16[160,1280]{1,0:T(8,128)(2,1)S(1)}, bf16[160,1280]{1,0:T(8,128)(2,1)}, u32[]{:S(2)}, u32[]{:S(2)}) collective-permute-start(bf16[160,1280]{1,0:T(8,128)(2,1)S(1)} %collective-permute-done.5.refs_5_.refs_6_), channel_id=1, source_target_pairs={{0,16},{1,17},{2,18},{3,19},{4,20},{5,21},{6,22},{7,23},{8,24},{9,... | collective-permute-start | bytes 1228808 | tf_op jit(solution)/shard_map/ppermute | solution.py:51
  28.8 8.1 %collective-permute-start.10 = (bf16[80,1280]{1,0:T(8,128)(2,1)S(1)}, bf16[80,1280]{1,0:T(8,128)(2,1)S(1)}, u32[]{:S(2)}, u32[]{:S(2)}) collective-permute-start(bf16[80,1280]{1,0:T(8,128)(2,1)S(1)} %slice.64), channel_id=1, source_target_pairs={{0,32},{1,33},{2,34},{3,35},{4,36},{5,37},{6,38},{7,39},{8,40},{9,... | collective-permute-start | bytes 614408 | tf_op jit(solution)/shard_map/ppermute | solution.py:51
  29.5 11.1 %collective-permute-start.11 = (bf16[80,1280]{1,0:T(8,128)(2,1)}, bf16[80,1280]{1,0:T(8,128)(2,1)S(1)}, u32[]{:S(2)}, u32[]{:S(2)}) collective-permute-start(bf16[80,1280]{1,0:T(8,128)(2,1)} %slice.65), channel_id=1, source_target_pairs={{0,4},{1,5},{2,6},{3,7},{4,8},{5,9},{6,10},{7,11},{8,12},{9,13},{1... | collective-permute-start | bytes 614408 | tf_op jit(solution)/shard_map/ppermute | solution.py:51
  32.0 9.3 %collective-permute-start.12 = (bf16[80,1280]{1,0:T(8,128)(2,1)S(1)}, bf16[80,1280]{1,0:T(8,128)(2,1)S(1)}, u32[]{:S(2)}, u32[]{:S(2)}) collective-permute-start(bf16[80,1280]{1,0:T(8,128)(2,1)S(1)} %slice.66), channel_id=1, source_target_pairs={{0,96},{1,97},{2,98},{3,99},{4,100},{5,101},{6,102},{7,103},{8,104... | collective-permute-start | bytes 614408 | tf_op jit(solution)/shard_map/ppermute | solution.py:51
  34.8 6.6 %collective-permute-start.13 = (bf16[80,1280]{1,0:T(8,128)(2,1)S(1)}, bf16[80,1280]{1,0:T(8,128)(2,1)S(1)}, u32[]{:S(2)}, u32[]{:S(2)}) collective-permute-start(bf16[80,1280]{1,0:T(8,128)(2,1)S(1)} %slice.67), channel_id=1, source_target_pairs={{0,12},{1,13},{2,14},{3,15},{4,0},{5,1},{6,2},{7,3},{8,4},{9,5},{1... | collective-permute-start | bytes 614408 | tf_op jit(solution)/shard_map/ppermute | solution.py:51
  36.9 7.0 %collective-permute-start.20 = (bf16[80,1280]{1,0:T(8,128)(2,1)S(1)}, bf16[80,1280]{1,0:T(8,128)(2,1)S(1)}, u32[]{:S(2)}, u32[]{:S(2)}) collective-permute-start(bf16[80,1280]{1,0:T(8,128)(2,1)S(1)} %collective-permute-done.10.refs_10_.refs_11_), channel_id=1, source_target_pairs={{0,16},{1,17},{2,18},{3,19},{4,20},{5,21},{6,22},{7,23},{8,24},{9,... | collective-permute-start | bytes 614408 | tf_op jit(solution)/shard_map/ppermute | solution.py:51
  40.7 4.0 %collective-permute-start.21 = (bf16[80,1280]{1,0:T(8,128)(2,1)S(1)}, bf16[80,1280]{1,0:T(8,128)(2,1)S(1)}, u32[]{:S(2)}, u32[]{:S(2)}) collective-permute-start(bf16[80,1280]{1,0:T(8,128)(2,1)S(1)} %collective-permute-done.11.refs_11_.refs_12_), channel_id=1, source_target_pairs={{0,16},{1,17},{2,18},{3,19},{4,20},{5,21},{6,22},{7,23},{8,24},{9,... | collective-permute-start | bytes 614408 | tf_op jit(solution)/shard_map/ppermute | solution.py:51
  40.8 14.9 %collective-permute-start.16 = (bf16[160,1280]{1,0:T(8,128)(2,1)S(1)}, bf16[160,1280]{1,0:T(8,128)(2,1)}, u32[]{:S(2)}, u32[]{:S(2)}) collective-permute-start(bf16[160,1280]{1,0:T(8,128)(2,1)S(1)} %collective-permute-done.6.refs_6_.refs_7_), channel_id=1, source_target_pairs={{0,16},{1,17},{2,18},{3,19},{4,20},{5,21},{6,22},{7,23},{8,24},{9,... | collective-permute-start | bytes 1228808 | tf_op jit(solution)/shard_map/ppermute | solution.py:51
  41.3 14.4 %collective-permute-start.17 = (bf16[160,1280]{1,0:T(8,128)(2,1)S(1)}, bf16[160,1280]{1,0:T(8,128)(2,1)}, u32[]{:S(2)}, u32[]{:S(2)}) collective-permute-start(bf16[160,1280]{1,0:T(8,128)(2,1)S(1)} %collective-permute-done.7.refs_7_.refs_8_), channel_id=1, source_target_pairs={{0,16},{1,17},{2,18},{3,19},{4,20},{5,21},{6,22},{7,23},{8,24},{9,... | collective-permute-start | bytes 1228808 | tf_op jit(solution)/shard_map/ppermute | solution.py:51
  41.4 14.3 %collective-permute-start.18 = (bf16[160,1280]{1,0:T(8,128)(2,1)S(1)}, bf16[160,1280]{1,0:T(8,128)(2,1)}, u32[]{:S(2)}, u32[]{:S(2)}) collective-permute-start(bf16[160,1280]{1,0:T(8,128)(2,1)S(1)} %collective-permute-done.8.refs_8_.refs_9_), channel_id=1, source_target_pairs={{0,16},{1,17},{2,18},{3,19},{4,20},{5,21},{6,22},{7,23},{8,24},{9,... | collective-permute-start | bytes 1228808 | tf_op jit(solution)/shard_map/ppermute | solution.py:51
  44.6 11.1 %collective-permute-start.19 = (bf16[160,1280]{1,0:T(8,128)(2,1)S(1)}, bf16[160,1280]{1,0:T(8,128)(2,1)}, u32[]{:S(2)}, u32[]{:S(2)}) collective-permute-start(bf16[160,1280]{1,0:T(8,128)(2,1)S(1)} %collective-permute-done.9.refs_9_.refs_10_), channel_id=1, source_target_pairs={{0,16},{1,17},{2,18},{3,19},{4,20},{5,21},{6,22},{7,23},{8,24},{9,... | collective-permute-start | bytes 1228808 | tf_op jit(solution)/shard_map/ppermute | solution.py:51
  45.3 5.4 %collective-permute-start.22 = (bf16[80,1280]{1,0:T(8,128)(2,1)S(1)}, bf16[80,1280]{1,0:T(8,128)(2,1)}, u32[]{:S(2)}, u32[]{:S(2)}) collective-permute-start(bf16[80,1280]{1,0:T(8,128)(2,1)S(1)} %collective-permute-done.12.refs_12_.refs_13_), channel_id=1, source_target_pairs={{0,16},{1,17},{2,18},{3,19},{4,20},{5,21},{6,22},{7,23},{8,24},{9,... | collective-permute-start | bytes 614408 | tf_op jit(solution)/shard_map/ppermute | solution.py:51
  50.7 1.5 collective-permute-start.23
  52.2 31.8 %collective-permute-start.3 = (bf16[512,1280]{1,0:T(8,128)(2,1)}, bf16[512,1280]{1,0:T(8,128)(2,1)S(1)}, u32[]{:S(2)}, u32[]{:S(2)}) collective-permute-start(bf16[512,1280]{1,0:T(8,128)(2,1)} %bitcast.46), channel_id=1, source_target_pairs={{0,2},{2,4},{4,6},{6,8},{8,10},{10,12},{12,14},{14,16},{16,18},{18... | collective-permute-start | bytes 3932168 | tf_op jit(solution)/shard_map/ppermute | solution.py:412
  110.7 69.9 %collective-permute-start.24 = (bf16[512,1280]{1,0:T(8,128)(2,1)}, bf16[512,1280]{1,0:T(8,128)(2,1)S(1)}, u32[]{:S(2)}, u32[]{:S(2)}) collective-permute-start(bf16[512,1280]{1,0:T(8,128)(2,1)} %get-tuple-element.128), channel_id=1, source_target_pairs={{2,0},{4,2},{6,4},{8,6},{10,8},{12,10},{14,12},{16,14},{18,16},{20... | collective-permute-start | bytes 3932168 | tf_op jit(solution)/shard_map/ppermute | solution.py:455
  114.1 27.4 %collective-permute-start.25 = (f32[8,128]{1,0:T(8,128)S(1)}, f32[8,128]{1,0:T(8,128)S(1)}, u32[]{:S(2)}, u32[]{:S(2)}) collective-permute-start(f32[8,128]{1,0:T(8,128)S(1)} %broadcast_in_dim.74), channel_id=1, source_target_pairs={{0,1},{1,0},{2,3},{3,2},{4,5},{5,4},{6,7},{7,6},{8,9},{9,8},{10,11... | collective-permute-start | bytes 12296 | tf_op jit(solution)/shard_map/ppermute | solution.py:442
  172.8 5.8 %collective-permute-start.2 = (bf16[512,1280]{1,0:T(8,128)(2,1)S(1)}, bf16[512,1280]{1,0:T(8,128)(2,1)S(1)}, u32[]{:S(2)}, u32[]{:S(2)}) collective-permute-start(bf16[512,1280]{1,0:T(8,128)(2,1)S(1)} %bitcast.33), channel_id=1, source_target_pairs={{0,16},{16,0},{1,17},{17,1},{2,18},{18,2},{3,19},{19,3},{4,20},{20... | collective-permute-start | bytes 3932168 | tf_op jit(solution)/shard_map/cond/branch_1_fun/ppermute | solution.py:461
  (9 other events, 140.9 us)

commit v8 on v7

--- a/solution.py
+++ b/solution.py
@@ -68,7 +68,7 @@
         lens_ref, hin_ref, sum_ref, refs = *refs[:3], refs[3:]
         hprev_ref, hown_ref, pooled_ref, few_ref, refs = *refs[:4], refs[4:]
     else:
-        image_ref, hown_ref, sum_ref, refs = *refs[:3], refs[3:]
+        image_ref, lens_ref, hown_ref, sum_ref, few_ref, refs = *refs[:5], refs[5:]
     if edge:
         wide_ref, refs = refs[0], refs[1:]
     (
@@ -304,15 +304,9 @@
             preferred_element_type=jnp.float32,
         )
         label = lax.broadcasted_iota(jnp.int32, (IMAGES, D), 0)
-        sums = sum_ref[...] + jnp.where(label == place_ref[6], extra[0:1, :], 0.0)
-        pooled = (sums / lens_ref[...]).astype(jnp.bfloat16)
-        pooled_ref[...] = pooled
-        label = lax.broadcasted_iota(jnp.int32, (SLOTS, IMAGES), 0) + place_ref[6]
-        pick = lax.broadcasted_iota(jnp.int32, (SLOTS, IMAGES), 1) == label
-        few_ref[...] = jnp.dot(
-            jnp.where(pick, 1.0, 0.0).astype(jnp.bfloat16), pooled,
-            preferred_element_type=jnp.float32,
-        ).astype(jnp.bfloat16)
+        alone = jnp.where(label == place_ref[6], extra[0:1, :] / lens_ref[...], 0.0)
+        pooled_ref[...] = sum_ref[...] + alone.astype(jnp.bfloat16)
+        few_ref[...] = jnp.sum(alone, axis=0, keepdims=True).astype(jnp.bfloat16)
         return
     hown_ref[...] = hid_ref[0:LOCAL, :]
     label = lax.broadcasted_iota(jnp.int32, (IMAGES, LOCAL), 0)
@@ -322,30 +316,38 @@
         jnp.where(member, 1.0, 0.0).astype(jnp.bfloat16), hid_ref[0:LOCAL, :],
         preferred_element_type=jnp.float32,
     )
-    sum_ref[...] = sums
-
-
-def unpack_kernel(near_ref, far_ref, slot_ref, out_ref):
-    at = lax.broadcasted_iota(jnp.int32, (32 * SLOTS, IMAGES), 0)
+    means = (sums / lens_ref[...]).astype(jnp.bfloat16)
+    sum_ref[...] = means
+    label = lax.broadcasted_iota(jnp.int32, (SLOTS, IMAGES), 0) + place_ref[6]
+    pick = lax.broadcasted_iota(jnp.int32, (SLOTS, IMAGES), 1) == label
+    few_ref[...] = jnp.dot(
+        jnp.where(pick, 1.0, 0.0).astype(jnp.bfloat16), means, preferred_element_type=jnp.float32
+    ).astype(jnp.bfloat16)
+
+
+def unpack_kernel(near_ref, far_ref, near_edge_ref, far_edge_ref, slot_ref, out_ref):
     means = jnp.zeros((IMAGES, D), jnp.float32)
-    for i, ref in enumerate((near_ref, far_ref)):
-        pick = jnp.where(slot_ref[...] == at + i * 32 * SLOTS, 1.0, 0.0).astype(jnp.bfloat16)
-        means = means + lax.dot_general(
-            pick, ref[...], (((0,), (0,)), ((), ())), preferred_element_type=jnp.float32
-        )
+    for row, refs in ((0, (near_ref, far_ref)), (1, (near_edge_ref, far_edge_ref))):
+        for i, ref in enumerate(refs):
+            count = ref.shape[0]
+            at = lax.broadcasted_iota(jnp.int32, (count, IMAGES), 0) + i * count
+            pick = jnp.where(slot_ref[row : row + 1, :] == at, 1.0, 0.0).astype(jnp.bfloat16)
+            means = means + lax.dot_general(
+                pick, ref[...], (((0,), (0,)), ((), ())), preferred_element_type=jnp.float32
+            )
     out_ref[...] = means
 
 
-def unpack(near, far, slot):
+def unpack(near, far, near_edge, far_edge, slot):
     vmem = pl.BlockSpec(memory_space=pltpu.VMEM)
     return pl.pallas_call(
         unpack_kernel,
         out_shape=jax.ShapeDtypeStruct((IMAGES, D), jnp.float32),
-        in_specs=[vmem] * 3,
+        in_specs=[vmem] * 5,
         out_specs=vmem,
         compiler_params=pltpu.CompilerParams(vmem_limit_bytes=16 * 2**20),
         name="unpack",
-    )(near, far, slot)
+    )(near, far, near_edge, far_edge, slot)
 
 
 def attention(edge, place, spans, inputs, gain, weights, extra):
@@ -355,14 +357,13 @@
     rows = LOCAL + 256
     width = WIDTHS[-1]
     hidden = jax.ShapeDtypeStruct((LOCAL, D), jnp.bfloat16)
-    sums = jax.ShapeDtypeStruct((IMAGES, D), jnp.float32)
-    if edge:
-        pooled = jax.ShapeDtypeStruct((IMAGES, D), jnp.bfloat16)
-        outs = (hidden, hidden, pooled, jax.ShapeDtypeStruct((SLOTS, D), jnp.bfloat16))
+    pooled = jax.ShapeDtypeStruct((IMAGES, D), jnp.bfloat16)
+    if edge:
+        outs = (hidden, hidden, pooled, jax.ShapeDtypeStruct((1, D), jnp.bfloat16))
         tail = [vmem, vmem, vmem]
     else:
-        outs = (hidden, sums)
-        tail = [vmem]
+        outs = (hidden, pooled, jax.ShapeDtypeStruct((SLOTS, D), jnp.bfloat16))
+        tail = [vmem, vmem]
     return pl.pallas_call(
         functools.partial(attention_kernel, edge),
         out_shape=outs,
@@ -437,7 +438,8 @@
     rank = jnp.arange(IMAGES, dtype=jnp.int32) - leader
     group = owner // 16 * 8 + owner % 8
     slot = jnp.where(owner // 8 % 2 == co, 0, 32 * SLOTS) + group * SLOTS + rank
-    slot = slot[None]
+    edge_slot = jnp.where(owner // 8 % 2 == co, 0, 32) + group
+    slot = jnp.stack([slot, jnp.where(rank == 0, edge_slot, -1)])
     crowded = jnp.full((8, 128), jnp.max(rank) >= SLOTS).astype(jnp.float32)
     elsewhere = lax.ppermute(crowded, "dp", SWAP)
     fits = crowded[0, 0] + elsewhere[0, 0] == 0.0
@@ -445,23 +447,26 @@
     gain = ln_gain[None]
     weights = [w_qkv, w_out, *mine, *other]
 
-    hown, sums = attention(
-        False, places[1], spans[:, LOCAL:] - LOCAL, [own], gain, weights, [image[None, LOCAL:WIN]]
+    column = lens.astype(jnp.float32)[:, None]
+    hown, means, few = attention(
+        False, places[1], spans[:, LOCAL:] - LOCAL, [own], gain, weights,
+        [image[None, LOCAL:WIN], column],
     )
-    hprev, hown, part, few = attention(
-        True, places[0], spans, [prev, own], gain, weights,
-        [lens.astype(jnp.float32)[:, None], hown, sums],
+    near = lax.all_to_all(
+        jnp.broadcast_to(few[None], (32, SLOTS, D)), GROUP, 0, 0, tiled=True
+    ).reshape(32 * SLOTS, D)
+    hprev, hown, part, alone = attention(
+        True, places[0], spans, [prev, own], gain, weights, [column, hown, means]
     )
     back = lax.ppermute(hprev, TOKEN_AXES, [(i + 1, i) for i in range(63)])
-
-    def pooled_directly(few, part):
-        near = lax.all_to_all(
-            jnp.broadcast_to(few[None], (32, SLOTS, D)), GROUP, 0, 0, tiled=True
-        ).reshape(32 * SLOTS, D)
-        far = lax.ppermute(near, "co", SWAP)
-        return unpack(near, far, slot)
-
-    def pooled_by_sums(few, part):
+    far = lax.ppermute(near, "co", SWAP)
+    near_edge = lax.all_to_all(jnp.broadcast_to(alone, (32, D)), GROUP, 0, 0, tiled=True)
+    far_edge = lax.ppermute(near_edge, "co", SWAP)
+
+    def pooled_directly(part):
+        return unpack(near, far, near_edge, far_edge, slot)
+
+    def pooled_by_sums(part):
         part = part.reshape(2, IMAGES // 2, D)
         kept = lax.dynamic_index_in_dim(part, co, 0, keepdims=False)
         given = lax.dynamic_index_in_dim(part, 1 - co, 0, keepdims=False)
@@ -476,7 +481,7 @@
         pooled = jnp.where(co == 0, jnp.stack([half, rest]), jnp.stack([rest, half]))
         return pooled.reshape(IMAGES, D).astype(jnp.float32)
 
-    pooled = lax.cond(fits, pooled_directly, pooled_by_sums, few, part)[None]
+    pooled = lax.cond(fits, pooled_directly, pooled_by_sums, part)[None]
 
     here = jnp.arange(LOCAL, dtype=jnp.int32)[:, None] < limit - LOCAL
     hidden = jnp.where(here, hown, back)[None]

time: 182 us -> 159 us (0.87)
  blocking collectives: 30 us -> 0 us
  starting transfers between devices: 45.3 us -> 58.2 us
  waiting for transfers between devices: 38.1 us -> 27 us
  other arithmetic: 4.47 us -> 6.98 us
    all_to_all x1 -> x0, blocking collectives: 30 us -> none  [pooled_directly(): lax.all_to_all(jnp.broadcast_to(few[None], (32, SLOTS, D)), GROUP, 0, 0,...]
    all_to_all x0 -> x2, starting transfers between devices: none -> 10.4 us  [the longest x1 6.58 us: layer(): lax.all_to_all(jnp.broadcast_to(few[None], (32, SLOTS, D)), GROUP, 0, 0,...]
    ppermute x1, waiting for transfers between devices: 18.3 us -> 11.3 us  [layer(): elsewhere = lax.ppermute(crowded, 'dp', SWAP)]
    ppermute x1, waiting for transfers between devices: 4.75 us -> 0.01 us  [layer(): prev = lax.ppermute(own, TOKEN_AXES, [(i, i + 1) for i in range(63)])]
    all_to_all x0 -> x2, waiting for transfers between devices: none -> 2.7 us  [the longest x1 2.69 us: layer(): lax.all_to_all(jnp.broadcast_to(alone, (32, D)), GROUP, 0, 0, tiled=True)]
    ppermute x1 -> x2, waiting for transfers between devices: 2.64 us -> 0.01 us  [the longest x1 0.01 us: layer(): far_edge = lax.ppermute(near_edge, 'co', SWAP)]
    unnamed x18 -> x21, local copies, waits for them, and re-layouts: 4.29 us -> 3.66 us
  transfers between devices with their start and end apart: 24 -> 27, of which waited for: 7 -> 6; matrix products, arithmetic and copies ran while one was open for 4% -> 9% of each run, Pallas kernels for 13% -> 30%
where the time goes in v8:
time: 159 us; the launch traced here: 157 us
  starting transfers between devices  58.2 us (37%)
  Pallas kernels  49.3 us (31%)
  waiting for transfers between devices  27 us (17%)
  local copies, waits for them, and re-layouts  11.1 us (7%)
  other arithmetic  6.98 us (4%)
  between operations  4.82 us (3%)
    pallas_call x2, Pallas kernels, attention(): pl.pallas_call(functools.partial(attention_kernel, edge), out_shape=outs,...  46.7 us
    ppermute x20, starting transfers between devices, moved(): return lax.ppermute(piece, ALL_AXES, pairs)  28.2 us
    ppermute x20, waiting for transfers between devices, moved(): return lax.ppermute(piece, ALL_AXES, pairs)  12.9 us
    ppermute x1, waiting for transfers between devices, layer(): elsewhere = lax.ppermute(crowded, 'dp', SWAP)  11.3 us
    ppermute x1, starting transfers between devices, layer(): elsewhere = lax.ppermute(crowded, 'dp', SWAP)  10.5 us
    all_to_all x1, starting transfers between devices, layer(): lax.all_to_all(jnp.broadcast_to(few[None], (32, SLOTS, D)), GROUP, 0, 0,...  6.58 us
    ppermute x1, starting transfers between devices, layer(): prev = lax.ppermute(own, TOKEN_AXES, [(i, i + 1) for i in range(63)])  4.29 us
    all_to_all x1, starting transfers between devices, layer(): lax.all_to_all(jnp.broadcast_to(alone, (32, D)), GROUP, 0, 0, tiled=True)  3.86 us
  transfers between devices with their start and end apart: 27, of which 6 were waited for; matrix products, arithmetic and copies ran while one was open for 9% of the time, Pallas kernels for 30%

profile of v8, /device:TPU:1, one launch (start us, length us, event | category | flops | bytes accessed | tf_op | source)
XLA Modules:
  0.0 157.4 jit_solution(16748278218552985600)
XLA Ops:
  2.0 3.6 %collective-permute-start.4 = (bf16[160,1280]{1,0:T(8,128)(2,1)S(1)}, bf16[160,1280]{1,0:T(8,128)(2,1)S(1)}, u32[]{:S(2)}, u32[]{:S(2)}) collective-permute-start(bf16[160,1280]{1,0:T(8,128)(2,1)S(1)} %get-tuple-element.49), channel_id=1, source_target_pairs={{0,3},{1,0},{2,1},{3,2},{4,7},{5,4},{6,5},{7,6},{8,11},{9,8},{10,9... | collective-permute-start | bytes 1228808 | tf_op jit(solution)/shard_map/ppermute | solution.py:51
  6.3 7.5 %collective-permute-done.4.refs_5_.refs_6_ = bf16[160,1280]{1,0:T(8,128)(2,1)S(1)} collective-permute-done((bf16[160,1280]{1,0:T(8,128)(2,1)S(1)}, bf16[160,1280]{1,0:T(8,128)(2,1)S(1)}, u32[]{:S(2)}, u32[]{:S(2)}) %collective-permute-start.4) | collective-permute-done | bytes 409632 | tf_op jit(solution)/shard_map/ppermute | solution.py:51
  13.8 3.8 %collective-permute-start.8 = (bf16[160,1280]{1,0:T(8,128)(2,1)S(1)}, bf16[160,1280]{1,0:T(8,128)(2,1)}, u32[]{:S(2)}, u32[]{:S(2)}) collective-permute-start(bf16[160,1280]{1,0:T(8,128)(2,1)S(1)} %collective-permute-done.4.refs_5_.refs_6_), channel_id=1, source_target_pairs={{0,12},{1,13},{2,14},{3,15},{4,0},{5,1},{6,2},{7,3},{8,4},{9,5},{1... | collective-permute-start | bytes 1228808 | tf_op jit(solution)/shard_map/ppermute | solution.py:51
  18.1 1.9 %collective-permute-start.14 = (bf16[160,1280]{1,0:T(8,128)(2,1)S(1)}, bf16[160,1280]{1,0:T(8,128)(2,1)}, u32[]{:S(2)}, u32[]{:S(2)}) collective-permute-start(bf16[160,1280]{1,0:T(8,128)(2,1)S(1)} %collective-permute-done.4.refs_5_.refs_6_), channel_id=1, source_target_pairs={{0,16},{1,17},{2,18},{3,19},{4,20},{5,21},{6,22},{7,23},{8,24},{9,... | collective-permute-start | bytes 1228808 | tf_op jit(solution)/shard_map/ppermute | solution.py:51
  20.1 2.5 %collective-permute-start.7 = (bf16[160,1280]{1,0:T(8,128)(2,1)S(1)}, bf16[160,1280]{1,0:T(8,128)(2,1)S(1)}, u32[]{:S(2)}, u32[]{:S(2)}) collective-permute-start(bf16[160,1280]{1,0:T(8,128)(2,1)S(1)} %collective-permute-done.3.refs_4_.refs_5_), channel_id=1, source_target_pairs={{0,96},{1,97},{2,98},{3,99},{4,100},{5,101},{6,102},{7,103},{8,104... | collective-permute-start | bytes 1228808 | tf_op jit(solution)/shard_map/ppermute | solution.py:51
  22.6 2.3 %collective-permute-done.8.refs_9_.refs_10_ = bf16[160,1280]{1,0:T(8,128)(2,1)} collective-permute-done((bf16[160,1280]{1,0:T(8,128)(2,1)S(1)}, bf16[160,1280]{1,0:T(8,128)(2,1)}, u32[]{:S(2)}, u32[]{:S(2)}) %collective-permute-start.8) | collective-permute-done | bytes 409632 | tf_op jit(solution)/shard_map/ppermute | solution.py:51
  28.0 2.6 %collective-permute-start.12 = (bf16[80,1280]{1,0:T(8,128)(2,1)S(1)}, bf16[80,1280]{1,0:T(8,128)(2,1)S(1)}, u32[]{:S(2)}, u32[]{:S(2)}) collective-permute-start(bf16[80,1280]{1,0:T(8,128)(2,1)S(1)} %slice.67), channel_id=1, source_target_pairs={{0,12},{1,13},{2,14},{3,15},{4,0},{5,1},{6,2},{7,3},{8,4},{9,5},{1... | collective-permute-start | bytes 614408 | tf_op jit(solution)/shard_map/ppermute | solution.py:51
  32.6 2.1 %collective-permute-done.5.refs_6_.refs_7_ = bf16[160,1280]{1,0:T(8,128)(2,1)S(1)} collective-permute-done((bf16[160,1280]{1,0:T(8,128)(2,1)S(1)}, bf16[160,1280]{1,0:T(8,128)(2,1)S(1)}, u32[]{:S(2)}, u32[]{:S(2)}) %collective-permute-start.5) | collective-permute-done | bytes 409632 | tf_op jit(solution)/shard_map/ppermute | solution.py:51
  36.3 3.8 %collective-permute-start.18 = (bf16[160,1280]{1,0:T(8,128)(2,1)}, bf16[160,1280]{1,0:T(8,128)(2,1)}, u32[]{:S(2)}, u32[]{:S(2)}) collective-permute-start(bf16[160,1280]{1,0:T(8,128)(2,1)} %collective-permute-done.8.refs_9_.refs_10_), channel_id=1, source_target_pairs={{0,16},{1,17},{2,18},{3,19},{4,20},{5,21},{6,22},{7,23},{8,24},{9,... | collective-permute-start | bytes 1228808 | tf_op jit(solution)/shard_map/ppermute | solution.py:51
  40.2 2.3 %collective-permute-start.16 = (bf16[160,1280]{1,0:T(8,128)(2,1)S(1)}, bf16[160,1280]{1,0:T(8,128)(2,1)}, u32[]{:S(2)}, u32[]{:S(2)}) collective-permute-start(bf16[160,1280]{1,0:T(8,128)(2,1)S(1)} %collective-permute-done.6.refs_7_.refs_8_), channel_id=1, source_target_pairs={{0,16},{1,17},{2,18},{3,19},{4,20},{5,21},{6,22},{7,23},{8,24},{9,... | collective-permute-start | bytes 1228808 | tf_op jit(solution)/shard_map/ppermute | solution.py:51
  43.7 2.9 %collective-permute-start.15 = (bf16[160,1280]{1,0:T(8,128)(2,1)S(1)}, bf16[160,1280]{1,0:T(8,128)(2,1)}, u32[]{:S(2)}, u32[]{:S(2)}) collective-permute-start(bf16[160,1280]{1,0:T(8,128)(2,1)S(1)} %collective-permute-done.5.refs_6_.refs_7_), channel_id=1, source_target_pairs={{0,16},{1,17},{2,18},{3,19},{4,20},{5,21},{6,22},{7,23},{8,24},{9,... | collective-permute-start | bytes 1228808 | tf_op jit(solution)/shard_map/ppermute | solution.py:51
  52.0 4.3 %collective-permute-start.2 = (bf16[512,1280]{1,0:T(8,128)(2,1)}, bf16[512,1280]{1,0:T(8,128)(2,1)}, u32[]{:S(2)}, u32[]{:S(2)}) collective-permute-start(bf16[512,1280]{1,0:T(8,128)(2,1)} %bitcast.51), channel_id=1, source_target_pairs={{0,2},{2,4},{4,6},{6,8},{8,10},{10,12},{12,14},{14,16},{16,18},{18... | collective-permute-start | bytes 3932168 | tf_op jit(solution)/shard_map/ppermute | solution.py:413
  56.4 21.4 %own_attention.1 = (bf16[512,1280]{1,0:T(8,128)(2,1)}, bf16[256,1280]{1,0:T(8,128)(2,1)}, bf16[16,1280]{1,0:T(8,128)(2,1)S(1)}) custom-call(s32[7]{0:T(128)S(1)} %stack.51.place_ref, s32[2,768]{1,0:T(2,128)S(1)} %fusion.4.ends_ref.refs_24_, bf16[512,1280]{1,0:T(8,128)(2,1)} %bitcast.52, f32[1,1280]{1,0:T(1,128)S(1)} %broadcast_in_dim.81.refs_1_.refs_2_, ...), custom_call_target="tpu_custom_call" | custom-call | flops 15000000512 | bytes 20000000 | tf_op jit(solution)/shard_map/own_attention/pallas_call | solution.py:367
  78.9 6.6 %all-to-all-start.2 = ((bf16[32,16,1280]{2,1,0:T(8,128)(2,1)}), bf16[32,16,1280]{2,1,0:T(8,128)(2,1)}, u32[]{:S(2)}, u32[]{:S(2)}) async-start(bf16[32,16,1280]{2,1,0:T(8,128)(2,1)} %broadcast_in_dim.85), calls=%async_computation.2 | async-start | bytes 2621440 | tf_op jit(solution)/shard_map/all_to_all | solution.py:455
  87.4 25.4 %edge_attention.1 = (bf16[512,1280]{1,0:T(8,128)(2,1)}, bf16[512,1280]{1,0:T(8,128)(2,1)}, bf16[256,1280]{1,0:T(8,128)(2,1)}, bf16[1,1280]{1,0:T(2,128)(2,1)S(1)}) custom-call(s32[7]{0:T(128)S(1)} %stack.49.place_ref, s32[2,1280]{1,0:T(2,128)S(1)} %pad_add_fusion.ends_ref.refs_25_, bf16[512,1280]{1,0:T(8,128)(2,1)} %collective-permute-done.2.refs_0_, ...), custom_call_target="tpu_custom_call" | custom-call | flops 15000000512 | bytes 20000000 | tf_op jit(solution)/shard_map/edge_attention/pallas_call | solution.py:367
  112.8 2.1 %collective-permute-start.23 = (bf16[512,1280]{1,0:T(8,128)(2,1)}, bf16[512,1280]{1,0:T(8,128)(2,1)}, u32[]{:S(2)}, u32[]{:S(2)}) collective-permute-start(bf16[512,1280]{1,0:T(8,128)(2,1)} %get-tuple-element.37), channel_id=1, source_target_pairs={{2,0},{4,2},{6,4},{8,6},{10,8},{12,10},{14,12},{16,14},{18,16},{20... | collective-permute-start | bytes 3932168 | tf_op jit(solution)/shard_map/ppermute | solution.py:461
  116.5 10.5 %collective-permute-start.24 = (f32[8,128]{1,0:T(8,128)S(1)}, f32[8,128]{1,0:T(8,128)S(1)}, u32[]{:S(2)}, u32[]{:S(2)}) collective-permute-start(f32[8,128]{1,0:T(8,128)S(1)} %broadcast_in_dim.84), channel_id=1, source_target_pairs={{0,1},{1,0},{2,3},{3,2},{4,5},{5,4},{6,7},{7,6},{8,9},{9,8},{10,11... | collective-permute-start | bytes 12296 | tf_op jit(solution)/shard_map/ppermute | solution.py:444
  129.4 3.9 %all-to-all-start.3 = ((bf16[32,2,640]{2,1,0:T(2,128)(2,1)}), bf16[32,2,640]{2,1,0:T(2,128)(2,1)S(1)}, u32[]{:S(2)}, u32[]{:S(2)}) async-start(bf16[32,2,640]{2,1,0:T(2,128)(2,1)} %reshape.436), calls=%async_computation.3 | async-start | bytes 163840 | tf_op jit(solution)/shard_map/all_to_all | solution.py:463
  133.3 11.3 %collective-permute-done.24 = f32[8,128]{1,0:T(8,128)S(1)} collective-permute-done((f32[8,128]{1,0:T(8,128)S(1)}, f32[8,128]{1,0:T(8,128)S(1)}, u32[]{:S(2)}, u32[]{:S(2)}) %collective-permute-start.24) | collective-permute-done | bytes 4128 | tf_op jit(solution)/shard_map/ppermute | solution.py:444
  145.8 2.7 %all-to-all-done.3 = bf16[32,2,640]{2,1,0:T(2,128)(2,1)S(1)} async-done(((bf16[32,2,640]{2,1,0:T(2,128)(2,1)}), bf16[32,2,640]{2,1,0:T(2,128)(2,1)S(1)}, u32[]{:S(2)}, u32[]{:S(2)}) %all-to-all-start.3) | async-done | bytes 81952 | tf_op jit(solution)/shard_map/all_to_all | solution.py:463
  148.6 2.6 %collective-permute-start.26 = (bf16[32,1280]{1,0:T(8,128)(2,1)S(1)}, bf16[32,1280]{1,0:T(8,128)(2,1)S(1)}, u32[]{:S(2)}, u32[]{:S(2)}) collective-permute-start(bf16[32,1280]{1,0:T(8,128)(2,1)S(1)} %bitcast.42), channel_id=1, source_target_pairs={{0,16},{16,0},{1,17},{17,1},{2,18},{18,2},{3,19},{19,3},{4,20},{20... | collective-permute-start | bytes 245768 | tf_op jit(solution)/shard_map/ppermute | solution.py:464
  151.2 2.6 %select_bitcast_fusion = bf16[1,512,1280]{2,1,0:T(8,128)(2,1)} fusion(bf16[512,1280]{1,0:T(8,128)(2,1)S(1)} %copy-done.4, bf16[512,1280]{1,0:T(8,128)(2,1)} %collective-permute-done.23, pred[512]{0:T(512)(128)(4,1)S(1)} %iota_compare_fusion), kind=kLoop, calls=%fused_computation.9 | loop fusion | flops 655360 | bytes 3932672 | tf_op jit(solution)/shard_map/broadcast_in_dim | solution.py:487
  153.8 2.6 %conditional.1 = (f32[1,256,1280]{2,1,0:T(8,128)S(1)}) conditional(s32[]{:T(128)} %convert_element_type.56, (s32[]{:T(128)}, bf16[256,1280]{1,0:T(8,128)(2,1)S(1)}) %tuple.33, (bf16[512,1280]{1,0:T(8,128)(2,1)}, bf16[512,1280]{1,0:T(8,128)(2,1)S(1)}, bf16[32,1280]{1,0:T(8,128)(2,1)S(1)}, bf16[32,1280]{1,0:T(8,128)(2,1)S(1)}, ...), branch_computations={%region_7.9_spmd, %region_9.10_spmd} | conditional | flops 2124808 | bytes 11489468 | solution.py:484
  153.8 2.5 %unpack.1 = f32[256,1280]{1,0:T(8,128)S(1)} custom-call(bf16[512,1280]{1,0:T(8,128)(2,1)} %get-tuple-element.20.near_ref, bf16[512,1280]{1,0:T(8,128)(2,1)S(1)} %get-tuple-element.21.far_ref, bf16[32,1280]{1,0:T(8,128)(2,1)S(1)} %get-tuple-element.22.near_edge_ref, bf16[32,1280]{1,0:T(8,128)(2,1)S(1)} %get-tuple-element.23.far_edge_ref, ...), custom_call_target="tpu_custom_call" | custom-call | tf_op jit(solution)/shard_map/cond/branch_1_fun/unpack/pallas_call | solution.py:343
  (97 shorter events, 21.6 us)
Async XLA Ops:
  2.0 11.8 %collective-permute-start.4 = (bf16[160,1280]{1,0:T(8,128)(2,1)S(1)}, bf16[160,1280]{1,0:T(8,128)(2,1)S(1)}, u32[]{:S(2)}, u32[]{:S(2)}) collective-permute-start(bf16[160,1280]{1,0:T(8,128)(2,1)S(1)} %get-tuple-element.49), channel_id=1, source_target_pairs={{0,3},{1,0},{2,1},{3,2},{4,7},{5,4},{6,5},{7,6},{8,11},{9,8},{10,9... | collective-permute-start | bytes 1228808 | tf_op jit(solution)/shard_map/ppermute | solution.py:51
  5.6 14.3 %collective-permute-start.3 = (bf16[160,1280]{1,0:T(8,128)(2,1)S(1)}, bf16[160,1280]{1,0:T(8,128)(2,1)S(1)}, u32[]{:S(2)}, u32[]{:S(2)}) collective-permute-start(bf16[160,1280]{1,0:T(8,128)(2,1)S(1)} %get-tuple-element.50), channel_id=1, source_target_pairs={{0,1},{1,2},{2,3},{3,0},{4,5},{5,6},{6,7},{7,4},{8,9},{9,10},{10,1... | collective-permute-start | bytes 1228808 | tf_op jit(solution)/shard_map/ppermute | solution.py:51
  13.8 11.1 %collective-permute-start.8 = (bf16[160,1280]{1,0:T(8,128)(2,1)S(1)}, bf16[160,1280]{1,0:T(8,128)(2,1)}, u32[]{:S(2)}, u32[]{:S(2)}) collective-permute-start(bf16[160,1280]{1,0:T(8,128)(2,1)S(1)} %collective-permute-done.4.refs_5_.refs_6_), channel_id=1, source_target_pairs={{0,12},{1,13},{2,14},{3,15},{4,0},{5,1},{6,2},{7,3},{8,4},{9,5},{1... | collective-permute-start | bytes 1228808 | tf_op jit(solution)/shard_map/ppermute | solution.py:51
  17.6 10.4 %collective-permute-start.6 = (bf16[160,1280]{1,0:T(8,128)(2,1)S(1)}, bf16[160,1280]{1,0:T(8,128)(2,1)S(1)}, u32[]{:S(2)}, u32[]{:S(2)}) collective-permute-start(bf16[160,1280]{1,0:T(8,128)(2,1)S(1)} %collective-permute-done.4.refs_5_.refs_6_), channel_id=1, source_target_pairs={{0,4},{1,5},{2,6},{3,7},{4,8},{5,9},{6,10},{7,11},{8,12},{9,13},{1... | collective-permute-start | bytes 1228808 | tf_op jit(solution)/shard_map/ppermute | solution.py:51
  18.1 17.9 %collective-permute-start.14 = (bf16[160,1280]{1,0:T(8,128)(2,1)S(1)}, bf16[160,1280]{1,0:T(8,128)(2,1)}, u32[]{:S(2)}, u32[]{:S(2)}) collective-permute-start(bf16[160,1280]{1,0:T(8,128)(2,1)S(1)} %collective-permute-done.4.refs_5_.refs_6_), channel_id=1, source_target_pairs={{0,16},{1,17},{2,18},{3,19},{4,20},{5,21},{6,22},{7,23},{8,24},{9,... | collective-permute-start | bytes 1228808 | tf_op jit(solution)/shard_map/ppermute | solution.py:51
  20.0 16.3 %collective-permute-start.13 = (bf16[160,1280]{1,0:T(8,128)(2,1)S(1)}, bf16[160,1280]{1,0:T(8,128)(2,1)}, u32[]{:S(2)}, u32[]{:S(2)}) collective-permute-start(bf16[160,1280]{1,0:T(8,128)(2,1)S(1)} %collective-permute-done.3.refs_4_.refs_5_), channel_id=1, source_target_pairs={{0,16},{1,17},{2,18},{3,19},{4,20},{5,21},{6,22},{7,23},{8,24},{9,... | collective-permute-start | bytes 1228808 | tf_op jit(solution)/shard_map/ppermute | solution.py:51
  20.1 12.4 %collective-permute-start.7 = (bf16[160,1280]{1,0:T(8,128)(2,1)S(1)}, bf16[160,1280]{1,0:T(8,128)(2,1)S(1)}, u32[]{:S(2)}, u32[]{:S(2)}) collective-permute-start(bf16[160,1280]{1,0:T(8,128)(2,1)S(1)} %collective-permute-done.3.refs_4_.refs_5_), channel_id=1, source_target_pairs={{0,96},{1,97},{2,98},{3,99},{4,100},{5,101},{6,102},{7,103},{8,104... | collective-permute-start | bytes 1228808 | tf_op jit(solution)/shard_map/ppermute | solution.py:51
  24.8 9.8 %collective-permute-start.5 = (bf16[160,1280]{1,0:T(8,128)(2,1)S(1)}, bf16[160,1280]{1,0:T(8,128)(2,1)S(1)}, u32[]{:S(2)}, u32[]{:S(2)}) collective-permute-start(bf16[160,1280]{1,0:T(8,128)(2,1)S(1)} %collective-permute-done.3.refs_4_.refs_5_), channel_id=1, source_target_pairs={{0,32},{1,33},{2,34},{3,35},{4,36},{5,37},{6,38},{7,39},{8,40},{9,... | collective-permute-start | bytes 1228808 | tf_op jit(solution)/shard_map/ppermute | solution.py:51
  28.0 12.1 %collective-permute-start.12 = (bf16[80,1280]{1,0:T(8,128)(2,1)S(1)}, bf16[80,1280]{1,0:T(8,128)(2,1)S(1)}, u32[]{:S(2)}, u32[]{:S(2)}) collective-permute-start(bf16[80,1280]{1,0:T(8,128)(2,1)S(1)} %slice.67), channel_id=1, source_target_pairs={{0,12},{1,13},{2,14},{3,15},{4,0},{5,1},{6,2},{7,3},{8,4},{9,5},{1... | collective-permute-start | bytes 614408 | tf_op jit(solution)/shard_map/ppermute | solution.py:51
  32.5 7.7 %collective-permute-start.10 = (bf16[80,1280]{1,0:T(8,128)(2,1)S(1)}, bf16[80,1280]{1,0:T(8,128)(2,1)S(1)}, u32[]{:S(2)}, u32[]{:S(2)}) collective-permute-start(bf16[80,1280]{1,0:T(8,128)(2,1)S(1)} %slice.65), channel_id=1, source_target_pairs={{0,4},{1,5},{2,6},{3,7},{4,8},{5,9},{6,10},{7,11},{8,12},{9,13},{1... | collective-permute-start | bytes 614408 | tf_op jit(solution)/shard_map/ppermute | solution.py:51
  34.7 7.7 %collective-permute-start.11 = (bf16[80,1280]{1,0:T(8,128)(2,1)S(1)}, bf16[80,1280]{1,0:T(8,128)(2,1)S(1)}, u32[]{:S(2)}, u32[]{:S(2)}) collective-permute-start(bf16[80,1280]{1,0:T(8,128)(2,1)S(1)} %slice.66), channel_id=1, source_target_pairs={{0,96},{1,97},{2,98},{3,99},{4,100},{5,101},{6,102},{7,103},{8,104... | collective-permute-start | bytes 614408 | tf_op jit(solution)/shard_map/ppermute | solution.py:51
  36.0 7.7 %collective-permute-start.9 = (bf16[80,1280]{1,0:T(8,128)(2,1)S(1)}, bf16[80,1280]{1,0:T(8,128)(2,1)S(1)}, u32[]{:S(2)}, u32[]{:S(2)}) collective-permute-start(bf16[80,1280]{1,0:T(8,128)(2,1)S(1)} %slice.64), channel_id=1, source_target_pairs={{0,32},{1,33},{2,34},{3,35},{4,36},{5,37},{6,38},{7,39},{8,40},{9,... | collective-permute-start | bytes 614408 | tf_op jit(solution)/shard_map/ppermute | solution.py:51
  36.3 15.1 %collective-permute-start.18 = (bf16[160,1280]{1,0:T(8,128)(2,1)}, bf16[160,1280]{1,0:T(8,128)(2,1)}, u32[]{:S(2)}, u32[]{:S(2)}) collective-permute-start(bf16[160,1280]{1,0:T(8,128)(2,1)} %collective-permute-done.8.refs_9_.refs_10_), channel_id=1, source_target_pairs={{0,16},{1,17},{2,18},{3,19},{4,20},{5,21},{6,22},{7,23},{8,24},{9,... | collective-permute-start | bytes 1228808 | tf_op jit(solution)/shard_map/ppermute | solution.py:51
  40.1 6.5 %collective-permute-start.22 = (bf16[80,1280]{1,0:T(8,128)(2,1)S(1)}, bf16[80,1280]{1,0:T(8,128)(2,1)S(1)}, u32[]{:S(2)}, u32[]{:S(2)}) collective-permute-start(bf16[80,1280]{1,0:T(8,128)(2,1)S(1)} %collective-permute-done.12.refs_13_.refs_14_), channel_id=1, source_target_pairs={{0,16},{1,17},{2,18},{3,19},{4,20},{5,21},{6,22},{7,23},{8,24},{9,... | collective-permute-start | bytes 614408 | tf_op jit(solution)/shard_map/ppermute | solution.py:51
  40.2 11.9 %collective-permute-start.16 = (bf16[160,1280]{1,0:T(8,128)(2,1)S(1)}, bf16[160,1280]{1,0:T(8,128)(2,1)}, u32[]{:S(2)}, u32[]{:S(2)}) collective-permute-start(bf16[160,1280]{1,0:T(8,128)(2,1)S(1)} %collective-permute-done.6.refs_7_.refs_8_), channel_id=1, source_target_pairs={{0,16},{1,17},{2,18},{3,19},{4,20},{5,21},{6,22},{7,23},{8,24},{9,... | collective-permute-start | bytes 1228808 | tf_op jit(solution)/shard_map/ppermute | solution.py:51
  42.4 13.9 %collective-permute-start.17 = (bf16[160,1280]{1,0:T(8,128)(2,1)S(1)}, bf16[160,1280]{1,0:T(8,128)(2,1)}, u32[]{:S(2)}, u32[]{:S(2)}) collective-permute-start(bf16[160,1280]{1,0:T(8,128)(2,1)S(1)} %collective-permute-done.7.refs_8_.refs_9_), channel_id=1, source_target_pairs={{0,16},{1,17},{2,18},{3,19},{4,20},{5,21},{6,22},{7,23},{8,24},{9,... | collective-permute-start | bytes 1228808 | tf_op jit(solution)/shard_map/ppermute | solution.py:51
  43.7 12.7 %collective-permute-start.15 = (bf16[160,1280]{1,0:T(8,128)(2,1)S(1)}, bf16[160,1280]{1,0:T(8,128)(2,1)}, u32[]{:S(2)}, u32[]{:S(2)}) collective-permute-start(bf16[160,1280]{1,0:T(8,128)(2,1)S(1)} %collective-permute-done.5.refs_6_.refs_7_), channel_id=1, source_target_pairs={{0,16},{1,17},{2,18},{3,19},{4,20},{5,21},{6,22},{7,23},{8,24},{9,... | collective-permute-start | bytes 1228808 | tf_op jit(solution)/shard_map/ppermute | solution.py:51
  46.6 5.4 %collective-permute-start.20 = (bf16[80,1280]{1,0:T(8,128)(2,1)S(1)}, bf16[80,1280]{1,0:T(8,128)(2,1)S(1)}, u32[]{:S(2)}, u32[]{:S(2)}) collective-permute-start(bf16[80,1280]{1,0:T(8,128)(2,1)S(1)} %collective-permute-done.10.refs_11_.refs_12_), channel_id=1, source_target_pairs={{0,16},{1,17},{2,18},{3,19},{4,20},{5,21},{6,22},{7,23},{8,24},{9,... | collective-permute-start | bytes 614408 | tf_op jit(solution)/shard_map/ppermute | solution.py:51
  52.0 33.5 %collective-permute-start.2 = (bf16[512,1280]{1,0:T(8,128)(2,1)}, bf16[512,1280]{1,0:T(8,128)(2,1)}, u32[]{:S(2)}, u32[]{:S(2)}) collective-permute-start(bf16[512,1280]{1,0:T(8,128)(2,1)} %bitcast.51), channel_id=1, source_target_pairs={{0,2},{2,4},{4,6},{6,8},{8,10},{10,12},{12,14},{14,16},{16,18},{18... | collective-permute-start | bytes 3932168 | tf_op jit(solution)/shard_map/ppermute | solution.py:413
  78.9 36.1 %all-to-all-start.2 = ((bf16[32,16,1280]{2,1,0:T(8,128)(2,1)}), bf16[32,16,1280]{2,1,0:T(8,128)(2,1)}, u32[]{:S(2)}, u32[]{:S(2)}) async-start(bf16[32,16,1280]{2,1,0:T(8,128)(2,1)} %broadcast_in_dim.85), calls=%async_computation.2 | async-start | bytes 2621440 | tf_op jit(solution)/shard_map/all_to_all | solution.py:455
  112.8 38.3 %collective-permute-start.23 = (bf16[512,1280]{1,0:T(8,128)(2,1)}, bf16[512,1280]{1,0:T(8,128)(2,1)}, u32[]{:S(2)}, u32[]{:S(2)}) collective-permute-start(bf16[512,1280]{1,0:T(8,128)(2,1)} %get-tuple-element.37), channel_id=1, source_target_pairs={{2,0},{4,2},{6,4},{8,6},{10,8},{12,10},{14,12},{16,14},{18,16},{20... | collective-permute-start | bytes 3932168 | tf_op jit(solution)/shard_map/ppermute | solution.py:461
  115.1 38.7 %collective-permute-start.25 = (bf16[512,1280]{1,0:T(8,128)(2,1)}, bf16[512,1280]{1,0:T(8,128)(2,1)S(1)}, u32[]{:S(2)}, u32[]{:S(2)}) collective-permute-start(bf16[512,1280]{1,0:T(8,128)(2,1)} %bitcast.23), channel_id=1, source_target_pairs={{0,16},{16,0},{1,17},{17,1},{2,18},{18,2},{3,19},{19,3},{4,20},{20... | collective-permute-start | bytes 3932168 | tf_op jit(solution)/shard_map/ppermute | solution.py:462
  116.5 28.2 %collective-permute-start.24 = (f32[8,128]{1,0:T(8,128)S(1)}, f32[8,128]{1,0:T(8,128)S(1)}, u32[]{:S(2)}, u32[]{:S(2)}) collective-permute-start(f32[8,128]{1,0:T(8,128)S(1)} %broadcast_in_dim.84), channel_id=1, source_target_pairs={{0,1},{1,0},{2,3},{3,2},{4,5},{5,4},{6,7},{7,6},{8,9},{9,8},{10,11... | collective-permute-start | bytes 12296 | tf_op jit(solution)/shard_map/ppermute | solution.py:444
  129.4 19.0 %all-to-all-start.3 = ((bf16[32,2,640]{2,1,0:T(2,128)(2,1)}), bf16[32,2,640]{2,1,0:T(2,128)(2,1)S(1)}, u32[]{:S(2)}, u32[]{:S(2)}) async-start(bf16[32,2,640]{2,1,0:T(2,128)(2,1)} %reshape.436), calls=%async_computation.3 | async-start | bytes 163840 | tf_op jit(solution)/shard_map/all_to_all | solution.py:463
  (12 other events, 137.0 us)

commit v9 on v6

--- a/solution.py
+++ b/solution.py
@@ -325,37 +325,36 @@
     )
     label = lax.broadcasted_iota(jnp.int32, (IMAGES, D), 0)
     sums = sums + jnp.where(label == place_ref[6], sum_ref[0:1, :], 0.0)
-    pooled_ref[...] = (sums / lens_ref[...]).astype(jnp.bfloat16)
-    label = lax.broadcasted_iota(jnp.int32, (SLOTS, LOCAL), 0) + place_ref[6]
-    at = lax.broadcasted_iota(jnp.int32, (SLOTS, LOCAL), 1)
-    member = (label == image_ref[...]) & (at >= lo) & (at < hi)
-    sums = jnp.dot(
-        jnp.where(member, 1.0, 0.0).astype(jnp.bfloat16), hid_ref[0:LOCAL, :],
-        preferred_element_type=jnp.float32,
-    )
-    label = lax.broadcasted_iota(jnp.int32, (SLOTS, D), 0)
-    sums = sums + jnp.where(label == 0, sum_ref[0:1, :], 0.0)
-    few_ref[...] = sums.astype(jnp.bfloat16)
-
-
-def unpack_kernel(near_ref, far_ref, slot_ref, lens_ref, out_ref):
-    at = lax.broadcasted_iota(jnp.int32, (IMAGES, 32 * SLOTS), 1)
-    sums = jnp.zeros((IMAGES, D), jnp.float32)
+    means = (sums / lens_ref[...]).astype(jnp.bfloat16)
+    pooled_ref[...] = means
+    label = lax.broadcasted_iota(jnp.int32, (SLOTS, IMAGES), 0) + place_ref[6]
+    pick = lax.broadcasted_iota(jnp.int32, (SLOTS, IMAGES), 1) == label
+    few_ref[...] = jnp.dot(
+        jnp.where(pick, 1.0, 0.0).astype(jnp.bfloat16), means, preferred_element_type=jnp.float32
+    ).astype(jnp.bfloat16)
+
+
+def unpack_kernel(near_ref, far_ref, slot_ref, out_ref):
+    at = lax.broadcasted_iota(jnp.int32, (32 * SLOTS, IMAGES), 0)
+    means = jnp.zeros((IMAGES, D), jnp.float32)
     for i, ref in enumerate((near_ref, far_ref)):
         pick = jnp.where(slot_ref[...] == at + i * 32 * SLOTS, 1.0, 0.0).astype(jnp.bfloat16)
-        sums = sums + jnp.dot(pick, ref[...], preferred_element_type=jnp.float32)
-    out_ref[...] = sums / lens_ref[...]
-
-
-def unpack(near, far, slot, lens):
+        means = means + lax.dot_general(
+            pick, ref[...], (((0,), (0,)), ((), ())), preferred_element_type=jnp.float32
+        )
+    out_ref[...] = means
+
+
+def unpack(near, far, slot):
     vmem = pl.BlockSpec(memory_space=pltpu.VMEM)
     return pl.pallas_call(
         unpack_kernel,
         out_shape=jax.ShapeDtypeStruct((IMAGES, D), jnp.float32),
-        in_specs=[vmem] * 4,
+        in_specs=[vmem] * 3,
         out_specs=vmem,
+        compiler_params=pltpu.CompilerParams(vmem_limit_bytes=16 * 2**20),
         name="unpack",
-    )(near, far, slot, lens)
+    )(near, far, slot)
 
 
 def attention(edge, place, spans, inputs, gain, weights, extra):
@@ -454,7 +453,7 @@
     rank = jnp.arange(IMAGES, dtype=jnp.int32) - leader
     group = owner // 16 * 8 + owner % 8
     slot = jnp.where(owner // 8 % 2 == co, 0, 32 * SLOTS) + group * SLOTS + rank
-    slot = slot[:, None]
+    slot = slot[None]
     crowded = jnp.full((8, 128), jnp.max(rank) >= SLOTS).astype(jnp.float32)
     elsewhere = lax.ppermute(crowded, "dp", SWAP)
     fits = crowded[0, 0] + elsewhere[0, 0] == 0.0
@@ -469,14 +468,12 @@
         [image[None, LOCAL:WIN], lens.astype(jnp.float32)[:, None], hedge, total],
     )
 
-    lens_column = lens.astype(jnp.float32)[:, None]
-
     def pooled_directly(few, part):
         near = lax.all_to_all(
             jnp.broadcast_to(few[None], (32, SLOTS, D)), GROUP, 0, 0, tiled=True
         ).reshape(32 * SLOTS, D)
         far = lax.ppermute(near, "co", SWAP)
-        return unpack(near, far, slot, lens_column)
+        return unpack(near, far, slot)
 
     def pooled_by_sums(few, part):
         part = part.reshape(2, IMAGES // 2, D)

time: 164 us -> 162 us (0.988)
  waiting for transfers between devices: 16.3 us -> 22.8 us
  other arithmetic: 9.94 us -> 6.25 us
  local copies, waits for them, and re-layouts: 7.91 us -> 4.91 us
  Pallas kernels: 48.9 us -> 46.2 us
    pallas_call x1, Pallas kernels: 3.7 us -> 0.86 us  [unpack(): pl.pallas_call(unpack_kernel, out_shape=jax.ShapeDtypeStruct((IMAGES, D),...]
    ppermute x1, waiting for transfers between devices: 4.92 us -> 7.65 us  [layer(): lax.ppermute(own, TOKEN_AXES, [(i, i + 1) for i in range(63) if i not in...]
    ppermute x1, waiting for transfers between devices: 0.01 us -> 2.64 us  [pooled_directly(): far = lax.ppermute(near, 'co', SWAP)]
    add x1, other arithmetic: 1.81 us -> 0.02 us  [layer(): slot = jnp.where(owner // 8 % 2 == co, 0, 32 * SLOTS) + group * SLOTS + rank]
    rem x2, other arithmetic: 1.67 us -> 0.02 us  [layer(): slot = jnp.where(owner // 8 % 2 == co, 0, 32 * SLOTS) + group * SLOTS + rank]
  transfers between devices with their start and end apart: 22 -> 22, of which waited for: 5 -> 9; matrix products, arithmetic and copies ran while one was open for 8% -> 4% of each run, Pallas kernels for 15% -> 14%
where the time goes in v9:
time: 162 us; the launch traced here: 161 us
  Pallas kernels  46.2 us (29%)
  starting transfers between devices  40.1 us (25%)
  blocking collectives  36.3 us (22%)
  waiting for transfers between devices  22.8 us (14%)
  other arithmetic  6.25 us (4%)
  local copies, waits for them, and re-layouts  4.91 us (3%)
  between operations  4.69 us (3%)
    pallas_call x2, Pallas kernels, attention(): pl.pallas_call(functools.partial(attention_kernel, edge), out_shape=outs,...  45.3 us
    all_to_all x1, blocking collectives, pooled_directly(): lax.all_to_all(jnp.broadcast_to(few[None], (32, SLOTS, D)), GROUP, 0, 0,...  36.3 us
    ppermute x16, starting transfers between devices, moved(): return lax.ppermute(piece, ALL_AXES, pairs)  22.2 us
    ppermute x16, waiting for transfers between devices, moved(): return lax.ppermute(piece, ALL_AXES, pairs)  11.7 us
    ppermute x1, starting transfers between devices, layer(): back = lax.ppermute(hprev, TOKEN_AXES, [(i + 1, i) for i in range(63)])  9.58 us
    ppermute x1, waiting for transfers between devices, layer(): lax.ppermute(own, TOKEN_AXES, [(i, i + 1) for i in range(63) if i not in...  7.65 us
    ppermute x1, starting transfers between devices, layer(): lax.ppermute(own, TOKEN_AXES, [(i, i + 1) for i in range(63) if i not in...  3.54 us
  transfers between devices with their start and end apart: 22, of which 9 were waited for; matrix products, arithmetic and copies ran while one was open for 4% of the time, Pallas kernels for 14%

profile of v9, /device:TPU:1, one launch (start us, length us, event | category | flops | bytes accessed | tf_op | source)
XLA Modules:
  0.0 161.2 jit_solution(12033367977959293243)
XLA Ops:
  0.7 1.4 dynamic-slice_select_fusion
  2.0 2.2 %collective-permute-start.3 = (bf16[160,1280]{1,0:T(8,128)(2,1)S(1)}, bf16[160,1280]{1,0:T(8,128)(2,1)S(1)}, u32[]{:S(2)}, u32[]{:S(2)}) collective-permute-start(bf16[160,1280]{1,0:T(8,128)(2,1)S(1)} %get-tuple-element.162), channel_id=1, source_target_pairs={{0,1},{1,2},{2,3},{3,0},{4,5},{5,6},{6,7},{7,4},{8,9},{9,10},{10,1... | collective-permute-start | bytes 1228808 | tf_op jit(solution)/shard_map/ppermute | solution.py:54
  4.2 1.5 collective-permute-start.4
  5.7 1.7 %collective-permute-start.20 = (bf16[512,1280]{1,0:T(8,128)(2,1)}, bf16[512,1280]{1,0:T(8,128)(2,1)}, u32[]{:S(2)}, u32[]{:S(2)}) collective-permute-start(bf16[512,1280]{1,0:T(8,128)(2,1)} %bitcast.18.refs_2_.refs_0_), channel_id=1, source_target_pairs={{30,46},{62,78},{94,110},{31,47},{63,79},{95,111}} | collective-permute-start | bytes 3932168 | tf_op jit(solution)/shard_map/ppermute | solution.py:416
  8.1 6.6 %collective-permute-done.3.refs_6_.refs_4_ = bf16[160,1280]{1,0:T(8,128)(2,1)S(1)} collective-permute-done((bf16[160,1280]{1,0:T(8,128)(2,1)S(1)}, bf16[160,1280]{1,0:T(8,128)(2,1)S(1)}, u32[]{:S(2)}, u32[]{:S(2)}) %collective-permute-start.3) | collective-permute-done | bytes 409632 | tf_op jit(solution)/shard_map/ppermute | solution.py:54
  17.4 1.6 %collective-permute-start.8 = (bf16[160,1280]{1,0:T(8,128)(2,1)S(1)}, bf16[160,1280]{1,0:T(8,128)(2,1)S(1)}, u32[]{:S(2)}, u32[]{:S(2)}) collective-permute-start(bf16[160,1280]{1,0:T(8,128)(2,1)S(1)} %collective-permute-done.4.refs_7_.refs_5_), channel_id=1, source_target_pairs={{0,96},{1,97},{2,98},{3,99},{4,100},{5,101},{6,102},{7,103},{8,104... | collective-permute-start | bytes 1228808 | tf_op jit(solution)/shard_map/ppermute | solution.py:54
  19.8 1.9 %collective-permute-start.7 = (bf16[160,1280]{1,0:T(8,128)(2,1)S(1)}, bf16[160,1280]{1,0:T(8,128)(2,1)S(1)}, u32[]{:S(2)}, u32[]{:S(2)}) collective-permute-start(bf16[160,1280]{1,0:T(8,128)(2,1)S(1)} %collective-permute-done.3.refs_6_.refs_4_), channel_id=1, source_target_pairs={{0,96},{1,97},{2,98},{3,99},{4,100},{5,101},{6,102},{7,103},{8,104... | collective-permute-start | bytes 1228808 | tf_op jit(solution)/shard_map/ppermute | solution.py:54
  21.8 3.8 %collective-permute-done.5.refs_8_.refs_6_ = bf16[160,1280]{1,0:T(8,128)(2,1)S(1)} collective-permute-done((bf16[160,1280]{1,0:T(8,128)(2,1)S(1)}, bf16[160,1280]{1,0:T(8,128)(2,1)S(1)}, u32[]{:S(2)}, u32[]{:S(2)}) %collective-permute-start.5) | collective-permute-done | bytes 409632 | tf_op jit(solution)/shard_map/ppermute | solution.py:54
  25.6 4.0 %collective-permute-start.11 = (bf16[160,1280]{1,0:T(8,128)(2,1)S(1)}, bf16[160,1280]{1,0:T(8,128)(2,1)S(1)}, u32[]{:S(2)}, u32[]{:S(2)}) collective-permute-start(bf16[160,1280]{1,0:T(8,128)(2,1)S(1)} %collective-permute-done.3.refs_6_.refs_4_), channel_id=1, source_target_pairs={{0,16},{1,17},{2,18},{3,19},{4,20},{5,21},{6,22},{7,23},{8,24},{9,... | collective-permute-start | bytes 1228808 | tf_op jit(solution)/shard_map/ppermute | solution.py:54
  30.8 3.5 %collective-permute-start.19 = (bf16[512,1280]{1,0:T(8,128)(2,1)}, bf16[512,1280]{1,0:T(8,128)(2,1)}, u32[]{:S(2)}, u32[]{:S(2)}) collective-permute-start(bf16[512,1280]{1,0:T(8,128)(2,1)} %bitcast.18.refs_2_.refs_0_), channel_id=1, source_target_pairs={{0,2},{2,4},{4,6},{6,8},{8,10},{10,12},{12,14},{14,16},{16,18},{18... | collective-permute-start | bytes 3932168 | tf_op jit(solution)/shard_map/ppermute | solution.py:419
  34.4 3.3 %collective-permute-start.12 = (bf16[160,1280]{1,0:T(8,128)(2,1)S(1)}, bf16[160,1280]{1,0:T(8,128)(2,1)}, u32[]{:S(2)}, u32[]{:S(2)}) collective-permute-start(bf16[160,1280]{1,0:T(8,128)(2,1)S(1)} %collective-permute-done.4.refs_7_.refs_5_), channel_id=1, source_target_pairs={{0,16},{1,17},{2,18},{3,19},{4,20},{5,21},{6,22},{7,23},{8,24},{9,... | collective-permute-start | bytes 1228808 | tf_op jit(solution)/shard_map/ppermute | solution.py:54
  38.9 1.5 collective-permute-start.10
  40.4 1.7 %collective-permute-start.21 = (bf16[512,1280]{1,0:T(8,128)(2,1)}, bf16[512,1280]{1,0:T(8,128)(2,1)}, u32[]{:S(2)}, u32[]{:S(2)}) collective-permute-start(bf16[512,1280]{1,0:T(8,128)(2,1)} %collective-permute-done.20), channel_id=1, source_target_pairs={{46,32},{78,64},{110,96},{47,33},{79,65},{111,97}} | collective-permute-start | bytes 3932168 | tf_op jit(solution)/shard_map/ppermute | solution.py:422
  46.0 1.3 stack.50.place_ref
  49.4 1.3 collective-permute-start.16
  54.3 7.6 %collective-permute-done.19.refs_0_ = bf16[512,1280]{1,0:T(8,128)(2,1)} collective-permute-done((bf16[512,1280]{1,0:T(8,128)(2,1)}, bf16[512,1280]{1,0:T(8,128)(2,1)}, u32[]{:S(2)}, u32[]{:S(2)}) %collective-permute-start.19) | collective-permute-done | bytes 1310752 | tf_op jit(solution)/shard_map/ppermute | solution.py:419
  62.0 24.1 %edge_attention.1 = (bf16[512,1280]{1,0:T(8,128)(2,1)}, bf16[512,1280]{1,0:T(8,128)(2,1)}, f32[8,1280]{1,0:T(8,128)S(1)}) custom-call(s32[7]{0:T(128)S(1)} %stack.50.place_ref, s32[2,1280]{1,0:T(2,128)S(1)} %pad_add_fusion.ends_ref.refs_22_, bf16[512,1280]{1,0:T(8,128)(2,1)} %collective-permute-done.19.refs_0_, ...), custom_call_target="tpu_custom_call" | custom-call | flops 15000000512 | bytes 20000000 | tf_op jit(solution)/shard_map/edge_attention/pallas_call | solution.py:377
  86.1 9.6 %collective-permute-start.22 = (bf16[512,1280]{1,0:T(8,128)(2,1)}, bf16[512,1280]{1,0:T(8,128)(2,1)}, u32[]{:S(2)}, u32[]{:S(2)}) collective-permute-start(bf16[512,1280]{1,0:T(8,128)(2,1)} %get-tuple-element.128), channel_id=1, source_target_pairs={{2,0},{4,2},{6,4},{8,6},{10,8},{12,10},{14,12},{16,14},{18,16},{20... | collective-permute-start | bytes 3932168 | tf_op jit(solution)/shard_map/ppermute | solution.py:465
  95.6 21.2 %own_attention.1 = (bf16[512,1280]{1,0:T(8,128)(2,1)}, bf16[256,1280]{1,0:T(8,128)(2,1)}, bf16[16,1280]{1,0:T(8,128)(2,1)S(1)}) custom-call(s32[7]{0:T(128)S(1)} %stack.48.place_ref, s32[2,768]{1,0:T(2,128)S(1)} %fusion.9.ends_ref.refs_20_, bf16[512,1280]{1,0:T(8,128)(2,1)} %bitcast.18.refs_2_.refs_0_, f32[1,1280]{1,0:T(1,128)S(1)} %broadcast_in_dim.71.refs_3_.refs_1_, ...), custom_call_target="tpu_custom_call" | custom-call | flops 15000000512 | bytes 20000000 | tf_op jit(solution)/shard_map/own_attention/pallas_call | solution.py:377
  116.9 41.3 %conditional.1 = (f32[1,256,1280]{2,1,0:T(8,128)S(1)}) conditional(s32[]{:T(128)} %convert_element_type.58, (s32[]{:T(128)}, bf16[256,1280]{1,0:T(8,128)(2,1)}) %tuple.26, (bf16[16,1280]{1,0:T(8,128)(2,1)S(1)}, s32[1,256]{1,0:T(1,128)S(1)}, s32[]{:T(128)}, s32[]{:T(128)}, s32[1,256]{1,0:T(1,128)S(1)}, /*index=5*/pred[1,256]{1,0:T(4,128)(4,1)S(1)}, (), ...), branch_computations={%region_7.9_spmd, %region_9.10_spmd} | conditional | flops 2124808 | bytes 11489468 | solution.py:493
  117.0 36.3 %all_to_all.14 = bf16[32,16,1280]{2,1,0:T(8,128)(2,1)S(1)} all-to-all(bf16[32,16,1280]{2,1,0:T(8,128)(2,1)S(1)} %broadcast_in_dim.36), channel_id=1, replica_groups=mesh['x'=4,'co'=2,'z'=4,'yh'=2,'dp'=2] {'x','z','yh'}, dimensions={0} | all-to-all | bytes 2621440 | tf_op jit(solution)/shard_map/cond/branch_1_fun/all_to_all | solution.py:472
  153.3 1.3 collective-permute-start.2
  154.7 2.6 %collective-permute-done.2.far_ref = bf16[512,1280]{1,0:T(8,128)(2,1)S(1)} collective-permute-done((bf16[512,1280]{1,0:T(8,128)(2,1)S(1)}, bf16[512,1280]{1,0:T(8,128)(2,1)S(1)}, u32[]{:S(2)}, u32[]{:S(2)}) %collective-permute-start.2) | collective-permute-done | bytes 1310752 | tf_op jit(solution)/shard_map/cond/branch_1_fun/ppermute | solution.py:475
  158.2 3.0 %select_bitcast_fusion = bf16[1,512,1280]{2,1,0:T(8,128)(2,1)} fusion(bf16[512,1280]{1,0:T(8,128)(2,1)S(1)} %copy-done, bf16[512,1280]{1,0:T(8,128)(2,1)} %collective-permute-done.22, pred[512]{0:T(512)(128)(4,1)S(1)} %iota_compare_fusion), kind=kLoop, calls=%fused_computation.25 | loop fusion | flops 655360 | bytes 3932672 | tf_op jit(solution)/shard_map/broadcast_in_dim | solution.py:496
  (75 shorter events, 13.2 us)
Async XLA Ops:
  0.6 41.5 %copy-start.3 = (f32[1280]{0:T(1024)S(1)}, f32[1280]{0:T(1024)}, u32[]{:S(2)}) copy-start(f32[1280]{0:T(1024)} %param.9) | copy-start | bytes 15364
  2.0 12.7 %collective-permute-start.3 = (bf16[160,1280]{1,0:T(8,128)(2,1)S(1)}, bf16[160,1280]{1,0:T(8,128)(2,1)S(1)}, u32[]{:S(2)}, u32[]{:S(2)}) collective-permute-start(bf16[160,1280]{1,0:T(8,128)(2,1)S(1)} %get-tuple-element.162), channel_id=1, source_target_pairs={{0,1},{1,2},{2,3},{3,0},{4,5},{5,6},{6,7},{7,4},{8,9},{9,10},{10,1... | collective-permute-start | bytes 1228808 | tf_op jit(solution)/shard_map/ppermute | solution.py:54
  4.2 13.2 %collective-permute-start.4 = (bf16[160,1280]{1,0:T(8,128)(2,1)S(1)}, bf16[160,1280]{1,0:T(8,128)(2,1)S(1)}, u32[]{:S(2)}, u32[]{:S(2)}) collective-permute-start(bf16[160,1280]{1,0:T(8,128)(2,1)S(1)} %get-tuple-element.161), channel_id=1, source_target_pairs={{0,3},{1,0},{2,1},{3,2},{4,7},{5,4},{6,5},{7,6},{8,11},{9,8},{10,9... | collective-permute-start | bytes 1228808 | tf_op jit(solution)/shard_map/ppermute | solution.py:54
  5.7 34.7 %collective-permute-start.20 = (bf16[512,1280]{1,0:T(8,128)(2,1)}, bf16[512,1280]{1,0:T(8,128)(2,1)}, u32[]{:S(2)}, u32[]{:S(2)}) collective-permute-start(bf16[512,1280]{1,0:T(8,128)(2,1)} %bitcast.18.refs_2_.refs_0_), channel_id=1, source_target_pairs={{30,46},{62,78},{94,110},{31,47},{63,79},{95,111}} | collective-permute-start | bytes 3932168 | tf_op jit(solution)/shard_map/ppermute | solution.py:416
  14.7 10.9 %collective-permute-start.5 = (bf16[160,1280]{1,0:T(8,128)(2,1)S(1)}, bf16[160,1280]{1,0:T(8,128)(2,1)S(1)}, u32[]{:S(2)}, u32[]{:S(2)}) collective-permute-start(bf16[160,1280]{1,0:T(8,128)(2,1)S(1)} %collective-permute-done.3.refs_6_.refs_4_), channel_id=1, source_target_pairs={{0,32},{1,33},{2,34},{3,35},{4,36},{5,37},{6,38},{7,39},{8,40},{9,... | collective-permute-start | bytes 1228808 | tf_op jit(solution)/shard_map/ppermute | solution.py:54
  17.3 2.5 %collective-permute-start.23 = (f32[8,128]{1,0:T(8,128)S(1)}, f32[8,128]{1,0:T(8,128)S(1)}, u32[]{:S(2)}, u32[]{:S(2)}) collective-permute-start(f32[8,128]{1,0:T(8,128)S(1)} %broadcast_in_dim.74), channel_id=1, source_target_pairs={{0,1},{1,0},{2,3},{3,2},{4,5},{5,4},{6,7},{7,6},{8,9},{9,8},{10,11... | collective-permute-start | bytes 12296 | tf_op jit(solution)/shard_map/ppermute | solution.py:458
  17.4 13.3 %collective-permute-start.8 = (bf16[160,1280]{1,0:T(8,128)(2,1)S(1)}, bf16[160,1280]{1,0:T(8,128)(2,1)S(1)}, u32[]{:S(2)}, u32[]{:S(2)}) collective-permute-start(bf16[160,1280]{1,0:T(8,128)(2,1)S(1)} %collective-permute-done.4.refs_7_.refs_5_), channel_id=1, source_target_pairs={{0,96},{1,97},{2,98},{3,99},{4,100},{5,101},{6,102},{7,103},{8,104... | collective-permute-start | bytes 1228808 | tf_op jit(solution)/shard_map/ppermute | solution.py:54
  19.1 15.3 %collective-permute-start.6 = (bf16[160,1280]{1,0:T(8,128)(2,1)S(1)}, bf16[160,1280]{1,0:T(8,128)(2,1)S(1)}, u32[]{:S(2)}, u32[]{:S(2)}) collective-permute-start(bf16[160,1280]{1,0:T(8,128)(2,1)S(1)} %collective-permute-done.4.refs_7_.refs_5_), channel_id=1, source_target_pairs={{0,32},{1,33},{2,34},{3,35},{4,36},{5,37},{6,38},{7,39},{8,40},{9,... | collective-permute-start | bytes 1228808 | tf_op jit(solution)/shard_map/ppermute | solution.py:54
  19.8 17.8 %collective-permute-start.7 = (bf16[160,1280]{1,0:T(8,128)(2,1)S(1)}, bf16[160,1280]{1,0:T(8,128)(2,1)S(1)}, u32[]{:S(2)}, u32[]{:S(2)}) collective-permute-start(bf16[160,1280]{1,0:T(8,128)(2,1)S(1)} %collective-permute-done.3.refs_6_.refs_4_), channel_id=1, source_target_pairs={{0,96},{1,97},{2,98},{3,99},{4,100},{5,101},{6,102},{7,103},{8,104... | collective-permute-start | bytes 1228808 | tf_op jit(solution)/shard_map/ppermute | solution.py:54
  25.6 13.3 %collective-permute-start.11 = (bf16[160,1280]{1,0:T(8,128)(2,1)S(1)}, bf16[160,1280]{1,0:T(8,128)(2,1)S(1)}, u32[]{:S(2)}, u32[]{:S(2)}) collective-permute-start(bf16[160,1280]{1,0:T(8,128)(2,1)S(1)} %collective-permute-done.3.refs_6_.refs_4_), channel_id=1, source_target_pairs={{0,16},{1,17},{2,18},{3,19},{4,20},{5,21},{6,22},{7,23},{8,24},{9,... | collective-permute-start | bytes 1228808 | tf_op jit(solution)/shard_map/ppermute | solution.py:54
  30.8 31.2 %collective-permute-start.19 = (bf16[512,1280]{1,0:T(8,128)(2,1)}, bf16[512,1280]{1,0:T(8,128)(2,1)}, u32[]{:S(2)}, u32[]{:S(2)}) collective-permute-start(bf16[512,1280]{1,0:T(8,128)(2,1)} %bitcast.18.refs_2_.refs_0_), channel_id=1, source_target_pairs={{0,2},{2,4},{4,6},{6,8},{8,10},{10,12},{12,14},{14,16},{16,18},{18... | collective-permute-start | bytes 3932168 | tf_op jit(solution)/shard_map/ppermute | solution.py:419
  34.4 13.8 %collective-permute-start.12 = (bf16[160,1280]{1,0:T(8,128)(2,1)S(1)}, bf16[160,1280]{1,0:T(8,128)(2,1)}, u32[]{:S(2)}, u32[]{:S(2)}) collective-permute-start(bf16[160,1280]{1,0:T(8,128)(2,1)S(1)} %collective-permute-done.4.refs_7_.refs_5_), channel_id=1, source_target_pairs={{0,16},{1,17},{2,18},{3,19},{4,20},{5,21},{6,22},{7,23},{8,24},{9,... | collective-permute-start | bytes 1228808 | tf_op jit(solution)/shard_map/ppermute | solution.py:54
  37.7 11.7 %collective-permute-start.9 = (bf16[160,1280]{1,0:T(8,128)(2,1)S(1)}, bf16[160,1280]{1,0:T(8,128)(2,1)S(1)}, u32[]{:S(2)}, u32[]{:S(2)}) collective-permute-start(bf16[160,1280]{1,0:T(8,128)(2,1)S(1)} %collective-permute-done.5.refs_8_.refs_6_), channel_id=1, source_target_pairs={{0,32},{1,33},{2,34},{3,35},{4,36},{5,37},{6,38},{7,39},{8,40},{9,... | collective-permute-start | bytes 1228808 | tf_op jit(solution)/shard_map/ppermute | solution.py:54
  38.9 11.8 %collective-permute-start.10 = (bf16[160,1280]{1,0:T(8,128)(2,1)S(1)}, bf16[160,1280]{1,0:T(8,128)(2,1)}, u32[]{:S(2)}, u32[]{:S(2)}) collective-permute-start(bf16[160,1280]{1,0:T(8,128)(2,1)S(1)} %collective-permute-done.8.refs_11_.refs_9_), channel_id=1, source_target_pairs={{0,96},{1,97},{2,98},{3,99},{4,100},{5,101},{6,102},{7,103},{8,104... | collective-permute-start | bytes 1228808 | tf_op jit(solution)/shard_map/ppermute | solution.py:54
  40.4 21.5 %collective-permute-start.21 = (bf16[512,1280]{1,0:T(8,128)(2,1)}, bf16[512,1280]{1,0:T(8,128)(2,1)}, u32[]{:S(2)}, u32[]{:S(2)}) collective-permute-start(bf16[512,1280]{1,0:T(8,128)(2,1)} %collective-permute-done.20), channel_id=1, source_target_pairs={{46,32},{78,64},{110,96},{47,33},{79,65},{111,97}} | collective-permute-start | bytes 3932168 | tf_op jit(solution)/shard_map/ppermute | solution.py:422
  48.1 2.8 %collective-permute-start.13 = (bf16[160,1280]{1,0:T(8,128)(2,1)S(1)}, bf16[160,1280]{1,0:T(8,128)(2,1)S(1)}, u32[]{:S(2)}, u32[]{:S(2)}) collective-permute-start(bf16[160,1280]{1,0:T(8,128)(2,1)S(1)} %collective-permute-done.5.refs_8_.refs_6_), channel_id=1, source_target_pairs={{0,16},{1,17},{2,18},{3,19},{4,20},{5,21},{6,22},{7,23},{8,24},{9,... | collective-permute-start | bytes 1228808 | tf_op jit(solution)/shard_map/ppermute | solution.py:54
  49.4 2.7 %collective-permute-start.16 = (bf16[160,1280]{1,0:T(8,128)(2,1)S(1)}, bf16[160,1280]{1,0:T(8,128)(2,1)S(1)}, u32[]{:S(2)}, u32[]{:S(2)}) collective-permute-start(bf16[160,1280]{1,0:T(8,128)(2,1)S(1)} %collective-permute-done.8.refs_11_.refs_9_), channel_id=1, source_target_pairs={{0,16},{1,17},{2,18},{3,19},{4,20},{5,21},{6,22},{7,23},{8,24},{9,... | collective-permute-start | bytes 1228808 | tf_op jit(solution)/shard_map/ppermute | solution.py:54
  50.8 2.0 %collective-permute-start.14 = (bf16[160,1280]{1,0:T(8,128)(2,1)S(1)}, bf16[160,1280]{1,0:T(8,128)(2,1)S(1)}, u32[]{:S(2)}, u32[]{:S(2)}) collective-permute-start(bf16[160,1280]{1,0:T(8,128)(2,1)S(1)} %collective-permute-done.6.refs_9_.refs_7_), channel_id=1, source_target_pairs={{0,16},{1,17},{2,18},{3,19},{4,20},{5,21},{6,22},{7,23},{8,24},{9,... | collective-permute-start | bytes 1228808 | tf_op jit(solution)/shard_map/ppermute | solution.py:54
  51.0 3.3 %collective-permute-start.15 = (bf16[160,1280]{1,0:T(8,128)(2,1)S(1)}, bf16[160,1280]{1,0:T(8,128)(2,1)}, u32[]{:S(2)}, u32[]{:S(2)}) collective-permute-start(bf16[160,1280]{1,0:T(8,128)(2,1)S(1)} %collective-permute-done.7.refs_10_.refs_8_), channel_id=1, source_target_pairs={{0,16},{1,17},{2,18},{3,19},{4,20},{5,21},{6,22},{7,23},{8,24},{9,... | collective-permute-start | bytes 1228808 | tf_op jit(solution)/shard_map/ppermute | solution.py:54
  52.1 9.8 %collective-permute-start.17 = (bf16[160,1280]{1,0:T(8,128)(2,1)S(1)}, bf16[160,1280]{1,0:T(8,128)(2,1)}, u32[]{:S(2)}, u32[]{:S(2)}) collective-permute-start(bf16[160,1280]{1,0:T(8,128)(2,1)S(1)} %collective-permute-done.9.refs_12_.refs_10_), channel_id=1, source_target_pairs={{0,16},{1,17},{2,18},{3,19},{4,20},{5,21},{6,22},{7,23},{8,24},{9,... | collective-permute-start | bytes 1228808 | tf_op jit(solution)/shard_map/ppermute | solution.py:54
  52.7 9.2 %collective-permute-start.18 = (bf16[160,1280]{1,0:T(8,128)(2,1)}, bf16[160,1280]{1,0:T(8,128)(2,1)}, u32[]{:S(2)}, u32[]{:S(2)}) collective-permute-start(bf16[160,1280]{1,0:T(8,128)(2,1)} %collective-permute-done.10.refs_13_.refs_11_), channel_id=1, source_target_pairs={{0,16},{1,17},{2,18},{3,19},{4,20},{5,21},{6,22},{7,23},{8,24},{9,... | collective-permute-start | bytes 1228808 | tf_op jit(solution)/shard_map/ppermute | solution.py:54
  86.1 72.1 %collective-permute-start.22 = (bf16[512,1280]{1,0:T(8,128)(2,1)}, bf16[512,1280]{1,0:T(8,128)(2,1)}, u32[]{:S(2)}, u32[]{:S(2)}) collective-permute-start(bf16[512,1280]{1,0:T(8,128)(2,1)} %get-tuple-element.128), channel_id=1, source_target_pairs={{2,0},{4,2},{6,4},{8,6},{10,8},{12,10},{14,12},{16,14},{18,16},{20... | collective-permute-start | bytes 3932168 | tf_op jit(solution)/shard_map/ppermute | solution.py:465
  116.9 41.3 %copy-start = (bf16[512,1280]{1,0:T(8,128)(2,1)S(1)}, bf16[512,1280]{1,0:T(8,128)(2,1)}, u32[]{:S(2)}) copy-start(bf16[512,1280]{1,0:T(8,128)(2,1)} %get-tuple-element.127) | copy-start | bytes 3932164
  153.3 4.0 %collective-permute-start.2 = (bf16[512,1280]{1,0:T(8,128)(2,1)S(1)}, bf16[512,1280]{1,0:T(8,128)(2,1)S(1)}, u32[]{:S(2)}, u32[]{:S(2)}) collective-permute-start(bf16[512,1280]{1,0:T(8,128)(2,1)S(1)} %bitcast.33), channel_id=1, source_target_pairs={{0,16},{16,0},{1,17},{17,1},{2,18},{18,2},{3,19},{19,3},{4,20},{20... | collective-permute-start | bytes 3932168 | tf_op jit(solution)/shard_map/cond/branch_1_fun/ppermute | solution.py:475
  (5 other events, 14.5 us)

commit v10 on v9

--- a/solution.py
+++ b/solution.py
@@ -109,8 +109,7 @@
         def _():
             pltpu.make_async_copy(late_ref, wide_ref.at[pl.ds(0, LOCAL)], sem.at[0]).start()
     else:
-        inputs.append(pltpu.make_async_copy(hedge_ref, hid_ref.at[pl.ds(0, LOCAL)], sem.at[5]))
-        inputs[1].start()
+        edge_rows = pltpu.make_async_copy(hedge_ref, hid_ref.at[pl.ds(0, LOCAL)], sem.at[5])
 
     def near(part, target, cols):
         return pltpu.make_async_copy(
@@ -137,6 +136,9 @@
                     row = lax.rem(x + shift[slot], 4)
                     distant(part, held[slot * 2 + part % 2], row).start()
 
+    if not edge:
+        edge_rows.start()
+
     def arrived(part):
         near(part, targets[part], columns[part]).wait()
         for _ in range(4):
@@ -153,7 +155,7 @@
         return jnp.where(source == out + lag, 1.0, 0.0).astype(jnp.bfloat16)
 
     if edge:
-        wide_ref[WIN:, :] = jnp.zeros((wide_ref.shape[0] - WIN, D), jnp.bfloat16)
+        wide_ref[WIN : WIN + QB, :] = jnp.zeros((QB, D), jnp.bfloat16)
         pick = mover(offset)
 
         def align(j, carry):
@@ -178,11 +180,12 @@
         return carry
 
     lax.fori_loop(0, blocks, normalize, 0)
-    k_ref[...] = jnp.zeros_like(k_ref)
-    vt_ref[...] = jnp.zeros_like(vt_ref)
+    past = pl.ds(pl.multiple_of(jnp.minimum(base + blocks * QB, LOCAL), 128), QB)
+    k_ref[past, :] = jnp.zeros((QB, D), jnp.bfloat16)
+    vt_ref[:, past] = jnp.zeros((HEADS * VROWS, QB), jnp.bfloat16)
     if edge:
         hid_ref[...] = jnp.zeros_like(hid_ref)
-        wide_ref[...] = jnp.zeros_like(wide_ref)
+        wide_ref[0:WIN, :] = jnp.zeros((WIN, D), jnp.bfloat16)
 
     def project_q(j, carry):
         _, rows = block_rows(j)
@@ -211,6 +214,8 @@
         arrived(part)
         lax.fori_loop(0, blocks, project, 0)
     arrived(3)
+    if not edge:
+        edge_rows.wait()
 
     def attend(j, carry):
         row0, rows = block_rows(j)
@@ -274,7 +279,7 @@
                     mix(h, p0_ref)
                     return inner
 
-                lax.fori_loop(0, HEADS // 2, two_heads, 0)
+                lax.fori_loop(0, HEADS // 2, two_heads, 0, unroll=4)
                 mix(HEADS - 1, p1_ref)
 
         mixed = lax.dot_general(

time: 162 us -> 158 us (0.975)
  Pallas kernels: 46.2 us -> 42.9 us
    pallas_call x2, Pallas kernels: 45.3 us -> 42.1 us  [attention(): pl.pallas_call(functools.partial(attention_kernel, edge), out_shape=outs,...]
  transfers between devices with their start and end apart: 22 -> 22, of which waited for: 9 -> 9; matrix products, arithmetic and copies ran while one was open for 4% -> 4% of each run, Pallas kernels for 14% -> 13%
where the time goes in v10:
time: 158 us
  Pallas kernels  42.9 us (27%)
  starting transfers between devices  40.4 us (26%)
  blocking collectives  36 us (23%)
  waiting for transfers between devices  22.8 us (14%)
  other arithmetic  6.25 us (4%)
  local copies, waits for them, and re-layouts  4.91 us (3%)
  between operations  4.69 us (3%)
    pallas_call x2, Pallas kernels, attention(): pl.pallas_call(functools.partial(attention_kernel, edge), out_shape=outs,...  42.1 us
    all_to_all x1, blocking collectives, pooled_directly(): lax.all_to_all(jnp.broadcast_to(few[None], (32, SLOTS, D)), GROUP, 0, 0,...  36 us
    ppermute x16, starting transfers between devices, moved(): return lax.ppermute(piece, ALL_AXES, pairs)  22.2 us
    ppermute x16, waiting for transfers between devices, moved(): return lax.ppermute(piece, ALL_AXES, pairs)  11.7 us
    ppermute x1, starting transfers between devices, layer(): back = lax.ppermute(hprev, TOKEN_AXES, [(i + 1, i) for i in range(63)])  9.95 us
    ppermute x1, waiting for transfers between devices, layer(): lax.ppermute(own, TOKEN_AXES, [(i, i + 1) for i in range(63) if i not in...  7.65 us
    ppermute x1, starting transfers between devices, layer(): lax.ppermute(own, TOKEN_AXES, [(i, i + 1) for i in range(63) if i not in...  3.54 us
  transfers between devices with their start and end apart: 22, of which 9 were waited for; matrix products, arithmetic and copies ran while one was open for 4% of the time, Pallas kernels for 13%

profile of v10, /device:TPU:1, one launch (start us, length us, event | category | flops | bytes accessed | tf_op | source)
XLA Modules:
  0.0 157.9 jit_solution(11048321091680538288)
XLA Ops:
  0.7 1.4 dynamic-slice_select_fusion
  2.0 2.2 %collective-permute-start.3 = (bf16[160,1280]{1,0:T(8,128)(2,1)S(1)}, bf16[160,1280]{1,0:T(8,128)(2,1)S(1)}, u32[]{:S(2)}, u32[]{:S(2)}) collective-permute-start(bf16[160,1280]{1,0:T(8,128)(2,1)S(1)} %get-tuple-element.162), channel_id=1, source_target_pairs={{0,1},{1,2},{2,3},{3,0},{4,5},{5,6},{6,7},{7,4},{8,9},{9,10},{10,1... | collective-permute-start | bytes 1228808 | tf_op jit(solution)/shard_map/ppermute | solution.py:54
  4.2 1.5 collective-permute-start.4
  5.7 1.7 %collective-permute-start.20 = (bf16[512,1280]{1,0:T(8,128)(2,1)}, bf16[512,1280]{1,0:T(8,128)(2,1)}, u32[]{:S(2)}, u32[]{:S(2)}) collective-permute-start(bf16[512,1280]{1,0:T(8,128)(2,1)} %bitcast.18.refs_2_.refs_0_), channel_id=1, source_target_pairs={{30,46},{62,78},{94,110},{31,47},{63,79},{95,111}} | collective-permute-start | bytes 3932168 | tf_op jit(solution)/shard_map/ppermute | solution.py:421
  8.1 6.6 %collective-permute-done.3.refs_6_.refs_4_ = bf16[160,1280]{1,0:T(8,128)(2,1)S(1)} collective-permute-done((bf16[160,1280]{1,0:T(8,128)(2,1)S(1)}, bf16[160,1280]{1,0:T(8,128)(2,1)S(1)}, u32[]{:S(2)}, u32[]{:S(2)}) %collective-permute-start.3) | collective-permute-done | bytes 409632 | tf_op jit(solution)/shard_map/ppermute | solution.py:54
  17.4 1.6 %collective-permute-start.8 = (bf16[160,1280]{1,0:T(8,128)(2,1)S(1)}, bf16[160,1280]{1,0:T(8,128)(2,1)S(1)}, u32[]{:S(2)}, u32[]{:S(2)}) collective-permute-start(bf16[160,1280]{1,0:T(8,128)(2,1)S(1)} %collective-permute-done.4.refs_7_.refs_5_), channel_id=1, source_target_pairs={{0,96},{1,97},{2,98},{3,99},{4,100},{5,101},{6,102},{7,103},{8,104... | collective-permute-start | bytes 1228808 | tf_op jit(solution)/shard_map/ppermute | solution.py:54
  19.8 1.9 %collective-permute-start.7 = (bf16[160,1280]{1,0:T(8,128)(2,1)S(1)}, bf16[160,1280]{1,0:T(8,128)(2,1)S(1)}, u32[]{:S(2)}, u32[]{:S(2)}) collective-permute-start(bf16[160,1280]{1,0:T(8,128)(2,1)S(1)} %collective-permute-done.3.refs_6_.refs_4_), channel_id=1, source_target_pairs={{0,96},{1,97},{2,98},{3,99},{4,100},{5,101},{6,102},{7,103},{8,104... | collective-permute-start | bytes 1228808 | tf_op jit(solution)/shard_map/ppermute | solution.py:54
  21.8 3.8 %collective-permute-done.5.refs_8_.refs_6_ = bf16[160,1280]{1,0:T(8,128)(2,1)S(1)} collective-permute-done((bf16[160,1280]{1,0:T(8,128)(2,1)S(1)}, bf16[160,1280]{1,0:T(8,128)(2,1)S(1)}, u32[]{:S(2)}, u32[]{:S(2)}) %collective-permute-start.5) | collective-permute-done | bytes 409632 | tf_op jit(solution)/shard_map/ppermute | solution.py:54
  25.6 4.0 %collective-permute-start.11 = (bf16[160,1280]{1,0:T(8,128)(2,1)S(1)}, bf16[160,1280]{1,0:T(8,128)(2,1)S(1)}, u32[]{:S(2)}, u32[]{:S(2)}) collective-permute-start(bf16[160,1280]{1,0:T(8,128)(2,1)S(1)} %collective-permute-done.3.refs_6_.refs_4_), channel_id=1, source_target_pairs={{0,16},{1,17},{2,18},{3,19},{4,20},{5,21},{6,22},{7,23},{8,24},{9,... | collective-permute-start | bytes 1228808 | tf_op jit(solution)/shard_map/ppermute | solution.py:54
  30.8 3.5 %collective-permute-start.19 = (bf16[512,1280]{1,0:T(8,128)(2,1)}, bf16[512,1280]{1,0:T(8,128)(2,1)}, u32[]{:S(2)}, u32[]{:S(2)}) collective-permute-start(bf16[512,1280]{1,0:T(8,128)(2,1)} %bitcast.18.refs_2_.refs_0_), channel_id=1, source_target_pairs={{0,2},{2,4},{4,6},{6,8},{8,10},{10,12},{12,14},{14,16},{16,18},{18... | collective-permute-start | bytes 3932168 | tf_op jit(solution)/shard_map/ppermute | solution.py:424
  34.4 3.3 %collective-permute-start.12 = (bf16[160,1280]{1,0:T(8,128)(2,1)S(1)}, bf16[160,1280]{1,0:T(8,128)(2,1)}, u32[]{:S(2)}, u32[]{:S(2)}) collective-permute-start(bf16[160,1280]{1,0:T(8,128)(2,1)S(1)} %collective-permute-done.4.refs_7_.refs_5_), channel_id=1, source_target_pairs={{0,16},{1,17},{2,18},{3,19},{4,20},{5,21},{6,22},{7,23},{8,24},{9,... | collective-permute-start | bytes 1228808 | tf_op jit(solution)/shard_map/ppermute | solution.py:54
  37.7 1.3 collective-permute-start.9
  38.9 1.5 collective-permute-start.10
  40.4 1.7 %collective-permute-start.21 = (bf16[512,1280]{1,0:T(8,128)(2,1)}, bf16[512,1280]{1,0:T(8,128)(2,1)}, u32[]{:S(2)}, u32[]{:S(2)}) collective-permute-start(bf16[512,1280]{1,0:T(8,128)(2,1)} %collective-permute-done.20), channel_id=1, source_target_pairs={{46,32},{78,64},{110,96},{47,33},{79,65},{111,97}} | collective-permute-start | bytes 3932168 | tf_op jit(solution)/shard_map/ppermute | solution.py:427
  46.0 1.3 stack.50.place_ref
  49.4 1.3 collective-permute-start.16
  54.3 7.6 %collective-permute-done.19.refs_0_ = bf16[512,1280]{1,0:T(8,128)(2,1)} collective-permute-done((bf16[512,1280]{1,0:T(8,128)(2,1)}, bf16[512,1280]{1,0:T(8,128)(2,1)}, u32[]{:S(2)}, u32[]{:S(2)}) %collective-permute-start.19) | collective-permute-done | bytes 1310752 | tf_op jit(solution)/shard_map/ppermute | solution.py:424
  62.0 22.4 %edge_attention.1 = (bf16[512,1280]{1,0:T(8,128)(2,1)}, bf16[512,1280]{1,0:T(8,128)(2,1)}, f32[8,1280]{1,0:T(8,128)S(1)}) custom-call(s32[7]{0:T(128)S(1)} %stack.50.place_ref, s32[2,1280]{1,0:T(2,128)S(1)} %pad_add_fusion.ends_ref.refs_22_, bf16[512,1280]{1,0:T(8,128)(2,1)} %collective-permute-done.19.refs_0_, ...), custom_call_target="tpu_custom_call" | custom-call | flops 15000000512 | bytes 20000000 | tf_op jit(solution)/shard_map/edge_attention/pallas_call | solution.py:382
  84.4 9.9 %collective-permute-start.22 = (bf16[512,1280]{1,0:T(8,128)(2,1)}, bf16[512,1280]{1,0:T(8,128)(2,1)}, u32[]{:S(2)}, u32[]{:S(2)}) collective-permute-start(bf16[512,1280]{1,0:T(8,128)(2,1)} %get-tuple-element.128), channel_id=1, source_target_pairs={{2,0},{4,2},{6,4},{8,6},{10,8},{12,10},{14,12},{16,14},{18,16},{20... | collective-permute-start | bytes 3932168 | tf_op jit(solution)/shard_map/ppermute | solution.py:470
  94.4 19.6 %own_attention.1 = (bf16[512,1280]{1,0:T(8,128)(2,1)}, bf16[256,1280]{1,0:T(8,128)(2,1)}, bf16[16,1280]{1,0:T(8,128)(2,1)S(1)}) custom-call(s32[7]{0:T(128)S(1)} %stack.48.place_ref, s32[2,768]{1,0:T(2,128)S(1)} %fusion.9.ends_ref.refs_20_, bf16[512,1280]{1,0:T(8,128)(2,1)} %bitcast.18.refs_2_.refs_0_, f32[1,1280]{1,0:T(1,128)S(1)} %broadcast_in_dim.71.refs_3_.refs_1_, ...), custom_call_target="tpu_custom_call" | custom-call | flops 15000000512 | bytes 20000000 | tf_op jit(solution)/shard_map/own_attention/pallas_call | solution.py:382
  114.0 40.8 %conditional.1 = (f32[1,256,1280]{2,1,0:T(8,128)S(1)}) conditional(s32[]{:T(128)} %convert_element_type.58, (s32[]{:T(128)}, bf16[256,1280]{1,0:T(8,128)(2,1)}) %tuple.26, (bf16[16,1280]{1,0:T(8,128)(2,1)S(1)}, s32[1,256]{1,0:T(1,128)S(1)}, s32[]{:T(128)}, s32[]{:T(128)}, s32[1,256]{1,0:T(1,128)S(1)}, /*index=5*/pred[1,256]{1,0:T(4,128)(4,1)S(1)}, (), ...), branch_computations={%region_7.9_spmd, %region_9.10_spmd} | conditional | flops 2124808 | bytes 11489468 | solution.py:498
  114.2 36.0 %all_to_all.14 = bf16[32,16,1280]{2,1,0:T(8,128)(2,1)S(1)} all-to-all(bf16[32,16,1280]{2,1,0:T(8,128)(2,1)S(1)} %broadcast_in_dim.36), channel_id=1, replica_groups=mesh['x'=4,'co'=2,'z'=4,'yh'=2,'dp'=2] {'x','z','yh'}, dimensions={0} | all-to-all | bytes 2621440 | tf_op jit(solution)/shard_map/cond/branch_1_fun/all_to_all | solution.py:477
  151.4 2.6 %collective-permute-done.2.far_ref = bf16[512,1280]{1,0:T(8,128)(2,1)S(1)} collective-permute-done((bf16[512,1280]{1,0:T(8,128)(2,1)S(1)}, bf16[512,1280]{1,0:T(8,128)(2,1)S(1)}, u32[]{:S(2)}, u32[]{:S(2)}) %collective-permute-start.2) | collective-permute-done | bytes 1310752 | tf_op jit(solution)/shard_map/cond/branch_1_fun/ppermute | solution.py:480
  154.9 3.0 %select_bitcast_fusion = bf16[1,512,1280]{2,1,0:T(8,128)(2,1)} fusion(bf16[512,1280]{1,0:T(8,128)(2,1)S(1)} %copy-done, bf16[512,1280]{1,0:T(8,128)(2,1)} %collective-permute-done.22, pred[512]{0:T(512)(128)(4,1)S(1)} %iota_compare_fusion), kind=kLoop, calls=%fused_computation.25 | loop fusion | flops 655360 | bytes 3932672 | tf_op jit(solution)/shard_map/broadcast_in_dim | solution.py:501
  (75 shorter events, 13.1 us)
Async XLA Ops:
  0.6 41.5 %copy-start.3 = (f32[1280]{0:T(1024)S(1)}, f32[1280]{0:T(1024)}, u32[]{:S(2)}) copy-start(f32[1280]{0:T(1024)} %param.9) | copy-start | bytes 15364
  2.0 12.7 %collective-permute-start.3 = (bf16[160,1280]{1,0:T(8,128)(2,1)S(1)}, bf16[160,1280]{1,0:T(8,128)(2,1)S(1)}, u32[]{:S(2)}, u32[]{:S(2)}) collective-permute-start(bf16[160,1280]{1,0:T(8,128)(2,1)S(1)} %get-tuple-element.162), channel_id=1, source_target_pairs={{0,1},{1,2},{2,3},{3,0},{4,5},{5,6},{6,7},{7,4},{8,9},{9,10},{10,1... | collective-permute-start | bytes 1228808 | tf_op jit(solution)/shard_map/ppermute | solution.py:54
  4.2 13.2 %collective-permute-start.4 = (bf16[160,1280]{1,0:T(8,128)(2,1)S(1)}, bf16[160,1280]{1,0:T(8,128)(2,1)S(1)}, u32[]{:S(2)}, u32[]{:S(2)}) collective-permute-start(bf16[160,1280]{1,0:T(8,128)(2,1)S(1)} %get-tuple-element.161), channel_id=1, source_target_pairs={{0,3},{1,0},{2,1},{3,2},{4,7},{5,4},{6,5},{7,6},{8,11},{9,8},{10,9... | collective-permute-start | bytes 1228808 | tf_op jit(solution)/shard_map/ppermute | solution.py:54
  5.7 34.7 %collective-permute-start.20 = (bf16[512,1280]{1,0:T(8,128)(2,1)}, bf16[512,1280]{1,0:T(8,128)(2,1)}, u32[]{:S(2)}, u32[]{:S(2)}) collective-permute-start(bf16[512,1280]{1,0:T(8,128)(2,1)} %bitcast.18.refs_2_.refs_0_), channel_id=1, source_target_pairs={{30,46},{62,78},{94,110},{31,47},{63,79},{95,111}} | collective-permute-start | bytes 3932168 | tf_op jit(solution)/shard_map/ppermute | solution.py:421
  14.7 10.9 %collective-permute-start.5 = (bf16[160,1280]{1,0:T(8,128)(2,1)S(1)}, bf16[160,1280]{1,0:T(8,128)(2,1)S(1)}, u32[]{:S(2)}, u32[]{:S(2)}) collective-permute-start(bf16[160,1280]{1,0:T(8,128)(2,1)S(1)} %collective-permute-done.3.refs_6_.refs_4_), channel_id=1, source_target_pairs={{0,32},{1,33},{2,34},{3,35},{4,36},{5,37},{6,38},{7,39},{8,40},{9,... | collective-permute-start | bytes 1228808 | tf_op jit(solution)/shard_map/ppermute | solution.py:54
  17.3 2.5 %collective-permute-start.23 = (f32[8,128]{1,0:T(8,128)S(1)}, f32[8,128]{1,0:T(8,128)S(1)}, u32[]{:S(2)}, u32[]{:S(2)}) collective-permute-start(f32[8,128]{1,0:T(8,128)S(1)} %broadcast_in_dim.74), channel_id=1, source_target_pairs={{0,1},{1,0},{2,3},{3,2},{4,5},{5,4},{6,7},{7,6},{8,9},{9,8},{10,11... | collective-permute-start | bytes 12296 | tf_op jit(solution)/shard_map/ppermute | solution.py:463
  17.4 13.3 %collective-permute-start.8 = (bf16[160,1280]{1,0:T(8,128)(2,1)S(1)}, bf16[160,1280]{1,0:T(8,128)(2,1)S(1)}, u32[]{:S(2)}, u32[]{:S(2)}) collective-permute-start(bf16[160,1280]{1,0:T(8,128)(2,1)S(1)} %collective-permute-done.4.refs_7_.refs_5_), channel_id=1, source_target_pairs={{0,96},{1,97},{2,98},{3,99},{4,100},{5,101},{6,102},{7,103},{8,104... | collective-permute-start | bytes 1228808 | tf_op jit(solution)/shard_map/ppermute | solution.py:54
  19.1 15.3 %collective-permute-start.6 = (bf16[160,1280]{1,0:T(8,128)(2,1)S(1)}, bf16[160,1280]{1,0:T(8,128)(2,1)S(1)}, u32[]{:S(2)}, u32[]{:S(2)}) collective-permute-start(bf16[160,1280]{1,0:T(8,128)(2,1)S(1)} %collective-permute-done.4.refs_7_.refs_5_), channel_id=1, source_target_pairs={{0,32},{1,33},{2,34},{3,35},{4,36},{5,37},{6,38},{7,39},{8,40},{9,... | collective-permute-start | bytes 1228808 | tf_op jit(solution)/shard_map/ppermute | solution.py:54
  19.8 17.8 %collective-permute-start.7 = (bf16[160,1280]{1,0:T(8,128)(2,1)S(1)}, bf16[160,1280]{1,0:T(8,128)(2,1)S(1)}, u32[]{:S(2)}, u32[]{:S(2)}) collective-permute-start(bf16[160,1280]{1,0:T(8,128)(2,1)S(1)} %collective-permute-done.3.refs_6_.refs_4_), channel_id=1, source_target_pairs={{0,96},{1,97},{2,98},{3,99},{4,100},{5,101},{6,102},{7,103},{8,104... | collective-permute-start | bytes 1228808 | tf_op jit(solution)/shard_map/ppermute | solution.py:54
  25.6 13.3 %collective-permute-start.11 = (bf16[160,1280]{1,0:T(8,128)(2,1)S(1)}, bf16[160,1280]{1,0:T(8,128)(2,1)S(1)}, u32[]{:S(2)}, u32[]{:S(2)}) collective-permute-start(bf16[160,1280]{1,0:T(8,128)(2,1)S(1)} %collective-permute-done.3.refs_6_.refs_4_), channel_id=1, source_target_pairs={{0,16},{1,17},{2,18},{3,19},{4,20},{5,21},{6,22},{7,23},{8,24},{9,... | collective-permute-start | bytes 1228808 | tf_op jit(solution)/shard_map/ppermute | solution.py:54
  30.8 31.2 %collective-permute-start.19 = (bf16[512,1280]{1,0:T(8,128)(2,1)}, bf16[512,1280]{1,0:T(8,128)(2,1)}, u32[]{:S(2)}, u32[]{:S(2)}) collective-permute-start(bf16[512,1280]{1,0:T(8,128)(2,1)} %bitcast.18.refs_2_.refs_0_), channel_id=1, source_target_pairs={{0,2},{2,4},{4,6},{6,8},{8,10},{10,12},{12,14},{14,16},{16,18},{18... | collective-permute-start | bytes 3932168 | tf_op jit(solution)/shard_map/ppermute | solution.py:424
  34.4 13.8 %collective-permute-start.12 = (bf16[160,1280]{1,0:T(8,128)(2,1)S(1)}, bf16[160,1280]{1,0:T(8,128)(2,1)}, u32[]{:S(2)}, u32[]{:S(2)}) collective-permute-start(bf16[160,1280]{1,0:T(8,128)(2,1)S(1)} %collective-permute-done.4.refs_7_.refs_5_), channel_id=1, source_target_pairs={{0,16},{1,17},{2,18},{3,19},{4,20},{5,21},{6,22},{7,23},{8,24},{9,... | collective-permute-start | bytes 1228808 | tf_op jit(solution)/shard_map/ppermute | solution.py:54
  37.7 11.7 %collective-permute-start.9 = (bf16[160,1280]{1,0:T(8,128)(2,1)S(1)}, bf16[160,1280]{1,0:T(8,128)(2,1)S(1)}, u32[]{:S(2)}, u32[]{:S(2)}) collective-permute-start(bf16[160,1280]{1,0:T(8,128)(2,1)S(1)} %collective-permute-done.5.refs_8_.refs_6_), channel_id=1, source_target_pairs={{0,32},{1,33},{2,34},{3,35},{4,36},{5,37},{6,38},{7,39},{8,40},{9,... | collective-permute-start | bytes 1228808 | tf_op jit(solution)/shard_map/ppermute | solution.py:54
  38.9 11.8 %collective-permute-start.10 = (bf16[160,1280]{1,0:T(8,128)(2,1)S(1)}, bf16[160,1280]{1,0:T(8,128)(2,1)}, u32[]{:S(2)}, u32[]{:S(2)}) collective-permute-start(bf16[160,1280]{1,0:T(8,128)(2,1)S(1)} %collective-permute-done.8.refs_11_.refs_9_), channel_id=1, source_target_pairs={{0,96},{1,97},{2,98},{3,99},{4,100},{5,101},{6,102},{7,103},{8,104... | collective-permute-start | bytes 1228808 | tf_op jit(solution)/shard_map/ppermute | solution.py:54
  40.4 21.5 %collective-permute-start.21 = (bf16[512,1280]{1,0:T(8,128)(2,1)}, bf16[512,1280]{1,0:T(8,128)(2,1)}, u32[]{:S(2)}, u32[]{:S(2)}) collective-permute-start(bf16[512,1280]{1,0:T(8,128)(2,1)} %collective-permute-done.20), channel_id=1, source_target_pairs={{46,32},{78,64},{110,96},{47,33},{79,65},{111,97}} | collective-permute-start | bytes 3932168 | tf_op jit(solution)/shard_map/ppermute | solution.py:427
  48.1 2.8 %collective-permute-start.13 = (bf16[160,1280]{1,0:T(8,128)(2,1)S(1)}, bf16[160,1280]{1,0:T(8,128)(2,1)S(1)}, u32[]{:S(2)}, u32[]{:S(2)}) collective-permute-start(bf16[160,1280]{1,0:T(8,128)(2,1)S(1)} %collective-permute-done.5.refs_8_.refs_6_), channel_id=1, source_target_pairs={{0,16},{1,17},{2,18},{3,19},{4,20},{5,21},{6,22},{7,23},{8,24},{9,... | collective-permute-start | bytes 1228808 | tf_op jit(solution)/shard_map/ppermute | solution.py:54
  49.4 2.7 %collective-permute-start.16 = (bf16[160,1280]{1,0:T(8,128)(2,1)S(1)}, bf16[160,1280]{1,0:T(8,128)(2,1)S(1)}, u32[]{:S(2)}, u32[]{:S(2)}) collective-permute-start(bf16[160,1280]{1,0:T(8,128)(2,1)S(1)} %collective-permute-done.8.refs_11_.refs_9_), channel_id=1, source_target_pairs={{0,16},{1,17},{2,18},{3,19},{4,20},{5,21},{6,22},{7,23},{8,24},{9,... | collective-permute-start | bytes 1228808 | tf_op jit(solution)/shard_map/ppermute | solution.py:54
  50.8 2.0 %collective-permute-start.14 = (bf16[160,1280]{1,0:T(8,128)(2,1)S(1)}, bf16[160,1280]{1,0:T(8,128)(2,1)S(1)}, u32[]{:S(2)}, u32[]{:S(2)}) collective-permute-start(bf16[160,1280]{1,0:T(8,128)(2,1)S(1)} %collective-permute-done.6.refs_9_.refs_7_), channel_id=1, source_target_pairs={{0,16},{1,17},{2,18},{3,19},{4,20},{5,21},{6,22},{7,23},{8,24},{9,... | collective-permute-start | bytes 1228808 | tf_op jit(solution)/shard_map/ppermute | solution.py:54
  51.0 3.3 %collective-permute-start.15 = (bf16[160,1280]{1,0:T(8,128)(2,1)S(1)}, bf16[160,1280]{1,0:T(8,128)(2,1)}, u32[]{:S(2)}, u32[]{:S(2)}) collective-permute-start(bf16[160,1280]{1,0:T(8,128)(2,1)S(1)} %collective-permute-done.7.refs_10_.refs_8_), channel_id=1, source_target_pairs={{0,16},{1,17},{2,18},{3,19},{4,20},{5,21},{6,22},{7,23},{8,24},{9,... | collective-permute-start | bytes 1228808 | tf_op jit(solution)/shard_map/ppermute | solution.py:54
  52.1 9.8 %collective-permute-start.17 = (bf16[160,1280]{1,0:T(8,128)(2,1)S(1)}, bf16[160,1280]{1,0:T(8,128)(2,1)}, u32[]{:S(2)}, u32[]{:S(2)}) collective-permute-start(bf16[160,1280]{1,0:T(8,128)(2,1)S(1)} %collective-permute-done.9.refs_12_.refs_10_), channel_id=1, source_target_pairs={{0,16},{1,17},{2,18},{3,19},{4,20},{5,21},{6,22},{7,23},{8,24},{9,... | collective-permute-start | bytes 1228808 | tf_op jit(solution)/shard_map/ppermute | solution.py:54
  52.7 9.2 %collective-permute-start.18 = (bf16[160,1280]{1,0:T(8,128)(2,1)}, bf16[160,1280]{1,0:T(8,128)(2,1)}, u32[]{:S(2)}, u32[]{:S(2)}) collective-permute-start(bf16[160,1280]{1,0:T(8,128)(2,1)} %collective-permute-done.10.refs_13_.refs_11_), channel_id=1, source_target_pairs={{0,16},{1,17},{2,18},{3,19},{4,20},{5,21},{6,22},{7,23},{8,24},{9,... | collective-permute-start | bytes 1228808 | tf_op jit(solution)/shard_map/ppermute | solution.py:54
  84.4 70.5 %collective-permute-start.22 = (bf16[512,1280]{1,0:T(8,128)(2,1)}, bf16[512,1280]{1,0:T(8,128)(2,1)}, u32[]{:S(2)}, u32[]{:S(2)}) collective-permute-start(bf16[512,1280]{1,0:T(8,128)(2,1)} %get-tuple-element.128), channel_id=1, source_target_pairs={{2,0},{4,2},{6,4},{8,6},{10,8},{12,10},{14,12},{16,14},{18,16},{20... | collective-permute-start | bytes 3932168 | tf_op jit(solution)/shard_map/ppermute | solution.py:470
  114.0 40.9 %copy-start = (bf16[512,1280]{1,0:T(8,128)(2,1)S(1)}, bf16[512,1280]{1,0:T(8,128)(2,1)}, u32[]{:S(2)}) copy-start(bf16[512,1280]{1,0:T(8,128)(2,1)} %get-tuple-element.127) | copy-start | bytes 3932164
  150.1 3.9 %collective-permute-start.2 = (bf16[512,1280]{1,0:T(8,128)(2,1)S(1)}, bf16[512,1280]{1,0:T(8,128)(2,1)S(1)}, u32[]{:S(2)}, u32[]{:S(2)}) collective-permute-start(bf16[512,1280]{1,0:T(8,128)(2,1)S(1)} %bitcast.33), channel_id=1, source_target_pairs={{0,16},{16,0},{1,17},{17,1},{2,18},{18,2},{3,19},{19,3},{4,20},{20... | collective-permute-start | bytes 3932168 | tf_op jit(solution)/shard_map/cond/branch_1_fun/ppermute | solution.py:480
  (5 other events, 14.5 us)
